TPU v7x, 32 devices: a whole 2x2x4 slice. The times are simulated.
32 devices in a mesh: rep: 4 (over y, x), shard: 8 (over z, core).
Axes of the slice: x: 2, y: 2, z: 4, core: 2. Of those that a mesh axis runs over, the one named last changes fastest.
Arguments:
- inputs: bfloat16 [8192, 768], P(('rep', 'shard')), may hold values from -6 to 6
- cotangent: bfloat16 [8192, 768], P(('rep', 'shard')), may hold values from -6 to 6
- lengths: int32 [4, 4], P('rep'), may hold values from 1 to 1024, 2048 in all within a row
- dealing: int32 [4, 2048], P('rep', 'shard'), may hold values from 0 to 2047, each once within a row
- key_mask: int32 [4, 2048], P('rep', 'shard'), may hold values 0 or 1
- entry_weight: float32 [2, 768, 2304], P(None, 'shard'), may hold values from -0.21875 to 0.21875
- exit_weight: float32 [2, 768, 768], P(None, 'shard'), may hold values from -6 to 6
- expand_weight: float32 [2, 768, 3072], P(None, 'shard'), may hold values from -0.21875 to 0.21875
- shrink_weight: float32 [2, 3072, 768], P(None, 'shard'), may hold values from -0.109375 to 0.109375
- vectors: float32 [2, 9216], P(None, 'shard'), may hold values from -1.2 to 1.4, as said below
Outputs:
- output: bfloat16 [8192, 768], P(('rep', 'shard'))
- input_grad: float32 [8192, 768], P(('rep', 'shard'))
- entry_grad: float32 [2, 768, 2304], P(None, 'shard')
- exit_grad: float32 [2, 768, 768], P(None, 'shard')
- expand_grad: float32 [2, 768, 3072], P(None, 'shard')
- shrink_grad: float32 [2, 3072, 768], P(None, 'shard')
- vector_grad: float32 [2, 9216], P(None, 'shard')
Inputs may be any that keep to these rules, and one draw needn't show every extreme that they name: The 4 lengths of a group sum to 2048; the longest of each group is exactly 1024. `dealing`: each row is a permutation of 0 to 2047. `vectors`: the norm gains lie in 0.6 to 1.4.
All inputs are finite; a program needn't handle non-finite values. No bound on the sum of `key_mask` on one device may be relied on, other than what follows from the above.
Results may differ from a plain program's by a relative error of at most 0.04.
Values may be sent and summed in bfloat16 or wider, within the bound.
No kernel may reach another device: no remote copies, remote signals or barrier semaphores. Data moves between devices by JAX's collectives and lax.ppermute only.
A program may use at most 192 MiB of HBM per device.

v0:
```python
import jax
import jax.numpy as jnp
from jax import lax
from jax.sharding import PartitionSpec as P

HEADS = 12
HEAD_DIM = 64


NEG_FILL = -1e30


def norm_forward(resid, gain, shift):
    center = jnp.mean(resid, axis=-1, keepdims=True)
    offsets = resid - center
    spread = jnp.mean(offsets * offsets, axis=-1, keepdims=True)
    factor = lax.rsqrt(spread + 1e-05)
    normed = offsets * factor
    return (normed * gain + shift, normed, factor)


def norm_backward(incoming, normed, factor, gain):
    scaled = incoming * gain
    resid_grad = factor * (
        scaled
        - jnp.mean(scaled, axis=-1, keepdims=True)
        - normed * jnp.mean(scaled * normed, axis=-1, keepdims=True)
    )
    return (resid_grad, jnp.sum(incoming * normed, axis=0), jnp.sum(incoming, axis=0))


def inner_rows(left, right):
    return lax.dot_general(
        left, right, (((0,), (0,)), ((), ())), preferred_element_type=jnp.float32
    )


def times_trans(left, right):
    return lax.dot_general(
        left, right, (((1,), (1,)), ((), ())), preferred_element_type=jnp.float32
    )


def gelu_exact(value):
    return jax.nn.gelu(value, approximate=False)


def sequence_ids(lengths, group_rows):
    ending = jnp.cumsum(lengths)
    opening = ending - lengths
    places = jnp.arange(group_rows, dtype=jnp.int32)
    member = jnp.sum((places[:, None] >= ending[None, :]).astype(jnp.int32), axis=1)
    leading = jnp.any(places[:, None] == opening[None, :], axis=1)
    return (member, leading)


def split_vector(vector, model_width):
    pieces = [vector[index * model_width : (index + 1) * model_width] for index in range(8)]
    pieces.append(vector[8 * model_width :])
    return pieces


def fetch_forward(entry_weight, exit_weight, expand_weight, shrink_weight, vectors, layer_index):
    return (
        lax.all_gather(entry_weight[layer_index].astype(jnp.bfloat16), "shard", axis=0, tiled=True),
        lax.all_gather(exit_weight[layer_index].astype(jnp.bfloat16), "shard", axis=0, tiled=True),
        lax.all_gather(
            expand_weight[layer_index].astype(jnp.bfloat16), "shard", axis=0, tiled=True
        ),
        lax.all_gather(
            shrink_weight[layer_index].astype(jnp.bfloat16), "shard", axis=0, tiled=True
        ),
        lax.all_gather(vectors[layer_index].astype(jnp.bfloat16), "shard", axis=0, tiled=True),
    )


def fetch_backward(entry_weight, exit_weight, expand_weight, shrink_weight, vectors, layer_index):
    return (
        lax.all_gather(entry_weight[layer_index].astype(jnp.bfloat16), "shard", axis=0, tiled=True),
        lax.all_gather(exit_weight[layer_index].astype(jnp.bfloat16), "shard", axis=0, tiled=True),
        lax.all_gather(
            expand_weight[layer_index].astype(jnp.bfloat16), "shard", axis=0, tiled=True
        ),
        lax.all_gather(
            shrink_weight[layer_index].astype(jnp.bfloat16), "shard", axis=0, tiled=True
        ),
        lax.all_gather(vectors[layer_index].astype(jnp.bfloat16), "shard", axis=0, tiled=True),
    )


def attend_forward(queries, keys, values, own_member, member, usable):
    local_rows = queries.shape[0]
    query_heads = queries.reshape(local_rows, HEADS, HEAD_DIM)
    factor_scale = HEAD_DIM ** (-0.5)
    start_state = (
        jnp.full((HEADS, local_rows), NEG_FILL, jnp.float32),
        jnp.zeros((HEADS, local_rows), jnp.float32),
        jnp.zeros((HEADS, local_rows, HEAD_DIM), jnp.float32),
    )
    key_piece = lax.all_gather(keys, "shard", axis=0, tiled=True)
    value_piece = lax.all_gather(values, "shard", axis=0, tiled=True)
    amount = key_piece.shape[0]
    block_rows = local_rows * max(1, 512 // local_rows)

    def fold_advance(block_index, running):
        running_max, running_total, weighted = running
        begin = block_index * block_rows
        key_block = lax.dynamic_slice_in_dim(key_piece, begin, block_rows, 0).reshape(
            block_rows, HEADS, HEAD_DIM
        )
        value_block = lax.dynamic_slice_in_dim(value_piece, begin, block_rows, 0).reshape(
            block_rows, HEADS, HEAD_DIM
        )
        key_member = lax.dynamic_slice_in_dim(member, begin, block_rows, 0)
        key_usable = lax.dynamic_slice_in_dim(usable, begin, block_rows, 0)
        allowed = ((own_member[:, None] == key_member[None, :]) & key_usable[None, :])[None]
        scores = (
            jnp.einsum("qhd,khd->hqk", query_heads, key_block, preferred_element_type=jnp.float32)
            * factor_scale
        )
        scores = jnp.where(allowed, scores, NEG_FILL)
        new_max = jnp.maximum(running_max, jnp.max(scores, axis=2))
        expos = jnp.where(allowed, jnp.exp(scores - new_max[:, :, None]), 0.0)
        shrink_by = jnp.exp(running_max - new_max)
        new_total = running_total * shrink_by + jnp.sum(expos, axis=2)
        new_weighted = weighted * shrink_by[:, :, None] + jnp.einsum(
            "hqk,khd->hqd",
            expos.astype(jnp.bfloat16),
            value_block,
            preferred_element_type=jnp.float32,
        )
        return (new_max, new_total, new_weighted)

    running_max, running_total, weighted = lax.fori_loop(
        0, amount // block_rows, fold_advance, start_state
    )
    attended = jnp.transpose(weighted / running_total[:, :, None], (1, 0, 2)).reshape(
        local_rows, HEADS * HEAD_DIM
    )
    return (attended, running_max + jnp.log(running_total))


def attend_backward(
    queries, attended_grad, log_total, deltas, keys_all, values_all, own_member, member, usable
):
    local_rows = queries.shape[0]
    group_rows = keys_all.shape[0]
    model_width = HEADS * HEAD_DIM
    factor_scale = HEAD_DIM ** (-0.5)
    query_heads = queries.reshape(local_rows, HEADS, HEAD_DIM)
    grad_heads = attended_grad.reshape(local_rows, HEADS, HEAD_DIM)
    block_rows = min(512, group_rows)

    def attend_advance(query_sum, block_index):
        begin = block_index * block_rows
        key_block = lax.dynamic_slice_in_dim(keys_all, begin, block_rows, 0).reshape(
            block_rows, HEADS, HEAD_DIM
        )
        value_block = lax.dynamic_slice_in_dim(values_all, begin, block_rows, 0).reshape(
            block_rows, HEADS, HEAD_DIM
        )
        key_member = lax.dynamic_slice_in_dim(member, begin, block_rows, 0)
        key_usable = lax.dynamic_slice_in_dim(usable, begin, block_rows, 0)
        allowed = ((own_member[:, None] == key_member[None, :]) & key_usable[None, :])[None]
        scores = (
            jnp.einsum("qhd,khd->hqk", query_heads, key_block, preferred_element_type=jnp.float32)
            * factor_scale
        )
        probs = jnp.where(allowed, jnp.exp(scores - log_total[:, :, None]), 0.0)
        prob_grad = jnp.einsum(
            "qhd,khd->hqk", grad_heads, value_block, preferred_element_type=jnp.float32
        )
        score_grad = (probs * (prob_grad - deltas[:, :, None])).astype(jnp.bfloat16)
        query_sum = (
            query_sum
            + jnp.einsum("hqk,khd->qhd", score_grad, key_block, preferred_element_type=jnp.float32)
            * factor_scale
        )
        key_grad = (
            jnp.einsum("hqk,qhd->khd", score_grad, query_heads, preferred_element_type=jnp.float32)
            * factor_scale
        )
        value_grad = jnp.einsum(
            "hqk,qhd->khd",
            probs.astype(jnp.bfloat16),
            grad_heads,
            preferred_element_type=jnp.float32,
        )
        joined = jnp.concatenate(
            [
                key_grad.reshape(block_rows, model_width),
                value_grad.reshape(block_rows, model_width),
            ],
            axis=1,
        )
        return (query_sum, joined)

    query_sum, key_value = lax.scan(
        attend_advance,
        jnp.zeros((local_rows, HEADS, HEAD_DIM), jnp.float32),
        jnp.arange(group_rows // block_rows, dtype=jnp.int32),
    )
    key_value = key_value.reshape(group_rows, 2 * model_width)
    return (query_sum.reshape(local_rows, model_width), key_value)


def layer_forward(hidden, weights, own_member, member, usable):
    entry, leaving, expand, shrink, vector = weights
    model_width = leaving.shape[0]
    pieces = split_vector(vector.astype(jnp.float32), model_width)
    flat = hidden.astype(jnp.bfloat16)
    mixed = jnp.dot(flat, entry, preferred_element_type=jnp.float32)
    queries = (mixed[:, 0:model_width] + pieces[0]).astype(jnp.bfloat16)
    keys = mixed[:, model_width : 2 * model_width].astype(jnp.bfloat16)
    values = (mixed[:, 2 * model_width : 3 * model_width] + pieces[1]).astype(jnp.bfloat16)
    attended, log_total = attend_forward(queries, keys, values, own_member, member, usable)
    attended_low = attended.astype(jnp.bfloat16)
    branch = jnp.dot(attended_low, leaving, preferred_element_type=jnp.float32) + pieces[2]
    middle, normed_one, factor_one = norm_forward(hidden + branch, pieces[3], pieces[4])
    middle_low = middle.astype(jnp.bfloat16)
    inner = jnp.dot(middle_low, expand, preferred_element_type=jnp.float32) + pieces[8]
    active = gelu_exact(inner).astype(jnp.bfloat16)
    branch_two = jnp.dot(active, shrink, preferred_element_type=jnp.float32) + pieces[5]
    result, normed_two, factor_two = norm_forward(middle + branch_two, pieces[6], pieces[7])
    record = (
        flat,
        queries,
        keys,
        values,
        attended,
        log_total,
        attended_low,
        normed_one,
        factor_one,
        middle_low,
        inner,
        active,
        normed_two,
        factor_two,
    )
    return (result, record)


def layer_backward(upstream, weights, record, keys_all, values_all, own_member, member, usable):
    entry, leaving, expand, shrink, vector = weights
    model_width = leaving.shape[0]
    pieces = split_vector(vector.astype(jnp.float32), model_width)
    (
        flat,
        queries,
        keys,
        values,
        attended,
        log_total,
        attended_low,
        normed_one,
        factor_one,
        middle_low,
        inner,
        active,
        normed_two,
        factor_two,
    ) = record
    local_rows = queries.shape[0]
    resid_two, gain_two_grad, shift_two_grad = norm_backward(
        upstream, normed_two, factor_two, pieces[6]
    )
    branch_two_grad = resid_two.astype(jnp.bfloat16)
    bias_down_grad = jnp.sum(branch_two_grad.astype(jnp.float32), axis=0)
    shrink_grad = inner_rows(active, branch_two_grad)
    active_grad = times_trans(branch_two_grad, shrink)
    unused_value, gelu_pull = jax.vjp(gelu_exact, inner)
    inner_grad = gelu_pull(active_grad)[0].astype(jnp.bfloat16)
    bias_up_grad = jnp.sum(inner_grad.astype(jnp.float32), axis=0)
    expand_grad = inner_rows(middle_low, inner_grad)
    middle_grad = resid_two + times_trans(inner_grad, expand)
    resid_one, gain_one_grad, shift_one_grad = norm_backward(
        middle_grad, normed_one, factor_one, pieces[3]
    )
    branch_grad = resid_one.astype(jnp.bfloat16)
    bias_out_grad = jnp.sum(branch_grad.astype(jnp.float32), axis=0)
    exit_grad = inner_rows(attended_low, branch_grad)
    attended_grad = times_trans(branch_grad, leaving).astype(jnp.bfloat16)
    deltas = jnp.sum(
        (attended_grad.astype(jnp.float32) * attended).reshape(local_rows, HEADS, HEAD_DIM), axis=2
    ).T
    query_grad, key_value_grad = attend_backward(
        queries, attended_grad, log_total, deltas, keys_all, values_all, own_member, member, usable
    )
    own_key_value = lax.psum_scatter(
        key_value_grad.astype(jnp.bfloat16), "shard", scatter_dimension=0, tiled=True
    ).astype(jnp.float32)
    mixed_grad = jnp.concatenate([query_grad, own_key_value], axis=1).astype(jnp.bfloat16)
    bias_query_grad = jnp.sum(mixed_grad[:, 0:model_width].astype(jnp.float32), axis=0)
    bias_value_grad = jnp.sum(
        mixed_grad[:, 2 * model_width : 3 * model_width].astype(jnp.float32), axis=0
    )
    entry_grad = inner_rows(flat, mixed_grad)
    hidden_grad = resid_one + times_trans(mixed_grad, entry)
    vector_grad = jnp.concatenate(
        [
            bias_query_grad,
            bias_value_grad,
            bias_out_grad,
            gain_one_grad,
            shift_one_grad,
            bias_down_grad,
            gain_two_grad,
            shift_two_grad,
            bias_up_grad,
        ]
    )
    return (hidden_grad, (entry_grad, exit_grad, expand_grad, shrink_grad, vector_grad))


def body(
    inputs,
    cotangent,
    lengths,
    dealing,
    key_mask,
    entry_weight,
    exit_weight,
    expand_weight,
    shrink_weight,
    vectors,
):
    local_rows = inputs.shape[0]
    group_rows = local_rows * lax.axis_size("shard")
    position = lax.axis_index("shard") * local_rows
    dealt_all, mask_all = (
        lax.all_gather(dealing, "shard", axis=1, tiled=True),
        lax.all_gather(key_mask, "shard", axis=1, tiled=True),
    )
    member, leading = sequence_ids(lengths[0], group_rows)
    usable = (mask_all[0] == 1) | leading
    own_member = lax.dynamic_slice_in_dim(member, position, local_rows, 0)
    inverse = (
        jnp.zeros((group_rows,), jnp.int32)
        .at[dealt_all[0]]
        .set(jnp.arange(group_rows, dtype=jnp.int32))
    )
    own_inverse = lax.dynamic_slice_in_dim(inverse, position, local_rows, 0)
    inputs_all, cotangent_all = (
        lax.all_gather(inputs, "shard", axis=0, tiled=True),
        lax.all_gather(cotangent, "shard", axis=0, tiled=True),
    )
    hidden = jnp.take(inputs_all, dealing[0], axis=0).astype(jnp.float32)
    upstream = jnp.take(cotangent_all, dealing[0], axis=0).astype(jnp.float32)
    layers = entry_weight.shape[0]
    saved = []
    kept = []
    for layer_index in range(layers):
        weights = fetch_forward(
            entry_weight, exit_weight, expand_weight, shrink_weight, vectors, layer_index
        )
        kept.append(weights)
        hidden, record = layer_forward(hidden, weights, own_member, member, usable)
        saved.append(record)
    output_all = lax.all_gather(hidden.astype(jnp.bfloat16), "shard", axis=0, tiled=True)
    output = jnp.take(output_all, own_inverse, axis=0)
    hidden_grad = upstream
    layer_grads = [None] * layers
    for layer_index in reversed(range(layers)):
        weights = fetch_backward(
            entry_weight, exit_weight, expand_weight, shrink_weight, vectors, layer_index
        )
        record = saved[layer_index]
        keys_all, values_all = (
            lax.all_gather(record[2], "shard", axis=0, tiled=True),
            lax.all_gather(record[3], "shard", axis=0, tiled=True),
        )
        hidden_grad, local_grads = layer_backward(
            hidden_grad, weights, record, keys_all, values_all, own_member, member, usable
        )
        entry_local, exit_local, expand_local, shrink_local, vector_local = local_grads
        entry_part, exit_part, expand_part, shrink_part, vector_part = (
            lax.psum_scatter(
                entry_local.astype(jnp.bfloat16), "shard", scatter_dimension=0, tiled=True
            ).astype(jnp.float32),
            lax.psum_scatter(
                exit_local.astype(jnp.bfloat16), "shard", scatter_dimension=0, tiled=True
            ).astype(jnp.float32),
            lax.psum_scatter(
                expand_local.astype(jnp.bfloat16), "shard", scatter_dimension=0, tiled=True
            ).astype(jnp.float32),
            lax.psum_scatter(
                shrink_local.astype(jnp.bfloat16), "shard", scatter_dimension=0, tiled=True
            ).astype(jnp.float32),
            lax.psum_scatter(
                vector_local.astype(jnp.bfloat16), "shard", scatter_dimension=0, tiled=True
            ).astype(jnp.float32),
        )
        entry_part, exit_part, expand_part, shrink_part, vector_part = (
            lax.psum(entry_part.astype(jnp.bfloat16), "rep").astype(jnp.float32),
            lax.psum(exit_part.astype(jnp.bfloat16), "rep").astype(jnp.float32),
            lax.psum(expand_part.astype(jnp.bfloat16), "rep").astype(jnp.float32),
            lax.psum(shrink_part.astype(jnp.bfloat16), "rep").astype(jnp.float32),
            lax.psum(vector_part.astype(jnp.bfloat16), "rep").astype(jnp.float32),
        )
        layer_grads[layer_index] = (entry_part, exit_part, expand_part, shrink_part, vector_part)
    entry_grad = jnp.stack([item[0] for item in layer_grads])
    exit_grad = jnp.stack([item[1] for item in layer_grads])
    expand_grad = jnp.stack([item[2] for item in layer_grads])
    shrink_grad = jnp.stack([item[3] for item in layer_grads])
    vector_grad = jnp.stack([item[4] for item in layer_grads])
    grads_all = lax.all_gather(
        hidden_grad.astype(jnp.bfloat16), "shard", axis=0, tiled=True
    ).astype(hidden_grad.dtype)
    input_grad = jnp.take(grads_all, own_inverse, axis=0)
    return (output, input_grad, entry_grad, exit_grad, expand_grad, shrink_grad, vector_grad)


def solution(mesh):
    placed = (
        P(("rep", "shard"), None),
        P(("rep", "shard"), None),
        P("rep", None),
        P("rep", "shard"),
        P("rep", "shard"),
        P(None, "shard", None),
        P(None, "shard", None),
        P(None, "shard", None),
        P(None, "shard", None),
        P(None, "shard"),
    )
    return jax.shard_map(
        body,
        mesh=mesh,
        in_specs=placed,
        out_specs=(
            P(("rep", "shard"), None),
            P(("rep", "shard"), None),
            P(None, "shard", None),
            P(None, "shard", None),
            P(None, "shard", None),
            P(None, "shard", None),
            P(None, "shard"),
        ),
        check_vma=False,
    )
```

profile of v0, /device:TPU:0, one launch (start us, length us, event | category | flops | bytes accessed | tf_op | source)
XLA Modules:
  0.0 1475.5 jit_solution(13386083691091691730)
XLA Ops:
  10.6 40.0 %all-gather.27.cloned.1.call-done = bf16[2048,768]{1,0:T(8,128)(2,1)} async-done(((bf16[256,768]{1,0:T(8,128)(2,1)}), bf16[2048,768]{1,0:T(8,128)(2,1)}) %all-gather.27.cloned.1.call-update) | async-done | bytes 3145744 | tf_op jit(solution)/shard_map/all_gather | solution.py:345
  54.3 38.9 %all-gather.43.cloned.1.call-done = bf16[1,768,2304]{2,1,0:T(8,128)(2,1)} async-done(((bf16[1,96,2304]{2,1,0:T(8,128)(2,1)}), bf16[1,768,2304]{2,1,0:T(8,128)(2,1)}) %all-gather.43.cloned.1.call-update) | async-done | bytes 3538960 | tf_op jit(solution)/shard_map/all_gather | solution.py:65
  97.2 14.1 all-gather.1
  120.7 10.4 all_gather.75
  134.5 4.7 copy.136
  139.2 34.5 %all-gather.31.cloned.1.call-done = bf16[2048,768]{1,0:T(8,128)(2,1)} async-done(((bf16[256,768]{1,0:T(8,128)(2,1)}), bf16[2048,768]{1,0:T(8,128)(2,1)}) %all-gather.31.cloned.1.call-update) | async-done | bytes 3145744 | tf_op jit(solution)/shard_map/all_gather | solution.py:101
  173.7 4.7 copy.137
  178.4 51.5 %while.62 = (s32[]{:T(128)}, f32[12,256]{1,0:T(8,128)S(1)}, f32[12,256]{1,0:T(8,128)S(1)}, f32[12,256,64]{1,2,0:T(8,128)S(1)}, s32[256]{0:T(256)S(1)}, /*index=5...) while((s32[]{:T(128)}, f32[12,256]{1,0:T(8,128)S(1)}, ...), condition=%wide.region_6.8_spmd.clone, body=%wide.region_3.7_spmd.clone.sunk | while | flops 423967744 | bytes 51454700 | solution.py:134
  223.4 4.5 fusion.269
  234.5 16.0 %all-gather.47.cloned.1.call-done = bf16[1,768,3072]{2,1,0:T(8,128)(2,1)} async-done(((bf16[1,96,3072]{2,1,0:T(8,128)(2,1)}), bf16[1,768,3072]{2,1,0:T(8,128)(2,1)}) %all-gather.47.cloned.1.call-update) | async-done | bytes 4718608 | tf_op jit(solution)/shard_map/all_gather | solution.py:67
  250.4 11.9 multiply_convert_fusion.1
  262.4 39.7 %all-gather.49.cloned.1.call-done = bf16[1,3072,768]{2,1,0:T(8,128)(2,1)} async-done(((bf16[1,384,768]{2,1,0:T(8,128)(2,1)}), bf16[1,3072,768]{2,1,0:T(8,128)(2,1)}) %all-gather.49.cloned.1.call-update) | async-done | bytes 4718608 | tf_op jit(solution)/shard_map/all_gather | solution.py:70
  306.7 37.3 %all-gather.51.cloned.1.call-done = bf16[1,768,2304]{2,1,0:T(8,128)(2,1)} async-done(((bf16[1,96,2304]{2,1,0:T(8,128)(2,1)}), bf16[1,768,2304]{2,1,0:T(8,128)(2,1)}) %all-gather.51.cloned.1.call-update) | async-done | bytes 3538960 | tf_op jit(solution)/shard_map/all_gather | solution.py:65
  348.0 14.4 all-gather.6
  366.2 16.6 %all-gather.39.cloned.1.call-done = bf16[2048,768]{1,0:T(8,128)(2,1)} async-done(((bf16[256,768]{1,0:T(8,128)(2,1)}), bf16[2048,768]{1,0:T(8,128)(2,1)}) %all-gather.39.cloned.1.call-update) | async-done | bytes 3145744 | tf_op jit(solution)/shard_map/all_gather | solution.py:346
  386.7 35.4 %all-gather.33.cloned.1.call-done = bf16[2048,768]{1,0:T(8,128)(2,1)} async-done(((bf16[256,768]{1,0:T(8,128)(2,1)}), bf16[2048,768]{1,0:T(8,128)(2,1)}) %all-gather.33.cloned.1.call-update) | async-done | bytes 3145744 | tf_op jit(solution)/shard_map/all_gather | solution.py:100
  422.1 4.7 copy.139
  426.8 34.7 %all-gather.35.cloned.1.call-done = bf16[2048,768]{1,0:T(8,128)(2,1)} async-done(((bf16[256,768]{1,0:T(8,128)(2,1)}), bf16[2048,768]{1,0:T(8,128)(2,1)}) %all-gather.35.cloned.1.call-update) | async-done | bytes 3145744 | tf_op jit(solution)/shard_map/all_gather | solution.py:101
  461.5 4.7 copy.140
  466.2 58.1 %while.63 = (s32[]{:T(128)}, f32[12,256]{1,0:T(8,128)S(1)}, f32[12,256]{1,0:T(8,128)S(1)}, f32[12,256,64]{1,2,0:T(8,128)}, s32[256]{0:T(256)S(1)}, /*index=5*/s3...) while((s32[]{:T(128)}, f32[12,256]{1,0:T(8,128)S(1)}, ...), condition=%wide.region_14.16_spmd.clone, body=%wide.region_11.15_spmd.clone.sunk | while | flops 423967744 | bytes 51454700 | solution.py:134
  472.6 4.4 fusion.277
  501.0 4.5 fusion.277
  529.0 8.8 all-gather.55.cloned.1.call-done
  537.8 11.7 multiply_convert_fusion
  549.5 40.3 %all-gather.57.cloned.1.call-done = bf16[1,3072,768]{2,1,0:T(8,128)(2,1)} async-done(((bf16[1,384,768]{2,1,0:T(8,128)(2,1)}), bf16[1,3072,768]{2,1,0:T(8,128)(2,1)}) %all-gather.57.cloned.1.call-update) | async-done | bytes 4718608 | tf_op jit(solution)/shard_map/all_gather | solution.py:70
  589.9 4.4 fusion.183
  609.5 69.5 %while.64 = (s32[]{:T(128)}, f32[256,12,64]{0,2,1:T(8,128)}, bf16[4,512,1536]{2,1,0:T(8,128)(2,1)}, s32[4]{0:T(128)S(1)}, bf16[2048,768]{0,1:T(8,128)(2,1)}, /*i...) while((s32[]{:T(128)}, f32[256,12,64]{0,2,1:T(8,128)}, ...), condition=%wide.region_26.28_spmd.clone, body=%wide.region_25.27_spmd.clone.sunk | while | flops 1027145728 | bytes 81065128 | solution.py:198
  682.8 64.8 %reduce-scatter.11.cloned.1.call-done = bf16[256,1536]{1,0:T(8,128)(2,1)} async-done(((bf16[2048,1536]{1,0:T(8,128)(2,1)}), bf16[256,1536]{1,0:T(8,128)(2,1)}) %reduce-scatter.11.cloned.1.call-update) | async-done | bytes 786448 | tf_op jit(solution)/shard_map/reduce_scatter | solution.py:290
  752.9 5.3 fusion.185
  767.9 69.8 %while.65 = (s32[]{:T(128)}, f32[256,12,64]{0,2,1:T(8,128)}, bf16[4,512,1536]{2,1,0:T(8,128)(2,1)}, s32[4]{0:T(128)S(1)}, bf16[2048,768]{0,1:T(8,128)(2,1)}, /*i...) while((s32[]{:T(128)}, f32[256,12,64]{0,2,1:T(8,128)}, ...), condition=%wide.region_34.36_spmd.clone, body=%wide.region_33.35_spmd.clone.sunk | while | flops 1027145728 | bytes 81065128 | solution.py:198
  840.6 5.2 convolution_convert_fusion.2
  858.2 5.1 convolution_convert_fusion.3
  870.1 36.0 %reduce-scatter.13.cloned.1.call-done = bf16[256,1536]{1,0:T(8,128)(2,1)} async-done(((bf16[2048,1536]{1,0:T(8,128)(2,1)}), bf16[256,1536]{1,0:T(8,128)(2,1)}) %reduce-scatter.13.cloned.1.call-update) | async-done | bytes 786448 | tf_op jit(solution)/shard_map/reduce_scatter | solution.py:290
  915.3 24.2 %reduce-scatter.21.cloned.1.call-done = bf16[96,768]{1,0:T(8,128)(2,1)} async-done(((bf16[768,768]{1,0:T(8,128)(2,1)}), bf16[96,768]{1,0:T(8,128)(2,1)}) %reduce-scatter.21.cloned.1.call-update) | async-done | bytes 147472 | tf_op jit(solution)/shard_map/reduce_scatter | solution.py:381
  939.5 55.3 %reduce-scatter.25.cloned.1.call-done = bf16[96,3072]{1,0:T(8,128)(2,1)} async-done(((bf16[768,3072]{1,0:T(8,128)(2,1)}), bf16[96,3072]{1,0:T(8,128)(2,1)}) %reduce-scatter.25.cloned.1.call-update) | async-done | bytes 589840 | tf_op jit(solution)/shard_map/reduce_scatter | solution.py:384
  994.9 55.7 %reduce-scatter.29.cloned.1.call-done = bf16[384,768]{1,0:T(8,128)(2,1)} async-done(((bf16[3072,768]{1,0:T(8,128)(2,1)}), bf16[384,768]{1,0:T(8,128)(2,1)}) %reduce-scatter.29.cloned.1.call-update) | async-done | bytes 589840 | tf_op jit(solution)/shard_map/reduce_scatter | solution.py:387
  1050.5 34.2 %reduce-scatter.19.cloned.1.call-done = bf16[96,768]{1,0:T(8,128)(2,1)} async-done(((bf16[768,768]{1,0:T(8,128)(2,1)}), bf16[96,768]{1,0:T(8,128)(2,1)}) %reduce-scatter.19.cloned.1.call-update) | async-done | bytes 147472 | tf_op jit(solution)/shard_map/reduce_scatter | solution.py:381
  1084.8 44.3 %reduce-scatter.17.cloned.1.call-done = bf16[96,2304]{1,0:T(8,128)(2,1)} async-done(((bf16[768,2304]{1,0:T(8,128)(2,1)}), bf16[96,2304]{1,0:T(8,128)(2,1)}) %reduce-scatter.17.cloned.1.call-update) | async-done | bytes 442384 | tf_op jit(solution)/shard_map/reduce_scatter | solution.py:378
  1129.0 55.7 %reduce-scatter.23.cloned.1.call-done = bf16[96,3072]{1,0:T(8,128)(2,1)} async-done(((bf16[768,3072]{1,0:T(8,128)(2,1)}), bf16[96,3072]{1,0:T(8,128)(2,1)}) %reduce-scatter.23.cloned.1.call-update) | async-done | bytes 589840 | tf_op jit(solution)/shard_map/reduce_scatter | solution.py:384
  1184.8 55.7 %reduce-scatter.27.cloned.1.call-done = bf16[384,768]{1,0:T(8,128)(2,1)} async-done(((bf16[3072,768]{1,0:T(8,128)(2,1)}), bf16[384,768]{1,0:T(8,128)(2,1)}) %reduce-scatter.27.cloned.1.call-update) | async-done | bytes 589840 | tf_op jit(solution)/shard_map/reduce_scatter | solution.py:387
  1240.5 44.4 %reduce-scatter.15.cloned.1.call-done = bf16[96,2304]{1,0:T(8,128)(2,1)} async-done(((bf16[768,2304]{1,0:T(8,128)(2,1)}), bf16[96,2304]{1,0:T(8,128)(2,1)}) %reduce-scatter.15.cloned.1.call-update) | async-done | bytes 442384 | tf_op jit(solution)/shard_map/reduce_scatter | solution.py:378
  1285.1 9.2 all_gather.91
  1294.3 8.3 scatter_custom_fusion
  1304.2 19.7 %all-gather.37.cloned.1.call-done = bf16[2048,768]{1,0:T(8,128)(2,1)} async-done(((bf16[256,768]{1,0:T(8,128)(2,1)}), bf16[2048,768]{1,0:T(8,128)(2,1)}) %all-gather.37.cloned.1.call-update) | async-done | bytes 3145744 | tf_op jit(solution)/shard_map/all_gather | solution.py:360
  1331.9 30.2 %all-reduce.2 = (bf16[9216]{0:T(1024)(128)(2,1)S(1)}, bf16[9216]{0:T(1024)(128)(2,1)S(1)}) all-reduce(bf16[9216]{0:T(1024)(128)(2,1)S(1)} %constant_dynamic-update-slice_fusion.3, bf16[9216]{0:T(1024)(128)(2,1)S(1)} %constant_dynamic-update-slice_fusion.2), channel_id=23, replica_groups=mesh['rep'=4,'shard'=8] {'shard'}, use_global_device_ids=true, to_apply=%region_72.74.clone | all-reduce | flops 18432 | bytes 73728
  1362.3 9.9 all-reduce.3
  1372.8 5.4 convert_element_type.312
  1383.4 77.4 %all-reduce.7.cloned.1.call-done = (bf16[1,96,2304]{2,1,0:T(8,128)(2,1)}, bf16[1,96,2304]{2,1,0:T(8,128)(2,1)}, bf16[1,96,768]{2,1,0:T(8,128)(2,1)}, bf16[1,96,7...) async-done(((bf16[1,96,2304]{2,1,0:T(8,128)(2,1)}, ...) | async-done | bytes 3538960 | tf_op jit(solution)/shard_map/psum | solution.py:395
  (820 shorter events, 363.8 us)
Async XLA Ops:
  7.2 43.4 %all-gather.27.cloned.1.call-start = ((), (), s32[]{:S(2)}) async-start(), calls=%async_computation.10 | async-start | bytes 3538944 | tf_op jit(solution)/shard_map/all_gather | solution.py:345
  7.9 85.3 %all-gather.43.cloned.1.call-start = ((), (), s32[]{:S(2)}) async-start(), calls=%async_computation.28 | async-start | bytes 3981312 | tf_op jit(solution)/shard_map/all_gather | solution.py:65
  10.5 124.0 %all-gather.29.cloned.1.call-start = ((), (), s32[]{:S(2)}) async-start(), calls=%async_computation.11 | async-start | bytes 3538944 | tf_op jit(solution)/shard_map/all_gather | solution.py:100
  10.6 221.5 %copy-start.92 = (pred[256]{0:T(512)(128)(4,1)}, pred[256]{0:T(512)(128)(4,1)S(1)}, u32[]{:S(2)}) copy-start(pred[256]{0:T(512)(128)(4,1)S(1)} %compare_and_fusion.5) | copy-start | bytes 772
  54.3 177.8 %copy-start.23 = (bf16[256,768]{1,0:T(8,128)(2,1)}, bf16[256,768]{1,0:T(8,128)(2,1)S(1)}, u32[]{:S(2)}) copy-start(bf16[256,768]{1,0:T(8,128)(2,1)S(1)} %gather_fusion.1) | copy-start | bytes 1179652
  97.1 76.6 %all-gather.31.cloned.1.call-start = ((), (), s32[]{:S(2)}) async-start(), calls=%async_computation.12 | async-start | bytes 3538944 | tf_op jit(solution)/shard_map/all_gather | solution.py:101
  111.5 190.6 %copy-start.69 = (f32[768]{0:T(1024)}, f32[768]{0:T(1024)S(1)}, u32[]{:S(2)}) copy-start(f32[768]{0:T(1024)S(1)} %get-tuple-element.902) | copy-start | bytes 9220
  111.5 190.6 %copy-start.74 = (f32[768]{0:T(1024)}, f32[768]{0:T(1024)S(1)}, u32[]{:S(2)}) copy-start(f32[768]{0:T(1024)S(1)} %get-tuple-element.901) | copy-start | bytes 9220
  111.5 232.5 %copy-start.66 = (f32[768]{0:T(1024)}, f32[768]{0:T(1024)S(1)}, u32[]{:S(2)}) copy-start(f32[768]{0:T(1024)S(1)} %get-tuple-element.906) | copy-start | bytes 9220
  112.4 119.7 %all-gather.45.cloned.1.call-start = ((), (), s32[]{:S(2)}) async-start(), calls=%async_computation.29 | async-start | bytes 1327104 | tf_op jit(solution)/shard_map/all_gather | solution.py:66
  114.3 136.1 %all-gather.47.cloned.1.call-start = ((), (), s32[]{:S(2)}) async-start(), calls=%async_computation.30 | async-start | bytes 5308416 | tf_op jit(solution)/shard_map/all_gather | solution.py:67
  117.5 184.5 %all-gather.49.cloned.1.call-start = ((), (), s32[]{:S(2)}) async-start(), calls=%async_computation.31 | async-start | bytes 5308416 | tf_op jit(solution)/shard_map/all_gather | solution.py:70
  118.8 225.1 %all-gather.51.cloned.1.call-start = ((), (), s32[]{:S(2)}) async-start(), calls=%async_computation.32 | async-start | bytes 3981312 | tf_op jit(solution)/shard_map/all_gather | solution.py:65
  119.6 263.3 %all-gather.39.cloned.1.call-start = ((), (), s32[]{:S(2)}) async-start(), calls=%async_computation.16 | async-start | bytes 3538944 | tf_op jit(solution)/shard_map/all_gather | solution.py:346
  120.3 301.8 %all-gather.33.cloned.1.call-start = ((), (), s32[]{:S(2)}) async-start(), calls=%async_computation.13 | async-start | bytes 3538944 | tf_op jit(solution)/shard_map/all_gather | solution.py:100
  234.2 67.9 %copy-start.13 = (f32[256,768]{1,0:T(8,128)}, f32[256,768]{1,0:T(8,128)S(1)}, u32[]{:S(2)}) copy-start(f32[256,768]{1,0:T(8,128)S(1)} %get-tuple-element.1062) | copy-start | bytes 2359300
  234.2 67.9 %copy-start.87 = (f32[256]{0:T(256)}, f32[256]{0:T(256)S(1)}, u32[]{:S(2)}) copy-start(f32[256]{0:T(256)S(1)} %broadcast_multiply_fusion.11) | copy-start | bytes 3076
  234.5 67.6 %copy-start.104 = (f32[256]{0:T(256)}, f32[256]{0:T(256)S(1)}, u32[]{:S(2)}) copy-start(f32[256]{0:T(256)S(1)} %add_rsqrt_fusion.3) | copy-start | bytes 3076
  306.4 220.4 %copy-start.10 = (f32[256,768]{1,0:T(8,128)}, f32[256,768]{1,0:T(8,128)S(1)}, u32[]{:S(2)}) copy-start(f32[256,768]{1,0:T(8,128)S(1)} %get-tuple-element.1065) | copy-start | bytes 2359300
  348.0 113.5 %all-gather.35.cloned.1.call-start = ((), (), s32[]{:S(2)}) async-start(), calls=%async_computation.14 | async-start | bytes 3538944 | tf_op jit(solution)/shard_map/all_gather | solution.py:101
  364.2 162.6 %all-gather.53.cloned.1.call-start = ((), (), s32[]{:S(2)}) async-start(), calls=%async_computation.33 | async-start | bytes 1327104 | tf_op jit(solution)/shard_map/all_gather | solution.py:66
  364.8 173.0 %all-gather.55.cloned.1.call-start = ((), (), s32[]{:S(2)}) async-start(), calls=%async_computation.34 | async-start | bytes 5308416 | tf_op jit(solution)/shard_map/all_gather | solution.py:67
  365.5 224.3 %all-gather.57.cloned.1.call-start = ((), (), s32[]{:S(2)}) async-start(), calls=%async_computation.35 | async-start | bytes 5308416 | tf_op jit(solution)/shard_map/all_gather | solution.py:70
  366.1 381.5 %reduce-scatter.11.cloned.1.call-start = ((), (), s32[]{:S(2)}) async-start(), calls=%async_computation.17 | async-start | bytes 7077888 | tf_op jit(solution)/shard_map/reduce_scatter | solution.py:290
  528.7 74.3 %copy-start.16 = (f32[256,768]{1,0:T(8,128)}, f32[256,768]{1,0:T(8,128)S(1)}, u32[]{:S(2)}) copy-start(f32[256,768]{1,0:T(8,128)S(1)} %get-tuple-element.1067) | copy-start | bytes 2359300
  528.7 74.3 %copy-start.90 = (f32[256]{0:T(256)}, f32[256]{0:T(256)S(1)}, u32[]{:S(2)}) copy-start(f32[256]{0:T(256)S(1)} %broadcast_multiply_fusion.9) | copy-start | bytes 3076
  529.0 74.0 %copy-start.107 = (f32[256]{0:T(256)}, f32[256]{0:T(256)S(1)}, u32[]{:S(2)}) copy-start(f32[256]{0:T(256)S(1)} %add_rsqrt_fusion.1) | copy-start | bytes 3076
  537.8 52.1 %copy-start.118 = (f32[768]{0:T(1024)S(1)}, f32[768]{0:T(1024)}, u32[]{:S(2)}) copy-start(f32[768]{0:T(1024)} %get-tuple-element.892) | copy-start | bytes 9220
  679.0 68.6 %copy-start.11 = (f32[256,768]{1,0:T(8,128)S(1)}, f32[256,768]{1,0:T(8,128)}, u32[]{:S(2)}) copy-start(f32[256,768]{1,0:T(8,128)} %copy-done.10) | copy-start | bytes 2359300
  679.0 68.6 %copy-start.26 = (f32[256,768]{1,0:T(8,128)S(1)}, f32[256,768]{1,0:T(8,128)}, u32[]{:S(2)}) copy-start(f32[256,768]{1,0:T(8,128)} %copy-done.25) | copy-start | bytes 2359300
  679.0 68.6 %copy-start.80 = (f32[256]{0:T(256)S(1)}, f32[256]{0:T(256)}, u32[]{:S(2)}) copy-start(f32[256]{0:T(256)} %copy-done.78) | copy-start | bytes 3076
  679.0 68.6 %copy-start.84 = (f32[256]{0:T(256)S(1)}, f32[256]{0:T(256)}, u32[]{:S(2)}) copy-start(f32[256]{0:T(256)} %copy-done.82) | copy-start | bytes 3076
  679.0 227.0 %reduce-scatter.13.cloned.1.call-start = ((), (), s32[]{:S(2)}) async-start(), calls=%async_computation.18 | async-start | bytes 7077888 | tf_op jit(solution)/shard_map/reduce_scatter | solution.py:290
  682.8 69.2 %copy-start.50 = (bf16[256,768]{1,0:T(8,128)(2,1)}, bf16[256,768]{1,0:T(8,128)(2,1)S(1)}, u32[]{:S(2)}) copy-start(bf16[256,768]{1,0:T(8,128)(2,1)S(1)} %copy.147) | copy-start | bytes 1179652
  837.7 101.8 %reduce-scatter.21.cloned.1.call-start = ((), (), s32[]{:S(2)}) async-start(), calls=%async_computation.23 | async-start | bytes 1327104 | tf_op jit(solution)/shard_map/reduce_scatter | solution.py:381
  840.5 154.3 %reduce-scatter.25.cloned.1.call-start = ((), (), s32[]{:S(2)}) async-start(), calls=%async_computation.25 | async-start | bytes 5308416 | tf_op jit(solution)/shard_map/reduce_scatter | solution.py:384
  845.9 204.7 %reduce-scatter.29.cloned.1.call-start = ((), (), s32[]{:S(2)}) async-start(), calls=%async_computation.27 | async-start | bytes 5308416 | tf_op jit(solution)/shard_map/reduce_scatter | solution.py:387
  851.1 233.7 %reduce-scatter.19.cloned.1.call-start = ((), (), s32[]{:S(2)}) async-start(), calls=%async_computation.22 | async-start | bytes 1327104 | tf_op jit(solution)/shard_map/reduce_scatter | solution.py:381
  853.9 275.1 %reduce-scatter.17.cloned.1.call-start = ((), (), s32[]{:S(2)}) async-start(), calls=%async_computation.21 | async-start | bytes 3981312 | tf_op jit(solution)/shard_map/reduce_scatter | solution.py:378
  857.1 327.7 %reduce-scatter.23.cloned.1.call-start = ((), (), s32[]{:S(2)}) async-start(), calls=%async_computation.24 | async-start | bytes 5308416 | tf_op jit(solution)/shard_map/reduce_scatter | solution.py:384
  863.3 377.1 %reduce-scatter.27.cloned.1.call-start = ((), (), s32[]{:S(2)}) async-start(), calls=%async_computation.26 | async-start | bytes 5308416 | tf_op jit(solution)/shard_map/reduce_scatter | solution.py:387
  868.6 416.3 %reduce-scatter.15.cloned.1.call-start = ((), (), s32[]{:S(2)}) async-start(), calls=%async_computation.20 | async-start | bytes 3981312 | tf_op jit(solution)/shard_map/reduce_scatter | solution.py:378
  910.2 413.7 %all-gather.37.cloned.1.call-start = ((), (), s32[]{:S(2)}) async-start(), calls=%async_computation.15 | async-start | bytes 3538944 | tf_op jit(solution)/shard_map/all_gather | solution.py:360
  910.9 461.8 %all-gather.41.cloned.1.call-start = ((), (), s32[]{:S(2)}) async-start(), calls=%async_computation.19 | async-start | bytes 3538944 | tf_op jit(solution)/shard_map/all_gather | solution.py:407
  915.3 369.8 %copy-start.120 = (s32[1,256]{1,0:T(1,128)S(1)}, s32[1,256]{1,0:T(1,128)}, u32[]{:S(2)}) copy-start(s32[1,256]{1,0:T(1,128)} %param.23) | copy-start | bytes 3076
  915.3 387.3 %copy-start.129 = (u32[32]{0:T(128)S(1)}, u32[32]{0:T(128)}, u32[]{:S(2)}) copy-start(u32[32]{0:T(128)} %constant.289) | copy-start | bytes 388
  915.3 388.7 %copy-start.96 = (bf16[12,64]{1,0:T(8,128)(2,1)S(1)}, bf16[12,64]{1,0:T(8,128)(2,1)}, u32[]{:S(2)}) copy-start(bf16[12,64]{1,0:T(8,128)(2,1)} %get-tuple-element.1025) | copy-start | bytes 4612
  915.3 545.5 %all-reduce.7.cloned.1.call-start = ((), (), s32[]{:S(2)}) async-start(), calls=%async_computation.36 | async-start | bytes 7077888 | tf_op jit(solution)/shard_map/psum | solution.py:395
  (195 other events, 1497.0 us)
Sparse Core Ops, SparseCore 0:
  9.6 40.9 all-gather.26
  52.8 40.3 all-gather.42
  97.3 37.1 all-gather.28
  136.6 37.0 all-gather.30
  175.8 21.6 all-gather.44
  199.6 50.8 all-gather.46
  252.1 49.9 all-gather.48
  303.7 40.2 all-gather.50
  345.6 37.1 all-gather.38
  384.9 37.1 all-gather.32
  424.3 37.1 all-gather.34
  463.0 21.6 all-gather.52
  486.9 50.8 all-gather.54
  539.9 49.9 all-gather.56
  679.1 68.4 reduce-scatter.10
  837.8 68.1 reduce-scatter.12
  908.2 31.3 reduce-scatter.20
  941.7 53.1 reduce-scatter.24
  997.2 53.3 reduce-scatter.28
  1053.3 31.4 reduce-scatter.18
  1087.1 41.8 reduce-scatter.16
  1131.3 53.3 reduce-scatter.22
  1187.1 53.3 reduce-scatter.26
  1242.7 42.1 reduce-scatter.14
  1287.1 36.7 all-gather.36
  1326.0 38.4 all-gather.40
  1368.1 92.6 all-reduce.6
where the time goes:
time: 1480 us
  waiting for transfers between devices  917 us (62%)
  matrix products  234 us (16%)
  local copies, waits for them, and re-layouts  135 us (9%)
  blocking collectives  88.2 us (6%)
  other arithmetic  75.5 us (5%)
  between operations  16.8 us (1%)
    reduce_scatter x2, waiting for transfers between devices, body(): lax.psum_scatter(shrink_local.astype(jnp.bfloat16), 'shard', scatter_dime...  111 us
    reduce_scatter x2, waiting for transfers between devices, body(): lax.psum_scatter(expand_local.astype(jnp.bfloat16), 'shard', scatter_dime...  111 us
    reduce_scatter x2, waiting for transfers between devices, layer_backward(): lax.psum_scatter(key_value_grad.astype(jnp.bfloat16), 'shard', scatter_di...  101 us
    reduce_scatter x2, waiting for transfers between devices, body(): lax.psum_scatter(entry_local.astype(jnp.bfloat16), 'shard', scatter_dimen...  88.7 us
    all_gather x2, waiting for transfers between devices, fetch_forward(): lax.all_gather(shrink_weight[layer_index].astype(jnp.bfloat16), 'shard',...  80 us
    psum x1, waiting for transfers between devices, body(): lax.psum(entry_part.astype(jnp.bfloat16), 'rep').astype(jnp.float32)  77.4 us
    all_gather x2, waiting for transfers between devices, fetch_forward(): lax.all_gather(entry_weight[layer_index].astype(jnp.bfloat16), 'shard', a...  76.2 us
    all_gather x2, waiting for transfers between devices, attend_forward(): value_piece = lax.all_gather(values, 'shard', axis=0, tiled=True)  69.2 us
  transfers between devices with their start and end apart: 27, of which 24 were waited for; matrix products, arithmetic and copies ran while one was open for 17% of the time, Pallas kernels for 0%

commit v1 on v0

--- a/solution.py
+++ b/solution.py
@@ -1,6 +1,10 @@
+import functools
+
 import jax
 import jax.numpy as jnp
 from jax import lax
+from jax.experimental import pallas as pl
+from jax.experimental.pallas import tpu as pltpu
 from jax.sharding import PartitionSpec as P
 
 HEADS = 12
@@ -411,6 +415,541 @@
     return (output, input_grad, entry_grad, exit_grad, expand_grad, shrink_grad, vector_grad)
 
 
+EDGE = (0, 1, 6, 7)
+CORE = (2, 3, 4, 5)
+ALL = tuple(range(8))
+BOTH = ("rep", "shard")
+
+
+def routes(rep_flip, shard_flip, shards):
+    return [
+        (rep * 8 + shard, (rep ^ rep_flip) * 8 + (shard ^ shard_flip))
+        for rep in range(4)
+        for shard in shards
+    ]
+
+
+TO_X = routes(1, 0, CORE)
+TO_Y = routes(2, 0, CORE)
+TO_TWIN = routes(0, 1, CORE)
+TO_MID = routes(0, 6, CORE)
+INWARD = routes(0, 2, EDGE)
+OUTWARD = routes(0, 2, CORE)
+ALL_X = routes(1, 0, ALL)
+ALL_Y = routes(2, 0, ALL)
+
+
+def send(value, route):
+    return lax.ppermute(value, BOTH, route)
+
+
+def vmem(count):
+    return [pl.BlockSpec(memory_space=pltpu.VMEM)] * count
+
+
+LIMIT = pltpu.CompilerParams(vmem_limit_bytes=60 * 1024 * 1024)
+
+
+def nt(left, right):
+    return lax.dot_general(left, right, (((1,), (1,)), ((), ())), preferred_element_type=jnp.float32)
+
+
+def nn(left, right):
+    return lax.dot_general(left, right, (((1,), (0,)), ((), ())), preferred_element_type=jnp.float32)
+
+
+def gather_kernel(count, ids_ref, want_ref, *refs):
+    out_ref = refs[count]
+    want = want_ref[...]
+    total = None
+    for index in range(count):
+        ids = ids_ref[index]
+        hit = (want == ids).astype(jnp.float32).astype(jnp.bfloat16)
+        part = nn(hit, refs[index][0 : ids.shape[1], :])
+        total = part if total is None else total + part
+    out_ref[...] = total.astype(jnp.bfloat16)
+
+
+def gather_rows(pieces, ids, want):
+    count = len(pieces)
+    return pl.pallas_call(
+        functools.partial(gather_kernel, count),
+        out_shape=jax.ShapeDtypeStruct((want.shape[0], pieces[0].shape[1]), jnp.bfloat16),
+        in_specs=vmem(2 + count),
+        out_specs=pl.BlockSpec(memory_space=pltpu.VMEM),
+        compiler_params=LIMIT,
+        name="gather_rows",
+    )(ids, want, *pieces)
+
+
+def assemble_kernel(where_ref, *refs):
+    parts, out_ref, sems = refs[:10], refs[10], refs[11]
+    depth, rep, twin = where_ref[0], where_ref[1], where_ref[2]
+    copies = []
+
+    def move(src, dst):
+        copies.append(pltpu.make_async_copy(src, dst, sems.at[len(copies)]))
+
+    for side in range(2):
+        own, first, over_x, over_y, over_d = parts[side * 5 : side * 5 + 5]
+        core = twin ^ side
+        move(own, out_ref.at[depth, core])
+        for slot, flip in enumerate((1, 3, 2)):
+            level = depth ^ flip
+            for piece, bits in ((first, 0), (over_x, 1), (over_y, 2), (over_d, 3)):
+                move(piece.at[slot], out_ref.at[level, core, rep ^ bits])
+    for item in copies:
+        item.start()
+    for item in copies:
+        item.wait()
+
+
+def assemble(where, parts):
+    quarter = parts[0].shape
+    result = pl.pallas_call(
+        assemble_kernel,
+        out_shape=jax.ShapeDtypeStruct((4, 2) + quarter, jnp.bfloat16),
+        in_specs=[pl.BlockSpec(memory_space=pltpu.SMEM)] + [pl.BlockSpec(memory_space=pl.ANY)] * 10,
+        out_specs=pl.BlockSpec(memory_space=pl.ANY),
+        scratch_shapes=[pltpu.SemaphoreType.DMA((26,))],
+        name="assemble",
+    )(where, *parts)
+    return result.reshape(8 * quarter[0] * quarter[1], quarter[2])
+
+
+def spread(own, rep, x_first):
+    rows, width = own.shape
+    quarter = own.reshape(4, rows // 4, width)
+    piece = lax.dynamic_index_in_dim(quarter, rep, 0, keepdims=False)
+    near = send(piece, INWARD)
+    middle = send(piece, TO_MID)
+    far = send(near, TO_MID)
+    first = jnp.stack([near, middle, far])
+    over_x = send(first, TO_X)
+    over_y = send(first, TO_Y)
+    over_d = send(over_x, TO_Y) if x_first else send(over_y, TO_X)
+    mine = (quarter, first, over_x, over_y, over_d)
+    return mine + tuple(send(item, TO_TWIN) for item in mine)
+
+
+def reduce_grad(chip_sum, rep, is_low, is_core, x_first):
+    piece, width = chip_sum.shape[2:]
+    axis = 2 if x_first else 1
+    bit = (rep & 1) if x_first else (rep >> 1)
+
+    def low(value):
+        return value.astype(jnp.bfloat16)
+
+    def wide(value):
+        return value.astype(jnp.float32)
+
+    view = chip_sum.reshape(4, 2, 2, piece, width)
+    keep = lax.dynamic_index_in_dim(view, bit, axis, keepdims=False)
+    give = lax.dynamic_index_in_dim(view, 1 - bit, axis, keepdims=False)
+    got = send(give, TO_X if x_first else TO_Y)
+    stage = low(wide(keep) + wide(got))
+    give = jnp.where(is_low, stage[2:4], stage[0:2])
+    keep = jnp.where(is_low, stage[0:2], stage[2:4])
+    got = send(give, TO_MID)
+    stage = low(wide(keep) + wide(got))
+    outer = jnp.where(is_low, stage[0], stage[1])
+    inner = jnp.where(is_low, stage[1], stage[0])
+    got = send(outer, OUTWARD)
+    stage = jnp.where(is_core, inner, got)
+    got = send(stage, ALL_Y if x_first else ALL_X)
+    stage = low(wide(stage) + wide(got))
+    got = send(stage, ALL_X if x_first else ALL_Y)
+    joined = jnp.where(
+        bit == 0, jnp.stack([stage, got], axis - 1), jnp.stack([got, stage], axis - 1)
+    )
+    return joined.astype(jnp.float32).reshape(4 * piece, width)
+
+
+def attend_kernel(q_ref, ka_ref, kb_ref, va_ref, vb_ref, code_ref, member_ref, o_ref, ot_ref, lse_ref, bias_ref):
+    half = q_ref.shape[0]
+
+    @pl.when(pl.program_id(0) == 0)
+    def _():
+        bias_ref[...] = jnp.where(code_ref[...] == member_ref[...], 0.0, NEG_FILL)
+
+    q = q_ref[...] * jnp.bfloat16(HEAD_DIM ** (-0.5))
+    lane = lax.broadcasted_iota(jnp.int32, q.shape, 1)
+    keys = (ka_ref[...], kb_ref[...])
+    values = (va_ref[...].T, vb_ref[...].T)
+    outs = []
+    for head in range(2):
+        q_head = jnp.where((lane >= HEAD_DIM) == (head == 1), q, jnp.bfloat16(0))
+        scores = [
+            nt(keys[side], q_head) + bias_ref[side * half : (side + 1) * half, :]
+            for side in range(2)
+        ]
+        top = jnp.maximum(
+            jnp.max(scores[0], axis=0, keepdims=True), jnp.max(scores[1], axis=0, keepdims=True)
+        )
+        total = None
+        mixed = None
+        for side in range(2):
+            expo = jnp.exp(scores[side] - top)
+            part = jnp.sum(expo, axis=0, keepdims=True)
+            value = values[side][head * HEAD_DIM : (head + 1) * HEAD_DIM, :]
+            product = nn(value, expo.astype(jnp.bfloat16))
+            total = part if total is None else total + part
+            mixed = product if mixed is None else mixed + product
+        outs.append(mixed / total)
+        lse_ref[0, head : head + 1, :] = top + jnp.log(total)
+    joined = jnp.concatenate(outs, axis=0)
+    ot_ref[...] = joined
+    o_ref[...] = joined.T.astype(jnp.bfloat16)
+
+
+def attend_fast(queries, keys, values, code, member):
+    half, width = queries.shape
+    column = pl.BlockSpec((half, 128), lambda pair: (0, pair))
+    whole = [
+        pl.BlockSpec((2 * half, 1), lambda pair: (0, 0)),
+        pl.BlockSpec((1, half), lambda pair: (0, 0)),
+    ]
+    return pl.pallas_call(
+        attend_kernel,
+        grid=(width // 128,),
+        in_specs=[column] * 5 + whole,
+        out_specs=[
+            column,
+            pl.BlockSpec((128, half), lambda pair: (pair, 0)),
+            pl.BlockSpec((1, 2, half), lambda pair: (pair, 0, 0)),
+        ],
+        out_shape=[
+            jax.ShapeDtypeStruct((half, width), jnp.bfloat16),
+            jax.ShapeDtypeStruct((width, half), jnp.float32),
+            jax.ShapeDtypeStruct((width // 128, 2, half), jnp.float32),
+        ],
+        scratch_shapes=[pltpu.VMEM((2 * half, half), jnp.float32)],
+        compiler_params=LIMIT,
+        name="attend_forward",
+    )(queries, keys[0], keys[1], values[0], values[1], code, member)
+
+
+def attend_back_kernel(
+    q_ref, g_ref, ka_ref, kb_ref, va_ref, vb_ref, ot_ref, lse_ref, code_ref, member_ref,
+    dq_ref, dka_ref, dkb_ref, dva_ref, dvb_ref, bias_ref,
+):
+    half = q_ref.shape[0]
+
+    @pl.when(pl.program_id(0) == 0)
+    def _():
+        bias_ref[...] = jnp.where(code_ref[...] == member_ref[...], 0.0, NEG_FILL)
+
+    scale = HEAD_DIM ** (-0.5)
+    q = q_ref[...] * jnp.bfloat16(scale)
+    grad = g_ref[...]
+    lane = lax.broadcasted_iota(jnp.int32, q.shape, 1)
+    keys = (ka_ref[...], kb_ref[...])
+    turned = (ka_ref[...].T, kb_ref[...].T)
+    values = (va_ref[...], vb_ref[...])
+    product = ot_ref[...] * grad.astype(jnp.float32).T
+    key_sums = [None, None]
+    value_sums = [None, None]
+    query_parts = []
+    for head in range(2):
+        rows = slice(head * HEAD_DIM, (head + 1) * HEAD_DIM)
+        chosen = (lane >= HEAD_DIM) == (head == 1)
+        q_head = jnp.where(chosen, q, jnp.bfloat16(0))
+        g_head = jnp.where(chosen, grad, jnp.bfloat16(0))
+        delta = jnp.sum(product[rows, :], axis=0, keepdims=True)
+        level = lse_ref[0, head : head + 1, :]
+        query_sum = None
+        for side in range(2):
+            scores = nt(keys[side], q_head) + bias_ref[side * half : (side + 1) * half, :]
+            prob = jnp.exp(scores - level)
+            slope = nt(values[side], g_head)
+            steep = (prob * (slope - delta)).astype(jnp.bfloat16)
+            value_part = nn(prob.astype(jnp.bfloat16), g_head)
+            key_part = nn(steep, q_head)
+            query_part = nn(turned[side][rows, :], steep)
+            value_sums[side] = value_part if head == 0 else value_sums[side] + value_part
+            key_sums[side] = key_part if head == 0 else key_sums[side] + key_part
+            query_sum = query_part if side == 0 else query_sum + query_part
+        query_parts.append(query_sum * scale)
+    dq_ref[...] = jnp.concatenate(query_parts, axis=0).T.astype(jnp.bfloat16)
+    dka_ref[...] = key_sums[0]
+    dkb_ref[...] = key_sums[1].astype(jnp.bfloat16)
+    dva_ref[...] = value_sums[0]
+    dvb_ref[...] = value_sums[1].astype(jnp.bfloat16)
+
+
+def attend_back_fast(queries, grad, keys, values, turned, level, code, member):
+    half, width = queries.shape
+    column = pl.BlockSpec((half, 128), lambda pair: (0, pair))
+    wide = jax.ShapeDtypeStruct((half, width), jnp.float32)
+    thin = jax.ShapeDtypeStruct((half, width), jnp.bfloat16)
+    return pl.pallas_call(
+        attend_back_kernel,
+        grid=(width // 128,),
+        in_specs=[column] * 6
+        + [
+            pl.BlockSpec((128, half), lambda pair: (pair, 0)),
+            pl.BlockSpec((1, 2, half), lambda pair: (pair, 0, 0)),
+            pl.BlockSpec((2 * half, 1), lambda pair: (0, 0)),
+            pl.BlockSpec((1, half), lambda pair: (0, 0)),
+        ],
+        out_specs=[column] * 5,
+        out_shape=[thin, wide, thin, wide, thin],
+        scratch_shapes=[pltpu.VMEM((2 * half, half), jnp.float32)],
+        compiler_params=LIMIT,
+        name="attend_backward",
+    )(queries, grad, keys[0], keys[1], values[0], values[1], turned, level, code, member)
+
+
+def forward_fast(hidden, weights, pieces, code, member):
+    entry, leaving, expand, shrink = weights
+    width = leaving.shape[0]
+    flat = hidden.astype(jnp.bfloat16)
+    mixed = jnp.dot(flat, entry, preferred_element_type=jnp.float32)
+    queries = (mixed[:, 0:width] + pieces[0]).astype(jnp.bfloat16)
+    keys = mixed[:, width : 2 * width].astype(jnp.bfloat16)
+    values = (mixed[:, 2 * width : 3 * width] + pieces[1]).astype(jnp.bfloat16)
+    keys = (keys, send(keys, TO_TWIN))
+    values = (values, send(values, TO_TWIN))
+    attended, turned, level = attend_fast(queries, keys, values, code, member)
+    branch = jnp.dot(attended, leaving, preferred_element_type=jnp.float32) + pieces[2]
+    middle, normed_one, factor_one = norm_forward(hidden + branch, pieces[3], pieces[4])
+    middle_low = middle.astype(jnp.bfloat16)
+    inner = jnp.dot(middle_low, expand, preferred_element_type=jnp.float32) + pieces[8]
+    active = gelu_exact(inner).astype(jnp.bfloat16)
+    branch_two = jnp.dot(active, shrink, preferred_element_type=jnp.float32) + pieces[5]
+    result, normed_two, factor_two = norm_forward(middle + branch_two, pieces[6], pieces[7])
+    record = (
+        flat, queries, keys, values, attended, turned, level,
+        normed_one, factor_one, middle_low, inner, active, normed_two, factor_two,
+    )
+    return (result, record)
+
+
+def backward_fast(upstream, weights, pieces, record, code, member, twin, finish):
+    entry, leaving, expand, shrink = weights
+    width = leaving.shape[0]
+    (
+        flat, queries, keys, values, attended, turned, level,
+        normed_one, factor_one, middle_low, inner, active, normed_two, factor_two,
+    ) = record
+    rows = queries.shape[0]
+    block = jnp.arange(width, dtype=jnp.int32)
+    place = jnp.arange(width // 2, dtype=jnp.int32)
+    unit = width // 8
+
+    def halves(left):
+        if left.shape[1] == width:
+            source = (place // unit) * (2 * unit) + place % unit
+
+            def pick(core):
+                chosen = (block[:, None] == (source + core * unit)[None, :]).astype(jnp.bfloat16)
+                return jnp.dot(left, chosen, preferred_element_type=jnp.float32).astype(jnp.bfloat16)
+        else:
+            view = left.reshape(rows, 4, 2, left.shape[1] // 8)
+
+            def pick(core):
+                taken = lax.dynamic_index_in_dim(view, core, 2, keepdims=False)
+                return taken.reshape(rows, left.shape[1] // 2)
+
+        return pick(twin), pick(1 - twin)
+
+    def weight_grad(left, right):
+        mine, theirs = halves(left)
+        left_all = jnp.concatenate([mine, send(theirs, TO_TWIN)], axis=0)
+        right_all = jnp.concatenate([right, send(right, TO_TWIN)], axis=0)
+        product = inner_rows(left_all, right_all).astype(jnp.bfloat16)
+        return finish(product)
+
+    resid_two, gain_two_grad, shift_two_grad = norm_backward(
+        upstream, normed_two, factor_two, pieces[6]
+    )
+    branch_two_grad = resid_two.astype(jnp.bfloat16)
+    bias_down_grad = jnp.sum(branch_two_grad.astype(jnp.float32), axis=0)
+    shrink_grad = weight_grad(active, branch_two_grad)
+    active_grad = times_trans(branch_two_grad, shrink)
+    unused_value, gelu_pull = jax.vjp(gelu_exact, inner)
+    inner_grad = gelu_pull(active_grad)[0].astype(jnp.bfloat16)
+    bias_up_grad = jnp.sum(inner_grad.astype(jnp.float32), axis=0)
+    expand_grad = weight_grad(middle_low, inner_grad)
+    middle_grad = resid_two + times_trans(inner_grad, expand)
+    resid_one, gain_one_grad, shift_one_grad = norm_backward(
+        middle_grad, normed_one, factor_one, pieces[3]
+    )
+    branch_grad = resid_one.astype(jnp.bfloat16)
+    bias_out_grad = jnp.sum(branch_grad.astype(jnp.float32), axis=0)
+    exit_grad = weight_grad(attended, branch_grad)
+    attended_grad = times_trans(branch_grad, leaving).astype(jnp.bfloat16)
+    query_grad, key_own, key_twin, value_own, value_twin = attend_back_fast(
+        queries, attended_grad, keys, values, turned, level, code, member
+    )
+    key_grad = (key_own + send(key_twin, TO_TWIN).astype(jnp.float32)).astype(jnp.bfloat16)
+    value_grad = (value_own + send(value_twin, TO_TWIN).astype(jnp.float32)).astype(jnp.bfloat16)
+    mixed_grad = jnp.concatenate([query_grad, key_grad, value_grad], axis=1)
+    bias_query_grad = jnp.sum(query_grad.astype(jnp.float32), axis=0)
+    bias_value_grad = jnp.sum(value_grad.astype(jnp.float32), axis=0)
+    entry_grad = weight_grad(flat, mixed_grad)
+    hidden_grad = resid_one + times_trans(mixed_grad, entry)
+    vector_grad = jnp.concatenate(
+        [
+            bias_query_grad, bias_value_grad, bias_out_grad, gain_one_grad, shift_one_grad,
+            bias_down_grad, gain_two_grad, shift_two_grad, bias_up_grad,
+        ]
+    )
+    return (hidden_grad, (entry_grad, exit_grad, expand_grad, shrink_grad, vector_grad))
+
+
+def body_fast(
+    inputs, cotangent, lengths, dealing, key_mask,
+    entry_weight, exit_weight, expand_weight, shrink_weight, vectors,
+):
+    rows, width = inputs.shape
+    layers = entry_weight.shape[0]
+    group_rows = 8 * rows
+    half_rows = group_rows // 2
+    core_rows = half_rows // 2
+    rep = lax.axis_index("rep")
+    shard = lax.axis_index("shard")
+    depth, twin = shard // 2, shard % 2
+    is_low = depth <= 1
+    is_core = (depth == 1) | (depth == 2)
+    where = jnp.stack([depth, rep, twin]).astype(jnp.int32)
+
+    def relay(value):
+        near = send(value, INWARD)
+        mine = (value, near, send(value, TO_MID), send(near, TO_MID))
+        return mine, tuple(send(item, TO_TWIN) for item in mine)
+
+    def absolute(mine, theirs):
+        def order(four):
+            own, near, middle, far = four
+            return jnp.where(
+                is_low, jnp.stack([near, own, middle, far]), jnp.stack([far, middle, own, near])
+            )
+
+        one, two = order(mine), order(theirs)
+        return jnp.where(twin == 0, jnp.stack([one, two], 1), jnp.stack([two, one], 1))
+
+    flips = (0, 1, 3, 2)
+    table = absolute(*relay(jnp.concatenate([dealing, key_mask], axis=0)))
+    dealt_all = table[:, :, 0, :].reshape(group_rows)
+    mask_all = table[:, :, 1, :].reshape(group_rows)
+
+    extra = layers * vectors.shape[1] // width
+    tail = vectors.astype(jnp.bfloat16).reshape(extra, width)
+    packed = jnp.concatenate([inputs, tail, jnp.zeros((8 - extra % 8, width), jnp.bfloat16)], axis=0)
+    mine, theirs = relay(packed)
+    input_pieces = mine + theirs
+    vector_all = absolute(
+        tuple(item[rows : rows + extra] for item in mine),
+        tuple(item[rows : rows + extra] for item in theirs),
+    )
+    vector_all = jnp.transpose(
+        vector_all.reshape(8, layers, vectors.shape[1]), (1, 0, 2)
+    ).reshape(layers, 8 * vectors.shape[1]).astype(jnp.float32)
+
+    weights = []
+    for layer in range(layers):
+        made = []
+        for index, weight in enumerate((entry_weight, exit_weight, expand_weight, shrink_weight)):
+            x_first = (index != 2) == (layer == 0)
+            made.append(assemble(where, spread(weight[layer].astype(jnp.bfloat16), rep, x_first)))
+        weights.append(made)
+    pieces = [split_vector(vector_all[layer], width) for layer in range(layers)]
+
+    mine, theirs = relay(cotangent)
+    cotangent_pieces = mine + theirs
+
+    member, leading = sequence_ids(lengths[0], group_rows)
+    usable = (mask_all == 1) | leading
+    code = jnp.where(usable, member, -1)
+    longest = jnp.argmax(lengths[0])
+    begin = jnp.cumsum(lengths[0])[longest] - lengths[0][longest]
+    spot = jnp.arange(half_rows, dtype=jnp.int32)
+
+    def halve(values, low_side):
+        inside = lax.dynamic_slice_in_dim(values, begin, half_rows, 0)
+        outside = jnp.where(spot < begin, values[:half_rows], values[half_rows:])
+        return jnp.where(low_side, inside, outside)
+
+    def cores(values):
+        own = lax.dynamic_slice_in_dim(values, twin * core_rows, core_rows, 0)
+        other = lax.dynamic_slice_in_dim(values, (1 - twin) * core_rows, core_rows, 0)
+        return own, other
+
+    code_half = jnp.concatenate(cores(halve(code, is_low))).reshape(half_rows, 1)
+    member_own = cores(halve(member, is_low))[0].reshape(1, core_rows)
+    dealt_near = cores(halve(dealt_all, is_low))
+    dealt_far = cores(halve(dealt_all, ~is_low))
+
+    local = jnp.arange(rows, dtype=jnp.int32)
+    bases = jnp.stack(
+        [(depth ^ flip) * (2 * rows) + (twin ^ side) * rows for side in range(2) for flip in flips]
+    ).astype(jnp.int32)
+    source_ids = (bases[:, None] + local[None, :]).reshape(8, 1, rows)
+    want_in = dealt_near[0].reshape(core_rows, 1)
+    hidden = gather_rows(input_pieces, source_ids, want_in).astype(jnp.float32)
+    upstream = gather_rows(cotangent_pieces, source_ids, want_in).astype(jnp.float32)
+
+    result_ids = jnp.stack([dealt_near[0], dealt_far[0], dealt_near[1], dealt_far[1]]).reshape(
+        4, 1, core_rows
+    )
+    want_out = jnp.concatenate([source_ids[0, 0], source_ids[1, 0]]).reshape(2 * rows, 1)
+
+    def restore(value):
+        middle = send(value, TO_MID)
+        found = gather_rows(
+            (value, middle, send(value, TO_TWIN), send(middle, TO_TWIN)), result_ids, want_out
+        )
+        outer = send(found[rows:], OUTWARD)
+        return jnp.where(is_core, found[:rows], outer)
+
+    saved = []
+    for layer in range(layers):
+        hidden, record = forward_fast(hidden, weights[layer], pieces[layer], code_half, member_own)
+        saved.append(record)
+    output = restore(hidden.astype(jnp.bfloat16))
+
+    grad = upstream
+    layer_grads = [None] * layers
+    for layer in reversed(range(layers)):
+        order = iter((0, 1, 1, 0) if layer == 0 else (1, 0, 0, 1))
+
+        def finish(product):
+            x_first = next(order) == 0
+            return reduce_grad(
+                product.reshape(4, 4, product.shape[0] // 16, product.shape[1]),
+                rep, is_low, is_core, x_first,
+            )
+
+        grad, layer_grads[layer] = backward_fast(
+            grad, weights[layer], pieces[layer], saved[layer], code_half, member_own, twin, finish
+        )
+    input_grad = restore(grad.astype(jnp.bfloat16)).astype(jnp.float32)
+
+    joined = jnp.stack([item[4] for item in layer_grads])
+    joined = jnp.transpose(joined.reshape(layers, 4, 2, vectors.shape[1]), (1, 2, 0, 3))
+    keep = lax.dynamic_index_in_dim(joined, twin, 1, keepdims=False)
+    give = lax.dynamic_index_in_dim(joined, 1 - twin, 1, keepdims=False)
+    stage = keep + send(give, TO_TWIN)
+    stage = stage + send(stage, TO_X)
+    stage = stage + send(stage, TO_Y)
+    give = jnp.where(is_low, stage[2:4], stage[0:2])
+    keep = jnp.where(is_low, stage[0:2], stage[2:4])
+    stage = keep + send(give, TO_MID)
+    outer = jnp.where(is_low, stage[0], stage[1])
+    inner = jnp.where(is_low, stage[1], stage[0])
+    vector_grad = jnp.where(is_core, inner, send(outer, OUTWARD))
+    return (
+        output,
+        input_grad,
+        jnp.stack([item[0] for item in layer_grads]),
+        jnp.stack([item[1] for item in layer_grads]),
+        jnp.stack([item[2] for item in layer_grads]),
+        jnp.stack([item[3] for item in layer_grads]),
+        vector_grad,
+    )
+
+
 def solution(mesh):
     placed = (
         P(("rep", "shard"), None),
@@ -424,8 +963,9 @@
         P(None, "shard", None),
         P(None, "shard"),
     )
+    small = dict(mesh.shape) == {"rep": 4, "shard": 8}
     return jax.shard_map(
-        body,
+        body_fast if small else body,
         mesh=mesh,
         in_specs=placed,
         out_specs=(

time: 1480 us -> 1880 us (1.27)
  Pallas kernels: 0 us -> 965 us
  waiting for transfers between devices: 917 us -> 293 us
  starting transfers between devices: 1.52 us -> 269 us
  blocking collectives: 88.2 us -> 0 us
  matrix products: 234 us -> 156 us
  local copies, waits for them, and re-layouts: 135 us -> 99 us
    pallas_call x0 -> x16, Pallas kernels: none -> 965 us  [the longest x8 874 us: assemble(): pl.pallas_call(assemble_kernel, out_shape=jax.ShapeDtypeStruct((4, 2) + q...]
    reduce_scatter x10 -> x0, waiting for transfers between devices: 470 us -> none  [the longest x2 111 us: body(): lax.psum_scatter(shrink_local.astype(jnp.bfloat16), 'shard', scatter_dime...]
    all_gather x16 -> x0, waiting for transfers between devices: 364 us -> none  [the longest x2 80 us: fetch_forward(): lax.all_gather(shrink_weight[layer_index].astype(jnp.bfloat16), 'shard',...]
    ppermute x0 -> x186, waiting for transfers between devices: none -> 293 us  [send(): return lax.ppermute(value, BOTH, route)]
    ppermute x0 -> x186, starting transfers between devices: none -> 269 us  [send(): return lax.ppermute(value, BOTH, route)]
    dot_general x64 -> x20, matrix products: 184 us -> 82.3 us  [the longest x2 37.4 us: forward_fast(): jnp.dot(middle_low, expand, preferred_element_type=jnp.float32) + pieces[8]]
    psum x1 -> x0, waiting for transfers between devices: 77.4 us -> none  [body(): lax.psum(entry_part.astype(jnp.bfloat16), 'rep').astype(jnp.float32)]
    all_gather x4 -> x0, blocking collectives: 48.2 us -> none  [the longest x2 28.6 us: fetch_forward(): lax.all_gather(vectors[layer_index].astype(jnp.bfloat16), 'shard', axis=0...]
  transfers between devices with their start and end apart: 27 -> 186, of which waited for: 24 -> 22; matrix products, arithmetic and copies ran while one was open for 17% -> 14% of each run, Pallas kernels for 0% -> 51%
where the time goes in v1:
time: 1880 us; the launch traced here: 1860 us
  Pallas kernels  965 us (51%)
  waiting for transfers between devices  293 us (16%)
  starting transfers between devices  269 us (14%)
  matrix products  156 us (8%)
  local copies, waits for them, and re-layouts  99 us (5%)
  other arithmetic  72.3 us (4%)
    pallas_call x8, Pallas kernels, assemble(): pl.pallas_call(assemble_kernel, out_shape=jax.ShapeDtypeStruct((4, 2) + q...  874 us
    ppermute x186, waiting for transfers between devices, send(): return lax.ppermute(value, BOTH, route)  293 us
    ppermute x186, starting transfers between devices, send(): return lax.ppermute(value, BOTH, route)  269 us
    dot_general x8, matrix products, times_trans(): lax.dot_general(left, right, (((1,), (1,)), ((), ())), preferred_element_...  41.8 us
    pallas_call x2, Pallas kernels, attend_back_fast(): pl.pallas_call(attend_back_kernel, grid=(width // 128,), in_specs=[column...  41.1 us
    unnamed x379, local copies, waits for them, and re-layouts  40.9 us
  transfers between devices with their start and end apart: 186, of which 22 were waited for; matrix products, arithmetic and copies ran while one was open for 14% of the time, Pallas kernels for 51%

profile of v1, /device:TPU:0, one launch (start us, length us, event | category | flops | bytes accessed | tf_op | source)
XLA Modules:
  0.0 1863.9 jit_solution(7036660111804273235)
XLA Ops:
  1.9 5.5 collective-permute-start
  38.3 10.3 collective-permute-start.14
  51.3 5.9 collective-permute-start.49
  65.2 4.8 collective-permute-start.38
  74.7 5.1 collective-permute-start.84
  96.6 22.8 %collective-permute-start.110 = (bf16[256,768]{1,0:T(8,128)(2,1)}, bf16[256,768]{1,0:T(8,128)(2,1)}, u32[]{:S(2)}, u32[]{:S(2)}) collective-permute-start(bf16[256,768]{1,0:T(8,128)(2,1)} %refs_0_.1), channel_id=1, source_target_pairs={{0,2},{1,3},{6,4},{7,5},{8,10},{9,11},{14,12},{15,13},{16,18},{17,... | collective-permute-start | bytes 1179656 | tf_op jit(solution)/shard_map/ppermute | solution.py:443
  138.1 15.4 collective-permute-start.7
  215.0 37.7 %assemble.9 = bf16[4,2,4,24,768]{4,3,2,1,0:T(8,128)(2,1)} custom-call(s32[3]{0:T(128)} %pad_add_fusion.4.where_ref, bf16[4,24,768]{2,1,0:T(8,128)(2,1)} %bitcast.371, bf16[3,24,768]{2,1,0:T(8,128)(2,1)} %copy-done.80, bf16[3,24,768]{2,1,0:T(8,128)(2,1)} %collective-permute-done.30.refs_2_, bf16[3,24,768]{2,1,0:T(8,128)(2,1)} %collective-permute-done.31.refs_3_, ...), custom_call_target="tpu_custom_call" | custom-call | tf_op jit(solution)/shard_map/assemble/pallas_call | solution.py:509
  252.8 37.7 %assemble.13 = bf16[4,2,4,24,768]{4,3,2,1,0:T(8,128)(2,1)} custom-call(s32[3]{0:T(128)} %pad_add_fusion.4.where_ref, bf16[4,24,768]{2,1,0:T(8,128)(2,1)} %bitcast.368, bf16[3,24,768]{2,1,0:T(8,128)(2,1)} %copy-done.81, bf16[3,24,768]{2,1,0:T(8,128)(2,1)} %copy-done.118, bf16[3,24,768]{2,1,0:T(8,128)(2,1)} %copy-done.116, bf16[3,24,768]{2,1,0:T(8,128)(2,1)} %copy-done.123, ...), custom_call_target="tpu_custom_call" | custom-call | tf_op jit(solution)/shard_map/assemble/pallas_call | solution.py:509
  312.2 4.7 gather_rows.4
  317.6 109.3 %assemble.8 = bf16[4,2,4,24,2304]{4,3,2,1,0:T(8,128)(2,1)} custom-call(s32[3]{0:T(128)} %pad_add_fusion.4.where_ref, bf16[4,24,2304]{2,1,0:T(8,128)(2,1)} %bitcast.345, bf16[3,24,2304]{2,1,0:T(8,128)(2,1)} %pad_maximum_fusion.6.refs_1_, bf16[3,24,2304]{2,1,0:T(8,128)(2,1)} %copy-done.104, bf16[3,24,2304]{2,1,0:T(8,128)(2,1)} %copy-done.105, ...), custom_call_target="tpu_custom_call" | custom-call | tf_op jit(solution)/shard_map/assemble/pallas_call | solution.py:509
  448.9 109.2 %assemble.12 = bf16[4,2,4,24,2304]{4,3,2,1,0:T(8,128)(2,1)} custom-call(s32[3]{0:T(128)} %pad_add_fusion.4.where_ref, bf16[4,24,2304]{2,1,0:T(8,128)(2,1)} %bitcast.342, bf16[3,24,2304]{2,1,0:T(8,128)(2,1)} %pad_maximum_fusion.7.refs_1_, bf16[3,24,2304]{2,1,0:T(8,128)(2,1)} %collective-permute-done.63.refs_2_, ...), custom_call_target="tpu_custom_call" | custom-call | tf_op jit(solution)/shard_map/assemble/pallas_call | solution.py:509
  558.2 144.9 %assemble.11 = bf16[4,2,4,96,768]{4,3,2,1,0:T(8,128)(2,1)} custom-call(s32[3]{0:T(128)} %pad_add_fusion.4.where_ref, bf16[4,96,768]{2,1,0:T(8,128)(2,1)} %bitcast.327, bf16[3,96,768]{2,1,0:T(8,128)(2,1)} %copy-done.43, bf16[3,96,768]{2,1,0:T(8,128)(2,1)} %copy-done.82, bf16[3,96,768]{2,1,0:T(8,128)(2,1)} %copy-done.83, bf16[3,96,768]{2,1,0:T(8,128)(2,1)} %copy-done.87, ...), custom_call_target="tpu_custom_call" | custom-call | tf_op jit(solution)/shard_map/assemble/pallas_call | solution.py:509
  703.1 144.9 %assemble.10 = bf16[4,2,4,24,3072]{4,3,2,1,0:T(8,128)(2,1)} custom-call(s32[3]{0:T(128)} %pad_add_fusion.4.where_ref, bf16[4,24,3072]{2,1,0:T(8,128)(2,1)} %bitcast.324, bf16[3,24,3072]{2,1,0:T(8,128)(2,1)} %copy-done.44, bf16[3,24,3072]{2,1,0:T(8,128)(2,1)} %collective-permute-done.41.refs_2_, bf16[3,24,3072]{2,1,0:T(8,128)(2,1)} %copy-done.85, ...), custom_call_target="tpu_custom_call" | custom-call | tf_op jit(solution)/shard_map/assemble/pallas_call | solution.py:509
  848.1 144.9 %assemble.14 = bf16[4,2,4,24,3072]{4,3,2,1,0:T(8,128)(2,1)} custom-call(s32[3]{0:T(128)} %pad_add_fusion.4.where_ref, bf16[4,24,3072]{2,1,0:T(8,128)(2,1)} %bitcast.321, bf16[3,24,3072]{2,1,0:T(8,128)(2,1)} %copy-done.45, bf16[3,24,3072]{2,1,0:T(8,128)(2,1)} %collective-permute-done.87.refs_2_, bf16[3,24,3072]{2,1,0:T(8,128)(2,1)} %collective-permute-done.88.refs_3_, ...), custom_call_target="tpu_custom_call" | custom-call | tf_op jit(solution)/shard_map/assemble/pallas_call | solution.py:509
  993.1 144.9 %assemble.15 = bf16[4,2,4,96,768]{4,3,2,1,0:T(8,128)(2,1)} custom-call(s32[3]{0:T(128)} %pad_add_fusion.4.where_ref, bf16[4,96,768]{2,1,0:T(8,128)(2,1)} %bitcast.318, bf16[3,96,768]{2,1,0:T(8,128)(2,1)} %copy-done.46, bf16[3,96,768]{2,1,0:T(8,128)(2,1)} %collective-permute-done.98.refs_2_, bf16[3,96,768]{2,1,0:T(8,128)(2,1)} %collective-permute-done.99.refs_3_, ...), custom_call_target="tpu_custom_call" | custom-call | tf_op jit(solution)/shard_map/assemble/pallas_call | solution.py:509
  1139.2 15.4 attend_forward.2
  1160.3 18.5 multiply_convert_fusion.1
  1178.8 7.3 reshape.1026
  1186.2 6.5 fusion.171
  1203.2 9.1 constant_dynamic-slice_fusion.4
  1213.7 8.3 copy.85
  1224.2 6.1 copy.84
  1236.8 15.5 attend_forward.3
  1256.5 18.9 %multiply_convert_fusion = (bf16[512,3072]{1,0:T(8,128)(2,1)}, f32[512,3072]{1,0:T(8,128)}, f32[512,3072]{1,0:T(8,128)}) fusion(f32[3072]{0:T(1024)S(1)} %bitcast.416, bf16[512,768]{1,0:T(8,128)(2,1)S(1)} %fusion.87, bf16[768,3072]{1,0:T(8,128)(2,1)} %bitcast.306), kind=kOutput, calls=%fused_computation.16 | convolution fusion | flops 2519728128 | bytes 21245952 | tf_op jit(solution)/shard_map/dot_general | solution.py:717
  1275.4 7.2 reshape.1029
  1282.7 6.5 fusion.173
  1292.0 10.1 convert_reduce_fusion
  1302.1 5.3 multiply_reduce_fusion
  1313.8 20.6 %attend_backward.2 = (bf16[512,768]{1,0:T(8,128)(2,1)}, f32[512,768]{1,0:T(8,128)}, bf16[512,768]{1,0:T(8,128)(2,1)}, f32[512,768]{1,0:T(8,128)}, bf16[512,768]{1,0:T(8,128)(2,1)}) custom-call(bf16[512,768]{1,0:T(8,128)(2,1)} %get-tuple-element.97.q_ref, bf16[512,768]{1,0:T(8,128)(2,1)} %convolution_convert_fusion.3.g_ref, bf16[512,768]{1,0:T(8,128)(2,1)} %slice.663.ka_ref, ...), custom_call_target="tpu_custom_call" | custom-call | tf_op jit(solution)/shard_map/attend_backward/pallas_call | solution.py:685
  1338.9 9.1 constant_dynamic-slice_fusion.2
  1348.0 8.3 copy.87
  1358.2 6.2 copy.86
  1377.9 4.8 multiply_reduce_fusion.1
  1384.2 9.1 convert_reduce_fusion.1
  1393.4 5.0 multiply_reduce_fusion.2
  1401.8 20.6 %attend_backward.3 = (bf16[512,768]{1,0:T(8,128)(2,1)}, f32[512,768]{1,0:T(8,128)}, bf16[512,768]{1,0:T(8,128)(2,1)}, f32[512,768]{1,0:T(8,128)}, bf16[512,768]{1,0:T(8,128)(2,1)}) custom-call(bf16[512,768]{1,0:T(8,128)(2,1)} %get-tuple-element.99.q_ref, bf16[512,768]{1,0:T(8,128)(2,1)} %convolution_convert_fusion.2.g_ref, bf16[512,768]{1,0:T(8,128)(2,1)} %copy-done.11, ...), custom_call_target="tpu_custom_call" | custom-call | tf_op jit(solution)/shard_map/attend_backward/pallas_call | solution.py:685
  1431.3 116.9 %collective-permute-done.150 = bf16[2,24,768]{2,1,0:T(8,128)(2,1)S(1)} collective-permute-done((bf16[2,24,768]{2,1,0:T(8,128)(2,1)S(1)}, bf16[2,24,768]{2,1,0:T(8,128)(2,1)S(1)}, u32[]{:S(2)}, u32[]{:S(2)}) %collective-permute-start.150) | collective-permute-done | bytes 73760 | tf_op jit(solution)/shard_map/ppermute | solution.py:443
  1594.2 4.7 gather_rows.5
  1606.3 35.6 %collective-permute-done.143 = bf16[2,24,768]{2,1,0:T(8,128)(2,1)S(1)} collective-permute-done((bf16[2,24,768]{2,1,0:T(8,128)(2,1)S(1)}, bf16[2,24,768]{2,1,0:T(8,128)(2,1)S(1)}, u32[]{:S(2)}, u32[]{:S(2)}) %collective-permute-start.143) | collective-permute-done | bytes 73760 | tf_op jit(solution)/shard_map/ppermute | solution.py:443
  1673.0 6.9 fusion.42
  1684.4 4.7 gather_rows.7
  1700.4 26.4 %collective-permute-done.124 = bf16[256,768]{1,0:T(8,128)(2,1)S(1)} collective-permute-done((bf16[256,768]{1,0:T(8,128)(2,1)S(1)}, bf16[256,768]{1,0:T(8,128)(2,1)S(1)}, u32[]{:S(2)}, u32[]{:S(2)}) %collective-permute-start.124) | collective-permute-done | bytes 393248 | tf_op jit(solution)/shard_map/ppermute | solution.py:443
  1729.0 9.8 collective-permute-done.171
  1746.4 5.5 fusion.45
  1767.4 38.7 %collective-permute-done.136 = bf16[2,24,2304]{2,1,0:T(8,128)(2,1)S(1)} collective-permute-done((bf16[2,24,2304]{2,1,0:T(8,128)(2,1)S(1)}, bf16[2,24,2304]{2,1,0:T(8,128)(2,1)S(1)}, u32[]{:S(2)}, u32[]{:S(2)}) %collective-permute-start.136) | collective-permute-done | bytes 221216 | tf_op jit(solution)/shard_map/ppermute | solution.py:443
  1819.9 7.6 collective-permute-done.164
  1828.4 8.9 collective-permute-done.129
  (972 shorter events, 422.4 us)
Async XLA Ops:
  1.9 30.5 %collective-permute-start = (s32[2,256]{1,0:T(2,128)}, s32[2,256]{1,0:T(2,128)}, u32[]{:S(2)}, u32[]{:S(2)}) collective-permute-start(s32[2,256]{1,0:T(2,128)} %get-tuple-element.133), channel_id=1, source_target_pairs={{0,2},{1,3},{6,4},{7,5},{8,10},{9,11},{14,12},{15,13},{16,18},{17,... | collective-permute-start | bytes 6152 | tf_op jit(solution)/shard_map/ppermute | solution.py:443
  11.6 37.1 %collective-permute-start.27 = (bf16[24,768]{1,0:T(8,128)(2,1)}, bf16[24,768]{1,0:T(8,128)(2,1)}, u32[]{:S(2)}, u32[]{:S(2)}) collective-permute-start(bf16[24,768]{1,0:T(8,128)(2,1)} %dynamic-slice_bitcast_fusion.16), channel_id=1, source_target_pairs={{0,2},{1,3},{6,4},{7,5},{8,10},{9,11},{14,12},{15,13},{16,18},{17,... | collective-permute-start | bytes 110600 | tf_op jit(solution)/shard_map/ppermute | solution.py:443
  16.6 32.7 %collective-permute-start.73 = (bf16[24,768]{1,0:T(8,128)(2,1)}, bf16[24,768]{1,0:T(8,128)(2,1)}, u32[]{:S(2)}, u32[]{:S(2)}) collective-permute-start(bf16[24,768]{1,0:T(8,128)(2,1)} %dynamic-slice_bitcast_fusion.15), channel_id=1, source_target_pairs={{0,2},{1,3},{6,4},{7,5},{8,10},{9,11},{14,12},{15,13},{16,18},{17,... | collective-permute-start | bytes 110600 | tf_op jit(solution)/shard_map/ppermute | solution.py:443
  90.6 31.4 %collective-permute-start.51 = (bf16[96,768]{1,0:T(8,128)(2,1)}, bf16[96,768]{1,0:T(8,128)(2,1)}, u32[]{:S(2)}, u32[]{:S(2)}) collective-permute-start(bf16[96,768]{1,0:T(8,128)(2,1)} %collective-permute-done.49), channel_id=1, source_target_pairs={{2,4},{3,5},{4,2},{5,3},{10,12},{11,13},{12,10},{13,11},{18,20},{1... | collective-permute-start | bytes 442376 | tf_op jit(solution)/shard_map/ppermute | solution.py:443
  92.0 31.4 %collective-permute-start.40 = (bf16[24,3072]{1,0:T(8,128)(2,1)}, bf16[24,3072]{1,0:T(8,128)(2,1)}, u32[]{:S(2)}, u32[]{:S(2)}) collective-permute-start(bf16[24,3072]{1,0:T(8,128)(2,1)} %collective-permute-done.38), channel_id=1, source_target_pairs={{2,4},{3,5},{4,2},{5,3},{10,12},{11,13},{12,10},{13,11},{18,20},{1... | collective-permute-start | bytes 442376 | tf_op jit(solution)/shard_map/ppermute | solution.py:443
  96.6 59.1 %collective-permute-start.110 = (bf16[256,768]{1,0:T(8,128)(2,1)}, bf16[256,768]{1,0:T(8,128)(2,1)}, u32[]{:S(2)}, u32[]{:S(2)}) collective-permute-start(bf16[256,768]{1,0:T(8,128)(2,1)} %refs_0_.1), channel_id=1, source_target_pairs={{0,2},{1,3},{6,4},{7,5},{8,10},{9,11},{14,12},{15,13},{16,18},{17,... | collective-permute-start | bytes 1179656 | tf_op jit(solution)/shard_map/ppermute | solution.py:443
  119.4 34.2 %collective-permute-start.86 = (bf16[24,3072]{1,0:T(8,128)(2,1)}, bf16[24,3072]{1,0:T(8,128)(2,1)}, u32[]{:S(2)}, u32[]{:S(2)}) collective-permute-start(bf16[24,3072]{1,0:T(8,128)(2,1)} %collective-permute-done.84), channel_id=1, source_target_pairs={{2,4},{3,5},{4,2},{5,3},{10,12},{11,13},{12,10},{13,11},{18,20},{1... | collective-permute-start | bytes 442376 | tf_op jit(solution)/shard_map/ppermute | solution.py:443
  206.5 84.0 %collective-permute-start.9 = (bf16[264,768]{1,0:T(8,128)(2,1)}, bf16[264,768]{1,0:T(8,128)(2,1)}, u32[]{:S(2)}, u32[]{:S(2)}) collective-permute-start(bf16[264,768]{1,0:T(8,128)(2,1)} %collective-permute-done.7.refs_1_), channel_id=1, source_target_pairs={{2,4},{3,5},{4,2},{5,3},{10,12},{11,13},{12,10},{13,11},{18,20},{1... | collective-permute-start | bytes 1216520 | tf_op jit(solution)/shard_map/ppermute | solution.py:443
  208.0 83.3 %collective-permute-start.11 = (bf16[264,768]{1,0:T(8,128)(2,1)}, bf16[264,768]{1,0:T(8,128)(2,1)}, u32[]{:S(2)}, u32[]{:S(2)}) collective-permute-start(bf16[264,768]{1,0:T(8,128)(2,1)} %collective-permute-done.7.refs_1_), channel_id=1, source_target_pairs={{2,3},{3,2},{4,5},{5,4},{10,11},{11,10},{12,13},{13,12},{18,19},{1... | collective-permute-start | bytes 1216520 | tf_op jit(solution)/shard_map/ppermute | solution.py:443
  209.4 83.3 %collective-permute-start.12 = (bf16[264,768]{1,0:T(8,128)(2,1)}, bf16[264,768]{1,0:T(8,128)(2,1)}, u32[]{:S(2)}, u32[]{:S(2)}) collective-permute-start(bf16[264,768]{1,0:T(8,128)(2,1)} %copy-done.97), channel_id=1, source_target_pairs={{2,3},{3,2},{4,5},{5,4},{10,11},{11,10},{12,13},{13,12},{18,19},{1... | collective-permute-start | bytes 1216520 | tf_op jit(solution)/shard_map/ppermute | solution.py:443
  211.5 82.5 %collective-permute-start.19 = (bf16[3,24,2304]{2,1,0:T(8,128)(2,1)}, bf16[3,24,2304]{2,1,0:T(8,128)(2,1)}, u32[]{:S(2)}, u32[]{:S(2)}) collective-permute-start(bf16[3,24,2304]{2,1,0:T(8,128)(2,1)} %copy-done.104), channel_id=1, source_target_pairs={{2,18},{3,19},{4,20},{5,21},{10,26},{11,27},{12,28},{13,29},{18,2}... | collective-permute-start | bytes 995336 | tf_op jit(solution)/shard_map/ppermute | solution.py:443
  212.9 81.8 %collective-permute-start.22 = (bf16[3,24,2304]{2,1,0:T(8,128)(2,1)}, bf16[3,24,2304]{2,1,0:T(8,128)(2,1)}, u32[]{:S(2)}, u32[]{:S(2)}) collective-permute-start(bf16[3,24,2304]{2,1,0:T(8,128)(2,1)} %copy-done.104), channel_id=1, source_target_pairs={{2,3},{3,2},{4,5},{5,4},{10,11},{11,10},{12,13},{13,12},{18,19},{1... | collective-permute-start | bytes 995336 | tf_op jit(solution)/shard_map/ppermute | solution.py:443
  305.5 121.4 %collective-permute-start.57 = (bf16[3,96,768]{2,1,0:T(8,128)(2,1)S(1)}, bf16[3,96,768]{2,1,0:T(8,128)(2,1)}, u32[]{:S(2)}, u32[]{:S(2)}) collective-permute-start(bf16[3,96,768]{2,1,0:T(8,128)(2,1)S(1)} %collective-permute-done.52.refs_2_), channel_id=1, source_target_pairs={{2,3},{3,2},{4,5},{5,4},{10,11},{11,10},{12,13},{13,12},{18,19},{1... | collective-permute-start | bytes 1327112 | tf_op jit(solution)/shard_map/ppermute | solution.py:443
  307.0 121.4 %collective-permute-start.43 = (bf16[3,24,3072]{2,1,0:T(8,128)(2,1)S(1)}, bf16[3,24,3072]{2,1,0:T(8,128)(2,1)S(1)}, u32[]{:S(2)}, u32[]{:S(2)}) collective-permute-start(bf16[3,24,3072]{2,1,0:T(8,128)(2,1)S(1)} %collective-permute-done.42.refs_3_), channel_id=1, source_target_pairs={{2,10},{3,11},{4,12},{5,13},{10,2},{11,3},{12,4},{13,5},{18,26},{1... | collective-permute-start | bytes 1327112 | tf_op jit(solution)/shard_map/ppermute | solution.py:443
  307.7 121.4 %collective-permute-start.47 = (bf16[3,24,3072]{2,1,0:T(8,128)(2,1)S(1)}, bf16[3,24,3072]{2,1,0:T(8,128)(2,1)}, u32[]{:S(2)}, u32[]{:S(2)}) collective-permute-start(bf16[3,24,3072]{2,1,0:T(8,128)(2,1)S(1)} %collective-permute-done.42.refs_3_), channel_id=1, source_target_pairs={{2,3},{3,2},{4,5},{5,4},{10,11},{11,10},{12,13},{13,12},{18,19},{1... | collective-permute-start | bytes 1327112 | tf_op jit(solution)/shard_map/ppermute | solution.py:443
  309.2 118.5 %collective-permute-start.58 = (bf16[3,96,768]{2,1,0:T(8,128)(2,1)S(1)}, bf16[3,96,768]{2,1,0:T(8,128)(2,1)}, u32[]{:S(2)}, u32[]{:S(2)}) collective-permute-start(bf16[3,96,768]{2,1,0:T(8,128)(2,1)S(1)} %collective-permute-done.53.refs_3_), channel_id=1, source_target_pairs={{2,3},{3,2},{4,5},{5,4},{10,11},{11,10},{12,13},{13,12},{18,19},{1... | collective-permute-start | bytes 1327112 | tf_op jit(solution)/shard_map/ppermute | solution.py:443
  310.6 119.9 %collective-permute-start.46 = (bf16[3,24,3072]{2,1,0:T(8,128)(2,1)}, bf16[3,24,3072]{2,1,0:T(8,128)(2,1)}, u32[]{:S(2)}, u32[]{:S(2)}) collective-permute-start(bf16[3,24,3072]{2,1,0:T(8,128)(2,1)} %collective-permute-done.41.refs_2_), channel_id=1, source_target_pairs={{2,3},{3,2},{4,5},{5,4},{10,11},{11,10},{12,13},{13,12},{18,19},{1... | collective-permute-start | bytes 1327112 | tf_op jit(solution)/shard_map/ppermute | solution.py:443
  438.8 699.2 %collective-permute-start.26 = (bf16[512,768]{1,0:T(8,128)(2,1)S(1)}, bf16[512,768]{1,0:T(8,128)(2,1)S(1)}, u32[]{:S(2)}, u32[]{:S(2)}) collective-permute-start(bf16[512,768]{1,0:T(8,128)(2,1)S(1)} %get-tuple-element.98.va_ref), channel_id=1, source_target_pairs={{2,3},{3,2},{4,5},{5,4},{10,11},{11,10},{12,13},{13,12},{18,19},{1... | collective-permute-start | bytes 2359304 | tf_op jit(solution)/shard_map/ppermute | solution.py:443
  439.6 698.5 %collective-permute-start.25 = (bf16[512,768]{1,0:T(8,128)(2,1)S(1)}, bf16[512,768]{1,0:T(8,128)(2,1)S(1)}, u32[]{:S(2)}, u32[]{:S(2)}) collective-permute-start(bf16[512,768]{1,0:T(8,128)(2,1)S(1)} %slice.664.ka_ref), channel_id=1, source_target_pairs={{2,3},{3,2},{4,5},{5,4},{10,11},{11,10},{12,13},{13,12},{18,19},{1... | collective-permute-start | bytes 2359304 | tf_op jit(solution)/shard_map/ppermute | solution.py:443
  440.9 552.1 %collective-permute-start.104 = (bf16[3,96,768]{2,1,0:T(8,128)(2,1)}, bf16[3,96,768]{2,1,0:T(8,128)(2,1)}, u32[]{:S(2)}, u32[]{:S(2)}) collective-permute-start(bf16[3,96,768]{2,1,0:T(8,128)(2,1)} %collective-permute-done.99.refs_3_), channel_id=1, source_target_pairs={{2,3},{3,2},{4,5},{5,4},{10,11},{11,10},{12,13},{13,12},{18,19},{1... | collective-permute-start | bytes 1327112 | tf_op jit(solution)/shard_map/ppermute | solution.py:443
  442.3 550.7 %collective-permute-start.103 = (bf16[3,96,768]{2,1,0:T(8,128)(2,1)}, bf16[3,96,768]{2,1,0:T(8,128)(2,1)}, u32[]{:S(2)}, u32[]{:S(2)}) collective-permute-start(bf16[3,96,768]{2,1,0:T(8,128)(2,1)} %collective-permute-done.98.refs_2_), channel_id=1, source_target_pairs={{2,3},{3,2},{4,5},{5,4},{10,11},{11,10},{12,13},{13,12},{18,19},{1... | collective-permute-start | bytes 1327112 | tf_op jit(solution)/shard_map/ppermute | solution.py:443
  444.6 548.5 %collective-permute-start.105 = (bf16[3,96,768]{2,1,0:T(8,128)(2,1)}, bf16[3,96,768]{2,1,0:T(8,128)(2,1)}, u32[]{:S(2)}, u32[]{:S(2)}) collective-permute-start(bf16[3,96,768]{2,1,0:T(8,128)(2,1)} %collective-permute-done.100.refs_4_), channel_id=1, source_target_pairs={{2,3},{3,2},{4,5},{5,4},{10,11},{11,10},{12,13},{13,12},{18,19},{1... | collective-permute-start | bytes 1327112 | tf_op jit(solution)/shard_map/ppermute | solution.py:443
  1200.0 36.8 %collective-permute-start.72 = (bf16[512,768]{1,0:T(8,128)(2,1)}, bf16[512,768]{1,0:T(8,128)(2,1)}, u32[]{:S(2)}, u32[]{:S(2)}) collective-permute-start(bf16[512,768]{1,0:T(8,128)(2,1)} %get-tuple-element.96.va_ref), channel_id=1, source_target_pairs={{2,3},{3,2},{4,5},{5,4},{10,11},{11,10},{12,13},{13,12},{18,19},{1... | collective-permute-start | bytes 2359304 | tf_op jit(solution)/shard_map/ppermute | solution.py:443
  1201.7 35.2 %collective-permute-start.71 = (bf16[512,768]{1,0:T(8,128)(2,1)}, bf16[512,768]{1,0:T(8,128)(2,1)}, u32[]{:S(2)}, u32[]{:S(2)}) collective-permute-start(bf16[512,768]{1,0:T(8,128)(2,1)} %slice.663.ka_ref), channel_id=1, source_target_pairs={{2,3},{3,2},{4,5},{5,4},{10,11},{11,10},{12,13},{13,12},{18,19},{1... | collective-permute-start | bytes 2359304 | tf_op jit(solution)/shard_map/ppermute | solution.py:443
  1222.0 344.5 %collective-permute-start.167 = (bf16[512,1536]{0,1:T(8,128)(2,1)}, bf16[512,1536]{0,1:T(8,128)(2,1)}, u32[]{:S(2)}, u32[]{:S(2)}) collective-permute-start(bf16[512,1536]{0,1:T(8,128)(2,1)} %bitcast.353), channel_id=1, source_target_pairs={{2,3},{3,2},{4,5},{5,4},{10,11},{11,10},{12,13},{13,12},{18,19},{1... | collective-permute-start | bytes 4718600 | tf_op jit(solution)/shard_map/ppermute | solution.py:443
  1312.2 111.8 %collective-permute-start.147 = (bf16[512,768]{1,0:T(8,128)(2,1)}, bf16[512,768]{1,0:T(8,128)(2,1)}, u32[]{:S(2)}, u32[]{:S(2)}) collective-permute-start(bf16[512,768]{1,0:T(8,128)(2,1)} %get-tuple-element.78), channel_id=1, source_target_pairs={{2,3},{3,2},{4,5},{5,4},{10,11},{11,10},{12,13},{13,12},{18,19},{1... | collective-permute-start | bytes 2359304 | tf_op jit(solution)/shard_map/ppermute | solution.py:443
  1334.3 37.0 %collective-permute-start.118 = (bf16[512,768]{1,0:T(8,128)(2,1)}, bf16[512,768]{1,0:T(8,128)(2,1)}, u32[]{:S(2)}, u32[]{:S(2)}) collective-permute-start(bf16[512,768]{1,0:T(8,128)(2,1)} %get-tuple-element.33), channel_id=1, source_target_pairs={{2,3},{3,2},{4,5},{5,4},{10,11},{11,10},{12,13},{13,12},{18,19},{1... | collective-permute-start | bytes 2359304 | tf_op jit(solution)/shard_map/ppermute | solution.py:443
  1337.2 36.9 %collective-permute-start.117 = (bf16[512,768]{1,0:T(8,128)(2,1)}, bf16[512,768]{1,0:T(8,128)(2,1)}, u32[]{:S(2)}, u32[]{:S(2)}) collective-permute-start(bf16[512,768]{1,0:T(8,128)(2,1)} %get-tuple-element.31), channel_id=1, source_target_pairs={{2,3},{3,2},{4,5},{5,4},{10,11},{11,10},{12,13},{13,12},{18,19},{1... | collective-permute-start | bytes 2359304 | tf_op jit(solution)/shard_map/ppermute | solution.py:443
  1356.3 225.9 %collective-permute-start.174 = (bf16[512,1536]{0,1:T(8,128)(2,1)}, bf16[512,1536]{0,1:T(8,128)(2,1)}, u32[]{:S(2)}, u32[]{:S(2)}) collective-permute-start(bf16[512,1536]{0,1:T(8,128)(2,1)} %bitcast.355), channel_id=1, source_target_pairs={{2,3},{3,2},{4,5},{5,4},{10,11},{11,10},{12,13},{13,12},{18,19},{1... | collective-permute-start | bytes 4718600 | tf_op jit(solution)/shard_map/ppermute | solution.py:443
  1371.3 51.1 %collective-permute-start.146 = (bf16[512,384]{1,0:T(8,128)(2,1)S(1)}, bf16[512,384]{1,0:T(8,128)(2,1)S(1)}, u32[]{:S(2)}, u32[]{:S(2)}) collective-permute-start(bf16[512,384]{1,0:T(8,128)(2,1)S(1)} %convolution_convert_fusion.8), channel_id=1, source_target_pairs={{2,3},{3,2},{4,5},{5,4},{10,11},{11,10},{12,13},{13,12},{18,19},{1... | collective-permute-start | bytes 1179656 | tf_op jit(solution)/shard_map/ppermute | solution.py:443
  1374.1 201.0 %collective-permute-start.106 = (bf16[512,768]{1,0:T(8,128)(2,1)S(1)}, bf16[512,768]{1,0:T(8,128)(2,1)}, u32[]{:S(2)}, u32[]{:S(2)}) collective-permute-start(bf16[512,768]{1,0:T(8,128)(2,1)S(1)} %copy-done.23), channel_id=1, source_target_pairs={{2,4},{3,5},{4,2},{5,3},{10,12},{11,13},{12,10},{13,11},{18,20},{1... | collective-permute-start | bytes 2359304 | tf_op jit(solution)/shard_map/ppermute | solution.py:443
  1422.4 136.3 %collective-permute-start.120 = (bf16[512,768]{1,0:T(8,128)(2,1)}, bf16[512,768]{1,0:T(8,128)(2,1)}, u32[]{:S(2)}, u32[]{:S(2)}) collective-permute-start(bf16[512,768]{1,0:T(8,128)(2,1)} %get-tuple-element.40), channel_id=1, source_target_pairs={{2,3},{3,2},{4,5},{5,4},{10,11},{11,10},{12,13},{13,12},{18,19},{1... | collective-permute-start | bytes 2359304 | tf_op jit(solution)/shard_map/ppermute | solution.py:443
  1430.0 118.2 %collective-permute-start.150 = (bf16[2,24,768]{2,1,0:T(8,128)(2,1)S(1)}, bf16[2,24,768]{2,1,0:T(8,128)(2,1)S(1)}, u32[]{:S(2)}, u32[]{:S(2)}) collective-permute-start(bf16[2,24,768]{2,1,0:T(8,128)(2,1)S(1)} %select_bitcast_fusion.6), channel_id=1, source_target_pairs={{2,0},{3,1},{4,6},{5,7},{10,8},{11,9},{12,14},{13,15},{18,16},{19,... | collective-permute-start | bytes 221192 | tf_op jit(solution)/shard_map/ppermute | solution.py:443
  1572.7 98.0 %collective-permute-start.161 = (bf16[512,3072]{1,0:T(8,128)(2,1)}, bf16[512,3072]{1,0:T(8,128)(2,1)}, u32[]{:S(2)}, u32[]{:S(2)}) collective-permute-start(bf16[512,3072]{1,0:T(8,128)(2,1)} %get-tuple-element.74), channel_id=1, source_target_pairs={{2,3},{3,2},{4,5},{5,4},{10,11},{11,10},{12,13},{13,12},{18,19},{1... | collective-permute-start | bytes 9437192 | tf_op jit(solution)/shard_map/ppermute | solution.py:443
  1590.9 70.0 %collective-permute-start.169 = (bf16[4,2,96,768]{3,2,1,0:T(8,128)(2,1)S(1)}, bf16[4,2,96,768]{3,2,1,0:T(8,128)(2,1)}, u32[]{:S(2)}, u32[]{:S(2)}) collective-permute-start(bf16[4,2,96,768]{3,2,1,0:T(8,128)(2,1)S(1)} %dynamic-slice_bitcast_fusion.1), channel_id=1, source_target_pairs={{2,10},{3,11},{4,12},{5,13},{10,2},{11,3},{12,4},{13,5},{18,26},{1... | collective-permute-start | bytes 3538952 | tf_op jit(solution)/shard_map/ppermute | solution.py:443
  1593.5 70.6 %collective-permute-start.176 = (bf16[4,2,96,768]{3,2,1,0:T(8,128)(2,1)}, bf16[4,2,96,768]{3,2,1,0:T(8,128)(2,1)S(1)}, u32[]{:S(2)}, u32[]{:S(2)}) collective-permute-start(bf16[4,2,96,768]{3,2,1,0:T(8,128)(2,1)} %dynamic-slice_bitcast_fusion), channel_id=1, source_target_pairs={{2,18},{3,19},{4,20},{5,21},{10,26},{11,27},{12,28},{13,29},{18,2}... | collective-permute-start | bytes 3538952 | tf_op jit(solution)/shard_map/ppermute | solution.py:443
  1600.1 52.7 %collective-permute-start.109 = (bf16[256,768]{1,0:T(8,128)(2,1)S(1)}, bf16[256,768]{1,0:T(8,128)(2,1)S(1)}, u32[]{:S(2)}, u32[]{:S(2)}) collective-permute-start(bf16[256,768]{1,0:T(8,128)(2,1)S(1)} %slice.504), channel_id=1, source_target_pairs={{2,0},{3,1},{4,6},{5,7},{10,8},{11,9},{12,14},{13,15},{18,16},{19,... | collective-permute-start | bytes 1179656 | tf_op jit(solution)/shard_map/ppermute | solution.py:443
  1605.0 36.9 %collective-permute-start.143 = (bf16[2,24,768]{2,1,0:T(8,128)(2,1)S(1)}, bf16[2,24,768]{2,1,0:T(8,128)(2,1)S(1)}, u32[]{:S(2)}, u32[]{:S(2)}) collective-permute-start(bf16[2,24,768]{2,1,0:T(8,128)(2,1)S(1)} %select_bitcast_fusion.7), channel_id=1, source_target_pairs={{2,0},{3,1},{4,6},{5,7},{10,8},{11,9},{12,14},{13,15},{18,16},{19,... | collective-permute-start | bytes 221192 | tf_op jit(solution)/shard_map/ppermute | solution.py:443
  1657.2 35.2 %collective-permute-start.133 = (bf16[512,2304]{1,0:T(8,128)(2,1)}, bf16[512,2304]{1,0:T(8,128)(2,1)}, u32[]{:S(2)}, u32[]{:S(2)}) collective-permute-start(bf16[512,2304]{1,0:T(8,128)(2,1)} %pad_maximum_fusion), channel_id=1, source_target_pairs={{2,3},{3,2},{4,5},{5,4},{10,11},{11,10},{12,13},{13,12},{18,19},{1... | collective-permute-start | bytes 7077896 | tf_op jit(solution)/shard_map/ppermute | solution.py:443
  1670.7 74.8 %collective-permute-start.154 = (bf16[512,3072]{1,0:T(8,128)(2,1)}, bf16[512,3072]{1,0:T(8,128)(2,1)}, u32[]{:S(2)}, u32[]{:S(2)}) collective-permute-start(bf16[512,3072]{1,0:T(8,128)(2,1)} %get-tuple-element.83), channel_id=1, source_target_pairs={{2,3},{3,2},{4,5},{5,4},{10,11},{11,10},{12,13},{13,12},{18,19},{1... | collective-permute-start | bytes 9437192 | tf_op jit(solution)/shard_map/ppermute | solution.py:443
  1680.0 74.3 %collective-permute-start.125 = (bf16[512,384]{1,0:T(8,128)(2,1)}, bf16[512,384]{1,0:T(8,128)(2,1)}, u32[]{:S(2)}, u32[]{:S(2)}) collective-permute-start(bf16[512,384]{1,0:T(8,128)(2,1)} %convolution_convert_fusion.14), channel_id=1, source_target_pairs={{2,3},{3,2},{4,5},{5,4},{10,11},{11,10},{12,13},{13,12},{18,19},{1... | collective-permute-start | bytes 1179656 | tf_op jit(solution)/shard_map/ppermute | solution.py:443
  1682.3 73.3 %collective-permute-start.126 = (bf16[512,2304]{1,0:T(8,128)(2,1)}, bf16[512,2304]{1,0:T(8,128)(2,1)}, u32[]{:S(2)}, u32[]{:S(2)}) collective-permute-start(bf16[512,2304]{1,0:T(8,128)(2,1)} %pad_maximum_fusion.1), channel_id=1, source_target_pairs={{2,3},{3,2},{4,5},{5,4},{10,11},{11,10},{12,13},{13,12},{18,19},{1... | collective-permute-start | bytes 7077896 | tf_op jit(solution)/shard_map/ppermute | solution.py:443
  1697.0 29.7 %collective-permute-start.124 = (bf16[256,768]{1,0:T(8,128)(2,1)S(1)}, bf16[256,768]{1,0:T(8,128)(2,1)S(1)}, u32[]{:S(2)}, u32[]{:S(2)}) collective-permute-start(bf16[256,768]{1,0:T(8,128)(2,1)S(1)} %slice.506), channel_id=1, source_target_pairs={{2,0},{3,1},{4,6},{5,7},{10,8},{11,9},{12,14},{13,15},{18,16},{19,... | collective-permute-start | bytes 1179656 | tf_op jit(solution)/shard_map/ppermute | solution.py:443
  1698.6 40.2 %collective-permute-start.171 = (bf16[2,96,768]{2,1,0:T(8,128)(2,1)S(1)}, bf16[2,96,768]{2,1,0:T(8,128)(2,1)S(1)}, u32[]{:S(2)}, u32[]{:S(2)}) collective-permute-start(bf16[2,96,768]{2,1,0:T(8,128)(2,1)S(1)} %select_bitcast_fusion.1), channel_id=1, source_target_pairs={{2,0},{3,1},{4,6},{5,7},{10,8},{11,9},{12,14},{13,15},{18,16},{19,... | collective-permute-start | bytes 884744 | tf_op jit(solution)/shard_map/ppermute | solution.py:443
  1755.6 57.5 %collective-permute-start.155 = (bf16[4,2,24,3072]{3,2,1,0:T(8,128)(2,1)S(1)}, bf16[4,2,24,3072]{3,2,1,0:T(8,128)(2,1)S(1)}, u32[]{:S(2)}, u32[]{:S(2)}) collective-permute-start(bf16[4,2,24,3072]{3,2,1,0:T(8,128)(2,1)S(1)} %dynamic-slice_bitcast_fusion.3), channel_id=1, source_target_pairs={{2,18},{3,19},{4,20},{5,21},{10,26},{11,27},{12,28},{13,29},{18,2}... | collective-permute-start | bytes 3538952 | tf_op jit(solution)/shard_map/ppermute | solution.py:443
  1760.3 46.5 %collective-permute-start.127 = (bf16[4,2,24,2304]{3,2,1,0:T(8,128)(2,1)S(1)}, bf16[4,2,24,2304]{3,2,1,0:T(8,128)(2,1)S(1)}, u32[]{:S(2)}, u32[]{:S(2)}) collective-permute-start(bf16[4,2,24,2304]{3,2,1,0:T(8,128)(2,1)S(1)} %dynamic-slice_bitcast_fusion.5), channel_id=1, source_target_pairs={{2,10},{3,11},{4,12},{5,13},{10,2},{11,3},{12,4},{13,5},{18,26},{1... | collective-permute-start | bytes 2654216 | tf_op jit(solution)/shard_map/ppermute | solution.py:443
  1765.4 40.8 %collective-permute-start.136 = (bf16[2,24,2304]{2,1,0:T(8,128)(2,1)S(1)}, bf16[2,24,2304]{2,1,0:T(8,128)(2,1)S(1)}, u32[]{:S(2)}, u32[]{:S(2)}) collective-permute-start(bf16[2,24,2304]{2,1,0:T(8,128)(2,1)S(1)} %select_bitcast_fusion.4), channel_id=1, source_target_pairs={{2,0},{3,1},{4,6},{5,7},{10,8},{11,9},{12,14},{13,15},{18,16},{19,... | collective-permute-start | bytes 663560 | tf_op jit(solution)/shard_map/ppermute | solution.py:443
  1766.7 41.1 %collective-permute-start.163 = (bf16[2,2,24,3072]{3,2,1,0:T(8,128)(2,1)S(1)}, bf16[2,2,24,3072]{3,2,1,0:T(8,128)(2,1)S(1)}, u32[]{:S(2)}, u32[]{:S(2)}) collective-permute-start(bf16[2,2,24,3072]{3,2,1,0:T(8,128)(2,1)S(1)} %broadcast_select_fusion.2), channel_id=1, source_target_pairs={{2,4},{3,5},{4,2},{5,3},{10,12},{11,13},{12,10},{13,11},{18,20},{1... | collective-permute-start | bytes 1769480 | tf_op jit(solution)/shard_map/ppermute | solution.py:443
  (316 other events, 5440.1 us)

commit v2 on v0

--- a/solution.py
+++ b/solution.py
@@ -1,6 +1,10 @@
+import functools
+
 import jax
 import jax.numpy as jnp
 from jax import lax
+from jax.experimental import pallas as pl
+from jax.experimental.pallas import tpu as pltpu
 from jax.sharding import PartitionSpec as P
 
 HEADS = 12
@@ -411,6 +415,949 @@
     return (output, input_grad, entry_grad, exit_grad, expand_grad, shrink_grad, vector_grad)
 
 
+EDGE = (0, 1, 6, 7)
+CORE = (2, 3, 4, 5)
+ALL = tuple(range(8))
+BOTH = ("rep", "shard")
+UNIT = 24
+
+
+def routes(rep_flip, shard_flip, shards):
+    return [
+        (rep * 8 + shard, (rep ^ rep_flip) * 8 + (shard ^ shard_flip))
+        for rep in range(4)
+        for shard in shards
+    ]
+
+
+TO_X = routes(1, 0, ALL)
+TO_Y = routes(2, 0, ALL)
+TO_TWIN = routes(0, 1, ALL)
+TO_SIDE = routes(0, 2, ALL)
+TO_MID = routes(0, 6, CORE)
+
+
+def send(value, route):
+    return lax.ppermute(value, BOTH, route)
+
+
+def low(value):
+    return value.astype(jnp.bfloat16)
+
+
+def wide(value):
+    return value.astype(jnp.float32)
+
+
+VMEM = pl.BlockSpec(memory_space=pltpu.VMEM)
+SMEM = pl.BlockSpec(memory_space=pltpu.SMEM)
+LIMIT = pltpu.CompilerParams(vmem_limit_bytes=60 * 1024 * 1024)
+
+
+def shaped(shape, kind=jnp.bfloat16):
+    return jax.ShapeDtypeStruct(shape, kind)
+
+
+def nt(left, right):
+    return lax.dot_general(left, right, (((1,), (1,)), ((), ())), preferred_element_type=jnp.float32)
+
+
+def nn(left, right):
+    return lax.dot_general(left, right, (((1,), (0,)), ((), ())), preferred_element_type=jnp.float32)
+
+
+def fixed(*shape):
+    return pl.BlockSpec(shape, lambda step: (0,) * len(shape))
+
+
+def gather_kernel(ids_ref, want_ref, *refs):
+    out_ref = refs[-1]
+    want = want_ref[...]
+    total = None
+    index = 0
+    for piece_ref in refs[:-1]:
+        for slot in range(piece_ref.shape[0]):
+            ids = ids_ref[index]
+            hit = low(wide(want == ids))
+            part = nn(hit, piece_ref[slot, 0 : ids.shape[1], :])
+            total = part if total is None else total + part
+            index += 1
+    out_ref[...] = low(total)
+
+
+def gather_rows(pieces, ids, want):
+    return pl.pallas_call(
+        gather_kernel,
+        out_shape=shaped((want.shape[0], pieces[0].shape[2])),
+        in_specs=[VMEM] * (2 + len(pieces)),
+        out_specs=VMEM,
+        compiler_params=LIMIT,
+        name="gather_rows",
+    )(ids, want, *pieces)
+
+
+def assemble_kernel(where_ref, *refs):
+    out_ref = refs[10]
+    depth, rep, twin = where_ref[0], where_ref[1], where_ref[2]
+    for side in range(2):
+        own, first, over_x, over_y, over_d = refs[side * 5 : side * 5 + 5]
+        core = twin ^ side
+        for row in range(4):
+            out_ref[depth, core, row] = own[row]
+        for slot, flip in enumerate((1, 3, 2)):
+            level = depth ^ flip
+            for piece, bits in ((first, 0), (over_x, 1), (over_y, 2), (over_d, 3)):
+                out_ref[level, core, rep ^ bits] = piece[slot]
+
+
+def assemble(where, parts, start, by_rows):
+    def part_spec(part):
+        return pl.BlockSpec(
+            (part.shape[0], None) + part.shape[2:],
+            lambda unit, where_ref: (0, start + unit, 0, 0),
+        )
+
+    width = parts[0].shape[3]
+    if by_rows:
+        shape = (4, 2, 4, 4, UNIT, width)
+        spec = pl.BlockSpec(
+            (4, 2, 4, None, UNIT, width), lambda unit, where_ref: (0, 0, 0, unit, 0, 0)
+        )
+    else:
+        shape = (4, 4, 2, 4, UNIT, width)
+        spec = pl.BlockSpec(
+            (None, 4, 2, 4, UNIT, width), lambda unit, where_ref: (unit, 0, 0, 0, 0, 0)
+        )
+    result = pl.pallas_call(
+        assemble_kernel,
+        grid_spec=pltpu.PrefetchScalarGridSpec(
+            num_scalar_prefetch=1,
+            grid=(4,),
+            in_specs=[part_spec(part) for part in parts],
+            out_specs=spec,
+        ),
+        out_shape=shaped(shape),
+        compiler_params=LIMIT,
+        name="assemble",
+    )(where, *parts)
+    return result.reshape(4, 32 * UNIT, width)
+
+
+def pack_weights(entry, leaving, expand, shrink):
+    width = leaving.shape[1]
+
+    def by_columns(weight):
+        count = weight.shape[1] // width
+        return low(weight).reshape(4, UNIT, count, width).transpose(0, 2, 1, 3)
+
+    return (
+        jnp.concatenate([by_columns(entry), by_columns(leaving)], axis=1),
+        jnp.concatenate([by_columns(expand), low(shrink).reshape(4, 4, UNIT, width)], axis=1),
+    )
+
+
+def spread(own, near, middle, far):
+    units = own.shape[1]
+    first = jnp.stack([near, middle, far])
+    over_x = send(first, TO_X)
+    over_y = send(first, TO_Y)
+    half = units // 2
+    over_d = jnp.concatenate(
+        [send(over_x[:, :half], TO_Y), send(over_y[:, half:], TO_X)], axis=1
+    )
+    mine = (own, first, over_x, over_y, over_d)
+    return mine + tuple(send(item, TO_TWIN) for item in mine)
+
+
+def project_kernel(h_ref, w_ref, vec_ref, sel_ref, q_ref, kv_ref, mine_ref, theirs_ref):
+    unit = pl.program_id(0)
+    product = nn(h_ref[...], w_ref[...])
+
+    @pl.when(unit == 0)
+    def _():
+        q_ref[...] = low(product + vec_ref[0:1, :])
+        mine_ref[...] = low(nn(h_ref[...], sel_ref[0]))
+        theirs_ref[...] = low(nn(h_ref[...], sel_ref[1]))
+
+    @pl.when(unit == 1)
+    def _():
+        kv_ref[...] = low(product)
+
+    @pl.when(unit == 2)
+    def _():
+        kv_ref[...] = low(product + vec_ref[1:2, :])
+
+
+def project(hidden, weight, vec, sel):
+    rows, width = hidden.shape
+    return pl.pallas_call(
+        project_kernel,
+        grid=(3,),
+        in_specs=[
+            fixed(rows, width),
+            pl.BlockSpec((None, width, width), lambda unit: (unit, 0, 0)),
+            fixed(12, width),
+            fixed(2, width, width // 2),
+        ],
+        out_specs=[
+            fixed(rows, width),
+            pl.BlockSpec((None, rows, width), lambda unit: (jnp.maximum(unit - 1, 0), 0, 0)),
+            fixed(rows, width // 2),
+            fixed(rows, width // 2),
+        ],
+        out_shape=[
+            shaped((rows, width)),
+            shaped((2, rows, width)),
+            shaped((rows, width // 2)),
+            shaped((rows, width // 2)),
+        ],
+        compiler_params=LIMIT,
+        name="project",
+    )(hidden, weight, vec, sel)
+
+
+def attend_kernel(
+    q_ref, ka_ref, kb_ref, va_ref, vb_ref, code_ref, member_ref, o_ref, ot_ref, lse_ref, bias_ref
+):
+    half = q_ref.shape[0]
+
+    @pl.when(pl.program_id(0) == 0)
+    def _():
+        bias_ref[...] = jnp.where(code_ref[...] == member_ref[...], 0.0, NEG_FILL)
+
+    q = q_ref[...] * jnp.bfloat16(HEAD_DIM ** (-0.5))
+    lane = lax.broadcasted_iota(jnp.int32, q.shape, 1)
+    keys = (ka_ref[...], kb_ref[...])
+    values = (va_ref[...].T, vb_ref[...].T)
+    outs = []
+    for head in range(2):
+        q_head = jnp.where((lane >= HEAD_DIM) == (head == 1), q, jnp.bfloat16(0))
+        scores = [
+            nt(keys[side], q_head) + bias_ref[side * half : (side + 1) * half, :]
+            for side in range(2)
+        ]
+        top = jnp.maximum(
+            jnp.max(scores[0], axis=0, keepdims=True), jnp.max(scores[1], axis=0, keepdims=True)
+        )
+        total = None
+        mixed = None
+        for side in range(2):
+            expo = jnp.exp(scores[side] - top)
+            part = jnp.sum(expo, axis=0, keepdims=True)
+            value = values[side][head * HEAD_DIM : (head + 1) * HEAD_DIM, :]
+            product = nn(value, low(expo))
+            total = part if total is None else total + part
+            mixed = product if mixed is None else mixed + product
+        outs.append(mixed / total)
+        lse_ref[head : head + 1, :] = top + jnp.log(total)
+    joined = jnp.concatenate(outs, axis=0)
+    ot_ref[...] = joined
+    o_ref[...] = low(joined.T)
+
+
+def pair_specs(half):
+    column = pl.BlockSpec((half, 128), lambda pair: (0, pair))
+    key = pl.BlockSpec((None, half, 128), lambda pair: (0, 0, pair))
+    value = pl.BlockSpec((None, half, 128), lambda pair: (1, 0, pair))
+    turned = pl.BlockSpec((128, half), lambda pair: (pair, 0))
+    level = pl.BlockSpec((None, 2, half), lambda pair: (pair, 0, 0))
+    return column, key, value, turned, level
+
+
+def attend_fast(queries, kv, kv_twin, code, member):
+    half, width = queries.shape
+    column, key, value, turned, level = pair_specs(half)
+    return pl.pallas_call(
+        attend_kernel,
+        grid=(width // 128,),
+        in_specs=[column, key, key, value, value, fixed(2 * half, 1), fixed(1, half)],
+        out_specs=[column, turned, level],
+        out_shape=[
+            shaped((half, width)),
+            shaped((width, half), jnp.float32),
+            shaped((width // 128, 2, half), jnp.float32),
+        ],
+        scratch_shapes=[pltpu.VMEM((2 * half, half), jnp.float32)],
+        compiler_params=LIMIT,
+        name="attend_forward",
+    )(queries, kv, kv_twin, kv, kv_twin, code, member)
+
+
+def attend_back_kernel(
+    q_ref, g_ref, ka_ref, kb_ref, va_ref, vb_ref, ot_ref, lse_ref, code_ref, member_ref,
+    dq_ref, own_ref, twin_ref, bias_ref,
+):
+    half = q_ref.shape[0]
+
+    @pl.when(pl.program_id(0) == 0)
+    def _():
+        bias_ref[...] = jnp.where(code_ref[...] == member_ref[...], 0.0, NEG_FILL)
+
+    scale = HEAD_DIM ** (-0.5)
+    q = q_ref[...] * jnp.bfloat16(scale)
+    grad = g_ref[...]
+    lane = lax.broadcasted_iota(jnp.int32, q.shape, 1)
+    keys = (ka_ref[...], kb_ref[...])
+    turned = (keys[0].T, keys[1].T)
+    values = (va_ref[...], vb_ref[...])
+    product = ot_ref[...] * wide(grad).T
+    key_sums = [None, None]
+    value_sums = [None, None]
+    query_parts = []
+    for head in range(2):
+        rows = slice(head * HEAD_DIM, (head + 1) * HEAD_DIM)
+        chosen = (lane >= HEAD_DIM) == (head == 1)
+        q_head = jnp.where(chosen, q, jnp.bfloat16(0))
+        g_head = jnp.where(chosen, grad, jnp.bfloat16(0))
+        delta = jnp.sum(product[rows, :], axis=0, keepdims=True)
+        level = lse_ref[head : head + 1, :]
+        query_sum = None
+        for side in range(2):
+            scores = nt(keys[side], q_head) + bias_ref[side * half : (side + 1) * half, :]
+            prob = jnp.exp(scores - level)
+            slope = nt(values[side], g_head)
+            steep = low(prob * (slope - delta))
+            value_part = nn(low(prob), g_head)
+            key_part = nn(steep, q_head)
+            query_part = nn(turned[side][rows, :], steep)
+            value_sums[side] = value_part if head == 0 else value_sums[side] + value_part
+            key_sums[side] = key_part if head == 0 else key_sums[side] + key_part
+            query_sum = query_part if side == 0 else query_sum + query_part
+        query_parts.append(query_sum * scale)
+    dq_ref[...] = low(jnp.concatenate(query_parts, axis=0).T)
+    own_ref[0] = key_sums[0]
+    own_ref[1] = value_sums[0]
+    twin_ref[0] = low(key_sums[1])
+    twin_ref[1] = low(value_sums[1])
+
+
+def attend_back_fast(queries, grad, kv, kv_twin, ot, lse, code, member):
+    half, width = queries.shape
+    column, key, value, turned, level = pair_specs(half)
+    both = pl.BlockSpec((2, half, 128), lambda pair: (0, 0, pair))
+    return pl.pallas_call(
+        attend_back_kernel,
+        grid=(width // 128,),
+        in_specs=[column, column, key, key, value, value, turned, level]
+        + [fixed(2 * half, 1), fixed(1, half)],
+        out_specs=[column, both, both],
+        out_shape=[
+            shaped((half, width)),
+            shaped((2, half, width), jnp.float32),
+            shaped((2, half, width)),
+        ],
+        scratch_shapes=[pltpu.VMEM((2 * half, half), jnp.float32)],
+        compiler_params=LIMIT,
+        name="attend_backward",
+    )(queries, grad, kv, kv_twin, kv, kv_twin, ot, lse, code, member)
+
+
+def normal_parts(value):
+    scaled = value * 0.7071067811865476
+    size = jnp.abs(scaled)
+    square = size * size
+    t = 1.0 / (1.0 + 0.5 * size)
+    series = 0.17087277
+    for factor in (
+        -0.82215223, 1.48851587, -1.13520398, 0.27886807, -0.18628806,
+        0.09678418, 0.37409196, 1.00002368, -1.26551223,
+    ):
+        series = series * t + factor
+    tail = 0.5 * t * jnp.exp(series - square)
+    cumulative = jnp.where(value >= 0, 1.0 - tail, tail)
+    density = 0.3989422804014327 * jnp.exp(-square)
+    return cumulative, density
+
+
+def row_norm(resid):
+    offsets = resid - jnp.mean(resid, axis=-1, keepdims=True)
+    spread_of = jnp.mean(offsets * offsets, axis=-1, keepdims=True)
+    factor = lax.rsqrt(spread_of + 1e-05)
+    return offsets * factor, factor
+
+
+def post_kernel(
+    where_ref, o_ref, h_ref, wo_ref, up_ref, down_ref, vec_ref, sel_ref,
+    h_out, hl_out, n1_out, t1_out, n2_out, t2_out, slope_out,
+    om_out, ot_out, ym_out, yt_out, gm_out, gt_out,
+    y_ref, yl_ref, f_ref,
+):
+    step = pl.program_id(0)
+    half_width = om_out.shape[1]
+
+    @pl.when(step == 0)
+    def _():
+        attended = o_ref[...]
+        branch = nn(attended, wo_ref[...]) + vec_ref[2:3, :]
+        normed, factor = row_norm(wide(h_ref[...]) + branch)
+        middle = normed * vec_ref[3:4, :] + vec_ref[4:5, :]
+        n1_out[...] = normed
+        t1_out[...] = factor
+        y_ref[...] = middle
+        yl_ref[...] = low(middle)
+        om_out[...] = low(nn(attended, sel_ref[0]))
+        ot_out[...] = low(nn(attended, sel_ref[1]))
+        ym_out[...] = low(nn(yl_ref[...], sel_ref[0]))
+        yt_out[...] = low(nn(yl_ref[...], sel_ref[1]))
+
+    inner = nn(yl_ref[...], up_ref[...]) + vec_ref[pl.ds(8 + step, 1), :]
+    cumulative, density = normal_parts(inner)
+    slope_out[...] = low(cumulative + inner * density)
+    active = low(inner * cumulative)
+    first, second = active[:, :half_width], active[:, half_width:]
+    swap = where_ref[2] == 1
+    gm_out[...] = jnp.where(swap, second, first)
+    gt_out[...] = jnp.where(swap, first, second)
+    part = nn(active, down_ref[...])
+
+    @pl.when(step == 0)
+    def _():
+        f_ref[...] = part
+
+    @pl.when(step > 0)
+    def _():
+        f_ref[...] += part
+
+    @pl.when(step == 3)
+    def _():
+        normed, factor = row_norm(y_ref[...] + (f_ref[...] + vec_ref[5:6, :]))
+        result = normed * vec_ref[6:7, :] + vec_ref[7:8, :]
+        n2_out[...] = normed
+        t2_out[...] = factor
+        h_out[...] = result
+        hl_out[...] = low(result)
+
+
+def unit_spec(width, index):
+    return pl.BlockSpec((None, width, width), lambda step: (index, 0, 0))
+
+
+def step_spec(width):
+    return pl.BlockSpec((None, width, width), lambda step: (step, 0, 0))
+
+
+def column_spec(rows, width):
+    return pl.BlockSpec((rows, width), lambda step: (0, step))
+
+
+def post(where, attended, hidden, front, up, down, vec, sel):
+    rows, width = attended.shape
+    half = width // 2
+    full = fixed(rows, width)
+    thin = fixed(rows, 1)
+    return pl.pallas_call(
+        post_kernel,
+        grid=(4,),
+        in_specs=[
+            SMEM, full, full, unit_spec(width, 3), step_spec(width), step_spec(width),
+            fixed(12, width), fixed(2, width, half),
+        ],
+        out_specs=[full, full, full, thin, full, thin, column_spec(rows, width)]
+        + [fixed(rows, half)] * 4
+        + [column_spec(rows, half)] * 2,
+        out_shape=[
+            shaped((rows, width), jnp.float32),
+            shaped((rows, width)),
+            shaped((rows, width), jnp.float32),
+            shaped((rows, 1), jnp.float32),
+            shaped((rows, width), jnp.float32),
+            shaped((rows, 1), jnp.float32),
+            shaped((rows, 4 * width)),
+        ]
+        + [shaped((rows, half))] * 4
+        + [shaped((rows, 4 * half))] * 2,
+        scratch_shapes=[
+            pltpu.VMEM((rows, width), jnp.float32),
+            pltpu.VMEM((rows, width), jnp.bfloat16),
+            pltpu.VMEM((rows, width), jnp.float32),
+        ],
+        compiler_params=LIMIT,
+        name="post",
+    )(where, attended, hidden, front, up, down, vec, sel)
+
+
+def norm_back(incoming, normed, factor, gain):
+    scaled = incoming * gain
+    return factor * (
+        scaled
+        - jnp.mean(scaled, axis=-1, keepdims=True)
+        - normed * jnp.mean(scaled * normed, axis=-1, keepdims=True)
+    )
+
+
+def column_sum(value):
+    return jnp.sum(value, axis=0, keepdims=True)
+
+
+def post_back_kernel(
+    e_ref, n1_ref, t1_ref, n2_ref, t2_ref, slope_ref, wo_ref, up_ref, down_ref, vec_ref,
+    df_out, dz_out, da_out, do_out, dr_out, sums_out,
+    r_ref, y_ref,
+):
+    step = pl.program_id(0)
+
+    @pl.when(step == 0)
+    def _():
+        incoming = wide(e_ref[...])
+        normed = n2_ref[...]
+        resid = norm_back(incoming, normed, t2_ref[...], vec_ref[6:7, :])
+        r_ref[...] = resid
+        rounded = low(resid)
+        df_out[...] = rounded
+        sums_out[0:2, :] = jnp.zeros((2, sums_out.shape[1]), jnp.float32)
+        sums_out[5:6, :] = column_sum(wide(rounded))
+        sums_out[6:7, :] = column_sum(incoming * normed)
+        sums_out[7:8, :] = column_sum(incoming)
+
+    steep = low(nt(df_out[...], down_ref[...]) * wide(slope_ref[...]))
+    dz_out[...] = steep
+    sums_out[pl.ds(8 + step, 1), :] = column_sum(wide(steep))
+    part = nt(steep, up_ref[...])
+
+    @pl.when(step == 0)
+    def _():
+        y_ref[...] = part
+
+    @pl.when(step > 0)
+    def _():
+        y_ref[...] += part
+
+    @pl.when(step == 3)
+    def _():
+        incoming = r_ref[...] + y_ref[...]
+        normed = n1_ref[...]
+        resid = norm_back(incoming, normed, t1_ref[...], vec_ref[3:4, :])
+        dr_out[...] = resid
+        rounded = low(resid)
+        da_out[...] = rounded
+        do_out[...] = low(nt(rounded, wo_ref[...]))
+        sums_out[2:3, :] = column_sum(wide(rounded))
+        sums_out[3:4, :] = column_sum(incoming * normed)
+        sums_out[4:5, :] = column_sum(incoming)
+
+
+def post_back(upstream, n1, t1, n2, t2, slope, front, up, down, vec):
+    rows, width = upstream.shape
+    full = fixed(rows, width)
+    thin = fixed(rows, 1)
+    return pl.pallas_call(
+        post_back_kernel,
+        grid=(4,),
+        in_specs=[
+            full, full, thin, full, thin, column_spec(rows, width),
+            unit_spec(width, 3), step_spec(width), step_spec(width), fixed(12, width),
+        ],
+        out_specs=[full, column_spec(rows, width), full, full, full, fixed(12, width)],
+        out_shape=[
+            shaped((rows, width)),
+            shaped((rows, 4 * width)),
+            shaped((rows, width)),
+            shaped((rows, width)),
+            shaped((rows, width), jnp.float32),
+            shaped((12, width), jnp.float32),
+        ],
+        scratch_shapes=[
+            pltpu.VMEM((rows, width), jnp.float32),
+            pltpu.VMEM((rows, width), jnp.float32),
+        ],
+        compiler_params=LIMIT,
+        name="post_back",
+    )(upstream, n1, t1, n2, t2, slope, front, up, down, vec)
+
+
+def project_back_kernel(
+    dq_ref, own_ref, got_ref, w_ref, dr_ref, dm_out, dx_out, dxl_out, sums_out
+):
+    unit = pl.program_id(0)
+
+    @pl.when(unit == 0)
+    def _():
+        dm_out[...] = dq_ref[...]
+
+    @pl.when(unit > 0)
+    def _():
+        dm_out[...] = low(own_ref[...] + wide(got_ref[...]))
+
+    grad = dm_out[...]
+    part = nt(grad, w_ref[...])
+    total = column_sum(wide(grad))
+
+    @pl.when(unit == 0)
+    def _():
+        dx_out[...] = dr_ref[...] + part
+        sums_out[0:1, :] = total
+
+    @pl.when(unit > 0)
+    def _():
+        dx_out[...] += part
+        sums_out[1:2, :] = total
+
+    @pl.when(unit == 2)
+    def _():
+        dxl_out[...] = low(dx_out[...])
+
+
+def project_back(dq, own, got, front, dr):
+    rows, width = dq.shape
+    full = fixed(rows, width)
+    late = pl.BlockSpec((None, rows, width), lambda unit: (jnp.maximum(unit - 1, 0), 0, 0))
+    return pl.pallas_call(
+        project_back_kernel,
+        grid=(3,),
+        in_specs=[full, late, late, step_spec(width), full],
+        out_specs=[
+            pl.BlockSpec((None, rows, width), lambda unit: (unit, 0, 0)),
+            full, full, fixed(2, width),
+        ],
+        out_shape=[
+            shaped((3, rows, width)),
+            shaped((rows, width), jnp.float32),
+            shaped((rows, width)),
+            shaped((2, width), jnp.float32),
+        ],
+        compiler_params=LIMIT,
+        name="project_back",
+    )(dq, own, got, front, dr)
+
+
+def tn(left, right):
+    return nn(left.T, right)
+
+
+def split_store(keep_ref, give_ref, bit, x_first, piece_of, store):
+    for other in range(2):
+        pair = []
+        for side in range(2):
+            rep = (other * 2 + side) if x_first else (side * 2 + other)
+            pair.append(low(piece_of(rep)))
+        store(keep_ref, other, jnp.where(bit == 0, pair[0], pair[1]))
+        store(give_ref, other, jnp.where(bit == 0, pair[1], pair[0]))
+
+
+def front_grad_kernel(
+    x_first, bit_ref, xm_ref, xt_ref, om_ref, ot_ref, dm_ref, dmt_ref, da_ref, dat_ref,
+    keep_ref, give_ref,
+):
+    unit = pl.program_id(0)
+    bit = bit_ref[0]
+
+    def put(product):
+        for level in range(4):
+            base = level * 4 * UNIT
+
+            def piece_of(rep):
+                return product[base + rep * UNIT : base + (rep + 1) * UNIT, :]
+
+            def store(ref, other, value):
+                ref[level, other, unit] = value
+
+            split_store(keep_ref, give_ref, bit, x_first, piece_of, store)
+
+    @pl.when(unit < 3)
+    def _():
+        put(tn(xm_ref[...], dm_ref[...]) + tn(xt_ref[...], dmt_ref[...]))
+
+    @pl.when(unit == 3)
+    def _():
+        put(tn(om_ref[...], da_ref[...]) + tn(ot_ref[...], dat_ref[...]))
+
+
+def front_grad(x_first, bit, xm, xt, om, ot, dm, dmt, da, dat):
+    rows, half = xm.shape
+    width = da.shape[1]
+    late = pl.BlockSpec((None, rows, width), lambda unit: (jnp.minimum(unit, 2), 0, 0))
+    shape = (4, 2, 4, UNIT, width)
+    return pl.pallas_call(
+        functools.partial(front_grad_kernel, x_first),
+        grid=(4,),
+        in_specs=[SMEM]
+        + [fixed(rows, half)] * 4
+        + [late, late, fixed(rows, width), fixed(rows, width)],
+        out_specs=[fixed(*shape)] * 2,
+        out_shape=[shaped(shape)] * 2,
+        compiler_params=LIMIT,
+        name="front_grad",
+    )(bit, xm, xt, om, ot, dm, dmt, da, dat)
+
+
+def feed_grad_kernel(
+    x_first, bit_ref, ym_ref, yt_ref, gm_ref, gt_ref, dz_ref, dzt_ref, df_ref, dft_ref,
+    keep_ref, give_ref,
+):
+    step = pl.program_id(0)
+    bit = bit_ref[0]
+
+    @pl.when(step < 4)
+    def _():
+        product = tn(ym_ref[...], dz_ref[...]) + tn(yt_ref[...], dzt_ref[...])
+        for level in range(4):
+            base = level * 4 * UNIT
+
+            def piece_of(rep):
+                return product[base + rep * UNIT : base + (rep + 1) * UNIT, :]
+
+            def store(ref, other, value):
+                ref[level, other, step] = value
+
+            split_store(keep_ref, give_ref, bit, x_first, piece_of, store)
+
+    @pl.when(step >= 4)
+    def _():
+        product = tn(gm_ref[...], df_ref[...]) + tn(gt_ref[...], dft_ref[...])
+        for sub in range(4):
+
+            def piece_of(rep):
+                base = (rep * 4 + sub) * UNIT
+                return product[base : base + UNIT, :]
+
+            def store(ref, other, value):
+                ref[step - 4, other, 4 + sub] = value
+
+            split_store(keep_ref, give_ref, bit, x_first, piece_of, store)
+
+
+def feed_grad(x_first, bit, ym, yt, gm, gt, dz, dzt, df, dft):
+    rows, half = ym.shape
+    width = df.shape[1]
+    early = pl.BlockSpec((rows, width), lambda step: (0, jnp.minimum(step, 3)))
+    late = pl.BlockSpec((rows, half), lambda step: (0, jnp.maximum(step - 4, 0)))
+    shape = (4, 2, 8, UNIT, width)
+    return pl.pallas_call(
+        functools.partial(feed_grad_kernel, x_first),
+        grid=(8,),
+        in_specs=[SMEM]
+        + [fixed(rows, half)] * 2
+        + [late, late, early, early, fixed(rows, width), fixed(rows, width)],
+        out_specs=[fixed(*shape)] * 2,
+        out_shape=[shaped(shape)] * 2,
+        compiler_params=LIMIT,
+        name="feed_grad",
+    )(bit, ym, yt, gm, gt, dz, dzt, df, dft)
+
+
+def reduce_grad(keep, give, bit, is_low, is_core, x_first):
+    one, two = (TO_X, TO_Y) if x_first else (TO_Y, TO_X)
+    got = send(give, one)
+    stage = low(wide(keep) + wide(got))
+    give = jnp.where(is_low, stage[2:4], stage[0:2])
+    keep = jnp.where(is_low, stage[0:2], stage[2:4])
+    got = send(give, TO_MID)
+    stage = low(wide(keep) + wide(got))
+    outer = jnp.where(is_low, stage[0], stage[1])
+    inner = jnp.where(is_low, stage[1], stage[0])
+    got = send(outer, TO_SIDE)
+    stage = jnp.where(is_core, inner, got)
+    got = send(stage, two)
+    stage = low(wide(stage) + wide(got))
+    got = send(stage, one)
+    axis = 1 if x_first else 0
+    joined = jnp.where(bit == 0, jnp.stack([stage, got], axis), jnp.stack([got, stage], axis))
+    return wide(joined).reshape((4,) + stage.shape[1:])
+
+
+def body_fast(
+    inputs, cotangent, lengths, dealing, key_mask,
+    entry_weight, exit_weight, expand_weight, shrink_weight, vectors,
+):
+    rows, width = inputs.shape
+    layers = entry_weight.shape[0]
+    group_rows = 8 * rows
+    half_rows = group_rows // 2
+    core_rows = half_rows // 2
+    rep = lax.axis_index("rep")
+    shard = lax.axis_index("shard")
+    depth, twin = shard // 2, shard % 2
+    is_low = depth <= 1
+    is_core = (depth == 1) | (depth == 2)
+    where = jnp.stack([depth, rep, twin]).astype(jnp.int32)
+    bits = (rep & 1, rep >> 1)
+
+    def order(four):
+        own, near, middle, far = four
+        return jnp.where(
+            is_low, jnp.stack([near, own, middle, far]), jnp.stack([far, middle, own, near])
+        )
+
+    def absolute(mine, theirs):
+        one, two = order(mine), order(theirs)
+        return jnp.where(twin == 0, jnp.stack([one, two], 1), jnp.stack([two, one], 1))
+
+    packs = [
+        pack_weights(entry_weight[l], exit_weight[l], expand_weight[l], shrink_weight[l])
+        for l in range(layers)
+    ]
+
+    def own_piece(pack):
+        piece = lax.dynamic_index_in_dim(pack, rep, 0, keepdims=False)
+        return piece.reshape(-1, width)
+
+    extra = layers * vectors.shape[1] // width
+    tail = low(vectors).reshape(extra, width)
+    table = jnp.concatenate([dealing // 64, dealing % 64, key_mask], axis=0)
+    table = low(table).reshape(1, width)
+    filler = jnp.zeros((7 - extra, width), jnp.bfloat16)
+    front_rows = 4 * UNIT
+    zero = jnp.concatenate([inputs, tail, table, filler, own_piece(packs[0][0])], axis=0)
+    near = send(zero, TO_SIDE)
+    middle = send(zero, TO_MID)
+    far = send(near, TO_MID)
+    four = (zero, near, middle, far)
+    lead = rows + 8
+    mine = jnp.stack([item[:lead] for item in four])
+    theirs = send(mine, TO_TWIN)
+
+    def relay_units(pack, near, middle, far):
+        shape = (pack.shape[1], UNIT, width)
+        return spread(pack, *[item.reshape(shape) for item in (near, middle, far)])
+
+    parts = relay_units(packs[0][0], *[item[lead:] for item in four[1:]])
+    fronts = [assemble(where, parts, 0, False)]
+
+    piece = own_piece(packs[0][1])
+    near = send(piece, TO_SIDE)
+    parts = relay_units(packs[0][1], near, send(piece, TO_MID), send(near, TO_MID))
+    ups = [assemble(where, parts, 0, False)]
+    downs = [assemble(where, parts, 4, True)]
+
+    joined = jnp.concatenate([packs[1][0], packs[1][1]], axis=1)
+    piece = jnp.concatenate([own_piece(joined), cotangent], axis=0)
+    split = 12 * UNIT
+    near = send(piece, TO_SIDE)
+    four = (piece, near, send(piece, TO_MID), send(near, TO_MID))
+    parts = relay_units(joined, *[item[:split] for item in four[1:]])
+    fronts.append(assemble(where, parts, 0, False))
+    ups.append(assemble(where, parts, 4, False))
+    downs.append(assemble(where, parts, 8, True))
+    cotangent_mine = jnp.stack([item[split:] for item in four])
+    cotangent_theirs = send(cotangent_mine, TO_TWIN)
+
+    header = absolute(tuple(mine[:, rows:]), tuple(theirs[:, rows:]))
+    header = header.reshape(8, 8, width)
+    vector_all = wide(header[:, :extra]).reshape(8, layers, vectors.shape[1])
+    vector_all = jnp.transpose(vector_all, (1, 0, 2)).reshape(layers, 12, width)
+    numbers = wide(header[:, extra]).reshape(8, 3, rows)
+    dealt_all = (numbers[:, 0] * 64 + numbers[:, 1]).astype(jnp.int32).reshape(group_rows)
+    mask_all = numbers[:, 2].reshape(group_rows)
+
+    member, leading = sequence_ids(lengths[0], group_rows)
+    usable = (mask_all == 1) | leading
+    code = jnp.where(usable, member, -1)
+    longest = jnp.argmax(lengths[0])
+    begin = jnp.cumsum(lengths[0])[longest] - lengths[0][longest]
+    spot = jnp.arange(half_rows, dtype=jnp.int32)
+
+    def halve(values, low_side):
+        inside = lax.dynamic_slice_in_dim(values, begin, half_rows, 0)
+        outside = jnp.where(spot < begin, values[:half_rows], values[half_rows:])
+        return jnp.where(low_side, inside, outside)
+
+    def cores(values):
+        own = lax.dynamic_slice_in_dim(values, twin * core_rows, core_rows, 0)
+        other = lax.dynamic_slice_in_dim(values, (1 - twin) * core_rows, core_rows, 0)
+        return own, other
+
+    code_half = jnp.concatenate(cores(halve(code, is_low))).reshape(half_rows, 1)
+    member_own = cores(halve(member, is_low))[0].reshape(1, core_rows)
+    dealt_near = cores(halve(dealt_all, is_low))
+    dealt_far = cores(halve(dealt_all, ~is_low))
+
+    block = jnp.arange(width, dtype=jnp.int32)
+    place = jnp.arange(width // 2, dtype=jnp.int32)
+    chunk = 4 * UNIT
+    source = (place // chunk) * (2 * chunk) + place % chunk
+    cores_at = jnp.stack([twin, 1 - twin])
+    sel = low(block[None, :, None] == (source[None, :] + cores_at[:, None] * chunk)[:, None, :])
+
+    local = jnp.arange(rows, dtype=jnp.int32)
+    bases = jnp.stack(
+        [
+            (depth ^ flip) * (2 * rows) + (twin ^ side) * rows
+            for side in range(2)
+            for flip in (0, 1, 3, 2)
+        ]
+    ).astype(jnp.int32)
+    source_ids = (bases[:, None] + local[None, :]).reshape(8, 1, rows)
+    want_in = dealt_near[0].reshape(core_rows, 1)
+    hidden_low = gather_rows((mine, theirs), source_ids, want_in)
+    upstream = gather_rows((cotangent_mine, cotangent_theirs), source_ids, want_in)
+
+    result_ids = jnp.stack([dealt_near[0], dealt_far[0], dealt_near[1], dealt_far[1]]).reshape(
+        4, 1, core_rows
+    )
+    want_out = jnp.concatenate([source_ids[0, 0], source_ids[1, 0]]).reshape(2 * rows, 1)
+
+    def restore(value):
+        pair = jnp.stack([value, send(value, TO_MID)])
+        found = gather_rows((pair, send(pair, TO_TWIN)), result_ids, want_out)
+        outer = send(found[rows:], TO_SIDE)
+        return jnp.where(is_core, found[:rows], outer)
+
+    saved = []
+    hidden = hidden_low
+    for layer in range(layers):
+        vec = vector_all[layer]
+        queries, kv, xm, xt = project(hidden_low, fronts[layer], vec, sel)
+        kv_twin = send(kv, TO_TWIN)
+        attended, ot, lse = attend_fast(queries, kv, kv_twin, code_half, member_own)
+        (
+            hidden, hidden_low, n1, t1, n2, t2, slope, om, oo, ym, yo, gm, go,
+        ) = post(where, attended, hidden, fronts[layer], ups[layer], downs[layer], vec, sel)
+        others = tuple(send(item, TO_TWIN) for item in (xt, oo, yo, go))
+        saved.append((queries, kv, kv_twin, ot, lse, n1, t1, n2, t2, slope, xm, om, ym, gm, others))
+    output = restore(hidden_low)
+
+    grads = [None] * layers
+    grad = upstream
+    for layer in reversed(range(layers)):
+        vec = vector_all[layer]
+        x_first = layer == 0
+        bit = bits[0] if x_first else bits[1]
+        bit_word = bit.reshape(1).astype(jnp.int32)
+        queries, kv, kv_twin, ot, lse, n1, t1, n2, t2, slope, xm, om, ym, gm, others = saved[layer]
+        xt, oo, yo, go = others
+        df, dz, da, do, dr, sums = post_back(
+            grad, n1, t1, n2, t2, slope, fronts[layer], ups[layer], downs[layer], vec
+        )
+        keep, give = feed_grad(
+            x_first, bit_word, ym, yo, gm, go, dz, send(dz, TO_TWIN), df, send(df, TO_TWIN)
+        )
+        feed = reduce_grad(keep, give, bit, is_low, is_core, x_first)
+        dq, own, give = attend_back_fast(queries, do, kv, kv_twin, ot, lse, code_half, member_own)
+        dm, grad, grad_low, head_sums = project_back(
+            dq, own, send(give, TO_TWIN), fronts[layer], dr
+        )
+        keep, give = front_grad(
+            x_first, bit_word, xm, xt, om, oo, dm, send(dm, TO_TWIN), da, send(da, TO_TWIN)
+        )
+        front = reduce_grad(keep, give, bit, is_low, is_core, x_first)
+        grads[layer] = (front, feed, jnp.concatenate([head_sums, sums[2:]], axis=0))
+    input_grad = wide(restore(grad_low))
+
+    def columns(units):
+        count = units.shape[1]
+        return units.transpose(0, 2, 1, 3).reshape(4 * UNIT, count * width)
+
+    entry_grad = jnp.stack([columns(item[0][:, 0:3]) for item in grads])
+    exit_grad = jnp.stack([columns(item[0][:, 3:4]) for item in grads])
+    expand_grad = jnp.stack([columns(item[1][:, 0:4]) for item in grads])
+    shrink_grad = jnp.stack([item[1][:, 4:8].reshape(16 * UNIT, width) for item in grads])
+
+    joined = jnp.stack([item[2].reshape(-1) for item in grads])
+    joined = jnp.transpose(joined.reshape(layers, 4, 2, vectors.shape[1]), (1, 2, 0, 3))
+    keep = lax.dynamic_index_in_dim(joined, twin, 1, keepdims=False)
+    give = lax.dynamic_index_in_dim(joined, 1 - twin, 1, keepdims=False)
+    stage = keep + send(give, TO_TWIN)
+    stage = stage + send(stage, TO_X)
+    stage = stage + send(stage, TO_Y)
+    give = jnp.where(is_low, stage[2:4], stage[0:2])
+    keep = jnp.where(is_low, stage[0:2], stage[2:4])
+    stage = keep + send(give, TO_MID)
+    outer = jnp.where(is_low, stage[0], stage[1])
+    inner = jnp.where(is_low, stage[1], stage[0])
+    vector_grad = jnp.where(is_core, inner, send(outer, TO_SIDE))
+    return (output, input_grad, entry_grad, exit_grad, expand_grad, shrink_grad, vector_grad)
+
+
 def solution(mesh):
     placed = (
         P(("rep", "shard"), None),
@@ -424,8 +1371,9 @@
         P(None, "shard", None),
         P(None, "shard"),
     )
+    small = dict(mesh.shape) == {"rep": 4, "shard": 8}
     return jax.shard_map(
-        body,
+        body_fast if small else body,
         mesh=mesh,
         in_specs=placed,
         out_specs=(

time: 1480 us -> 734 us (0.50)
  waiting for transfers between devices: 917 us -> 200 us
  Pallas kernels: 0 us -> 279 us
  matrix products: 234 us -> 0 us
  starting transfers between devices: 1.52 us -> 104 us
  blocking collectives: 88.2 us -> 0 us
  local copies, waits for them, and re-layouts: 135 us -> 72.4 us
    reduce_scatter x10 -> x0, waiting for transfers between devices: 470 us -> none  [the longest x2 111 us: body(): lax.psum_scatter(shrink_local.astype(jnp.bfloat16), 'shard', scatter_dime...]
    all_gather x16 -> x0, waiting for transfers between devices: 364 us -> none  [the longest x2 80 us: fetch_forward(): lax.all_gather(shrink_weight[layer_index].astype(jnp.bfloat16), 'shard',...]
    pallas_call x0 -> x26, Pallas kernels: none -> 279 us  [the longest x2 47.2 us: post(): pl.pallas_call(post_kernel, grid=(4,), in_specs=[SMEM, full, full, unit_s...]
    dot_general x80 -> x0, matrix products: 234 us -> none  [the longest x8 33 us: attend_advance(): jnp.einsum('hqk,qhd->khd', probs.astype(jnp.bfloat16), grad_heads, prefer...]
    ppermute x0 -> x89, waiting for transfers between devices: none -> 200 us  [send(): return lax.ppermute(value, BOTH, route)]
    ppermute x0 -> x89, starting transfers between devices: none -> 104 us  [send(): return lax.ppermute(value, BOTH, route)]
    psum x1 -> x0, waiting for transfers between devices: 77.4 us -> none  [body(): lax.psum(entry_part.astype(jnp.bfloat16), 'rep').astype(jnp.float32)]
    all_gather x4 -> x0, blocking collectives: 48.2 us -> none  [the longest x2 28.6 us: fetch_forward(): lax.all_gather(vectors[layer_index].astype(jnp.bfloat16), 'shard', axis=0...]
  transfers between devices with their start and end apart: 27 -> 89, of which waited for: 24 -> 21; matrix products, arithmetic and copies ran while one was open for 17% -> 15% of each run, Pallas kernels for 0% -> 22%
where the time goes in v2:
time: 734 us; the launch traced here: 725 us
  Pallas kernels  279 us (38%)
  waiting for transfers between devices  200 us (27%)
  starting transfers between devices  104 us (14%)
  local copies, waits for them, and re-layouts  72.4 us (10%)
  other arithmetic  62.6 us (9%)
    ppermute x89, waiting for transfers between devices, send(): return lax.ppermute(value, BOTH, route)  200 us
    ppermute x89, starting transfers between devices, send(): return lax.ppermute(value, BOTH, route)  104 us
    pallas_call x2, Pallas kernels, post(): pl.pallas_call(post_kernel, grid=(4,), in_specs=[SMEM, full, full, unit_s...  47.2 us
    pallas_call x2, Pallas kernels, attend_back_fast(): pl.pallas_call(attend_back_kernel, grid=(width // 128,), in_specs=[column...  41.4 us
    pallas_call x6, Pallas kernels, assemble(): pl.pallas_call(assemble_kernel, grid_spec=pltpu.PrefetchScalarGridSpec(nu...  34.7 us
    pallas_call x2, Pallas kernels, post_back(): pl.pallas_call(post_back_kernel, grid=(4,), in_specs=[full, full, thin, f...  32.4 us
    pallas_call x2, Pallas kernels, attend_fast(): pl.pallas_call(attend_kernel, grid=(width // 128,), in_specs=[column, key...  31 us
    pallas_call x2, Pallas kernels, feed_grad(): pl.pallas_call(functools.partial(feed_grad_kernel, x_first), grid=(8,), i...  25.3 us
  transfers between devices with their start and end apart: 89, of which 21 were waited for; matrix products, arithmetic and copies ran while one was open for 15% of the time, Pallas kernels for 22%

profile of v2, /device:TPU:0, one launch (start us, length us, event | category | flops | bytes accessed | tf_op | source)
XLA Modules:
  0.0 725.4 jit_solution(3386683965764208542)
XLA Ops:
  19.0 3.9 concatenate.79
  22.9 3.5 collective-permute-start
  33.8 14.0 %collective-permute-done = bf16[360,768]{1,0:T(8,128)(2,1)} collective-permute-done((bf16[360,768]{1,0:T(8,128)(2,1)}, bf16[360,768]{1,0:T(8,128)(2,1)}, u32[]{:S(2)}, u32[]{:S(2)}) %collective-permute-start) | collective-permute-done | bytes 552992 | tf_op jit(solution)/shard_map/ppermute | solution.py:441
  58.3 4.2 collective-permute-done.4.refs_2_
  87.6 6.3 collective-permute-done.17.refs_2_
  104.1 5.8 assemble.6
  115.1 19.2 %collective-permute-done.29.refs_2_ = bf16[3,12,24,768]{3,2,1,0:T(8,128)(2,1)} collective-permute-done((bf16[3,12,24,768]{3,2,1,0:T(8,128)(2,1)}, bf16[3,12,24,768]{3,2,1,0:T(8,128)(2,1)}, u32[]{:S(2)}, u32[]{:S(2)}) %collective-permute-start.29) | collective-permute-done | bytes 1327136 | tf_op jit(solution)/shard_map/ppermute | solution.py:441
  141.0 4.7 gather_rows.4.h_ref
  145.7 7.3 %project.2 = (bf16[512,768]{1,0:T(8,128)(2,1)}, bf16[2,512,768]{2,1,0:T(8,128)(2,1)}, bf16[512,384]{1,0:T(8,128)(2,1)}, bf16[512,384]{1,0:T(8,128)(2,1)}) custom-call(bf16[512,768]{1,0:T(8,128)(2,1)} %gather_rows.4.h_ref, bf16[4,768,768]{2,1,0:T(8,128)(2,1)} %bitcast.183, f32[12,768]{1,0:T(8,128)} %squeeze.25.vec_ref, bf16[2,768,384]{2,1,0:T(8,128)(2,1)} %fusion.sel_ref), custom_call_target="tpu_custom_call" | custom-call | tf_op jit(solution)/shard_map/project/pallas_call | solution.py:593
  157.0 14.6 %collective-permute-done.32 = bf16[3,6,24,768]{3,2,1,0:T(8,128)(2,1)S(1)} collective-permute-done((bf16[3,6,24,768]{3,2,1,0:T(8,128)(2,1)S(1)}, bf16[3,6,24,768]{3,2,1,0:T(8,128)(2,1)S(1)}, u32[]{:S(2)}, u32[]{:S(2)}) %collective-permute-start.32) | collective-permute-done | bytes 663584 | tf_op jit(solution)/shard_map/ppermute | solution.py:441
  187.3 5.8 assemble.8
  193.1 5.7 assemble.7
  198.8 15.4 %attend_forward.2 = (bf16[512,768]{1,0:T(8,128)(2,1)}, f32[768,512]{1,0:T(8,128)}, f32[6,2,512]{2,1,0:T(2,128)}) custom-call(bf16[512,768]{1,0:T(8,128)(2,1)} %get-tuple-element.80.q_ref, bf16[2,512,768]{2,1,0:T(8,128)(2,1)} %get-tuple-element.81.ka_ref.va_ref, bf16[2,512,768]{2,1,0:T(8,128)(2,1)} %copy-done.1, ...), custom_call_target="tpu_custom_call" | custom-call | tf_op jit(solution)/shard_map/attend_forward/pallas_call | solution.py:670
  214.3 23.6 %post.2 = (f32[512,768]{1,0:T(8,128)}, bf16[512,768]{1,0:T(8,128)(2,1)}, f32[512,768]{1,0:T(8,128)}, f32[512,1]{1,0:T(8,128)}, f32[512,768]{1,0:T(8,128)}, /*ind...) custom-call(s32[3]{0:T(128)} %pad_add_fusion.3.where_ref, ...), custom_call_target="tpu_custom_call" | custom-call | tf_op jit(solution)/shard_map/post/pallas_call | solution.py:848
  238.3 5.8 assemble.9
  244.0 7.4 %project.3 = (bf16[512,768]{1,0:T(8,128)(2,1)}, bf16[2,512,768]{2,1,0:T(8,128)(2,1)}, bf16[512,384]{1,0:T(8,128)(2,1)}, bf16[512,384]{1,0:T(8,128)(2,1)}) custom-call(bf16[512,768]{1,0:T(8,128)(2,1)} %get-tuple-element.83.h_ref, bf16[4,768,768]{2,1,0:T(8,128)(2,1)} %bitcast.187, f32[12,768]{1,0:T(8,128)} %squeeze.26.vec_ref, bf16[2,768,384]{2,1,0:T(8,128)(2,1)} %fusion.sel_ref), custom_call_target="tpu_custom_call" | custom-call | tf_op jit(solution)/shard_map/project/pallas_call | solution.py:593
  251.7 4.7 gather_rows.6.e_ref
  256.4 5.8 assemble.11
  262.3 5.8 assemble.10
  269.2 15.6 %attend_forward.3 = (bf16[512,768]{1,0:T(8,128)(2,1)}, f32[768,512]{1,0:T(8,128)}, f32[6,2,512]{2,1,0:T(2,128)}) custom-call(bf16[512,768]{1,0:T(8,128)(2,1)} %get-tuple-element.84.q_ref, bf16[2,512,768]{2,1,0:T(8,128)(2,1)} %get-tuple-element.85.ka_ref.va_ref, bf16[2,512,768]{2,1,0:T(8,128)(2,1)} %copy-done.2, ...), custom_call_target="tpu_custom_call" | custom-call | tf_op jit(solution)/shard_map/attend_forward/pallas_call | solution.py:670
  284.9 23.6 %post.3 = (f32[512,768]{1,0:T(8,128)}, bf16[512,768]{1,0:T(8,128)(2,1)}, f32[512,768]{1,0:T(8,128)}, f32[512,1]{1,0:T(8,128)}, f32[512,768]{1,0:T(8,128)}, /*ind...) custom-call(s32[3]{0:T(128)} %pad_add_fusion.3.where_ref, ...), custom_call_target="tpu_custom_call" | custom-call | tf_op jit(solution)/shard_map/post/pallas_call | solution.py:848
  308.5 16.4 %post_back.2 = (bf16[512,768]{1,0:T(8,128)(2,1)}, bf16[512,3072]{1,0:T(8,128)(2,1)}, bf16[512,768]{1,0:T(8,128)(2,1)}, bf16[512,768]{1,0:T(8,128)(2,1)}, f32[512,768]{1,0:T(8,128)}, /*index=5*/f32[12,768]{1,0:T(8,128)}) custom-call(bf16[512,768]{1,0:T(8,128)(2,1)} %gather_rows.6.e_ref, f32[512,768]{1,0:T(8,128)} %get-tuple-element.89.n1_ref, ...), custom_call_target="tpu_custom_call" | custom-call | tf_op jit(solution)/shard_map/post_back/pallas_call | solution.py:943
  324.8 20.6 %attend_backward.2 = (bf16[512,768]{1,0:T(8,128)(2,1)}, f32[2,512,768]{2,1,0:T(8,128)}, bf16[2,512,768]{2,1,0:T(8,128)(2,1)}) custom-call(bf16[512,768]{1,0:T(8,128)(2,1)} %get-tuple-element.84.q_ref, bf16[512,768]{1,0:T(8,128)(2,1)} %get-tuple-element.94.g_ref, bf16[2,512,768]{2,1,0:T(8,128)(2,1)} %get-tuple-element.85.ka_ref.va_ref, ...), custom_call_target="tpu_custom_call" | custom-call | tf_op jit(solution)/shard_map/attend_backward/pallas_call | solution.py:738
  345.7 3.4 collective-permute-done.43.got_ref
  350.2 9.2 %project_back.2 = (bf16[3,512,768]{2,1,0:T(8,128)(2,1)}, f32[512,768]{1,0:T(8,128)}, bf16[512,768]{1,0:T(8,128)(2,1)}, f32[2,768]{1,0:T(2,128)}) custom-call(bf16[512,768]{1,0:T(8,128)(2,1)} %get-tuple-element.97.dq_ref, f32[2,512,768]{2,1,0:T(8,128)} %get-tuple-element.98.own_ref, bf16[2,512,768]{2,1,0:T(8,128)(2,1)} %copy-done.34, ...), custom_call_target="tpu_custom_call" | custom-call | tf_op jit(solution)/shard_map/project_back/pallas_call | solution.py:1004
  359.4 16.1 %post_back.3 = (bf16[512,768]{1,0:T(8,128)(2,1)}, bf16[512,3072]{1,0:T(8,128)(2,1)}, bf16[512,768]{1,0:T(8,128)(2,1)}, bf16[512,768]{1,0:T(8,128)(2,1)}, f32[512,768]{1,0:T(8,128)}, /*index=5*/f32[12,768]{1,0:T(8,128)}) custom-call(f32[512,768]{1,0:T(8,128)} %get-tuple-element.101.e_ref, f32[512,768]{1,0:T(8,128)} %get-tuple-element.102.n1_ref, ...), custom_call_target="tpu_custom_call" | custom-call | tf_op jit(solution)/shard_map/post_back/pallas_call | solution.py:943
  375.5 20.9 %attend_backward.3 = (bf16[512,768]{1,0:T(8,128)(2,1)}, f32[2,512,768]{2,1,0:T(8,128)}, bf16[2,512,768]{2,1,0:T(8,128)(2,1)}) custom-call(bf16[512,768]{1,0:T(8,128)(2,1)} %get-tuple-element.80.q_ref, bf16[512,768]{1,0:T(8,128)(2,1)} %get-tuple-element.107.g_ref, bf16[2,512,768]{2,1,0:T(8,128)(2,1)} %get-tuple-element.81.ka_ref.va_ref, ...), custom_call_target="tpu_custom_call" | custom-call | tf_op jit(solution)/shard_map/attend_backward/pallas_call | solution.py:738
  397.7 10.8 %collective-permute-done.57.xt_ref = bf16[512,384]{1,0:T(8,128)(2,1)S(1)} collective-permute-done((bf16[512,384]{1,0:T(8,128)(2,1)S(1)}, bf16[512,384]{1,0:T(8,128)(2,1)S(1)}, u32[]{:S(2)}, u32[]{:S(2)}) %collective-permute-start.57) | collective-permute-done | bytes 393248 | tf_op jit(solution)/shard_map/ppermute | solution.py:441
  416.0 9.2 %project_back.3 = (bf16[3,512,768]{2,1,0:T(8,128)(2,1)}, f32[512,768]{1,0:T(8,128)}, bf16[512,768]{1,0:T(8,128)(2,1)}, f32[2,768]{1,0:T(2,128)}) custom-call(bf16[512,768]{1,0:T(8,128)(2,1)} %get-tuple-element.110.dq_ref, f32[2,512,768]{2,1,0:T(8,128)} %get-tuple-element.111.own_ref, bf16[2,512,768]{2,1,0:T(8,128)(2,1)} %copy-done.33, ...), custom_call_target="tpu_custom_call" | custom-call | tf_op jit(solution)/shard_map/project_back/pallas_call | solution.py:1004
  430.8 3.4 collective-permute-done.85
  435.7 7.6 %front_grad.3 = (bf16[4,2,4,24,768]{4,3,2,1,0:T(8,128)(2,1)}, bf16[4,2,4,24,768]{4,3,2,1,0:T(8,128)(2,1)}) custom-call(s32[1]{0:T(128)} %bitcast.91.bit_ref, bf16[512,384]{1,0:T(8,128)(2,1)} %get-tuple-element.123.xm_ref, bf16[512,384]{1,0:T(8,128)(2,1)} %copy-done.57, bf16[512,384]{1,0:T(8,128)(2,1)} %get-tuple-element.125.om_ref, ...), custom_call_target="tpu_custom_call" | custom-call | tf_op jit(solution)/shard_map/front_grad/pallas_call | solution.py:1070
  446.1 4.7 gather_rows.5
  452.0 12.6 %feed_grad.3 = (bf16[4,2,8,24,768]{4,3,2,1,0:T(8,128)(2,1)}, bf16[4,2,8,24,768]{4,3,2,1,0:T(8,128)(2,1)}) custom-call(s32[1]{0:T(128)} %bitcast.91.bit_ref, bf16[512,384]{1,0:T(8,128)(2,1)} %get-tuple-element.139.ym_ref, bf16[512,384]{1,0:T(8,128)(2,1)} %copy-done.56, bf16[512,1536]{1,0:T(8,128)(2,1)} %get-tuple-element.141.gm_ref, ...), custom_call_target="tpu_custom_call" | custom-call | tf_op jit(solution)/shard_map/feed_grad/pallas_call | solution.py:1125
  464.6 19.8 %collective-permute-start.41 = (bf16[256,768]{1,0:T(8,128)(2,1)S(1)}, bf16[256,768]{1,0:T(8,128)(2,1)S(1)}, u32[]{:S(2)}, u32[]{:S(2)}) collective-permute-start(bf16[256,768]{1,0:T(8,128)(2,1)S(1)} %slice.405), channel_id=1, source_target_pairs={{0,2},{1,3},{2,0},{3,1},{4,6},{5,7},{6,4},{7,5},{8,10},{9,11},{10,... | collective-permute-start | bytes 1179656 | tf_op jit(solution)/shard_map/ppermute | solution.py:441
  485.5 8.6 %collective-permute-done.41 = bf16[256,768]{1,0:T(8,128)(2,1)S(1)} collective-permute-done((bf16[256,768]{1,0:T(8,128)(2,1)S(1)}, bf16[256,768]{1,0:T(8,128)(2,1)S(1)}, u32[]{:S(2)}, u32[]{:S(2)}) %collective-permute-start.41) | collective-permute-done | bytes 393248 | tf_op jit(solution)/shard_map/ppermute | solution.py:441
  502.9 12.7 %feed_grad.2 = (bf16[4,2,8,24,768]{4,3,2,1,0:T(8,128)(2,1)}, bf16[4,2,8,24,768]{4,3,2,1,0:T(8,128)(2,1)}) custom-call(s32[1]{0:T(128)} %bitcast.84.bit_ref, bf16[512,384]{1,0:T(8,128)(2,1)} %get-tuple-element.131.ym_ref, bf16[512,384]{1,0:T(8,128)(2,1)} %copy-done.58, bf16[512,1536]{1,0:T(8,128)(2,1)} %get-tuple-element.133.gm_ref, ...), custom_call_target="tpu_custom_call" | custom-call | tf_op jit(solution)/shard_map/feed_grad/pallas_call | solution.py:1125
  518.5 19.7 %collective-permute-done.79 = bf16[4,2,8,24,768]{4,3,2,1,0:T(8,128)(2,1)} collective-permute-done((bf16[4,2,8,24,768]{4,3,2,1,0:T(8,128)(2,1)}, bf16[4,2,8,24,768]{4,3,2,1,0:T(8,128)(2,1)}, u32[]{:S(2)}, u32[]{:S(2)}) %collective-permute-start.79) | collective-permute-done | bytes 2359328 | tf_op jit(solution)/shard_map/ppermute | solution.py:441
  538.2 4.9 collective-permute-start.63
  549.2 7.6 %front_grad.2 = (bf16[4,2,4,24,768]{4,3,2,1,0:T(8,128)(2,1)}, bf16[4,2,4,24,768]{4,3,2,1,0:T(8,128)(2,1)}) custom-call(s32[1]{0:T(128)} %bitcast.84.bit_ref, bf16[512,384]{1,0:T(8,128)(2,1)} %get-tuple-element.115.xm_ref, bf16[512,384]{1,0:T(8,128)(2,1)} %copy-done.59, bf16[512,384]{1,0:T(8,128)(2,1)} %get-tuple-element.117.om_ref, ...), custom_call_target="tpu_custom_call" | custom-call | tf_op jit(solution)/shard_map/front_grad/pallas_call | solution.py:1070
  558.0 4.7 gather_rows.7
  563.8 3.9 collective-permute-start.47
  571.0 3.8 collective-permute-done.47
  575.8 53.8 %collective-permute-done.64 = bf16[2,4,24,768]{3,2,1,0:T(8,128)(2,1)S(1)} collective-permute-done((bf16[2,4,24,768]{3,2,1,0:T(8,128)(2,1)S(1)}, bf16[2,4,24,768]{3,2,1,0:T(8,128)(2,1)S(1)}, u32[]{:S(2)}, u32[]{:S(2)}) %collective-permute-start.64) | collective-permute-done | bytes 294944 | tf_op jit(solution)/shard_map/ppermute | solution.py:441
  639.0 11.5 %collective-permute-start.54 = (bf16[2,4,24,768]{3,2,1,0:T(8,128)(2,1)S(1)}, bf16[2,4,24,768]{3,2,1,0:T(8,128)(2,1)S(1)}, u32[]{:S(2)}, u32[]{:S(2)}) collective-permute-start(bf16[2,4,24,768]{3,2,1,0:T(8,128)(2,1)S(1)} %select_bitcast_fusion.3), channel_id=1, source_target_pairs={{0,2},{1,3},{2,0},{3,1},{4,6},{5,7},{6,4},{7,5},{8,10},{9,11},{10,... | collective-permute-start | bytes 884744 | tf_op jit(solution)/shard_map/ppermute | solution.py:441
  651.5 6.9 collective-permute-done.54
  675.4 6.1 collective-permute-done.82
  696.6 7.8 %collective-permute-done.73 = bf16[2,8,24,768]{3,2,1,0:T(8,128)(2,1)} collective-permute-done((bf16[2,8,24,768]{3,2,1,0:T(8,128)(2,1)}, bf16[2,8,24,768]{3,2,1,0:T(8,128)(2,1)}, u32[]{:S(2)}, u32[]{:S(2)}) %collective-permute-start.73) | collective-permute-done | bytes 589856 | tf_op jit(solution)/shard_map/ppermute | solution.py:441
  709.1 8.6 %collective-permute-done.74 = bf16[2,8,24,768]{3,2,1,0:T(8,128)(2,1)S(1)} collective-permute-done((bf16[2,8,24,768]{3,2,1,0:T(8,128)(2,1)S(1)}, bf16[2,8,24,768]{3,2,1,0:T(8,128)(2,1)S(1)}, u32[]{:S(2)}, u32[]{:S(2)}) %collective-permute-start.74) | collective-permute-done | bytes 589856 | tf_op jit(solution)/shard_map/ppermute | solution.py:441
  (501 shorter events, 200.8 us)
Async XLA Ops:
  13.2 57.4 %collective-permute-start.26 = (bf16[544,768]{1,0:T(8,128)(2,1)}, bf16[544,768]{1,0:T(8,128)(2,1)}, u32[]{:S(2)}, u32[]{:S(2)}) collective-permute-start(bf16[544,768]{1,0:T(8,128)(2,1)} %pad_maximum_fusion.11), channel_id=1, source_target_pairs={{0,2},{1,3},{2,0},{3,1},{4,6},{5,7},{6,4},{7,5},{8,10},{9,11},{10,... | collective-permute-start | bytes 2506760 | tf_op jit(solution)/shard_map/ppermute | solution.py:441
  16.2 55.6 %collective-permute-start.27 = (bf16[544,768]{1,0:T(8,128)(2,1)}, bf16[544,768]{1,0:T(8,128)(2,1)}, u32[]{:S(2)}, u32[]{:S(2)}) collective-permute-start(bf16[544,768]{1,0:T(8,128)(2,1)} %pad_maximum_fusion.11), channel_id=1, source_target_pairs={{2,4},{3,5},{4,2},{5,3},{10,12},{11,13},{12,10},{13,11},{18,20},{1... | collective-permute-start | bytes 2506760 | tf_op jit(solution)/shard_map/ppermute | solution.py:441
  22.9 24.9 %collective-permute-start = (bf16[360,768]{1,0:T(8,128)(2,1)}, bf16[360,768]{1,0:T(8,128)(2,1)}, u32[]{:S(2)}, u32[]{:S(2)}) collective-permute-start(bf16[360,768]{1,0:T(8,128)(2,1)} %concatenate.79), channel_id=1, source_target_pairs={{0,2},{1,3},{2,0},{3,1},{4,6},{5,7},{6,4},{7,5},{8,10},{9,11},{10,... | collective-permute-start | bytes 1658888 | tf_op jit(solution)/shard_map/ppermute | solution.py:441
  26.4 24.5 %collective-permute-start.1 = (bf16[360,768]{1,0:T(8,128)(2,1)}, bf16[360,768]{1,0:T(8,128)(2,1)}, u32[]{:S(2)}, u32[]{:S(2)}) collective-permute-start(bf16[360,768]{1,0:T(8,128)(2,1)} %concatenate.79), channel_id=1, source_target_pairs={{2,4},{3,5},{4,2},{5,3},{10,12},{11,13},{12,10},{13,11},{18,20},{1... | collective-permute-start | bytes 1658888 | tf_op jit(solution)/shard_map/ppermute | solution.py:441
  30.4 27.2 %collective-permute-start.14 = (bf16[192,768]{1,0:T(8,128)(2,1)}, bf16[192,768]{1,0:T(8,128)(2,1)}, u32[]{:S(2)}, u32[]{:S(2)}) collective-permute-start(bf16[192,768]{1,0:T(8,128)(2,1)} %bitcast.59), channel_id=1, source_target_pairs={{0,2},{1,3},{2,0},{3,1},{4,6},{5,7},{6,4},{7,5},{8,10},{9,11},{10,... | collective-permute-start | bytes 884744 | tf_op jit(solution)/shard_map/ppermute | solution.py:441
  64.0 45.9 %collective-permute-start.3 = (bf16[4,264,768]{2,1,0:T(8,128)(2,1)S(1)}, bf16[4,264,768]{2,1,0:T(8,128)(2,1)}, u32[]{:S(2)}, u32[]{:S(2)}) collective-permute-start(bf16[4,264,768]{2,1,0:T(8,128)(2,1)S(1)} %pad_maximum_fusion.4.refs_0_), channel_id=1, source_target_pairs={{0,1},{1,0},{2,3},{3,2},{4,5},{5,4},{6,7},{7,6},{8,9},{9,8},{10,11... | collective-permute-start | bytes 4866056 | tf_op jit(solution)/shard_map/ppermute | solution.py:441
  70.6 23.3 %collective-permute-start.17 = (bf16[3,8,24,768]{3,2,1,0:T(8,128)(2,1)}, bf16[3,8,24,768]{3,2,1,0:T(8,128)(2,1)}, u32[]{:S(2)}, u32[]{:S(2)}) collective-permute-start(bf16[3,8,24,768]{3,2,1,0:T(8,128)(2,1)} %pad_maximum_fusion.10.refs_1_), channel_id=1, source_target_pairs={{0,8},{1,9},{2,10},{3,11},{4,12},{5,13},{6,14},{7,15},{8,0},{9,1},... | collective-permute-start | bytes 2654216 | tf_op jit(solution)/shard_map/ppermute | solution.py:441
  71.9 22.0 %collective-permute-start.18 = (bf16[3,8,24,768]{3,2,1,0:T(8,128)(2,1)}, bf16[3,8,24,768]{3,2,1,0:T(8,128)(2,1)}, u32[]{:S(2)}, u32[]{:S(2)}) collective-permute-start(bf16[3,8,24,768]{3,2,1,0:T(8,128)(2,1)} %pad_maximum_fusion.10.refs_1_), channel_id=1, source_target_pairs={{0,16},{1,17},{2,18},{3,19},{4,20},{5,21},{6,22},{7,23},{8,24},{9,... | collective-permute-start | bytes 2654216 | tf_op jit(solution)/shard_map/ppermute | solution.py:441
  72.4 22.0 %collective-permute-start.28 = (bf16[544,768]{1,0:T(8,128)(2,1)}, bf16[544,768]{1,0:T(8,128)(2,1)}, u32[]{:S(2)}, u32[]{:S(2)}) collective-permute-start(bf16[544,768]{1,0:T(8,128)(2,1)} %collective-permute-done.26), channel_id=1, source_target_pairs={{2,4},{3,5},{4,2},{5,3},{10,12},{11,13},{12,10},{13,11},{18,20},{1... | collective-permute-start | bytes 2506760 | tf_op jit(solution)/shard_map/ppermute | solution.py:441
  100.4 55.6 %collective-permute-start.21 = (bf16[4,8,24,768]{3,2,1,0:T(8,128)(2,1)}, bf16[4,8,24,768]{3,2,1,0:T(8,128)(2,1)}, u32[]{:S(2)}, u32[]{:S(2)}) collective-permute-start(bf16[4,8,24,768]{3,2,1,0:T(8,128)(2,1)} %pad_maximum_fusion.8.refs_0_), channel_id=1, source_target_pairs={{0,1},{1,0},{2,3},{3,2},{4,5},{5,4},{6,7},{7,6},{8,9},{9,8},{10,11... | collective-permute-start | bytes 3538952 | tf_op jit(solution)/shard_map/ppermute | solution.py:441
  100.9 55.3 %collective-permute-start.22 = (bf16[3,8,24,768]{3,2,1,0:T(8,128)(2,1)}, bf16[3,8,24,768]{3,2,1,0:T(8,128)(2,1)}, u32[]{:S(2)}, u32[]{:S(2)}) collective-permute-start(bf16[3,8,24,768]{3,2,1,0:T(8,128)(2,1)} %pad_maximum_fusion.10.refs_1_), channel_id=1, source_target_pairs={{0,1},{1,0},{2,3},{3,2},{4,5},{5,4},{6,7},{7,6},{8,9},{9,8},{10,11... | collective-permute-start | bytes 2654216 | tf_op jit(solution)/shard_map/ppermute | solution.py:441
  101.0 36.8 %collective-permute-start.19 = (bf16[3,4,24,768]{3,2,1,0:T(8,128)(2,1)}, bf16[3,4,24,768]{3,2,1,0:T(8,128)(2,1)}, u32[]{:S(2)}, u32[]{:S(2)}) collective-permute-start(bf16[3,4,24,768]{3,2,1,0:T(8,128)(2,1)} %slice.392), channel_id=1, source_target_pairs={{0,16},{1,17},{2,18},{3,19},{4,20},{5,21},{6,22},{7,23},{8,24},{9,... | collective-permute-start | bytes 1327112 | tf_op jit(solution)/shard_map/ppermute | solution.py:441
  102.6 31.7 %collective-permute-start.29 = (bf16[3,12,24,768]{3,2,1,0:T(8,128)(2,1)}, bf16[3,12,24,768]{3,2,1,0:T(8,128)(2,1)}, u32[]{:S(2)}, u32[]{:S(2)}) collective-permute-start(bf16[3,12,24,768]{3,2,1,0:T(8,128)(2,1)} %pad_maximum_fusion.9.refs_1_), channel_id=1, source_target_pairs={{0,8},{1,9},{2,10},{3,11},{4,12},{5,13},{6,14},{7,15},{8,0},{9,1},... | collective-permute-start | bytes 3981320 | tf_op jit(solution)/shard_map/ppermute | solution.py:441
  109.9 43.2 %collective-permute-start.30 = (bf16[3,12,24,768]{3,2,1,0:T(8,128)(2,1)}, bf16[3,12,24,768]{3,2,1,0:T(8,128)(2,1)}, u32[]{:S(2)}, u32[]{:S(2)}) collective-permute-start(bf16[3,12,24,768]{3,2,1,0:T(8,128)(2,1)} %pad_maximum_fusion.9.refs_1_), channel_id=1, source_target_pairs={{0,16},{1,17},{2,18},{3,19},{4,20},{5,21},{6,22},{7,23},{8,24},{9,... | collective-permute-start | bytes 3981320 | tf_op jit(solution)/shard_map/ppermute | solution.py:441
  134.3 19.9 %collective-permute-start.20 = (bf16[3,4,24,768]{3,2,1,0:T(8,128)(2,1)}, bf16[3,4,24,768]{3,2,1,0:T(8,128)(2,1)S(1)}, u32[]{:S(2)}, u32[]{:S(2)}) collective-permute-start(bf16[3,4,24,768]{3,2,1,0:T(8,128)(2,1)} %slice.393), channel_id=1, source_target_pairs={{0,8},{1,9},{2,10},{3,11},{4,12},{5,13},{6,14},{7,15},{8,0},{9,1},... | collective-permute-start | bytes 1327112 | tf_op jit(solution)/shard_map/ppermute | solution.py:441
  137.8 18.7 %collective-permute-start.31 = (bf16[3,6,24,768]{3,2,1,0:T(8,128)(2,1)}, bf16[3,6,24,768]{3,2,1,0:T(8,128)(2,1)}, u32[]{:S(2)}, u32[]{:S(2)}) collective-permute-start(bf16[3,6,24,768]{3,2,1,0:T(8,128)(2,1)} %slice.401), channel_id=1, source_target_pairs={{0,16},{1,17},{2,18},{3,19},{4,20},{5,21},{6,22},{7,23},{8,24},{9,... | collective-permute-start | bytes 1990664 | tf_op jit(solution)/shard_map/ppermute | solution.py:441
  153.0 23.7 %collective-permute-start.13 = (bf16[2,512,768]{2,1,0:T(8,128)(2,1)}, bf16[2,512,768]{2,1,0:T(8,128)(2,1)S(1)}, u32[]{:S(2)}, u32[]{:S(2)}) collective-permute-start(bf16[2,512,768]{2,1,0:T(8,128)(2,1)} %get-tuple-element.81.ka_ref.va_ref), channel_id=1, source_target_pairs={{0,1},{1,0},{2,3},{3,2},{4,5},{5,4},{6,7},{7,6},{8,9},{9,8},{10,11... | collective-permute-start | bytes 4718600 | tf_op jit(solution)/shard_map/ppermute | solution.py:441
  156.0 19.6 %collective-permute-start.23 = (bf16[3,8,24,768]{3,2,1,0:T(8,128)(2,1)}, bf16[3,8,24,768]{3,2,1,0:T(8,128)(2,1)S(1)}, u32[]{:S(2)}, u32[]{:S(2)}) collective-permute-start(bf16[3,8,24,768]{3,2,1,0:T(8,128)(2,1)} %collective-permute-done.17.refs_2_), channel_id=1, source_target_pairs={{0,1},{1,0},{2,3},{3,2},{4,5},{5,4},{6,7},{7,6},{8,9},{9,8},{10,11... | collective-permute-start | bytes 2654216 | tf_op jit(solution)/shard_map/ppermute | solution.py:441
  156.3 19.9 %collective-permute-start.24 = (bf16[3,8,24,768]{3,2,1,0:T(8,128)(2,1)}, bf16[3,8,24,768]{3,2,1,0:T(8,128)(2,1)S(1)}, u32[]{:S(2)}, u32[]{:S(2)}) collective-permute-start(bf16[3,8,24,768]{3,2,1,0:T(8,128)(2,1)} %collective-permute-done.18.refs_3_), channel_id=1, source_target_pairs={{0,1},{1,0},{2,3},{3,2},{4,5},{5,4},{6,7},{7,6},{8,9},{9,8},{10,11... | collective-permute-start | bytes 2654216 | tf_op jit(solution)/shard_map/ppermute | solution.py:441
  156.6 19.7 %collective-permute-start.25 = (bf16[3,8,24,768]{3,2,1,0:T(8,128)(2,1)S(1)}, bf16[3,8,24,768]{3,2,1,0:T(8,128)(2,1)S(1)}, u32[]{:S(2)}, u32[]{:S(2)}) collective-permute-start(bf16[3,8,24,768]{3,2,1,0:T(8,128)(2,1)S(1)} %constant_dynamic-update-slice_fusion.2.refs_4_), channel_id=1, source_target_pairs={{0,1},{1,0},{2,3},{3,2},{4,5},{5,4},{6,7},{7,6},{8,9},{9,8},{10,11... | collective-permute-start | bytes 2654216 | tf_op jit(solution)/shard_map/ppermute | solution.py:441
  171.6 66.3 %collective-permute-start.33 = (bf16[4,12,24,768]{3,2,1,0:T(8,128)(2,1)S(1)}, bf16[4,12,24,768]{3,2,1,0:T(8,128)(2,1)}, u32[]{:S(2)}, u32[]{:S(2)}) collective-permute-start(bf16[4,12,24,768]{3,2,1,0:T(8,128)(2,1)S(1)} %pad_maximum_fusion.2.refs_0_), channel_id=1, source_target_pairs={{0,1},{1,0},{2,3},{3,2},{4,5},{5,4},{6,7},{7,6},{8,9},{9,8},{10,11... | collective-permute-start | bytes 5308424 | tf_op jit(solution)/shard_map/ppermute | solution.py:441
  175.6 62.6 %collective-permute-start.34 = (bf16[3,12,24,768]{3,2,1,0:T(8,128)(2,1)}, bf16[3,12,24,768]{3,2,1,0:T(8,128)(2,1)}, u32[]{:S(2)}, u32[]{:S(2)}) collective-permute-start(bf16[3,12,24,768]{3,2,1,0:T(8,128)(2,1)} %pad_maximum_fusion.9.refs_1_), channel_id=1, source_target_pairs={{0,1},{1,0},{2,3},{3,2},{4,5},{5,4},{6,7},{7,6},{8,9},{9,8},{10,11... | collective-permute-start | bytes 3981320 | tf_op jit(solution)/shard_map/ppermute | solution.py:441
  176.2 62.1 %collective-permute-start.35 = (bf16[3,12,24,768]{3,2,1,0:T(8,128)(2,1)}, bf16[3,12,24,768]{3,2,1,0:T(8,128)(2,1)}, u32[]{:S(2)}, u32[]{:S(2)}) collective-permute-start(bf16[3,12,24,768]{3,2,1,0:T(8,128)(2,1)} %collective-permute-done.29.refs_2_), channel_id=1, source_target_pairs={{0,1},{1,0},{2,3},{3,2},{4,5},{5,4},{6,7},{7,6},{8,9},{9,8},{10,11... | collective-permute-start | bytes 3981320 | tf_op jit(solution)/shard_map/ppermute | solution.py:441
  176.3 62.0 %collective-permute-start.36 = (bf16[3,12,24,768]{3,2,1,0:T(8,128)(2,1)}, bf16[3,12,24,768]{3,2,1,0:T(8,128)(2,1)}, u32[]{:S(2)}, u32[]{:S(2)}) collective-permute-start(bf16[3,12,24,768]{3,2,1,0:T(8,128)(2,1)} %collective-permute-done.30.refs_3_), channel_id=1, source_target_pairs={{0,1},{1,0},{2,3},{3,2},{4,5},{5,4},{6,7},{7,6},{8,9},{9,8},{10,11... | collective-permute-start | bytes 3981320 | tf_op jit(solution)/shard_map/ppermute | solution.py:441
  177.3 60.9 %collective-permute-start.37 = (bf16[3,12,24,768]{3,2,1,0:T(8,128)(2,1)}, bf16[3,12,24,768]{3,2,1,0:T(8,128)(2,1)}, u32[]{:S(2)}, u32[]{:S(2)}) collective-permute-start(bf16[3,12,24,768]{3,2,1,0:T(8,128)(2,1)} %constant_dynamic-update-slice_fusion.4.refs_4_), channel_id=1, source_target_pairs={{0,1},{1,0},{2,3},{3,2},{4,5},{5,4},{6,7},{7,6},{8,9},{9,8},{10,11... | collective-permute-start | bytes 3981320 | tf_op jit(solution)/shard_map/ppermute | solution.py:441
  396.7 37.5 %collective-permute-start.59 = (bf16[3,512,768]{2,1,0:T(8,128)(2,1)}, bf16[3,512,768]{2,1,0:T(8,128)(2,1)}, u32[]{:S(2)}, u32[]{:S(2)}) collective-permute-start(bf16[3,512,768]{2,1,0:T(8,128)(2,1)} %get-tuple-element.127.dm_ref), channel_id=1, source_target_pairs={{0,1},{1,0},{2,3},{3,2},{4,5},{5,4},{6,7},{7,6},{8,9},{9,8},{10,11... | collective-permute-start | bytes 7077896 | tf_op jit(solution)/shard_map/ppermute | solution.py:441
  396.9 54.9 %collective-permute-start.77 = (bf16[512,3072]{1,0:T(8,128)(2,1)}, bf16[512,3072]{1,0:T(8,128)(2,1)}, u32[]{:S(2)}, u32[]{:S(2)}) collective-permute-start(bf16[512,3072]{1,0:T(8,128)(2,1)} %get-tuple-element.143.dz_ref), channel_id=1, source_target_pairs={{0,1},{1,0},{2,3},{3,2},{4,5},{5,4},{6,7},{7,6},{8,9},{9,8},{10,11... | collective-permute-start | bytes 9437192 | tf_op jit(solution)/shard_map/ppermute | solution.py:441
  410.1 18.8 %collective-permute-start.78 = (bf16[512,768]{1,0:T(8,128)(2,1)S(1)}, bf16[512,768]{1,0:T(8,128)(2,1)S(1)}, u32[]{:S(2)}, u32[]{:S(2)}) collective-permute-start(bf16[512,768]{1,0:T(8,128)(2,1)S(1)} %copy-done.46), channel_id=1, source_target_pairs={{0,1},{1,0},{2,3},{3,2},{4,5},{5,4},{6,7},{7,6},{8,9},{9,8},{10,11... | collective-permute-start | bytes 2359304 | tf_op jit(solution)/shard_map/ppermute | solution.py:441
  434.2 61.4 %collective-permute-start.67 = (bf16[512,1536]{1,0:T(8,128)(2,1)}, bf16[512,1536]{1,0:T(8,128)(2,1)}, u32[]{:S(2)}, u32[]{:S(2)}) collective-permute-start(bf16[512,1536]{1,0:T(8,128)(2,1)} %get-tuple-element.134), channel_id=1, source_target_pairs={{0,1},{1,0},{2,3},{3,2},{4,5},{5,4},{6,7},{7,6},{8,9},{9,8},{10,11... | collective-permute-start | bytes 4718600 | tf_op jit(solution)/shard_map/ppermute | solution.py:441
  434.2 68.5 %collective-permute-start.68 = (bf16[512,3072]{1,0:T(8,128)(2,1)}, bf16[512,3072]{1,0:T(8,128)(2,1)}, u32[]{:S(2)}, u32[]{:S(2)}) collective-permute-start(bf16[512,3072]{1,0:T(8,128)(2,1)} %get-tuple-element.135.dz_ref), channel_id=1, source_target_pairs={{0,1},{1,0},{2,3},{3,2},{4,5},{5,4},{6,7},{7,6},{8,9},{9,8},{10,11... | collective-permute-start | bytes 9437192 | tf_op jit(solution)/shard_map/ppermute | solution.py:441
  443.4 21.2 %collective-permute-start.86 = (f32[4,2,1152]{2,1,0:T(2,128)S(1)}, f32[4,2,1152]{2,1,0:T(2,128)S(1)}, u32[]{:S(2)}, u32[]{:S(2)}) collective-permute-start(f32[4,2,1152]{2,1,0:T(2,128)S(1)} %add.234), channel_id=1, source_target_pairs={{0,16},{1,17},{2,18},{3,19},{4,20},{5,21},{6,22},{7,23},{8,24},{9,... | collective-permute-start | bytes 110600 | tf_op jit(solution)/shard_map/ppermute | solution.py:441
  444.5 51.9 %collective-permute-start.61 = (bf16[4,2,4,24,768]{4,3,2,1,0:T(8,128)(2,1)}, bf16[4,2,4,24,768]{4,3,2,1,0:T(8,128)(2,1)S(1)}, u32[]{:S(2)}, u32[]{:S(2)}) collective-permute-start(bf16[4,2,4,24,768]{4,3,2,1,0:T(8,128)(2,1)} %get-tuple-element.130), channel_id=1, source_target_pairs={{0,16},{1,17},{2,18},{3,19},{4,20},{5,21},{6,22},{7,23},{8,24},{9,... | collective-permute-start | bytes 3538952 | tf_op jit(solution)/shard_map/ppermute | solution.py:441
  451.9 32.6 %collective-permute-start.66 = (bf16[512,384]{1,0:T(8,128)(2,1)}, bf16[512,384]{1,0:T(8,128)(2,1)S(1)}, u32[]{:S(2)}, u32[]{:S(2)}) collective-permute-start(bf16[512,384]{1,0:T(8,128)(2,1)} %get-tuple-element.132), channel_id=1, source_target_pairs={{0,1},{1,0},{2,3},{3,2},{4,5},{5,4},{6,7},{7,6},{8,9},{9,8},{10,11... | collective-permute-start | bytes 1179656 | tf_op jit(solution)/shard_map/ppermute | solution.py:441
  464.6 29.5 %collective-permute-start.41 = (bf16[256,768]{1,0:T(8,128)(2,1)S(1)}, bf16[256,768]{1,0:T(8,128)(2,1)S(1)}, u32[]{:S(2)}, u32[]{:S(2)}) collective-permute-start(bf16[256,768]{1,0:T(8,128)(2,1)S(1)} %slice.405), channel_id=1, source_target_pairs={{0,2},{1,3},{2,0},{3,1},{4,6},{5,7},{6,4},{7,5},{8,10},{9,11},{10,... | collective-permute-start | bytes 1179656 | tf_op jit(solution)/shard_map/ppermute | solution.py:441
  484.4 53.7 %collective-permute-start.79 = (bf16[4,2,8,24,768]{4,3,2,1,0:T(8,128)(2,1)}, bf16[4,2,8,24,768]{4,3,2,1,0:T(8,128)(2,1)}, u32[]{:S(2)}, u32[]{:S(2)}) collective-permute-start(bf16[4,2,8,24,768]{4,3,2,1,0:T(8,128)(2,1)} %get-tuple-element.146), channel_id=1, source_target_pairs={{0,16},{1,17},{2,18},{3,19},{4,20},{5,21},{6,22},{7,23},{8,24},{9,... | collective-permute-start | bytes 7077896 | tf_op jit(solution)/shard_map/ppermute | solution.py:441
  496.4 51.1 %collective-permute-start.50 = (bf16[3,512,768]{2,1,0:T(8,128)(2,1)}, bf16[3,512,768]{2,1,0:T(8,128)(2,1)}, u32[]{:S(2)}, u32[]{:S(2)}) collective-permute-start(bf16[3,512,768]{2,1,0:T(8,128)(2,1)} %get-tuple-element.119.dm_ref), channel_id=1, source_target_pairs={{0,1},{1,0},{2,3},{3,2},{4,5},{5,4},{6,7},{7,6},{8,9},{9,8},{10,11... | collective-permute-start | bytes 7077896 | tf_op jit(solution)/shard_map/ppermute | solution.py:441
  501.5 55.2 %collective-permute-start.46 = (bf16[2,512,768]{2,1,0:T(8,128)(2,1)S(1)}, bf16[2,512,768]{2,1,0:T(8,128)(2,1)}, u32[]{:S(2)}, u32[]{:S(2)}) collective-permute-start(bf16[2,512,768]{2,1,0:T(8,128)(2,1)S(1)} %pad_maximum_fusion.7.refs_0_), channel_id=1, source_target_pairs={{0,1},{1,0},{2,3},{3,2},{4,5},{5,4},{6,7},{7,6},{8,9},{9,8},{10,11... | collective-permute-start | bytes 4718600 | tf_op jit(solution)/shard_map/ppermute | solution.py:441
  515.6 31.9 %collective-permute-start.51 = (bf16[512,768]{1,0:T(8,128)(2,1)}, bf16[512,768]{1,0:T(8,128)(2,1)}, u32[]{:S(2)}, u32[]{:S(2)}) collective-permute-start(bf16[512,768]{1,0:T(8,128)(2,1)} %get-tuple-element.120.da_ref), channel_id=1, source_target_pairs={{0,1},{1,0},{2,3},{3,2},{4,5},{5,4},{6,7},{7,6},{8,9},{9,8},{10,11... | collective-permute-start | bytes 2359304 | tf_op jit(solution)/shard_map/ppermute | solution.py:441
  518.4 26.9 %collective-permute-start.49 = (bf16[512,384]{1,0:T(8,128)(2,1)S(1)}, bf16[512,384]{1,0:T(8,128)(2,1)S(1)}, u32[]{:S(2)}, u32[]{:S(2)}) collective-permute-start(bf16[512,384]{1,0:T(8,128)(2,1)S(1)} %copy-done.75), channel_id=1, source_target_pairs={{0,1},{1,0},{2,3},{3,2},{4,5},{5,4},{6,7},{7,6},{8,9},{9,8},{10,11... | collective-permute-start | bytes 1179656 | tf_op jit(solution)/shard_map/ppermute | solution.py:441
  538.2 25.6 %collective-permute-start.63 = (bf16[2,4,24,768]{3,2,1,0:T(8,128)(2,1)}, bf16[2,4,24,768]{3,2,1,0:T(8,128)(2,1)}, u32[]{:S(2)}, u32[]{:S(2)}) collective-permute-start(bf16[2,4,24,768]{3,2,1,0:T(8,128)(2,1)} %select_bitcast_fusion.2), channel_id=1, source_target_pairs={{0,2},{1,3},{2,0},{3,1},{4,6},{5,7},{6,4},{7,5},{8,10},{9,11},{10,... | collective-permute-start | bytes 884744 | tf_op jit(solution)/shard_map/ppermute | solution.py:441
  545.3 88.3 %collective-permute-start.70 = (bf16[4,2,8,24,768]{4,3,2,1,0:T(8,128)(2,1)}, bf16[4,2,8,24,768]{4,3,2,1,0:T(8,128)(2,1)}, u32[]{:S(2)}, u32[]{:S(2)}) collective-permute-start(bf16[4,2,8,24,768]{4,3,2,1,0:T(8,128)(2,1)} %get-tuple-element.138), channel_id=1, source_target_pairs={{0,8},{1,9},{2,10},{3,11},{4,12},{5,13},{6,14},{7,15},{8,0},{9,1},... | collective-permute-start | bytes 7077896 | tf_op jit(solution)/shard_map/ppermute | solution.py:441
  547.5 21.3 %collective-permute-start.88 = (f32[2,1152]{1,0:T(2,128)}, f32[2,1152]{1,0:T(2,128)}, u32[]{:S(2)}, u32[]{:S(2)}) collective-permute-start(f32[2,1152]{1,0:T(2,128)} %select_bitcast_fusion.4), channel_id=1, source_target_pairs={{0,2},{1,3},{2,0},{3,1},{4,6},{5,7},{6,4},{7,5},{8,10},{9,11},{10,... | collective-permute-start | bytes 27656 | tf_op jit(solution)/shard_map/ppermute | solution.py:441
  547.5 84.5 %collective-permute-start.80 = (bf16[2,2,8,24,768]{4,3,2,1,0:T(8,128)(2,1)}, bf16[2,2,8,24,768]{4,3,2,1,0:T(8,128)(2,1)}, u32[]{:S(2)}, u32[]{:S(2)}) collective-permute-start(bf16[2,2,8,24,768]{4,3,2,1,0:T(8,128)(2,1)} %broadcast_select_fusion), channel_id=1, source_target_pairs={{2,4},{3,5},{4,2},{5,3},{10,12},{11,13},{12,10},{13,11},{18,20},{1... | collective-permute-start | bytes 3538952 | tf_op jit(solution)/shard_map/ppermute | solution.py:441
  556.8 73.9 %collective-permute-start.52 = (bf16[4,2,4,24,768]{4,3,2,1,0:T(8,128)(2,1)}, bf16[4,2,4,24,768]{4,3,2,1,0:T(8,128)(2,1)S(1)}, u32[]{:S(2)}, u32[]{:S(2)}) collective-permute-start(bf16[4,2,4,24,768]{4,3,2,1,0:T(8,128)(2,1)} %get-tuple-element.122), channel_id=1, source_target_pairs={{0,8},{1,9},{2,10},{3,11},{4,12},{5,13},{6,14},{7,15},{8,0},{9,1},... | collective-permute-start | bytes 3538952 | tf_op jit(solution)/shard_map/ppermute | solution.py:441
  568.7 60.8 %collective-permute-start.64 = (bf16[2,4,24,768]{3,2,1,0:T(8,128)(2,1)S(1)}, bf16[2,4,24,768]{3,2,1,0:T(8,128)(2,1)S(1)}, u32[]{:S(2)}, u32[]{:S(2)}) collective-permute-start(bf16[2,4,24,768]{3,2,1,0:T(8,128)(2,1)S(1)} %bitcast_select_fusion.2), channel_id=1, source_target_pairs={{0,8},{1,9},{2,10},{3,11},{4,12},{5,13},{6,14},{7,15},{8,0},{9,1},... | collective-permute-start | bytes 884744 | tf_op jit(solution)/shard_map/ppermute | solution.py:441
  629.6 21.8 %collective-permute-start.65 = (bf16[2,4,24,768]{3,2,1,0:T(8,128)(2,1)S(1)}, bf16[2,4,24,768]{3,2,1,0:T(8,128)(2,1)S(1)}, u32[]{:S(2)}, u32[]{:S(2)}) collective-permute-start(bf16[2,4,24,768]{3,2,1,0:T(8,128)(2,1)S(1)} %add_convert_fusion.10), channel_id=1, source_target_pairs={{0,16},{1,17},{2,18},{3,19},{4,20},{5,21},{6,22},{7,23},{8,24},{9,... | collective-permute-start | bytes 884744 | tf_op jit(solution)/shard_map/ppermute | solution.py:441
  637.1 33.8 %collective-permute-start.71 = (bf16[2,2,8,24,768]{4,3,2,1,0:T(8,128)(2,1)}, bf16[2,2,8,24,768]{4,3,2,1,0:T(8,128)(2,1)}, u32[]{:S(2)}, u32[]{:S(2)}) collective-permute-start(bf16[2,2,8,24,768]{4,3,2,1,0:T(8,128)(2,1)} %broadcast_select_fusion.1), channel_id=1, source_target_pairs={{2,4},{3,5},{4,2},{5,3},{10,12},{11,13},{12,10},{13,11},{18,20},{1... | collective-permute-start | bytes 3538952 | tf_op jit(solution)/shard_map/ppermute | solution.py:441
  639.0 19.4 %collective-permute-start.54 = (bf16[2,4,24,768]{3,2,1,0:T(8,128)(2,1)S(1)}, bf16[2,4,24,768]{3,2,1,0:T(8,128)(2,1)S(1)}, u32[]{:S(2)}, u32[]{:S(2)}) collective-permute-start(bf16[2,4,24,768]{3,2,1,0:T(8,128)(2,1)S(1)} %select_bitcast_fusion.3), channel_id=1, source_target_pairs={{0,2},{1,3},{2,0},{3,1},{4,6},{5,7},{6,4},{7,5},{8,10},{9,11},{10,... | collective-permute-start | bytes 884744 | tf_op jit(solution)/shard_map/ppermute | solution.py:441
  (121 other events, 1412.9 us)

commit v3 on v2

--- a/solution.py
+++ b/solution.py
@@ -458,6 +458,12 @@
     return jax.ShapeDtypeStruct(shape, kind)
 
 
+def cost(micros):
+    return pl.CostEstimate(
+        flops=int(micros * 1e9), bytes_accessed=int(micros * 1e6), transcendentals=0
+    )
+
+
 def nt(left, right):
     return lax.dot_general(left, right, (((1,), (1,)), ((), ())), preferred_element_type=jnp.float32)
 
@@ -492,6 +498,7 @@
         in_specs=[VMEM] * (2 + len(pieces)),
         out_specs=VMEM,
         compiler_params=LIMIT,
+        cost_estimate=cost(5),
         name="gather_rows",
     )(ids, want, *pieces)
 
@@ -538,33 +545,18 @@
         ),
         out_shape=shaped(shape),
         compiler_params=LIMIT,
+        cost_estimate=cost(6),
         name="assemble",
     )(where, *parts)
     return result.reshape(4, 32 * UNIT, width)
 
 
-def pack_weights(entry, leaving, expand, shrink):
-    width = leaving.shape[1]
-
-    def by_columns(weight):
-        count = weight.shape[1] // width
-        return low(weight).reshape(4, UNIT, count, width).transpose(0, 2, 1, 3)
-
-    return (
-        jnp.concatenate([by_columns(entry), by_columns(leaving)], axis=1),
-        jnp.concatenate([by_columns(expand), low(shrink).reshape(4, 4, UNIT, width)], axis=1),
-    )
-
-
-def spread(own, near, middle, far):
-    units = own.shape[1]
-    first = jnp.stack([near, middle, far])
-    over_x = send(first, TO_X)
-    over_y = send(first, TO_Y)
-    half = units // 2
-    over_d = jnp.concatenate(
-        [send(over_x[:, :half], TO_Y), send(over_y[:, half:], TO_X)], axis=1
-    )
+def tie(value, *others):
+    return lax.optimization_barrier((value,) + others)[0]
+
+
+def spread(own, first, over_x, over_y, x_last):
+    over_d = send(over_y, TO_X) if x_last else send(over_x, TO_Y)
     mine = (own, first, over_x, over_y, over_d)
     return mine + tuple(send(item, TO_TWIN) for item in mine)
 
@@ -612,6 +604,7 @@
             shaped((rows, width // 2)),
         ],
         compiler_params=LIMIT,
+        cost_estimate=cost(7),
         name="project",
     )(hidden, weight, vec, sel)
 
@@ -679,6 +672,7 @@
         ],
         scratch_shapes=[pltpu.VMEM((2 * half, half), jnp.float32)],
         compiler_params=LIMIT,
+        cost_estimate=cost(15),
         name="attend_forward",
     )(queries, kv, kv_twin, kv, kv_twin, code, member)
 
@@ -748,6 +742,7 @@
         ],
         scratch_shapes=[pltpu.VMEM((2 * half, half), jnp.float32)],
         compiler_params=LIMIT,
+        cost_estimate=cost(20),
         name="attend_backward",
     )(queries, grad, kv, kv_twin, kv, kv_twin, ot, lse, code, member)
 
@@ -778,12 +773,11 @@
 
 def post_kernel(
     where_ref, o_ref, h_ref, wo_ref, up_ref, down_ref, vec_ref, sel_ref,
-    h_out, hl_out, n1_out, t1_out, n2_out, t2_out, slope_out,
-    om_out, ot_out, ym_out, yt_out, gm_out, gt_out,
+    h_out, hl_out, n1_out, t1_out, n2_out, t2_out, slope_out, mine_out, theirs_out,
     y_ref, yl_ref, f_ref,
 ):
     step = pl.program_id(0)
-    half_width = om_out.shape[1]
+    half_width = mine_out.shape[2]
 
     @pl.when(step == 0)
     def _():
@@ -795,10 +789,10 @@
         t1_out[...] = factor
         y_ref[...] = middle
         yl_ref[...] = low(middle)
-        om_out[...] = low(nn(attended, sel_ref[0]))
-        ot_out[...] = low(nn(attended, sel_ref[1]))
-        ym_out[...] = low(nn(yl_ref[...], sel_ref[0]))
-        yt_out[...] = low(nn(yl_ref[...], sel_ref[1]))
+        mine_out[4] = low(nn(yl_ref[...], sel_ref[0]))
+        theirs_out[4] = low(nn(yl_ref[...], sel_ref[1]))
+        mine_out[5] = low(nn(attended, sel_ref[0]))
+        theirs_out[5] = low(nn(attended, sel_ref[1]))
 
     inner = nn(yl_ref[...], up_ref[...]) + vec_ref[pl.ds(8 + step, 1), :]
     cumulative, density = normal_parts(inner)
@@ -806,8 +800,8 @@
     active = low(inner * cumulative)
     first, second = active[:, :half_width], active[:, half_width:]
     swap = where_ref[2] == 1
-    gm_out[...] = jnp.where(swap, second, first)
-    gt_out[...] = jnp.where(swap, first, second)
+    mine_out[step] = jnp.where(swap, second, first)
+    theirs_out[step] = jnp.where(swap, first, second)
     part = nn(active, down_ref[...])
 
     @pl.when(step == 0)
@@ -853,8 +847,7 @@
             fixed(12, width), fixed(2, width, half),
         ],
         out_specs=[full, full, full, thin, full, thin, column_spec(rows, width)]
-        + [fixed(rows, half)] * 4
-        + [column_spec(rows, half)] * 2,
+        + [fixed(6, rows, half)] * 2,
         out_shape=[
             shaped((rows, width), jnp.float32),
             shaped((rows, width)),
@@ -864,14 +857,14 @@
             shaped((rows, 1), jnp.float32),
             shaped((rows, 4 * width)),
         ]
-        + [shaped((rows, half))] * 4
-        + [shaped((rows, 4 * half))] * 2,
+        + [shaped((6, rows, half))] * 2,
         scratch_shapes=[
             pltpu.VMEM((rows, width), jnp.float32),
             pltpu.VMEM((rows, width), jnp.bfloat16),
             pltpu.VMEM((rows, width), jnp.float32),
         ],
         compiler_params=LIMIT,
+        cost_estimate=cost(23),
         name="post",
     )(where, attended, hidden, front, up, down, vec, sel)
 
@@ -891,7 +884,7 @@
 
 def post_back_kernel(
     e_ref, n1_ref, t1_ref, n2_ref, t2_ref, slope_ref, wo_ref, up_ref, down_ref, vec_ref,
-    df_out, dz_out, da_out, do_out, dr_out, sums_out,
+    all_out, do_out, dr_out, sums_out,
     r_ref, y_ref,
 ):
     step = pl.program_id(0)
@@ -903,14 +896,14 @@
         resid = norm_back(incoming, normed, t2_ref[...], vec_ref[6:7, :])
         r_ref[...] = resid
         rounded = low(resid)
-        df_out[...] = rounded
+        all_out[4] = rounded
         sums_out[0:2, :] = jnp.zeros((2, sums_out.shape[1]), jnp.float32)
         sums_out[5:6, :] = column_sum(wide(rounded))
         sums_out[6:7, :] = column_sum(incoming * normed)
         sums_out[7:8, :] = column_sum(incoming)
 
-    steep = low(nt(df_out[...], down_ref[...]) * wide(slope_ref[...]))
-    dz_out[...] = steep
+    steep = low(nt(all_out[4], down_ref[...]) * wide(slope_ref[...]))
+    all_out[step] = steep
     sums_out[pl.ds(8 + step, 1), :] = column_sum(wide(steep))
     part = nt(steep, up_ref[...])
 
@@ -929,7 +922,7 @@
         resid = norm_back(incoming, normed, t1_ref[...], vec_ref[3:4, :])
         dr_out[...] = resid
         rounded = low(resid)
-        da_out[...] = rounded
+        all_out[5] = rounded
         do_out[...] = low(nt(rounded, wo_ref[...]))
         sums_out[2:3, :] = column_sum(wide(rounded))
         sums_out[3:4, :] = column_sum(incoming * normed)
@@ -947,11 +940,9 @@
             full, full, thin, full, thin, column_spec(rows, width),
             unit_spec(width, 3), step_spec(width), step_spec(width), fixed(12, width),
         ],
-        out_specs=[full, column_spec(rows, width), full, full, full, fixed(12, width)],
+        out_specs=[fixed(6, rows, width), full, full, fixed(12, width)],
         out_shape=[
-            shaped((rows, width)),
-            shaped((rows, 4 * width)),
-            shaped((rows, width)),
+            shaped((6, rows, width)),
             shaped((rows, width)),
             shaped((rows, width), jnp.float32),
             shaped((12, width), jnp.float32),
@@ -961,6 +952,7 @@
             pltpu.VMEM((rows, width), jnp.float32),
         ],
         compiler_params=LIMIT,
+        cost_estimate=cost(16),
         name="post_back",
     )(upstream, n1, t1, n2, t2, slope, front, up, down, vec)
 
@@ -1016,6 +1008,7 @@
             shaped((2, width), jnp.float32),
         ],
         compiler_params=LIMIT,
+        cost_estimate=cost(9),
         name="project_back",
     )(dq, own, got, front, dr)
 
@@ -1034,72 +1027,74 @@
         store(give_ref, other, jnp.where(bit == 0, pair[1], pair[0]))
 
 
+def column_store(ref_pair, bit, x_first, product, unit):
+    keep_ref, give_ref = ref_pair
+    for level in range(4):
+        base = level * 4 * UNIT
+
+        def piece_of(rep):
+            return product[base + rep * UNIT : base + (rep + 1) * UNIT, :]
+
+        def store(ref, other, value):
+            ref[level, other, unit] = value
+
+        split_store(keep_ref, give_ref, bit, x_first, piece_of, store)
+
+
 def front_grad_kernel(
     x_first, bit_ref, xm_ref, xt_ref, om_ref, ot_ref, dm_ref, dmt_ref, da_ref, dat_ref,
     keep_ref, give_ref,
 ):
     unit = pl.program_id(0)
-    bit = bit_ref[0]
-
-    def put(product):
-        for level in range(4):
-            base = level * 4 * UNIT
-
-            def piece_of(rep):
-                return product[base + rep * UNIT : base + (rep + 1) * UNIT, :]
-
-            def store(ref, other, value):
-                ref[level, other, unit] = value
-
-            split_store(keep_ref, give_ref, bit, x_first, piece_of, store)
+    bit = bit_ref[0 if x_first else 1]
 
     @pl.when(unit < 3)
     def _():
-        put(tn(xm_ref[...], dm_ref[...]) + tn(xt_ref[...], dmt_ref[...]))
+        product = tn(xm_ref[...], dm_ref[...]) + tn(xt_ref[...], dmt_ref[...])
+        column_store((keep_ref, give_ref), bit, x_first, product, unit)
 
     @pl.when(unit == 3)
     def _():
-        put(tn(om_ref[...], da_ref[...]) + tn(ot_ref[...], dat_ref[...]))
-
-
-def front_grad(x_first, bit, xm, xt, om, ot, dm, dmt, da, dat):
+        product = tn(om_ref[...], da_ref[...]) + tn(ot_ref[...], dat_ref[...])
+        column_store((keep_ref, give_ref), bit, x_first, product, unit)
+
+
+def block_spec(rows, width, index):
+    return pl.BlockSpec((None, rows, width), lambda step: (index, 0, 0))
+
+
+def front_grad(x_first, bits, xm, xt, mine, theirs, dm, dmt, da, dat):
     rows, half = xm.shape
-    width = da.shape[1]
+    width = da.shape[2]
     late = pl.BlockSpec((None, rows, width), lambda unit: (jnp.minimum(unit, 2), 0, 0))
     shape = (4, 2, 4, UNIT, width)
     return pl.pallas_call(
         functools.partial(front_grad_kernel, x_first),
         grid=(4,),
-        in_specs=[SMEM]
-        + [fixed(rows, half)] * 4
-        + [late, late, fixed(rows, width), fixed(rows, width)],
+        in_specs=[SMEM, fixed(rows, half), fixed(rows, half)]
+        + [block_spec(rows, half, 5)] * 2
+        + [late, late]
+        + [block_spec(rows, width, 5)] * 2,
         out_specs=[fixed(*shape)] * 2,
         out_shape=[shaped(shape)] * 2,
         compiler_params=LIMIT,
+        cost_estimate=cost(7),
         name="front_grad",
-    )(bit, xm, xt, om, ot, dm, dmt, da, dat)
+    )(bits, xm, xt, mine, theirs, dm, dmt, da, dat)
 
 
 def feed_grad_kernel(
     x_first, bit_ref, ym_ref, yt_ref, gm_ref, gt_ref, dz_ref, dzt_ref, df_ref, dft_ref,
-    keep_ref, give_ref,
+    keep_up, give_up, keep_down, give_down,
 ):
     step = pl.program_id(0)
-    bit = bit_ref[0]
+    up_bit = bit_ref[0 if x_first else 1]
+    down_bit = bit_ref[1 if x_first else 0]
 
     @pl.when(step < 4)
     def _():
         product = tn(ym_ref[...], dz_ref[...]) + tn(yt_ref[...], dzt_ref[...])
-        for level in range(4):
-            base = level * 4 * UNIT
-
-            def piece_of(rep):
-                return product[base + rep * UNIT : base + (rep + 1) * UNIT, :]
-
-            def store(ref, other, value):
-                ref[level, other, step] = value
-
-            split_store(keep_ref, give_ref, bit, x_first, piece_of, store)
+        column_store((keep_up, give_up), up_bit, x_first, product, step)
 
     @pl.when(step >= 4)
     def _():
@@ -1111,48 +1106,71 @@
                 return product[base : base + UNIT, :]
 
             def store(ref, other, value):
-                ref[step - 4, other, 4 + sub] = value
-
-            split_store(keep_ref, give_ref, bit, x_first, piece_of, store)
-
-
-def feed_grad(x_first, bit, ym, yt, gm, gt, dz, dzt, df, dft):
-    rows, half = ym.shape
-    width = df.shape[1]
-    early = pl.BlockSpec((rows, width), lambda step: (0, jnp.minimum(step, 3)))
-    late = pl.BlockSpec((rows, half), lambda step: (0, jnp.maximum(step - 4, 0)))
-    shape = (4, 2, 8, UNIT, width)
+                ref[step - 4, other, sub] = value
+
+            split_store(keep_down, give_down, down_bit, not x_first, piece_of, store)
+
+
+def feed_grad(x_first, bits, mine, theirs, slopes, slopes_twin):
+    rows, half = mine.shape[1:]
+    width = slopes.shape[2]
+    early = pl.BlockSpec((None, rows, width), lambda step: (jnp.minimum(step, 3), 0, 0))
+    late = pl.BlockSpec((None, rows, half), lambda step: (jnp.maximum(step - 4, 0), 0, 0))
+    shape = (4, 2, 4, UNIT, width)
     return pl.pallas_call(
         functools.partial(feed_grad_kernel, x_first),
         grid=(8,),
         in_specs=[SMEM]
-        + [fixed(rows, half)] * 2
-        + [late, late, early, early, fixed(rows, width), fixed(rows, width)],
-        out_specs=[fixed(*shape)] * 2,
-        out_shape=[shaped(shape)] * 2,
+        + [block_spec(rows, half, 4)] * 2
+        + [late, late, early, early]
+        + [block_spec(rows, width, 4)] * 2,
+        out_specs=[fixed(*shape)] * 4,
+        out_shape=[shaped(shape)] * 4,
         compiler_params=LIMIT,
+        cost_estimate=cost(12),
         name="feed_grad",
-    )(bit, ym, yt, gm, gt, dz, dzt, df, dft)
-
-
-def reduce_grad(keep, give, bit, is_low, is_core, x_first):
-    one, two = (TO_X, TO_Y) if x_first else (TO_Y, TO_X)
-    got = send(give, one)
-    stage = low(wide(keep) + wide(got))
-    give = jnp.where(is_low, stage[2:4], stage[0:2])
-    keep = jnp.where(is_low, stage[0:2], stage[2:4])
-    got = send(give, TO_MID)
-    stage = low(wide(keep) + wide(got))
-    outer = jnp.where(is_low, stage[0], stage[1])
-    inner = jnp.where(is_low, stage[1], stage[0])
-    got = send(outer, TO_SIDE)
-    stage = jnp.where(is_core, inner, got)
-    got = send(stage, two)
-    stage = low(wide(stage) + wide(got))
-    got = send(stage, one)
-    axis = 1 if x_first else 0
-    joined = jnp.where(bit == 0, jnp.stack([stage, got], axis), jnp.stack([got, stage], axis))
-    return wide(joined).reshape((4,) + stage.shape[1:])
+    )(bits, mine, theirs, mine, theirs, slopes, slopes_twin, slopes, slopes_twin)
+
+
+class Reduction:
+    def __init__(self, pairs, bits, is_low, is_core):
+        self.streams = pairs
+        self.bits, self.is_low, self.is_core = bits, is_low, is_core
+        self.got = [
+            send(give, TO_X if x_first else TO_Y) for keep, give, x_first in self.streams
+        ]
+
+    def across(self):
+        stage = jnp.stack(
+            [low(wide(item[0]) + wide(got)) for item, got in zip(self.streams, self.got)]
+        )
+        give = jnp.where(self.is_low, stage[:, 2:4], stage[:, 0:2])
+        self.keep = jnp.where(self.is_low, stage[:, 0:2], stage[:, 2:4])
+        self.mid = send(give, TO_MID)
+        return self.keep
+
+    def outward(self):
+        stage = low(wide(self.keep) + wide(self.mid))
+        outer = jnp.where(self.is_low, stage[:, 0], stage[:, 1])
+        self.inner = jnp.where(self.is_low, stage[:, 1], stage[:, 0])
+        self.side = send(outer, TO_SIDE)
+        return self.inner
+
+    def finish(self):
+        stage = jnp.where(self.is_core, self.inner, self.side)
+        results = []
+        for index, (keep, give, x_first) in enumerate(self.streams):
+            one, two = (TO_X, TO_Y) if x_first else (TO_Y, TO_X)
+            piece = stage[index]
+            piece = low(wide(piece) + wide(send(piece, two)))
+            got = send(piece, one)
+            axis = 1 if x_first else 0
+            bit = self.bits[0] if x_first else self.bits[1]
+            joined = jnp.where(
+                bit == 0, jnp.stack([piece, got], axis), jnp.stack([got, piece], axis)
+            )
+            results.append(wide(joined).reshape((4,) + piece.shape[1:]))
+        return results
 
 
 def body_fast(
@@ -1171,6 +1189,7 @@
     is_core = (depth == 1) | (depth == 2)
     where = jnp.stack([depth, rep, twin]).astype(jnp.int32)
     bits = (rep & 1, rep >> 1)
+    bit_words = jnp.stack(bits).astype(jnp.int32)
 
     def order(four):
         own, near, middle, far = four
@@ -1182,52 +1201,80 @@
         one, two = order(mine), order(theirs)
         return jnp.where(twin == 0, jnp.stack([one, two], 1), jnp.stack([two, one], 1))
 
-    packs = [
-        pack_weights(entry_weight[l], exit_weight[l], expand_weight[l], shrink_weight[l])
-        for l in range(layers)
-    ]
-
     def own_piece(pack):
         piece = lax.dynamic_index_in_dim(pack, rep, 0, keepdims=False)
         return piece.reshape(-1, width)
+
+    def units_of(item):
+        return item.reshape(-1, UNIT, width)
+
+    def pack_front(entry, leaving):
+        return jnp.concatenate([by_columns(entry), by_columns(leaving)], axis=1)
+
+    def pack_feed(expand, shrink):
+        return jnp.concatenate([by_columns(expand), low(shrink).reshape(4, 4, UNIT, width)], axis=1)
+
+    def by_columns(weight):
+        count = weight.shape[1] // width
+        return low(weight).reshape(4, UNIT, count, width).transpose(0, 2, 1, 3)
 
     extra = layers * vectors.shape[1] // width
     tail = low(vectors).reshape(extra, width)
     table = jnp.concatenate([dealing // 64, dealing % 64, key_mask], axis=0)
     table = low(table).reshape(1, width)
     filler = jnp.zeros((7 - extra, width), jnp.bfloat16)
-    front_rows = 4 * UNIT
-    zero = jnp.concatenate([inputs, tail, table, filler, own_piece(packs[0][0])], axis=0)
-    near = send(zero, TO_SIDE)
-    middle = send(zero, TO_MID)
+    rows_in = jnp.concatenate([inputs, tail, table, filler], axis=0)
+
+    front_zero = pack_front(entry_weight[0], exit_weight[0])
+    piece = own_piece(front_zero)
+    near = send(piece, TO_SIDE)
+    middle = send(piece, TO_MID)
+    near_in = send(rows_in, TO_SIDE)
+    middle_in = send(rows_in, TO_MID)
     far = send(near, TO_MID)
-    four = (zero, near, middle, far)
-    lead = rows + 8
-    mine = jnp.stack([item[:lead] for item in four])
+    far_in = send(near_in, TO_MID)
+    first = jnp.stack([units_of(item) for item in (near, middle, far)])
+    over_x, over_y = send(first, TO_X), send(first, TO_Y)
+    parts = spread(front_zero, first, over_x, over_y, False)
+    fronts = [assemble(where, parts, 0, False)]
+    mine = jnp.stack([rows_in, near_in, middle_in, far_in])
     theirs = send(mine, TO_TWIN)
 
-    def relay_units(pack, near, middle, far):
-        shape = (pack.shape[1], UNIT, width)
-        return spread(pack, *[item.reshape(shape) for item in (near, middle, far)])
-
-    parts = relay_units(packs[0][0], *[item[lead:] for item in four[1:]])
-    fronts = [assemble(where, parts, 0, False)]
-
-    piece = own_piece(packs[0][1])
+    expand_late, shrink_late = lax.optimization_barrier(
+        (expand_weight[0], shrink_weight[0], near, middle)
+    )[:2]
+    feed_zero = pack_feed(expand_late, shrink_late)
+    piece = own_piece(feed_zero)
     near = send(piece, TO_SIDE)
-    parts = relay_units(packs[0][1], near, send(piece, TO_MID), send(near, TO_MID))
+    middle = send(piece, TO_MID)
+    far = send(near, TO_MID)
+    first = jnp.stack([units_of(item) for item in (near, middle, far)])
+    first = tie(first, over_x, over_y)
+    over_x, over_y = send(first, TO_X), send(first, TO_Y)
+    parts = spread(feed_zero, first, over_x, over_y, True)
     ups = [assemble(where, parts, 0, False)]
     downs = [assemble(where, parts, 4, True)]
 
-    joined = jnp.concatenate([packs[1][0], packs[1][1]], axis=1)
-    piece = jnp.concatenate([own_piece(joined), cotangent], axis=0)
-    split = 12 * UNIT
+    entry_late, exit_late, expand_late, shrink_late, cotangent_late = lax.optimization_barrier(
+        (entry_weight[1], exit_weight[1], expand_weight[1], shrink_weight[1], cotangent, near, middle)
+    )[:5]
+    front_one = pack_front(entry_late, exit_late)
+    feed_one = pack_feed(expand_late, shrink_late)
+    piece = jnp.concatenate([own_piece(front_one), own_piece(feed_one), cotangent_late], axis=0)
     near = send(piece, TO_SIDE)
     four = (piece, near, send(piece, TO_MID), send(near, TO_MID))
-    parts = relay_units(joined, *[item[:split] for item in four[1:]])
+    first_split, split = 4 * UNIT, 12 * UNIT
+    first = jnp.stack([units_of(item[:first_split]) for item in four[1:]])
+    first = tie(first, over_x, over_y)
+    over_x, over_y = send(first, TO_X), send(first, TO_Y)
+    parts = spread(front_one, first, over_x, over_y, True)
     fronts.append(assemble(where, parts, 0, False))
-    ups.append(assemble(where, parts, 4, False))
-    downs.append(assemble(where, parts, 8, True))
+    first = jnp.stack([units_of(item[first_split:split]) for item in four[1:]])
+    first = tie(first, over_x, over_y)
+    over_x, over_y = send(first, TO_X), send(first, TO_Y)
+    parts = spread(feed_one, first, over_x, over_y, False)
+    ups.append(assemble(where, parts, 0, False))
+    downs.append(assemble(where, parts, 4, True))
     cotangent_mine = jnp.stack([item[split:] for item in four])
     cotangent_theirs = send(cotangent_mine, TO_TWIN)
 
@@ -1286,11 +1333,14 @@
     )
     want_out = jnp.concatenate([source_ids[0, 0], source_ids[1, 0]]).reshape(2 * rows, 1)
 
-    def restore(value):
+    def collect(value):
         pair = jnp.stack([value, send(value, TO_MID)])
-        found = gather_rows((pair, send(pair, TO_TWIN)), result_ids, want_out)
+        return pair, send(pair, TO_TWIN)
+
+    def deliver(pair, other):
+        found = gather_rows((pair, other), result_ids, want_out)
         outer = send(found[rows:], TO_SIDE)
-        return jnp.where(is_core, found[:rows], outer)
+        return found, jnp.where(is_core, found[:rows], outer)
 
     saved = []
     hidden = hidden_low
@@ -1298,40 +1348,81 @@
         vec = vector_all[layer]
         queries, kv, xm, xt = project(hidden_low, fronts[layer], vec, sel)
         kv_twin = send(kv, TO_TWIN)
+        xo = send(xt, TO_TWIN)
         attended, ot, lse = attend_fast(queries, kv, kv_twin, code_half, member_own)
-        (
-            hidden, hidden_low, n1, t1, n2, t2, slope, om, oo, ym, yo, gm, go,
-        ) = post(where, attended, hidden, fronts[layer], ups[layer], downs[layer], vec, sel)
-        others = tuple(send(item, TO_TWIN) for item in (xt, oo, yo, go))
-        saved.append((queries, kv, kv_twin, ot, lse, n1, t1, n2, t2, slope, xm, om, ym, gm, others))
-    output = restore(hidden_low)
-
-    grads = [None] * layers
-    grad = upstream
-    for layer in reversed(range(layers)):
-        vec = vector_all[layer]
-        x_first = layer == 0
-        bit = bits[0] if x_first else bits[1]
-        bit_word = bit.reshape(1).astype(jnp.int32)
-        queries, kv, kv_twin, ot, lse, n1, t1, n2, t2, slope, xm, om, ym, gm, others = saved[layer]
-        xt, oo, yo, go = others
-        df, dz, da, do, dr, sums = post_back(
-            grad, n1, t1, n2, t2, slope, fronts[layer], ups[layer], downs[layer], vec
-        )
-        keep, give = feed_grad(
-            x_first, bit_word, ym, yo, gm, go, dz, send(dz, TO_TWIN), df, send(df, TO_TWIN)
-        )
-        feed = reduce_grad(keep, give, bit, is_low, is_core, x_first)
-        dq, own, give = attend_back_fast(queries, do, kv, kv_twin, ot, lse, code_half, member_own)
-        dm, grad, grad_low, head_sums = project_back(
-            dq, own, send(give, TO_TWIN), fronts[layer], dr
-        )
+        hidden, hidden_low, n1, t1, n2, t2, slope, mine, theirs = post(
+            where, attended, hidden, fronts[layer], ups[layer], downs[layer], vec, sel
+        )
+        others = send(theirs, TO_TWIN)
+        saved.append((queries, kv, kv_twin, ot, lse, n1, t1, n2, t2, slope, xm, xo, mine, others))
+    results = collect(hidden_low)
+
+    def start_back(layer, grad):
+        n1, t1, n2, t2, slope = saved[layer][5:10]
+        slopes, do, dr, sums = post_back(
+            grad, n1, t1, n2, t2, slope,
+            fronts[layer], ups[layer], downs[layer], vector_all[layer],
+        )
+        return slopes, send(slopes, TO_TWIN), do, dr, sums
+
+    def attention_back(layer, do):
+        queries, kv, kv_twin, ot, lse = saved[layer][:5]
+        return attend_back_fast(queries, do, kv, kv_twin, ot, lse, code_half, member_own)
+
+    def feed_part(layer, x_first, slopes, slopes_twin):
+        mine, others = saved[layer][12:14]
+        keep_up, give_up, keep_down, give_down = feed_grad(
+            x_first, bit_words, mine, others, slopes, slopes_twin
+        )
+        work = Reduction(
+            [(keep_up, give_up, x_first), (keep_down, give_down, not x_first)],
+            bits, is_low, is_core,
+        )
+        return work, keep_up
+
+    def front_part(layer, x_first, slopes, slopes_twin, dm, dm_twin):
+        xm, xo, mine, others = saved[layer][10:14]
         keep, give = front_grad(
-            x_first, bit_word, xm, xt, om, oo, dm, send(dm, TO_TWIN), da, send(da, TO_TWIN)
-        )
-        front = reduce_grad(keep, give, bit, is_low, is_core, x_first)
-        grads[layer] = (front, feed, jnp.concatenate([head_sums, sums[2:]], axis=0))
-    input_grad = wide(restore(grad_low))
+            x_first, bit_words, xm, xo, mine, others, dm, dm_twin, slopes, slopes_twin
+        )
+        return Reduction([(keep, give, x_first)], bits, is_low, is_core), keep
+
+    upstream = tie(upstream, saved[0][11], saved[0][13])
+    slopes_b, slopes_tb, do, dr, sums_b = start_back(1, upstream)
+    do = tie(do, saved[1][11], saved[1][13])
+    dq, own, give = attention_back(1, do)
+    got = send(give, TO_TWIN)
+    slopes_late = tie(slopes_tb, dq)
+    feed_b, mark = feed_part(1, True, slopes_b, slopes_late)
+    found, output = deliver(*tie(results, dq))
+    dr = tie(dr, mark, found)
+    dm_b, grad, _, head_b = project_back(dq, own, got, fronts[1], dr)
+    dm_tb = send(dm_b, TO_TWIN)
+    slopes_a, slopes_ta, do, dr, sums_a = start_back(0, grad)
+    front_b, mark = front_part(1, True, slopes_b, slopes_tb, dm_b, tie(dm_tb, do))
+    feed_a, mark = feed_part(0, False, slopes_a, tie(slopes_ta, mark))
+    do = tie(do, mark, feed_b.across())
+    dq, own, give = attention_back(0, do)
+    got = send(give, TO_TWIN)
+    dm_a, grad, grad_low, head_a = project_back(dq, own, got, fronts[0], dr)
+    dm_ta = send(dm_a, TO_TWIN)
+    dm_ta = tie(dm_ta, feed_b.outward(), front_b.across())
+    front_a, mark = front_part(0, False, slopes_a, slopes_ta, dm_a, dm_ta)
+    found, input_grad = deliver(*collect(grad_low))
+    input_grad = wide(input_grad)
+    feed_a.across()
+    front_b.outward()
+    feed_a.outward()
+    front_a.across()
+    front_a.outward()
+    grads = []
+    for front, feed, head_sums, sums in (
+        (front_a, feed_a, head_a, sums_a),
+        (front_b, feed_b, head_b, sums_b),
+    ):
+        up_grad, down_grad = feed.finish()
+        vector = jnp.concatenate([head_sums, sums[2:]], axis=0)
+        grads.append((front.finish()[0], up_grad, down_grad, vector))
 
     def columns(units):
         count = units.shape[1]
@@ -1339,10 +1430,10 @@
 
     entry_grad = jnp.stack([columns(item[0][:, 0:3]) for item in grads])
     exit_grad = jnp.stack([columns(item[0][:, 3:4]) for item in grads])
-    expand_grad = jnp.stack([columns(item[1][:, 0:4]) for item in grads])
-    shrink_grad = jnp.stack([item[1][:, 4:8].reshape(16 * UNIT, width) for item in grads])
-
-    joined = jnp.stack([item[2].reshape(-1) for item in grads])
+    expand_grad = jnp.stack([columns(item[1]) for item in grads])
+    shrink_grad = jnp.stack([item[2].reshape(16 * UNIT, width) for item in grads])
+
+    joined = jnp.stack([item[3].reshape(-1) for item in grads])
     joined = jnp.transpose(joined.reshape(layers, 4, 2, vectors.shape[1]), (1, 2, 0, 3))
     keep = lax.dynamic_index_in_dim(joined, twin, 1, keepdims=False)
     give = lax.dynamic_index_in_dim(joined, 1 - twin, 1, keepdims=False)

time: 734 us -> 720 us (0.981)
  starting transfers between devices: 104 us -> 161 us
  waiting for transfers between devices: 200 us -> 158 us
  local copies, waits for them, and re-layouts: 72.4 us -> 45.8 us
    ppermute x89 -> x95, starting transfers between devices: 104 us -> 161 us  [send(): return lax.ppermute(value, BOTH, route)]
    ppermute x89 -> x95, waiting for transfers between devices: 200 us -> 158 us  [send(): return lax.ppermute(value, BOTH, route)]
    slice x22 -> x12, local copies, waits for them, and re-layouts: 21.3 us -> 4.3 us  [the longest x2 1.25 us: body_fast(): vector = jnp.concatenate([head_sums, sums[2:]], axis=0)]
    convert_element_type x14 -> x10, other arithmetic: 15.6 us -> 8.44 us  [low(): return value.astype(jnp.bfloat16)]
    another operation x17 -> x21, other arithmetic: 14.4 us -> 19.6 us  [the longest x6 6.86 us: across(): jnp.stack([low(wide(item[0]) + wide(got)) for item, got in zip(self.strea...]
  transfers between devices with their start and end apart: 89 -> 95, of which waited for: 21 -> 23; matrix products, arithmetic and copies ran while one was open for 15% -> 12% of each run, Pallas kernels for 22% -> 37%
where the time goes in v3:
time: 720 us; the launch traced here: 712 us
  Pallas kernels  282 us (39%)
  starting transfers between devices  161 us (22%)
  waiting for transfers between devices  158 us (22%)
  other arithmetic  58.5 us (8%)
  local copies, waits for them, and re-layouts  45.8 us (6%)
    ppermute x95, starting transfers between devices, send(): return lax.ppermute(value, BOTH, route)  161 us
    ppermute x95, waiting for transfers between devices, send(): return lax.ppermute(value, BOTH, route)  158 us
    pallas_call x2, Pallas kernels, post(): pl.pallas_call(post_kernel, grid=(4,), in_specs=[SMEM, full, full, unit_s...  49.4 us
    pallas_call x2, Pallas kernels, attend_back_fast(): pl.pallas_call(attend_back_kernel, grid=(width // 128,), in_specs=[column...  41.6 us
    pallas_call x6, Pallas kernels, assemble(): pl.pallas_call(assemble_kernel, grid_spec=pltpu.PrefetchScalarGridSpec(nu...  34.8 us
    pallas_call x2, Pallas kernels, post_back(): pl.pallas_call(post_back_kernel, grid=(4,), in_specs=[full, full, thin, f...  32.9 us
    pallas_call x2, Pallas kernels, attend_fast(): pl.pallas_call(attend_kernel, grid=(width // 128,), in_specs=[column, key...  31 us
    pallas_call x2, Pallas kernels, feed_grad(): pl.pallas_call(functools.partial(feed_grad_kernel, x_first), grid=(8,), i...  25 us
  transfers between devices with their start and end apart: 95, of which 23 were waited for; matrix products, arithmetic and copies ran while one was open for 12% of the time, Pallas kernels for 37%

profile of v3, /device:TPU:0, one launch (start us, length us, event | category | flops | bytes accessed | tf_op | source)
XLA Modules:
  0.0 712.4 jit_solution(7355118581702519903)
XLA Ops:
  9.4 3.8 collective-permute-start
  30.9 3.8 collective-permute-start.16
  47.9 19.9 %collective-permute-start.27 = (bf16[544,768]{1,0:T(8,128)(2,1)S(1)}, bf16[544,768]{1,0:T(8,128)(2,1)}, u32[]{:S(2)}, u32[]{:S(2)}) collective-permute-start(bf16[544,768]{1,0:T(8,128)(2,1)S(1)} %pad_maximum_fusion.11), channel_id=1, source_target_pairs={{0,2},{1,3},{2,0},{3,1},{4,6},{5,7},{6,4},{7,5},{8,10},{9,11},{10,... | collective-permute-start | bytes 2506760 | tf_op jit(solution)/shard_map/ppermute | solution.py:441
  74.0 9.2 %collective-permute-done.9.refs_4_ = bf16[3,4,24,768]{3,2,1,0:T(8,128)(2,1)S(1)} collective-permute-done((bf16[3,4,24,768]{3,2,1,0:T(8,128)(2,1)}, bf16[3,4,24,768]{3,2,1,0:T(8,128)(2,1)S(1)}, u32[]{:S(2)}, u32[]{:S(2)}) %collective-permute-start.9) | collective-permute-done | bytes 442400 | tf_op jit(solution)/shard_map/ppermute | solution.py:441
  90.9 5.8 assemble.6
  96.7 8.0 %collective-permute-done.20.refs_3_ = bf16[3,8,24,768]{3,2,1,0:T(8,128)(2,1)} collective-permute-done((bf16[3,8,24,768]{3,2,1,0:T(8,128)(2,1)}, bf16[3,8,24,768]{3,2,1,0:T(8,128)(2,1)}, u32[]{:S(2)}, u32[]{:S(2)}) %collective-permute-start.20) | collective-permute-done | bytes 884768 | tf_op jit(solution)/shard_map/ppermute | solution.py:441
  106.2 4.3 collective-permute-done.19.refs_2_
  117.3 4.7 gather_rows.4.h_ref
  123.2 6.2 collective-permute-done.21.refs_4_
  130.3 8.0 %collective-permute-done.30.refs_2_ = bf16[3,4,24,768]{3,2,1,0:T(8,128)(2,1)S(1)} collective-permute-done((bf16[3,4,24,768]{3,2,1,0:T(8,128)(2,1)}, bf16[3,4,24,768]{3,2,1,0:T(8,128)(2,1)S(1)}, u32[]{:S(2)}, u32[]{:S(2)}) %collective-permute-start.30) | collective-permute-done | bytes 442400 | tf_op jit(solution)/shard_map/ppermute | solution.py:441
  139.1 7.4 %project.2 = (bf16[512,768]{1,0:T(8,128)(2,1)}, bf16[2,512,768]{2,1,0:T(8,128)(2,1)}, bf16[512,384]{1,0:T(8,128)(2,1)}, bf16[512,384]{1,0:T(8,128)(2,1)}) custom-call(bf16[512,768]{1,0:T(8,128)(2,1)} %gather_rows.4.h_ref, bf16[4,768,768]{2,1,0:T(8,128)(2,1)} %bitcast.314, f32[12,768]{1,0:T(8,128)} %squeeze.49.vec_ref, bf16[2,768,384]{2,1,0:T(8,128)(2,1)} %fusion.sel_ref), custom_call_target="tpu_custom_call" | custom-call | flops 7000000000 | bytes 7000000 | tf_op jit(solution)/shard_map/project/pallas_call | solution.py:585
  146.5 3.7 collective-permute-done.31.refs_3_
  155.9 5.9 assemble.8
  162.3 22.7 %collective-permute-done.32.refs_4_ = bf16[3,4,24,768]{3,2,1,0:T(8,128)(2,1)} collective-permute-done((bf16[3,4,24,768]{3,2,1,0:T(8,128)(2,1)}, bf16[3,4,24,768]{3,2,1,0:T(8,128)(2,1)}, u32[]{:S(2)}, u32[]{:S(2)}) %collective-permute-start.32) | collective-permute-done | bytes 442400 | tf_op jit(solution)/shard_map/ppermute | solution.py:441
  185.0 5.7 assemble.7
  191.8 5.8 assemble.9
  199.5 15.4 %attend_forward.2 = (bf16[512,768]{1,0:T(8,128)(2,1)}, f32[768,512]{1,0:T(8,128)}, f32[6,2,512]{2,1,0:T(2,128)}) custom-call(bf16[512,768]{1,0:T(8,128)(2,1)} %get-tuple-element.92.q_ref, bf16[2,512,768]{2,1,0:T(8,128)(2,1)} %get-tuple-element.93.ka_ref.va_ref, bf16[2,512,768]{2,1,0:T(8,128)(2,1)} %collective-permute-done.15.kb_ref.vb_ref, ...), custom_call_target="tpu_custom_call" | custom-call | flops 15000000512 | bytes 15000000 | tf_op jit(solution)/shard_map/attend_forward/pallas_call | solution.py:663
  214.9 24.6 %post.2 = (f32[512,768]{1,0:T(8,128)}, bf16[512,768]{1,0:T(8,128)(2,1)}, f32[512,768]{1,0:T(8,128)}, f32[512,1]{1,0:T(8,128)}, f32[512,768]{1,0:T(8,128)}, /*ind...) custom-call(s32[3]{0:T(128)} %pad_add_fusion.3.where_ref, ...), custom_call_target="tpu_custom_call" | custom-call | flops 23000000512 | bytes 23000000 | tf_op jit(solution)/shard_map/post/pallas_call | solution.py:842
  240.2 7.3 %project.3 = (bf16[512,768]{1,0:T(8,128)(2,1)}, bf16[2,512,768]{2,1,0:T(8,128)(2,1)}, bf16[512,384]{1,0:T(8,128)(2,1)}, bf16[512,384]{1,0:T(8,128)(2,1)}) custom-call(bf16[512,768]{1,0:T(8,128)(2,1)} %get-tuple-element.98.h_ref, bf16[4,768,768]{2,1,0:T(8,128)(2,1)} %bitcast.322, f32[12,768]{1,0:T(8,128)} %squeeze.106.vec_ref, bf16[2,768,384]{2,1,0:T(8,128)(2,1)} %fusion.sel_ref), custom_call_target="tpu_custom_call" | custom-call | flops 7000000000 | bytes 7000000 | tf_op jit(solution)/shard_map/project/pallas_call | solution.py:585
  248.0 4.7 gather_rows.5.e_ref
  254.1 5.8 assemble.11
  259.9 5.8 assemble.10
  266.9 15.6 %attend_forward.3 = (bf16[512,768]{1,0:T(8,128)(2,1)}, f32[768,512]{1,0:T(8,128)}, f32[6,2,512]{2,1,0:T(2,128)}) custom-call(bf16[512,768]{1,0:T(8,128)(2,1)} %get-tuple-element.105.q_ref, bf16[2,512,768]{2,1,0:T(8,128)(2,1)} %get-tuple-element.106.ka_ref.va_ref, bf16[2,512,768]{2,1,0:T(8,128)(2,1)} %copy-done.58, ...), custom_call_target="tpu_custom_call" | custom-call | flops 15000000512 | bytes 15000000 | tf_op jit(solution)/shard_map/attend_forward/pallas_call | solution.py:663
  282.5 24.7 %post.3 = (f32[512,768]{1,0:T(8,128)}, bf16[512,768]{1,0:T(8,128)(2,1)}, f32[512,768]{1,0:T(8,128)}, f32[512,1]{1,0:T(8,128)}, f32[512,768]{1,0:T(8,128)}, /*ind...) custom-call(s32[3]{0:T(128)} %pad_add_fusion.3.where_ref, ...), custom_call_target="tpu_custom_call" | custom-call | flops 23000000512 | bytes 23000000 | tf_op jit(solution)/shard_map/post/pallas_call | solution.py:842
  308.7 16.4 %post_back.2 = (bf16[6,512,768]{2,1,0:T(8,128)(2,1)}, bf16[512,768]{1,0:T(8,128)(2,1)}, f32[512,768]{1,0:T(8,128)}, f32[12,768]{1,0:T(8,128)}) custom-call(bf16[512,768]{1,0:T(8,128)(2,1)} %gather_rows.5.e_ref, f32[512,768]{1,0:T(8,128)} %get-tuple-element.114.n1_ref, f32[512,1]{1,0:T(8,128)} %get-tuple-element.115.t1_ref, ...), custom_call_target="tpu_custom_call" | custom-call | flops 16000000000 | bytes 16000000 | tf_op jit(solution)/shard_map/post_back/pallas_call | solution.py:936
  329.4 7.8 %collective-permute-done.52.xt_ref = bf16[512,384]{1,0:T(8,128)(2,1)S(1)} collective-permute-done((bf16[512,384]{1,0:T(8,128)(2,1)S(1)}, bf16[512,384]{1,0:T(8,128)(2,1)S(1)}, u32[]{:S(2)}, u32[]{:S(2)}) %collective-permute-start.52) | collective-permute-done | bytes 393248 | tf_op jit(solution)/shard_map/ppermute | solution.py:441
  337.2 21.0 %attend_backward.2 = (bf16[512,768]{1,0:T(8,128)(2,1)}, f32[2,512,768]{2,1,0:T(8,128)}, bf16[2,512,768]{2,1,0:T(8,128)(2,1)}) custom-call(bf16[512,768]{1,0:T(8,128)(2,1)} %get-tuple-element.105.q_ref, bf16[512,768]{1,0:T(8,128)(2,1)} %get-tuple-element.122.g_ref, bf16[2,512,768]{2,1,0:T(8,128)(2,1)} %get-tuple-element.106.ka_ref.va_ref, ...), custom_call_target="tpu_custom_call" | custom-call | flops 20000000000 | bytes 20000000 | tf_op jit(solution)/shard_map/attend_backward/pallas_call | solution.py:732
  359.4 4.7 gather_rows.6
  364.2 12.5 %feed_grad.2 = (bf16[4,2,4,24,768]{4,3,2,1,0:T(8,128)(2,1)}, bf16[4,2,4,24,768]{4,3,2,1,0:T(8,128)(2,1)}, bf16[4,2,4,24,768]{4,3,2,1,0:T(8,128)(2,1)}, bf16[4,2,4,24,768]{4,3,2,1,0:T(8,128)(2,1)}) custom-call(s32[2]{0:T(128)} %pad_add_fusion.4.bit_ref, bf16[6,512,384]{2,1,0:T(8,128)(2,1)} %get-tuple-element.131.ym_ref.gm_ref.om_ref, ...), custom_call_target="tpu_custom_call" | custom-call | flops 12000000000 | bytes 12000000 | tf_op jit(solution)/shard_map/feed_grad/pallas_call | solution.py:1120
  378.6 9.2 %project_back.2 = (bf16[3,512,768]{2,1,0:T(8,128)(2,1)}, f32[512,768]{1,0:T(8,128)}, bf16[512,768]{1,0:T(8,128)(2,1)}, f32[2,768]{1,0:T(2,128)}) custom-call(bf16[512,768]{1,0:T(8,128)(2,1)} %get-tuple-element.125.dq_ref, f32[2,512,768]{2,1,0:T(8,128)} %get-tuple-element.128.own_ref, bf16[2,512,768]{2,1,0:T(8,128)(2,1)} %copy-done.59, ...), custom_call_target="tpu_custom_call" | custom-call | flops 8999999488 | bytes 9000000 | tf_op jit(solution)/shard_map/project_back/pallas_call | solution.py:996
  388.0 16.5 %post_back.3 = (bf16[6,512,768]{2,1,0:T(8,128)(2,1)}, bf16[512,768]{1,0:T(8,128)(2,1)}, f32[512,768]{1,0:T(8,128)}, f32[12,768]{1,0:T(8,128)}) custom-call(f32[512,768]{1,0:T(8,128)} %get-tuple-element.136.e_ref, f32[512,768]{1,0:T(8,128)} %get-tuple-element.137.n1_ref, f32[512,1]{1,0:T(8,128)} %get-tuple-element.138.t1_ref, ...), custom_call_target="tpu_custom_call" | custom-call | flops 16000000000 | bytes 16000000 | tf_op jit(solution)/shard_map/post_back/pallas_call | solution.py:936
  410.0 7.8 %front_grad.2 = (bf16[4,2,4,24,768]{4,3,2,1,0:T(8,128)(2,1)}, bf16[4,2,4,24,768]{4,3,2,1,0:T(8,128)(2,1)}) custom-call(s32[2]{0:T(128)} %pad_add_fusion.4.bit_ref, bf16[512,384]{1,0:T(8,128)(2,1)} %get-tuple-element.145.xm_ref, bf16[512,384]{1,0:T(8,128)(2,1)} %copy-done.69, bf16[6,512,384]{2,1,0:T(8,128)(2,1)} %get-tuple-element.131.ym_ref.gm_ref.om_ref, ...), custom_call_target="tpu_custom_call" | custom-call | flops 7000000000 | bytes 7000000 | tf_op jit(solution)/shard_map/front_grad/pallas_call | solution.py:1071
  421.9 32.6 %collective-permute-start.83 = (bf16[2,2,4,24,768]{4,3,2,1,0:T(8,128)(2,1)}, bf16[2,2,4,24,768]{4,3,2,1,0:T(8,128)(2,1)}, u32[]{:S(2)}, u32[]{:S(2)}) collective-permute-start(bf16[2,2,4,24,768]{4,3,2,1,0:T(8,128)(2,1)} %select_bitcast_fusion), channel_id=1, source_target_pairs={{0,2},{1,3},{2,0},{3,1},{4,6},{5,7},{6,4},{7,5},{8,10},{9,11},{10,... | collective-permute-start | bytes 1769480 | tf_op jit(solution)/shard_map/ppermute | solution.py:441
  457.9 7.6 %collective-permute-start.54 = (bf16[256,768]{1,0:T(8,128)(2,1)S(1)}, bf16[256,768]{1,0:T(8,128)(2,1)}, u32[]{:S(2)}, u32[]{:S(2)}) collective-permute-start(bf16[256,768]{1,0:T(8,128)(2,1)S(1)} %slice.349), channel_id=1, source_target_pairs={{0,2},{1,3},{2,0},{3,1},{4,6},{5,7},{6,4},{7,5},{8,10},{9,11},{10,... | collective-permute-start | bytes 1179656 | tf_op jit(solution)/shard_map/ppermute | solution.py:441
  474.2 4.9 collective-permute-start.74
  479.0 12.5 %feed_grad.3 = (bf16[4,2,4,24,768]{4,3,2,1,0:T(8,128)(2,1)}, bf16[4,2,4,24,768]{4,3,2,1,0:T(8,128)(2,1)}, bf16[4,2,4,24,768]{4,3,2,1,0:T(8,128)(2,1)}, bf16[4,2,4,24,768]{4,3,2,1,0:T(8,128)(2,1)}) custom-call(s32[2]{0:T(128)} %pad_add_fusion.4.bit_ref, bf16[6,512,384]{2,1,0:T(8,128)(2,1)} %get-tuple-element.143.ym_ref.gm_ref.om_ref, ...), custom_call_target="tpu_custom_call" | custom-call | flops 12000000000 | bytes 12000000 | tf_op jit(solution)/shard_map/feed_grad/pallas_call | solution.py:1120
  491.6 20.6 %attend_backward.3 = (bf16[512,768]{1,0:T(8,128)(2,1)}, f32[2,512,768]{2,1,0:T(8,128)}, bf16[2,512,768]{2,1,0:T(8,128)(2,1)}) custom-call(bf16[512,768]{1,0:T(8,128)(2,1)} %get-tuple-element.92.q_ref, bf16[512,768]{1,0:T(8,128)(2,1)} %get-tuple-element.154.g_ref, bf16[2,512,768]{2,1,0:T(8,128)(2,1)} %get-tuple-element.93.ka_ref.va_ref, ...), custom_call_target="tpu_custom_call" | custom-call | flops 20000000000 | bytes 20000000 | tf_op jit(solution)/shard_map/attend_backward/pallas_call | solution.py:732
  521.1 5.1 collective-permute-done.85
  527.8 19.9 %collective-permute-done.89 = bf16[2,4,24,768]{3,2,1,0:T(8,128)(2,1)S(1)} collective-permute-done((bf16[2,4,24,768]{3,2,1,0:T(8,128)(2,1)S(1)}, bf16[2,4,24,768]{3,2,1,0:T(8,128)(2,1)S(1)}, u32[]{:S(2)}, u32[]{:S(2)}) %collective-permute-start.89) | collective-permute-done | bytes 294944 | tf_op jit(solution)/shard_map/ppermute | solution.py:441
  548.7 4.8 collective-permute-done.75
  557.9 9.3 %project_back.3 = (bf16[3,512,768]{2,1,0:T(8,128)(2,1)}, f32[512,768]{1,0:T(8,128)}, bf16[512,768]{1,0:T(8,128)(2,1)}, f32[2,768]{1,0:T(2,128)}) custom-call(bf16[512,768]{1,0:T(8,128)(2,1)} %get-tuple-element.157.dq_ref, f32[2,512,768]{2,1,0:T(8,128)} %get-tuple-element.158.own_ref, bf16[2,512,768]{2,1,0:T(8,128)(2,1)} %collective-permute-done.61.got_ref, ...), custom_call_target="tpu_custom_call" | custom-call | flops 8999999488 | bytes 9000000 | tf_op jit(solution)/shard_map/project_back/pallas_call | solution.py:996
  571.6 16.6 %collective-permute-done.78 = bf16[4,2,4,24,768]{4,3,2,1,0:T(8,128)(2,1)S(1)} collective-permute-done((bf16[4,2,4,24,768]{4,3,2,1,0:T(8,128)(2,1)}, bf16[4,2,4,24,768]{4,3,2,1,0:T(8,128)(2,1)S(1)}, u32[]{:S(2)}, u32[]{:S(2)}) %collective-permute-start.78) | collective-permute-done | bytes 1179680 | tf_op jit(solution)/shard_map/ppermute | solution.py:441
  609.2 19.3 %collective-permute-start.80 = (bf16[2,2,4,24,768]{4,3,2,1,0:T(8,128)(2,1)S(1)}, bf16[2,2,4,24,768]{4,3,2,1,0:T(8,128)(2,1)S(1)}, u32[]{:S(2)}, u32[]{:S(2)}) collective-permute-start(bf16[2,2,4,24,768]{4,3,2,1,0:T(8,128)(2,1)S(1)} %select_bitcast_fusion.1), channel_id=1, source_target_pairs={{0,2},{1,3},{2,0},{3,1},{4,6},{5,7},{6,4},{7,5},{8,10},{9,11},{10,... | collective-permute-start | bytes 1769480 | tf_op jit(solution)/shard_map/ppermute | solution.py:441
  628.5 7.7 %front_grad.3 = (bf16[4,2,4,24,768]{4,3,2,1,0:T(8,128)(2,1)}, bf16[4,2,4,24,768]{4,3,2,1,0:T(8,128)(2,1)}) custom-call(s32[2]{0:T(128)} %pad_add_fusion.4.bit_ref, bf16[512,384]{1,0:T(8,128)(2,1)} %get-tuple-element.162.xm_ref, bf16[512,384]{1,0:T(8,128)(2,1)} %collective-permute-done.50.xt_ref, ...), custom_call_target="tpu_custom_call" | custom-call | flops 7000000000 | bytes 7000000 | tf_op jit(solution)/shard_map/front_grad/pallas_call | solution.py:1071
  636.9 3.6 collective-permute-done.80
  647.7 21.2 %collective-permute-done.86 = bf16[2,4,24,768]{3,2,1,0:T(8,128)(2,1)S(1)} collective-permute-done((bf16[2,4,24,768]{3,2,1,0:T(8,128)(2,1)S(1)}, bf16[2,4,24,768]{3,2,1,0:T(8,128)(2,1)S(1)}, u32[]{:S(2)}, u32[]{:S(2)}) %collective-permute-start.86) | collective-permute-done | bytes 294944 | tf_op jit(solution)/shard_map/ppermute | solution.py:441
  677.4 9.3 %collective-permute-start.70 = (bf16[1,2,4,24,768]{4,3,2,1,0:T(8,128)(2,1)S(1)}, bf16[1,2,4,24,768]{4,3,2,1,0:T(8,128)(2,1)S(1)}, u32[]{:S(2)}, u32[]{:S(2)}) collective-permute-start(bf16[1,2,4,24,768]{4,3,2,1,0:T(8,128)(2,1)S(1)} %select_bitcast_fusion.4), channel_id=1, source_target_pairs={{0,2},{1,3},{2,0},{3,1},{4,6},{5,7},{6,4},{7,5},{8,10},{9,11},{10,... | collective-permute-start | bytes 884744 | tf_op jit(solution)/shard_map/ppermute | solution.py:441
  693.0 4.7 gather_rows.7
  (490 shorter events, 181.5 us)
Async XLA Ops:
  9.4 30.5 %collective-permute-start = (bf16[264,768]{1,0:T(8,128)(2,1)}, bf16[264,768]{1,0:T(8,128)(2,1)}, u32[]{:S(2)}, u32[]{:S(2)}) collective-permute-start(bf16[264,768]{1,0:T(8,128)(2,1)} %maximum_maximum_fusion), channel_id=1, source_target_pairs={{0,2},{1,3},{2,0},{3,1},{4,6},{5,7},{6,4},{7,5},{8,10},{9,11},{10,... | collective-permute-start | bytes 1216520 | tf_op jit(solution)/shard_map/ppermute | solution.py:441
  15.5 56.1 %collective-permute-start.10 = (bf16[4,4,24,768]{3,2,1,0:T(8,128)(2,1)}, bf16[4,4,24,768]{3,2,1,0:T(8,128)(2,1)}, u32[]{:S(2)}, u32[]{:S(2)}) collective-permute-start(bf16[4,4,24,768]{3,2,1,0:T(8,128)(2,1)} %pad_maximum_fusion.12.refs_0_), channel_id=1, source_target_pairs={{0,1},{1,0},{2,3},{3,2},{4,5},{5,4},{6,7},{7,6},{8,9},{9,8},{10,11... | collective-permute-start | bytes 1769480 | tf_op jit(solution)/shard_map/ppermute | solution.py:441
  37.2 30.6 %collective-permute-start.7 = (bf16[3,4,24,768]{3,2,1,0:T(8,128)(2,1)}, bf16[3,4,24,768]{3,2,1,0:T(8,128)(2,1)}, u32[]{:S(2)}, u32[]{:S(2)}) collective-permute-start(bf16[3,4,24,768]{3,2,1,0:T(8,128)(2,1)} %pad_maximum_fusion.15.refs_1_), channel_id=1, source_target_pairs={{0,8},{1,9},{2,10},{3,11},{4,12},{5,13},{6,14},{7,15},{8,0},{9,1},... | collective-permute-start | bytes 1327112 | tf_op jit(solution)/shard_map/ppermute | solution.py:441
  40.0 29.4 %collective-permute-start.8 = (bf16[3,4,24,768]{3,2,1,0:T(8,128)(2,1)}, bf16[3,4,24,768]{3,2,1,0:T(8,128)(2,1)}, u32[]{:S(2)}, u32[]{:S(2)}) collective-permute-start(bf16[3,4,24,768]{3,2,1,0:T(8,128)(2,1)} %pad_maximum_fusion.15.refs_1_), channel_id=1, source_target_pairs={{0,16},{1,17},{2,18},{3,19},{4,20},{5,21},{6,22},{7,23},{8,24},{9,... | collective-permute-start | bytes 1327112 | tf_op jit(solution)/shard_map/ppermute | solution.py:441
  42.8 27.6 %collective-permute-start.2 = (bf16[264,768]{1,0:T(8,128)(2,1)}, bf16[264,768]{1,0:T(8,128)(2,1)S(1)}, u32[]{:S(2)}, u32[]{:S(2)}) collective-permute-start(bf16[264,768]{1,0:T(8,128)(2,1)} %collective-permute-done), channel_id=1, source_target_pairs={{2,4},{3,5},{4,2},{5,3},{10,12},{11,13},{12,10},{13,11},{18,20},{1... | collective-permute-start | bytes 1216520 | tf_op jit(solution)/shard_map/ppermute | solution.py:441
  47.9 36.7 %collective-permute-start.27 = (bf16[544,768]{1,0:T(8,128)(2,1)S(1)}, bf16[544,768]{1,0:T(8,128)(2,1)}, u32[]{:S(2)}, u32[]{:S(2)}) collective-permute-start(bf16[544,768]{1,0:T(8,128)(2,1)S(1)} %pad_maximum_fusion.11), channel_id=1, source_target_pairs={{0,2},{1,3},{2,0},{3,1},{4,6},{5,7},{6,4},{7,5},{8,10},{9,11},{10,... | collective-permute-start | bytes 2506760 | tf_op jit(solution)/shard_map/ppermute | solution.py:441
  83.7 28.3 %collective-permute-start.3 = (bf16[4,264,768]{2,1,0:T(8,128)(2,1)S(1)}, bf16[4,264,768]{2,1,0:T(8,128)(2,1)}, u32[]{:S(2)}, u32[]{:S(2)}) collective-permute-start(bf16[4,264,768]{2,1,0:T(8,128)(2,1)S(1)} %pad_maximum_fusion.1.refs_0_), channel_id=1, source_target_pairs={{0,1},{1,0},{2,3},{3,2},{4,5},{5,4},{6,7},{7,6},{8,9},{9,8},{10,11... | collective-permute-start | bytes 4866056 | tf_op jit(solution)/shard_map/ppermute | solution.py:441
  90.7 32.1 %collective-permute-start.22 = (bf16[4,8,24,768]{3,2,1,0:T(8,128)(2,1)}, bf16[4,8,24,768]{3,2,1,0:T(8,128)(2,1)}, u32[]{:S(2)}, u32[]{:S(2)}) collective-permute-start(bf16[4,8,24,768]{3,2,1,0:T(8,128)(2,1)} %pad_maximum_fusion.5.refs_0_), channel_id=1, source_target_pairs={{0,1},{1,0},{2,3},{3,2},{4,5},{5,4},{6,7},{7,6},{8,9},{9,8},{10,11... | collective-permute-start | bytes 3538952 | tf_op jit(solution)/shard_map/ppermute | solution.py:441
  104.8 48.5 %collective-permute-start.23 = (bf16[3,8,24,768]{3,2,1,0:T(8,128)(2,1)}, bf16[3,8,24,768]{3,2,1,0:T(8,128)(2,1)}, u32[]{:S(2)}, u32[]{:S(2)}) collective-permute-start(bf16[3,8,24,768]{3,2,1,0:T(8,128)(2,1)} %pad_maximum_fusion.9.refs_1_), channel_id=1, source_target_pairs={{0,1},{1,0},{2,3},{3,2},{4,5},{5,4},{6,7},{7,6},{8,9},{9,8},{10,11... | collective-permute-start | bytes 2654216 | tf_op jit(solution)/shard_map/ppermute | solution.py:441
  110.4 42.9 %collective-permute-start.25 = (bf16[3,8,24,768]{3,2,1,0:T(8,128)(2,1)}, bf16[3,8,24,768]{3,2,1,0:T(8,128)(2,1)}, u32[]{:S(2)}, u32[]{:S(2)}) collective-permute-start(bf16[3,8,24,768]{3,2,1,0:T(8,128)(2,1)} %collective-permute-done.20.refs_3_), channel_id=1, source_target_pairs={{0,1},{1,0},{2,3},{3,2},{4,5},{5,4},{6,7},{7,6},{8,9},{9,8},{10,11... | collective-permute-start | bytes 2654216 | tf_op jit(solution)/shard_map/ppermute | solution.py:441
  112.0 26.2 %collective-permute-start.30 = (bf16[3,4,24,768]{3,2,1,0:T(8,128)(2,1)}, bf16[3,4,24,768]{3,2,1,0:T(8,128)(2,1)S(1)}, u32[]{:S(2)}, u32[]{:S(2)}) collective-permute-start(bf16[3,4,24,768]{3,2,1,0:T(8,128)(2,1)} %pad_maximum_fusion.16.refs_1_), channel_id=1, source_target_pairs={{0,8},{1,9},{2,10},{3,11},{4,12},{5,13},{6,14},{7,15},{8,0},{9,1},... | collective-permute-start | bytes 1327112 | tf_op jit(solution)/shard_map/ppermute | solution.py:441
  122.8 31.0 %collective-permute-start.24 = (bf16[3,8,24,768]{3,2,1,0:T(8,128)(2,1)}, bf16[3,8,24,768]{3,2,1,0:T(8,128)(2,1)}, u32[]{:S(2)}, u32[]{:S(2)}) collective-permute-start(bf16[3,8,24,768]{3,2,1,0:T(8,128)(2,1)} %collective-permute-done.19.refs_2_), channel_id=1, source_target_pairs={{0,1},{1,0},{2,3},{3,2},{4,5},{5,4},{6,7},{7,6},{8,9},{9,8},{10,11... | collective-permute-start | bytes 2654216 | tf_op jit(solution)/shard_map/ppermute | solution.py:441
  153.3 44.4 %collective-permute-start.15 = (bf16[2,512,768]{2,1,0:T(8,128)(2,1)}, bf16[2,512,768]{2,1,0:T(8,128)(2,1)}, u32[]{:S(2)}, u32[]{:S(2)}) collective-permute-start(bf16[2,512,768]{2,1,0:T(8,128)(2,1)} %get-tuple-element.93.ka_ref.va_ref), channel_id=1, source_target_pairs={{0,1},{1,0},{2,3},{3,2},{4,5},{5,4},{6,7},{7,6},{8,9},{9,8},{10,11... | collective-permute-start | bytes 4718600 | tf_op jit(solution)/shard_map/ppermute | solution.py:441
  153.8 43.7 %collective-permute-start.39 = (bf16[3,8,24,768]{3,2,1,0:T(8,128)(2,1)S(1)}, bf16[3,8,24,768]{3,2,1,0:T(8,128)(2,1)}, u32[]{:S(2)}, u32[]{:S(2)}) collective-permute-start(bf16[3,8,24,768]{3,2,1,0:T(8,128)(2,1)S(1)} %copy-done.24), channel_id=1, source_target_pairs={{0,8},{1,9},{2,10},{3,11},{4,12},{5,13},{6,14},{7,15},{8,0},{9,1},... | collective-permute-start | bytes 2654216 | tf_op jit(solution)/shard_map/ppermute | solution.py:441
  154.4 30.7 %collective-permute-start.32 = (bf16[3,4,24,768]{3,2,1,0:T(8,128)(2,1)}, bf16[3,4,24,768]{3,2,1,0:T(8,128)(2,1)}, u32[]{:S(2)}, u32[]{:S(2)}) collective-permute-start(bf16[3,4,24,768]{3,2,1,0:T(8,128)(2,1)} %copy-done.63), channel_id=1, source_target_pairs={{0,8},{1,9},{2,10},{3,11},{4,12},{5,13},{6,14},{7,15},{8,0},{9,1},... | collective-permute-start | bytes 1327112 | tf_op jit(solution)/shard_map/ppermute | solution.py:441
  161.7 29.1 %collective-permute-start.35 = (bf16[3,4,24,768]{3,2,1,0:T(8,128)(2,1)}, bf16[3,4,24,768]{3,2,1,0:T(8,128)(2,1)}, u32[]{:S(2)}, u32[]{:S(2)}) collective-permute-start(bf16[3,4,24,768]{3,2,1,0:T(8,128)(2,1)} %copy-done.62), channel_id=1, source_target_pairs={{0,1},{1,0},{2,3},{3,2},{4,5},{5,4},{6,7},{7,6},{8,9},{9,8},{10,11... | collective-permute-start | bytes 1327112 | tf_op jit(solution)/shard_map/ppermute | solution.py:441
  161.8 29.6 %collective-permute-start.36 = (bf16[3,4,24,768]{3,2,1,0:T(8,128)(2,1)}, bf16[3,4,24,768]{3,2,1,0:T(8,128)(2,1)}, u32[]{:S(2)}, u32[]{:S(2)}) collective-permute-start(bf16[3,4,24,768]{3,2,1,0:T(8,128)(2,1)} %copy-done.63), channel_id=1, source_target_pairs={{0,1},{1,0},{2,3},{3,2},{4,5},{5,4},{6,7},{7,6},{8,9},{9,8},{10,11... | collective-permute-start | bytes 1327112 | tf_op jit(solution)/shard_map/ppermute | solution.py:441
  190.8 48.7 %collective-permute-start.42 = (bf16[4,8,24,768]{3,2,1,0:T(8,128)(2,1)S(1)}, bf16[4,8,24,768]{3,2,1,0:T(8,128)(2,1)}, u32[]{:S(2)}, u32[]{:S(2)}) collective-permute-start(bf16[4,8,24,768]{3,2,1,0:T(8,128)(2,1)S(1)} %copy-done.21), channel_id=1, source_target_pairs={{0,1},{1,0},{2,3},{3,2},{4,5},{5,4},{6,7},{7,6},{8,9},{9,8},{10,11... | collective-permute-start | bytes 3538952 | tf_op jit(solution)/shard_map/ppermute | solution.py:441
  191.4 56.2 %collective-permute-start.49 = (bf16[4,256,768]{2,1,0:T(8,128)(2,1)S(1)}, bf16[4,256,768]{2,1,0:T(8,128)(2,1)}, u32[]{:S(2)}, u32[]{:S(2)}) collective-permute-start(bf16[4,256,768]{2,1,0:T(8,128)(2,1)S(1)} %pad_maximum_fusion.3.refs_0_), channel_id=1, source_target_pairs={{0,1},{1,0},{2,3},{3,2},{4,5},{5,4},{6,7},{7,6},{8,9},{9,8},{10,11... | collective-permute-start | bytes 4718600 | tf_op jit(solution)/shard_map/ppermute | solution.py:441
  191.5 48.2 %collective-permute-start.40 = (bf16[3,8,24,768]{3,2,1,0:T(8,128)(2,1)S(1)}, bf16[3,8,24,768]{3,2,1,0:T(8,128)(2,1)}, u32[]{:S(2)}, u32[]{:S(2)}) collective-permute-start(bf16[3,8,24,768]{3,2,1,0:T(8,128)(2,1)S(1)} %copy-done.24), channel_id=1, source_target_pairs={{0,16},{1,17},{2,18},{3,19},{4,20},{5,21},{6,22},{7,23},{8,24},{9,... | collective-permute-start | bytes 2654216 | tf_op jit(solution)/shard_map/ppermute | solution.py:441
  197.6 55.2 %collective-permute-start.43 = (bf16[3,8,24,768]{3,2,1,0:T(8,128)(2,1)S(1)}, bf16[3,8,24,768]{3,2,1,0:T(8,128)(2,1)}, u32[]{:S(2)}, u32[]{:S(2)}) collective-permute-start(bf16[3,8,24,768]{3,2,1,0:T(8,128)(2,1)S(1)} %copy-done.24), channel_id=1, source_target_pairs={{0,1},{1,0},{2,3},{3,2},{4,5},{5,4},{6,7},{7,6},{8,9},{9,8},{10,11... | collective-permute-start | bytes 2654216 | tf_op jit(solution)/shard_map/ppermute | solution.py:441
  197.8 42.4 %collective-permute-start.41 = (bf16[3,8,24,768]{3,2,1,0:T(8,128)(2,1)}, bf16[3,8,24,768]{3,2,1,0:T(8,128)(2,1)}, u32[]{:S(2)}, u32[]{:S(2)}) collective-permute-start(bf16[3,8,24,768]{3,2,1,0:T(8,128)(2,1)} %collective-permute-done.39.refs_2_), channel_id=1, source_target_pairs={{0,16},{1,17},{2,18},{3,19},{4,20},{5,21},{6,22},{7,23},{8,24},{9,... | collective-permute-start | bytes 2654216 | tf_op jit(solution)/shard_map/ppermute | solution.py:441
  252.7 54.5 %collective-permute-start.50 = (bf16[512,384]{1,0:T(8,128)(2,1)}, bf16[512,384]{1,0:T(8,128)(2,1)}, u32[]{:S(2)}, u32[]{:S(2)}) collective-permute-start(bf16[512,384]{1,0:T(8,128)(2,1)} %get-tuple-element.111), channel_id=1, source_target_pairs={{0,1},{1,0},{2,3},{3,2},{4,5},{5,4},{6,7},{7,6},{8,9},{9,8},{10,11... | collective-permute-start | bytes 1179656 | tf_op jit(solution)/shard_map/ppermute | solution.py:441
  253.7 53.5 %collective-permute-start.51 = (bf16[6,512,384]{2,1,0:T(8,128)(2,1)}, bf16[6,512,384]{2,1,0:T(8,128)(2,1)S(1)}, u32[]{:S(2)}, u32[]{:S(2)}) collective-permute-start(bf16[6,512,384]{2,1,0:T(8,128)(2,1)} %get-tuple-element.112), channel_id=1, source_target_pairs={{0,1},{1,0},{2,3},{3,2},{4,5},{5,4},{6,7},{7,6},{8,9},{9,8},{10,11... | collective-permute-start | bytes 7077896 | tf_op jit(solution)/shard_map/ppermute | solution.py:441
  325.2 39.0 %collective-permute-start.56 = (bf16[6,512,768]{2,1,0:T(8,128)(2,1)}, bf16[6,512,768]{2,1,0:T(8,128)(2,1)}, u32[]{:S(2)}, u32[]{:S(2)}) collective-permute-start(bf16[6,512,768]{2,1,0:T(8,128)(2,1)} %get-tuple-element.132.dz_ref.df_ref.da_ref), channel_id=1, source_target_pairs={{0,1},{1,0},{2,3},{3,2},{4,5},{5,4},{6,7},{7,6},{8,9},{9,8},{10,11... | collective-permute-start | bytes 14155784 | tf_op jit(solution)/shard_map/ppermute | solution.py:441
  328.9 29.3 %collective-permute-start.48 = (bf16[2,512,768]{2,1,0:T(8,128)(2,1)S(1)}, bf16[2,512,768]{2,1,0:T(8,128)(2,1)S(1)}, u32[]{:S(2)}, u32[]{:S(2)}) collective-permute-start(bf16[2,512,768]{2,1,0:T(8,128)(2,1)S(1)} %pad_maximum_fusion.2.refs_0_), channel_id=1, source_target_pairs={{0,1},{1,0},{2,3},{3,2},{4,5},{5,4},{6,7},{7,6},{8,9},{9,8},{10,11... | collective-permute-start | bytes 4718600 | tf_op jit(solution)/shard_map/ppermute | solution.py:441
  376.7 28.3 %collective-permute-start.59 = (bf16[4,2,4,24,768]{4,3,2,1,0:T(8,128)(2,1)}, bf16[4,2,4,24,768]{4,3,2,1,0:T(8,128)(2,1)}, u32[]{:S(2)}, u32[]{:S(2)}) collective-permute-start(bf16[4,2,4,24,768]{4,3,2,1,0:T(8,128)(2,1)} %get-tuple-element.151), channel_id=1, source_target_pairs={{0,8},{1,9},{2,10},{3,11},{4,12},{5,13},{6,14},{7,15},{8,0},{9,1},... | collective-permute-start | bytes 3538952 | tf_op jit(solution)/shard_map/ppermute | solution.py:441
  377.2 29.4 %collective-permute-start.60 = (bf16[4,2,4,24,768]{4,3,2,1,0:T(8,128)(2,1)}, bf16[4,2,4,24,768]{4,3,2,1,0:T(8,128)(2,1)}, u32[]{:S(2)}, u32[]{:S(2)}) collective-permute-start(bf16[4,2,4,24,768]{4,3,2,1,0:T(8,128)(2,1)} %get-tuple-element.153), channel_id=1, source_target_pairs={{0,16},{1,17},{2,18},{3,19},{4,20},{5,21},{6,22},{7,23},{8,24},{9,... | collective-permute-start | bytes 3538952 | tf_op jit(solution)/shard_map/ppermute | solution.py:441
  404.4 74.6 %collective-permute-start.57 = (bf16[6,512,768]{2,1,0:T(8,128)(2,1)}, bf16[6,512,768]{2,1,0:T(8,128)(2,1)}, u32[]{:S(2)}, u32[]{:S(2)}) collective-permute-start(bf16[6,512,768]{2,1,0:T(8,128)(2,1)} %get-tuple-element.144.dz_ref.df_ref.da_ref), channel_id=1, source_target_pairs={{0,1},{1,0},{2,3},{3,2},{4,5},{5,4},{6,7},{7,6},{8,9},{9,8},{10,11... | collective-permute-start | bytes 14155784 | tf_op jit(solution)/shard_map/ppermute | solution.py:441
  417.8 36.7 %collective-permute-start.67 = (bf16[4,2,4,24,768]{4,3,2,1,0:T(8,128)(2,1)}, bf16[4,2,4,24,768]{4,3,2,1,0:T(8,128)(2,1)S(1)}, u32[]{:S(2)}, u32[]{:S(2)}) collective-permute-start(bf16[4,2,4,24,768]{4,3,2,1,0:T(8,128)(2,1)} %get-tuple-element.164), channel_id=1, source_target_pairs={{0,8},{1,9},{2,10},{3,11},{4,12},{5,13},{6,14},{7,15},{8,0},{9,1},... | collective-permute-start | bytes 3538952 | tf_op jit(solution)/shard_map/ppermute | solution.py:441
  421.9 47.1 %collective-permute-start.83 = (bf16[2,2,4,24,768]{4,3,2,1,0:T(8,128)(2,1)}, bf16[2,2,4,24,768]{4,3,2,1,0:T(8,128)(2,1)}, u32[]{:S(2)}, u32[]{:S(2)}) collective-permute-start(bf16[2,2,4,24,768]{4,3,2,1,0:T(8,128)(2,1)} %select_bitcast_fusion), channel_id=1, source_target_pairs={{0,2},{1,3},{2,0},{3,1},{4,6},{5,7},{6,4},{7,5},{8,10},{9,11},{10,... | collective-permute-start | bytes 1769480 | tf_op jit(solution)/shard_map/ppermute | solution.py:441
  457.9 54.4 %collective-permute-start.54 = (bf16[256,768]{1,0:T(8,128)(2,1)S(1)}, bf16[256,768]{1,0:T(8,128)(2,1)}, u32[]{:S(2)}, u32[]{:S(2)}) collective-permute-start(bf16[256,768]{1,0:T(8,128)(2,1)S(1)} %slice.349), channel_id=1, source_target_pairs={{0,2},{1,3},{2,0},{3,1},{4,6},{5,7},{6,4},{7,5},{8,10},{9,11},{10,... | collective-permute-start | bytes 1179656 | tf_op jit(solution)/shard_map/ppermute | solution.py:441
  471.1 43.8 %collective-permute-start.84 = (bf16[2,4,24,768]{3,2,1,0:T(8,128)(2,1)}, bf16[2,4,24,768]{3,2,1,0:T(8,128)(2,1)S(1)}, u32[]{:S(2)}, u32[]{:S(2)}) collective-permute-start(bf16[2,4,24,768]{3,2,1,0:T(8,128)(2,1)} %get-tuple-element.204), channel_id=1, source_target_pairs={{0,16},{1,17},{2,18},{3,19},{4,20},{5,21},{6,22},{7,23},{8,24},{9,... | collective-permute-start | bytes 884744 | tf_op jit(solution)/shard_map/ppermute | solution.py:441
  471.4 43.6 %collective-permute-start.88 = (bf16[2,4,24,768]{3,2,1,0:T(8,128)(2,1)}, bf16[2,4,24,768]{3,2,1,0:T(8,128)(2,1)}, u32[]{:S(2)}, u32[]{:S(2)}) collective-permute-start(bf16[2,4,24,768]{3,2,1,0:T(8,128)(2,1)} %get-tuple-element.203), channel_id=1, source_target_pairs={{0,8},{1,9},{2,10},{3,11},{4,12},{5,13},{6,14},{7,15},{8,0},{9,1},... | collective-permute-start | bytes 884744 | tf_op jit(solution)/shard_map/ppermute | solution.py:441
  474.2 44.7 %collective-permute-start.74 = (bf16[1,2,4,24,768]{4,3,2,1,0:T(8,128)(2,1)S(1)}, bf16[1,2,4,24,768]{4,3,2,1,0:T(8,128)(2,1)S(1)}, u32[]{:S(2)}, u32[]{:S(2)}) collective-permute-start(bf16[1,2,4,24,768]{4,3,2,1,0:T(8,128)(2,1)S(1)} %select_bitcast_fusion.3), channel_id=1, source_target_pairs={{0,2},{1,3},{2,0},{3,1},{4,6},{5,7},{6,4},{7,5},{8,10},{9,11},{10,... | collective-permute-start | bytes 884744 | tf_op jit(solution)/shard_map/ppermute | solution.py:441
  512.2 45.7 %collective-permute-start.61 = (bf16[2,512,768]{2,1,0:T(8,128)(2,1)}, bf16[2,512,768]{2,1,0:T(8,128)(2,1)}, u32[]{:S(2)}, u32[]{:S(2)}) collective-permute-start(bf16[2,512,768]{2,1,0:T(8,128)(2,1)} %get-tuple-element.159), channel_id=1, source_target_pairs={{0,1},{1,0},{2,3},{3,2},{4,5},{5,4},{6,7},{7,6},{8,9},{9,8},{10,11... | collective-permute-start | bytes 4718600 | tf_op jit(solution)/shard_map/ppermute | solution.py:441
  512.3 44.0 %collective-permute-start.77 = (bf16[4,2,4,24,768]{4,3,2,1,0:T(8,128)(2,1)}, bf16[4,2,4,24,768]{4,3,2,1,0:T(8,128)(2,1)}, u32[]{:S(2)}, u32[]{:S(2)}) collective-permute-start(bf16[4,2,4,24,768]{4,3,2,1,0:T(8,128)(2,1)} %get-tuple-element.168), channel_id=1, source_target_pairs={{0,16},{1,17},{2,18},{3,19},{4,20},{5,21},{6,22},{7,23},{8,24},{9,... | collective-permute-start | bytes 3538952 | tf_op jit(solution)/shard_map/ppermute | solution.py:441
  516.0 31.7 %collective-permute-start.89 = (bf16[2,4,24,768]{3,2,1,0:T(8,128)(2,1)S(1)}, bf16[2,4,24,768]{3,2,1,0:T(8,128)(2,1)S(1)}, u32[]{:S(2)}, u32[]{:S(2)}) collective-permute-start(bf16[2,4,24,768]{3,2,1,0:T(8,128)(2,1)S(1)} %get-tuple-element.201), channel_id=1, source_target_pairs={{0,16},{1,17},{2,18},{3,19},{4,20},{5,21},{6,22},{7,23},{8,24},{9,... | collective-permute-start | bytes 884744 | tf_op jit(solution)/shard_map/ppermute | solution.py:441
  518.9 34.6 %collective-permute-start.75 = (bf16[2,4,24,768]{3,2,1,0:T(8,128)(2,1)S(1)}, bf16[2,4,24,768]{3,2,1,0:T(8,128)(2,1)S(1)}, u32[]{:S(2)}, u32[]{:S(2)}) collective-permute-start(bf16[2,4,24,768]{3,2,1,0:T(8,128)(2,1)S(1)} %fusion.13), channel_id=1, source_target_pairs={{0,16},{1,17},{2,18},{3,19},{4,20},{5,21},{6,22},{7,23},{8,24},{9,... | collective-permute-start | bytes 884744 | tf_op jit(solution)/shard_map/ppermute | solution.py:441
  554.3 42.2 %collective-permute-start.76 = (bf16[2,4,24,768]{3,2,1,0:T(8,128)(2,1)}, bf16[2,4,24,768]{3,2,1,0:T(8,128)(2,1)}, u32[]{:S(2)}, u32[]{:S(2)}) collective-permute-start(bf16[2,4,24,768]{3,2,1,0:T(8,128)(2,1)} %add_convert_fusion.14), channel_id=1, source_target_pairs={{0,8},{1,9},{2,10},{3,11},{4,12},{5,13},{6,14},{7,15},{8,0},{9,1},... | collective-permute-start | bytes 884744 | tf_op jit(solution)/shard_map/ppermute | solution.py:441
  555.8 32.5 %collective-permute-start.78 = (bf16[4,2,4,24,768]{4,3,2,1,0:T(8,128)(2,1)}, bf16[4,2,4,24,768]{4,3,2,1,0:T(8,128)(2,1)S(1)}, u32[]{:S(2)}, u32[]{:S(2)}) collective-permute-start(bf16[4,2,4,24,768]{4,3,2,1,0:T(8,128)(2,1)} %get-tuple-element.170), channel_id=1, source_target_pairs={{0,8},{1,9},{2,10},{3,11},{4,12},{5,13},{6,14},{7,15},{8,0},{9,1},... | collective-permute-start | bytes 3538952 | tf_op jit(solution)/shard_map/ppermute | solution.py:441
  590.8 37.6 %collective-permute-start.65 = (bf16[3,512,768]{2,1,0:T(8,128)(2,1)}, bf16[3,512,768]{2,1,0:T(8,128)(2,1)}, u32[]{:S(2)}, u32[]{:S(2)}) collective-permute-start(bf16[3,512,768]{2,1,0:T(8,128)(2,1)} %get-tuple-element.163.dm_ref), channel_id=1, source_target_pairs={{0,1},{1,0},{2,3},{3,2},{4,5},{5,4},{6,7},{7,6},{8,9},{9,8},{10,11... | collective-permute-start | bytes 7077896 | tf_op jit(solution)/shard_map/ppermute | solution.py:441
  604.5 39.4 %collective-permute-start.62 = (bf16[512,768]{1,0:T(8,128)(2,1)}, bf16[512,768]{1,0:T(8,128)(2,1)}, u32[]{:S(2)}, u32[]{:S(2)}) collective-permute-start(bf16[512,768]{1,0:T(8,128)(2,1)} %get-tuple-element.161), channel_id=1, source_target_pairs={{2,4},{3,5},{4,2},{5,3},{10,12},{11,13},{12,10},{13,11},{18,20},{1... | collective-permute-start | bytes 2359304 | tf_op jit(solution)/shard_map/ppermute | solution.py:441
  609.2 31.3 %collective-permute-start.80 = (bf16[2,2,4,24,768]{4,3,2,1,0:T(8,128)(2,1)S(1)}, bf16[2,2,4,24,768]{4,3,2,1,0:T(8,128)(2,1)S(1)}, u32[]{:S(2)}, u32[]{:S(2)}) collective-permute-start(bf16[2,2,4,24,768]{4,3,2,1,0:T(8,128)(2,1)S(1)} %select_bitcast_fusion.1), channel_id=1, source_target_pairs={{0,2},{1,3},{2,0},{3,1},{4,6},{5,7},{6,4},{7,5},{8,10},{9,11},{10,... | collective-permute-start | bytes 1769480 | tf_op jit(solution)/shard_map/ppermute | solution.py:441
  636.2 34.2 %collective-permute-start.68 = (bf16[4,2,4,24,768]{4,3,2,1,0:T(8,128)(2,1)}, bf16[4,2,4,24,768]{4,3,2,1,0:T(8,128)(2,1)S(1)}, u32[]{:S(2)}, u32[]{:S(2)}) collective-permute-start(bf16[4,2,4,24,768]{4,3,2,1,0:T(8,128)(2,1)} %get-tuple-element.167), channel_id=1, source_target_pairs={{0,16},{1,17},{2,18},{3,19},{4,20},{5,21},{6,22},{7,23},{8,24},{9,... | collective-permute-start | bytes 3538952 | tf_op jit(solution)/shard_map/ppermute | solution.py:441
  641.3 27.6 %collective-permute-start.86 = (bf16[2,4,24,768]{3,2,1,0:T(8,128)(2,1)S(1)}, bf16[2,4,24,768]{3,2,1,0:T(8,128)(2,1)S(1)}, u32[]{:S(2)}, u32[]{:S(2)}) collective-permute-start(bf16[2,4,24,768]{3,2,1,0:T(8,128)(2,1)S(1)} %get-tuple-element.199), channel_id=1, source_target_pairs={{0,16},{1,17},{2,18},{3,19},{4,20},{5,21},{6,22},{7,23},{8,24},{9,... | collective-permute-start | bytes 884744 | tf_op jit(solution)/shard_map/ppermute | solution.py:441
  642.0 30.2 %collective-permute-start.94 = (f32[2,1152]{1,0:T(2,128)S(1)}, f32[2,1152]{1,0:T(2,128)S(1)}, u32[]{:S(2)}, u32[]{:S(2)}) collective-permute-start(f32[2,1152]{1,0:T(2,128)S(1)} %select_bitcast_fusion.5), channel_id=1, source_target_pairs={{0,2},{1,3},{2,0},{3,1},{4,6},{5,7},{6,4},{7,5},{8,10},{9,11},{10,... | collective-permute-start | bytes 27656 | tf_op jit(solution)/shard_map/ppermute | solution.py:441
  646.3 46.7 %collective-permute-start.63 = (bf16[2,512,768]{2,1,0:T(8,128)(2,1)}, bf16[2,512,768]{2,1,0:T(8,128)(2,1)}, u32[]{:S(2)}, u32[]{:S(2)}) collective-permute-start(bf16[2,512,768]{2,1,0:T(8,128)(2,1)} %pad_maximum_fusion.4.refs_0_), channel_id=1, source_target_pairs={{0,1},{1,0},{2,3},{3,2},{4,5},{5,4},{6,7},{7,6},{8,9},{9,8},{10,11... | collective-permute-start | bytes 4718600 | tf_op jit(solution)/shard_map/ppermute | solution.py:441
  (122 other events, 1281.1 us)

commit v4 on v3

--- a/solution.py
+++ b/solution.py
@@ -491,14 +491,14 @@
     out_ref[...] = low(total)
 
 
-def gather_rows(pieces, ids, want):
+def gather_rows(pieces, ids, want, spend):
     return pl.pallas_call(
         gather_kernel,
         out_shape=shaped((want.shape[0], pieces[0].shape[2])),
         in_specs=[VMEM] * (2 + len(pieces)),
         out_specs=VMEM,
         compiler_params=LIMIT,
-        cost_estimate=cost(5),
+        cost_estimate=cost(spend),
         name="gather_rows",
     )(ids, want, *pieces)
 
@@ -555,10 +555,18 @@
     return lax.optimization_barrier((value,) + others)[0]
 
 
+def after(values, *others):
+    return list(lax.optimization_barrier(tuple(values) + others)[: len(values)])
+
+
 def spread(own, first, over_x, over_y, x_last):
+    others = [send(own, TO_TWIN), send(first, TO_TWIN)]
+    over_x, over_y = after([over_x, over_y], *others)
     over_d = send(over_y, TO_X) if x_last else send(over_x, TO_Y)
-    mine = (own, first, over_x, over_y, over_d)
-    return mine + tuple(send(item, TO_TWIN) for item in mine)
+    others += [send(over_x, TO_TWIN), send(over_y, TO_TWIN)]
+    over_d = after([over_d], *others)[0]
+    others.append(send(over_d, TO_TWIN))
+    return (own, first, over_x, over_y, over_d) + tuple(others)
 
 
 def project_kernel(h_ref, w_ref, vec_ref, sel_ref, q_ref, kv_ref, mine_ref, theirs_ref):
@@ -725,7 +733,7 @@
     twin_ref[1] = low(value_sums[1])
 
 
-def attend_back_fast(queries, grad, kv, kv_twin, ot, lse, code, member):
+def attend_back_fast(queries, grad, kv, kv_twin, ot, lse, code, member, spend):
     half, width = queries.shape
     column, key, value, turned, level = pair_specs(half)
     both = pl.BlockSpec((2, half, 128), lambda pair: (0, 0, pair))
@@ -742,7 +750,7 @@
         ],
         scratch_shapes=[pltpu.VMEM((2 * half, half), jnp.float32)],
         compiler_params=LIMIT,
-        cost_estimate=cost(20),
+        cost_estimate=cost(spend),
         name="attend_backward",
     )(queries, grad, kv, kv_twin, kv, kv_twin, ot, lse, code, member)
 
@@ -929,7 +937,7 @@
         sums_out[4:5, :] = column_sum(incoming)
 
 
-def post_back(upstream, n1, t1, n2, t2, slope, front, up, down, vec):
+def post_back(upstream, n1, t1, n2, t2, slope, front, up, down, vec, spend):
     rows, width = upstream.shape
     full = fixed(rows, width)
     thin = fixed(rows, 1)
@@ -952,7 +960,7 @@
             pltpu.VMEM((rows, width), jnp.float32),
         ],
         compiler_params=LIMIT,
-        cost_estimate=cost(16),
+        cost_estimate=cost(spend),
         name="post_back",
     )(upstream, n1, t1, n2, t2, slope, front, up, down, vec)
 
@@ -989,7 +997,7 @@
         dxl_out[...] = low(dx_out[...])
 
 
-def project_back(dq, own, got, front, dr):
+def project_back(dq, own, got, front, dr, spend):
     rows, width = dq.shape
     full = fixed(rows, width)
     late = pl.BlockSpec((None, rows, width), lambda unit: (jnp.maximum(unit - 1, 0), 0, 0))
@@ -1008,7 +1016,7 @@
             shaped((2, width), jnp.float32),
         ],
         compiler_params=LIMIT,
-        cost_estimate=cost(9),
+        cost_estimate=cost(spend),
         name="project_back",
     )(dq, own, got, front, dr)
 
@@ -1042,43 +1050,48 @@
 
 
 def front_grad_kernel(
-    x_first, bit_ref, xm_ref, xt_ref, om_ref, ot_ref, dm_ref, dmt_ref, da_ref, dat_ref,
-    keep_ref, give_ref,
+    bit_ref, xm_ref, xt_ref, om_ref, ot_ref, dm_ref, dmt_ref, da_ref, dat_ref,
+    keep_x, give_x, keep_y, give_y,
 ):
     unit = pl.program_id(0)
-    bit = bit_ref[0 if x_first else 1]
-
-    @pl.when(unit < 3)
-    def _():
-        product = tn(xm_ref[...], dm_ref[...]) + tn(xt_ref[...], dmt_ref[...])
-        column_store((keep_ref, give_ref), bit, x_first, product, unit)
+
+    def store(product, index, x_first):
+        pair = (keep_x, give_x) if x_first else (keep_y, give_y)
+        column_store(pair, bit_ref[0 if x_first else 1], x_first, product, index)
+
+    @pl.when(unit < 2)
+    def _():
+        store(tn(xm_ref[...], dm_ref[...]) + tn(xt_ref[...], dmt_ref[...]), unit, True)
+
+    @pl.when(unit == 2)
+    def _():
+        store(tn(xm_ref[...], dm_ref[...]) + tn(xt_ref[...], dmt_ref[...]), 0, False)
 
     @pl.when(unit == 3)
     def _():
-        product = tn(om_ref[...], da_ref[...]) + tn(ot_ref[...], dat_ref[...])
-        column_store((keep_ref, give_ref), bit, x_first, product, unit)
+        store(tn(om_ref[...], da_ref[...]) + tn(ot_ref[...], dat_ref[...]), 1, False)
 
 
 def block_spec(rows, width, index):
     return pl.BlockSpec((None, rows, width), lambda step: (index, 0, 0))
 
 
-def front_grad(x_first, bits, xm, xt, mine, theirs, dm, dmt, da, dat):
+def front_grad(bits, xm, xt, mine, theirs, dm, dmt, da, dat, spend):
     rows, half = xm.shape
     width = da.shape[2]
     late = pl.BlockSpec((None, rows, width), lambda unit: (jnp.minimum(unit, 2), 0, 0))
-    shape = (4, 2, 4, UNIT, width)
+    shape = (4, 2, 2, UNIT, width)
     return pl.pallas_call(
-        functools.partial(front_grad_kernel, x_first),
+        front_grad_kernel,
         grid=(4,),
         in_specs=[SMEM, fixed(rows, half), fixed(rows, half)]
         + [block_spec(rows, half, 5)] * 2
         + [late, late]
         + [block_spec(rows, width, 5)] * 2,
-        out_specs=[fixed(*shape)] * 2,
-        out_shape=[shaped(shape)] * 2,
+        out_specs=[fixed(*shape)] * 4,
+        out_shape=[shaped(shape)] * 4,
         compiler_params=LIMIT,
-        cost_estimate=cost(7),
+        cost_estimate=cost(spend),
         name="front_grad",
     )(bits, xm, xt, mine, theirs, dm, dmt, da, dat)
 
@@ -1111,7 +1124,7 @@
             split_store(keep_down, give_down, down_bit, not x_first, piece_of, store)
 
 
-def feed_grad(x_first, bits, mine, theirs, slopes, slopes_twin):
+def feed_grad(x_first, bits, mine, theirs, slopes, slopes_twin, spend):
     rows, half = mine.shape[1:]
     width = slopes.shape[2]
     early = pl.BlockSpec((None, rows, width), lambda step: (jnp.minimum(step, 3), 0, 0))
@@ -1127,45 +1140,83 @@
         out_specs=[fixed(*shape)] * 4,
         out_shape=[shaped(shape)] * 4,
         compiler_params=LIMIT,
-        cost_estimate=cost(12),
+        cost_estimate=cost(spend),
         name="feed_grad",
     )(bits, mine, theirs, mine, theirs, slopes, slopes_twin, slopes, slopes_twin)
 
 
+def halve_kernel(low_ref, keep_x, got_x, keep_y, got_y, keep_out, give_out):
+    start = jnp.where(low_ref[0] == 1, 0, 2)
+    for index, (keep, got) in enumerate(((keep_x, got_x), (keep_y, got_y))):
+        for out, begin in ((keep_out, start), (give_out, 2 - start)):
+            for level in range(2):
+                out[index, level] = low(wide(keep[begin + level]) + wide(got[begin + level]))
+
+
+def halve_sum(is_low, keeps, gots, spend):
+    count, width = keeps[0].shape[2], keeps[0].shape[4]
+    whole = pl.BlockSpec((4, None, count, UNIT, width), lambda other: (0, other, 0, 0, 0))
+    half = pl.BlockSpec((2, 2, None, count, UNIT, width), lambda other: (0, 0, other, 0, 0, 0))
+    return pl.pallas_call(
+        halve_kernel,
+        grid=(2,),
+        in_specs=[SMEM] + [whole] * 4,
+        out_specs=[half] * 2,
+        out_shape=[shaped((2, 2, 2, count, UNIT, width))] * 2,
+        compiler_params=LIMIT,
+        cost_estimate=cost(spend),
+        name="halve_sum",
+    )(is_low.astype(jnp.int32).reshape(1), keeps[0], gots[0], keeps[1], gots[1])
+
+
 class Reduction:
     def __init__(self, pairs, bits, is_low, is_core):
-        self.streams = pairs
+        self.keeps = [pair[0] for pair in pairs]
+        self.firsts = [pair[2] for pair in pairs]
         self.bits, self.is_low, self.is_core = bits, is_low, is_core
-        self.got = [
-            send(give, TO_X if x_first else TO_Y) for keep, give, x_first in self.streams
-        ]
-
-    def across(self):
-        stage = jnp.stack(
-            [low(wide(item[0]) + wide(got)) for item, got in zip(self.streams, self.got)]
-        )
-        give = jnp.where(self.is_low, stage[:, 2:4], stage[:, 0:2])
-        self.keep = jnp.where(self.is_low, stage[:, 0:2], stage[:, 2:4])
+        self.got = [send(pair[1], TO_X if pair[2] else TO_Y) for pair in pairs]
+
+    def across(self, spend, *others):
+        got = after(self.got, *others)
+        self.keep, give = halve_sum(self.is_low, self.keeps, got, spend)
         self.mid = send(give, TO_MID)
-        return self.keep
-
-    def outward(self):
-        stage = low(wide(self.keep) + wide(self.mid))
+        return give
+
+    def join(self, other):
+        self.keep = jnp.concatenate([self.keep, other.keep], axis=3)
+        self.mid = jnp.concatenate([self.mid, other.mid], axis=3)
+
+    def outward(self, *others):
+        mid = after([self.mid], *others)[0]
+        stage = low(wide(self.keep) + wide(mid))
         outer = jnp.where(self.is_low, stage[:, 0], stage[:, 1])
         self.inner = jnp.where(self.is_low, stage[:, 1], stage[:, 0])
         self.side = send(outer, TO_SIDE)
-        return self.inner
-
-    def finish(self):
-        stage = jnp.where(self.is_core, self.inner, self.side)
+        return outer
+
+    def turn(self, *others):
+        side = after([self.side], *others)[0]
+        stage = jnp.where(self.is_core, self.inner, side)
+        self.pieces = [stage[index] for index in range(len(self.firsts))]
+        self.over = [
+            send(piece, TO_Y if first else TO_X)
+            for piece, first in zip(self.pieces, self.firsts)
+        ]
+        return stage
+
+    def share(self, *others):
+        over = after(self.over, *others)
+        self.sums = [low(wide(piece) + wide(item)) for piece, item in zip(self.pieces, over)]
+        self.got = [
+            send(piece, TO_X if first else TO_Y) for piece, first in zip(self.sums, self.firsts)
+        ]
+        return self.sums[0]
+
+    def finish(self, *others):
         results = []
-        for index, (keep, give, x_first) in enumerate(self.streams):
-            one, two = (TO_X, TO_Y) if x_first else (TO_Y, TO_X)
-            piece = stage[index]
-            piece = low(wide(piece) + wide(send(piece, two)))
-            got = send(piece, one)
-            axis = 1 if x_first else 0
-            bit = self.bits[0] if x_first else self.bits[1]
+        for piece, got, first in zip(self.sums, after(self.got, *others), self.firsts):
+            axis = 1 if first else 0
+            bit = self.bits[0] if first else self.bits[1]
             joined = jnp.where(
                 bit == 0, jnp.stack([piece, got], axis), jnp.stack([got, piece], axis)
             )
@@ -1232,45 +1283,50 @@
     near_in = send(rows_in, TO_SIDE)
     middle_in = send(rows_in, TO_MID)
     far = send(near, TO_MID)
-    far_in = send(near_in, TO_MID)
     first = jnp.stack([units_of(item) for item in (near, middle, far)])
     over_x, over_y = send(first, TO_X), send(first, TO_Y)
+    expand_late, shrink_late, twin_late, near_in = after(
+        [expand_weight[0], shrink_weight[0], twin, near_in], first
+    )
+    far_in = send(near_in, TO_MID)
     parts = spread(front_zero, first, over_x, over_y, False)
-    fronts = [assemble(where, parts, 0, False)]
+
+    feed_zero = pack_feed(expand_late, shrink_late)
+    piece = tie(own_piece(feed_zero), parts[5], parts[6])
+    near = send(piece, TO_SIDE)
+    middle = send(piece, TO_MID)
     mine = jnp.stack([rows_in, near_in, middle_in, far_in])
     theirs = send(mine, TO_TWIN)
-
-    expand_late, shrink_late = lax.optimization_barrier(
-        (expand_weight[0], shrink_weight[0], near, middle)
-    )[:2]
-    feed_zero = pack_feed(expand_late, shrink_late)
-    piece = own_piece(feed_zero)
+    far = send(near, TO_MID)
+    first = jnp.stack([units_of(item) for item in (near, middle, far)])
+    first = tie(first, parts[7], parts[8], theirs)
+    over_x, over_y = send(first, TO_X), send(first, TO_Y)
+    feed_parts = spread(feed_zero, first, over_x, over_y, True)
+    fronts = [assemble(where, parts, 0, False)]
+
+    entry_late, exit_late, expand_late, shrink_late, cotangent_late = after(
+        [entry_weight[1], exit_weight[1], expand_weight[1], shrink_weight[1], cotangent], first
+    )
+    front_one = pack_front(entry_late, exit_late)
+    feed_one = pack_feed(expand_late, shrink_late)
+    piece = jnp.concatenate([own_piece(front_one), own_piece(feed_one), cotangent_late], axis=0)
+    piece = tie(piece, feed_parts[5], feed_parts[6])
     near = send(piece, TO_SIDE)
     middle = send(piece, TO_MID)
     far = send(near, TO_MID)
-    first = jnp.stack([units_of(item) for item in (near, middle, far)])
-    first = tie(first, over_x, over_y)
-    over_x, over_y = send(first, TO_X), send(first, TO_Y)
-    parts = spread(feed_zero, first, over_x, over_y, True)
+    four = (piece, near, middle, far)
+    parts = feed_parts
     ups = [assemble(where, parts, 0, False)]
     downs = [assemble(where, parts, 4, True)]
 
-    entry_late, exit_late, expand_late, shrink_late, cotangent_late = lax.optimization_barrier(
-        (entry_weight[1], exit_weight[1], expand_weight[1], shrink_weight[1], cotangent, near, middle)
-    )[:5]
-    front_one = pack_front(entry_late, exit_late)
-    feed_one = pack_feed(expand_late, shrink_late)
-    piece = jnp.concatenate([own_piece(front_one), own_piece(feed_one), cotangent_late], axis=0)
-    near = send(piece, TO_SIDE)
-    four = (piece, near, send(piece, TO_MID), send(near, TO_MID))
     first_split, split = 4 * UNIT, 12 * UNIT
     first = jnp.stack([units_of(item[:first_split]) for item in four[1:]])
-    first = tie(first, over_x, over_y)
+    first = tie(first, parts[7], parts[8])
     over_x, over_y = send(first, TO_X), send(first, TO_Y)
     parts = spread(front_one, first, over_x, over_y, True)
     fronts.append(assemble(where, parts, 0, False))
     first = jnp.stack([units_of(item[first_split:split]) for item in four[1:]])
-    first = tie(first, over_x, over_y)
+    first = tie(first, parts[7], parts[8])
     over_x, over_y = send(first, TO_X), send(first, TO_Y)
     parts = spread(feed_one, first, over_x, over_y, False)
     ups.append(assemble(where, parts, 0, False))
@@ -1312,7 +1368,7 @@
     place = jnp.arange(width // 2, dtype=jnp.int32)
     chunk = 4 * UNIT
     source = (place // chunk) * (2 * chunk) + place % chunk
-    cores_at = jnp.stack([twin, 1 - twin])
+    cores_at = jnp.stack([twin_late, 1 - twin_late])
     sel = low(block[None, :, None] == (source[None, :] + cores_at[:, None] * chunk)[:, None, :])
 
     local = jnp.arange(rows, dtype=jnp.int32)
@@ -1325,22 +1381,18 @@
     ).astype(jnp.int32)
     source_ids = (bases[:, None] + local[None, :]).reshape(8, 1, rows)
     want_in = dealt_near[0].reshape(core_rows, 1)
-    hidden_low = gather_rows((mine, theirs), source_ids, want_in)
-    upstream = gather_rows((cotangent_mine, cotangent_theirs), source_ids, want_in)
+    hidden_low = gather_rows((mine, theirs), source_ids, want_in, 5)
+    upstream = gather_rows((cotangent_mine, cotangent_theirs), source_ids, want_in, 5)
 
     result_ids = jnp.stack([dealt_near[0], dealt_far[0], dealt_near[1], dealt_far[1]]).reshape(
         4, 1, core_rows
     )
     want_out = jnp.concatenate([source_ids[0, 0], source_ids[1, 0]]).reshape(2 * rows, 1)
 
-    def collect(value):
-        pair = jnp.stack([value, send(value, TO_MID)])
-        return pair, send(pair, TO_TWIN)
-
-    def deliver(pair, other):
-        found = gather_rows((pair, other), result_ids, want_out)
-        outer = send(found[rows:], TO_SIDE)
-        return found, jnp.where(is_core, found[:rows], outer)
+    def deliver(pieces, spend):
+        pieces = [piece[None] for piece in pieces]
+        found = gather_rows(pieces, result_ids, want_out, spend)
+        return found, send(found[rows:], TO_SIDE)
 
     saved = []
     hidden = hidden_low
@@ -1355,24 +1407,27 @@
         )
         others = send(theirs, TO_TWIN)
         saved.append((queries, kv, kv_twin, ot, lse, n1, t1, n2, t2, slope, xm, xo, mine, others))
-    results = collect(hidden_low)
-
-    def start_back(layer, grad):
+    result_mid = send(hidden_low, TO_MID)
+    result_twin = send(hidden_low, TO_TWIN)
+
+    def start_back(layer, grad, spend):
         n1, t1, n2, t2, slope = saved[layer][5:10]
         slopes, do, dr, sums = post_back(
             grad, n1, t1, n2, t2, slope,
-            fronts[layer], ups[layer], downs[layer], vector_all[layer],
+            fronts[layer], ups[layer], downs[layer], vector_all[layer], spend,
         )
         return slopes, send(slopes, TO_TWIN), do, dr, sums
 
-    def attention_back(layer, do):
+    def attention_back(layer, do, spend):
         queries, kv, kv_twin, ot, lse = saved[layer][:5]
-        return attend_back_fast(queries, do, kv, kv_twin, ot, lse, code_half, member_own)
-
-    def feed_part(layer, x_first, slopes, slopes_twin):
+        return attend_back_fast(
+            queries, do, kv, kv_twin, ot, lse, code_half, member_own, spend
+        )
+
+    def feed_part(layer, x_first, slopes, slopes_twin, spend):
         mine, others = saved[layer][12:14]
         keep_up, give_up, keep_down, give_down = feed_grad(
-            x_first, bit_words, mine, others, slopes, slopes_twin
+            x_first, bit_words, mine, others, slopes, slopes_twin, spend
         )
         work = Reduction(
             [(keep_up, give_up, x_first), (keep_down, give_down, not x_first)],
@@ -1380,49 +1435,91 @@
         )
         return work, keep_up
 
-    def front_part(layer, x_first, slopes, slopes_twin, dm, dm_twin):
+    def front_part(layer, slopes, slopes_twin, dm, dm_twin, spend):
         xm, xo, mine, others = saved[layer][10:14]
-        keep, give = front_grad(
-            x_first, bit_words, xm, xo, mine, others, dm, dm_twin, slopes, slopes_twin
-        )
-        return Reduction([(keep, give, x_first)], bits, is_low, is_core), keep
+        keep_x, give_x, keep_y, give_y = front_grad(
+            bit_words, xm, xo, mine, others, dm, dm_twin, slopes, slopes_twin, spend
+        )
+        work = Reduction(
+            [(keep_x, give_x, True), (keep_y, give_y, False)], bits, is_low, is_core
+        )
+        return work, keep_x
 
     upstream = tie(upstream, saved[0][11], saved[0][13])
-    slopes_b, slopes_tb, do, dr, sums_b = start_back(1, upstream)
-    do = tie(do, saved[1][11], saved[1][13])
-    dq, own, give = attention_back(1, do)
+    slopes_b, slopes_tb, do, dr, sums_b = start_back(1, upstream, 16)
+    dq, own, give = attention_back(1, do, 21)
     got = send(give, TO_TWIN)
-    slopes_late = tie(slopes_tb, dq)
-    feed_b, mark = feed_part(1, True, slopes_b, slopes_late)
-    found, output = deliver(*tie(results, dq))
-    dr = tie(dr, mark, found)
-    dm_b, grad, _, head_b = project_back(dq, own, got, fronts[1], dr)
+    feed_b, mark = feed_part(1, True, slopes_b, tie(slopes_tb, dq, saved[1][11], result_twin), 12)
+    pair = (hidden_low, tie(result_mid, mark))
+    pair += (result_twin, send(pair[1], TO_TWIN))
+    dm_b, grad, _, head_b = project_back(dq, own, got, fronts[1], tie(dr, mark, pair[1]), 0.5)
     dm_tb = send(dm_b, TO_TWIN)
-    slopes_a, slopes_ta, do, dr, sums_a = start_back(0, grad)
-    front_b, mark = front_part(1, True, slopes_b, slopes_tb, dm_b, tie(dm_tb, do))
-    feed_a, mark = feed_part(0, False, slopes_a, tie(slopes_ta, mark))
-    do = tie(do, mark, feed_b.across())
-    dq, own, give = attention_back(0, do)
+    found, output_side = deliver(after(pair, head_b), 0.5)
+    slopes_a, slopes_ta, do, dr, sums_a = start_back(0, tie(grad, found), 0.5)
+    ready = feed_b.across(3, do)
+    dq, own, give = attention_back(0, tie(do, ready), 45)
     got = send(give, TO_TWIN)
-    dm_a, grad, grad_low, head_a = project_back(dq, own, got, fronts[0], dr)
+    front_b, mark = front_part(1, slopes_b, slopes_tb, dm_b, tie(dm_tb, dq), 0.5)
+    feed_a, mark = feed_part(0, False, slopes_a, tie(slopes_ta, mark, output_side, feed_b.mid), 12)
+    ready = front_b.across(2, mark)
+    dm_a, grad, grad_low, head_a = project_back(
+        dq, own, got, fronts[0], tie(dr, ready), 0.5
+    )
     dm_ta = send(dm_a, TO_TWIN)
-    dm_ta = tie(dm_ta, feed_b.outward(), front_b.across())
-    front_a, mark = front_part(0, False, slopes_a, slopes_ta, dm_a, dm_ta)
-    found, input_grad = deliver(*collect(grad_low))
-    input_grad = wide(input_grad)
-    feed_a.across()
-    front_b.outward()
-    feed_a.outward()
-    front_a.across()
-    front_a.outward()
-    grads = []
-    for front, feed, head_sums, sums in (
-        (front_a, feed_a, head_a, sums_a),
-        (front_b, feed_b, head_b, sums_b),
-    ):
-        up_grad, down_grad = feed.finish()
-        vector = jnp.concatenate([head_sums, sums[2:]], axis=0)
-        grads.append((front.finish()[0], up_grad, down_grad, vector))
+    grad_mid = send(grad_low, TO_MID)
+    grad_twin = send(grad_low, TO_TWIN)
+
+    vectors_all = [
+        jnp.concatenate([head_sums, sums[2:]], axis=0)
+        for head_sums, sums in ((head_a, sums_a), (head_b, sums_b))
+    ]
+    joined = jnp.stack([item.reshape(-1) for item in vectors_all])
+    joined = jnp.transpose(joined.reshape(layers, 4, 2, vectors.shape[1]), (1, 2, 0, 3))
+    vector_keep = lax.dynamic_index_in_dim(joined, twin, 1, keepdims=False)
+    vector_give = lax.dynamic_index_in_dim(joined, 1 - twin, 1, keepdims=False)
+    vector_twin = send(vector_give, TO_TWIN)
+
+    ready = feed_a.across(25, grad_low, front_b.mid)
+    front_a, mark = front_part(0, slopes_a, slopes_ta, dm_a, tie(dm_ta, vector_give, ready, grad_twin), 0.5)
+
+    feed_b.join(front_b)
+    ready = feed_b.outward(mark)
+    vector_stage = vector_keep + tie(vector_twin, ready)
+    vector_over = send(vector_stage, TO_X)
+    pair = (grad_low, tie(grad_mid, vector_stage), grad_twin)
+    pair += (send(pair[1], TO_TWIN),)
+    found_in, input_side = deliver(pair, 0.5)
+    ready = feed_b.turn(found_in)
+    vector_stage = vector_stage + tie(vector_over, ready)
+    vector_over = send(vector_stage, TO_Y)
+
+    ready = front_a.across(0.5, vector_stage)
+    ready = feed_b.share(ready)
+    vector_stage = vector_stage + tie(vector_over, ready)
+    vector_give = jnp.where(is_low, vector_stage[2:4], vector_stage[0:2])
+    vector_keep = jnp.where(is_low, vector_stage[0:2], vector_stage[2:4])
+    vector_mid = send(vector_give, TO_MID)
+    ready = feed_a.outward(vector_give)
+    done_b = feed_b.finish(ready)
+    up_b, down_b = (item[:, :4] for item in done_b)
+    front_grad_b = jnp.concatenate([item[:, 4:] for item in done_b], axis=1)
+
+    ready = front_a.outward(up_b, down_b, front_grad_b)
+    vector_stage = vector_keep + tie(vector_mid, ready)
+    vector_outer = jnp.where(is_low, vector_stage[0], vector_stage[1])
+    vector_inner = jnp.where(is_low, vector_stage[1], vector_stage[0])
+    vector_side = send(vector_outer, TO_SIDE)
+    ready = feed_a.turn(vector_outer)
+    output = jnp.where(is_core, found[:rows], output_side)
+    input_grad = wide(jnp.where(is_core, found_in[:rows], tie(input_side, ready)))
+
+    ready = front_a.turn(ready)
+    ready_two = feed_a.share(ready)
+    ready = front_a.share(ready_two)
+    up_a, down_a = feed_a.finish(ready)
+    front_grad_a = jnp.concatenate(front_a.finish(up_a, down_a), axis=1)
+    vector_grad = jnp.where(is_core, vector_inner, tie(vector_side, ready))
+    grads = [(front_grad_a, up_a, down_a), (front_grad_b, up_b, down_b)]
 
     def columns(units):
         count = units.shape[1]
@@ -1432,20 +1529,6 @@
     exit_grad = jnp.stack([columns(item[0][:, 3:4]) for item in grads])
     expand_grad = jnp.stack([columns(item[1]) for item in grads])
     shrink_grad = jnp.stack([item[2].reshape(16 * UNIT, width) for item in grads])
-
-    joined = jnp.stack([item[3].reshape(-1) for item in grads])
-    joined = jnp.transpose(joined.reshape(layers, 4, 2, vectors.shape[1]), (1, 2, 0, 3))
-    keep = lax.dynamic_index_in_dim(joined, twin, 1, keepdims=False)
-    give = lax.dynamic_index_in_dim(joined, 1 - twin, 1, keepdims=False)
-    stage = keep + send(give, TO_TWIN)
-    stage = stage + send(stage, TO_X)
-    stage = stage + send(stage, TO_Y)
-    give = jnp.where(is_low, stage[2:4], stage[0:2])
-    keep = jnp.where(is_low, stage[0:2], stage[2:4])
-    stage = keep + send(give, TO_MID)
-    outer = jnp.where(is_low, stage[0], stage[1])
-    inner = jnp.where(is_low, stage[1], stage[0])
-    vector_grad = jnp.where(is_core, inner, send(outer, TO_SIDE))
     return (output, input_grad, entry_grad, exit_grad, expand_grad, shrink_grad, vector_grad)
 
 

time: 720 us -> 600 us (0.83)
  waiting for transfers between devices: 158 us -> 81.5 us
  starting transfers between devices: 161 us -> 108 us
  Pallas kernels: 282 us -> 295 us
  other arithmetic: 58.5 us -> 46.5 us
    ppermute x95 -> x98, waiting for transfers between devices: 158 us -> 81.5 us  [send(): return lax.ppermute(value, BOTH, route)]
    ppermute x95 -> x98, starting transfers between devices: 161 us -> 108 us  [send(): return lax.ppermute(value, BOTH, route)]
    pallas_call x2 -> x6, Pallas kernels: 15.5 us -> 27.8 us  [the longest x2 15.3 us: front_grad(): pl.pallas_call(front_grad_kernel, grid=(4,), in_specs=[SMEM, fixed(rows,...]
    another operation x12 -> x4, other arithmetic: 9.63 us -> 0.2 us  [the longest x6 6.86 us: across(): jnp.stack([low(wide(item[0]) + wide(got)) for item, got in zip(self.strea...]
  transfers between devices with their start and end apart: 95 -> 98, of which waited for: 23 -> 20; matrix products, arithmetic and copies ran while one was open for 12% -> 13% of each run, Pallas kernels for 37% -> 41%
where the time goes in v4:
time: 600 us; the launch traced here: 589 us
  Pallas kernels  295 us (49%)
  starting transfers between devices  108 us (18%)
  waiting for transfers between devices  81.5 us (14%)
  local copies, waits for them, and re-layouts  52.4 us (9%)
  other arithmetic  46.5 us (8%)
  between operations  6.22 us (1%)
    ppermute x98, starting transfers between devices, send(): return lax.ppermute(value, BOTH, route)  108 us
    ppermute x98, waiting for transfers between devices, send(): return lax.ppermute(value, BOTH, route)  81.5 us
    pallas_call x2, Pallas kernels, post(): pl.pallas_call(post_kernel, grid=(4,), in_specs=[SMEM, full, full, unit_s...  49.1 us
    pallas_call x2, Pallas kernels, attend_back_fast(): pl.pallas_call(attend_back_kernel, grid=(width // 128,), in_specs=[column...  41.5 us
    pallas_call x6, Pallas kernels, assemble(): pl.pallas_call(assemble_kernel, grid_spec=pltpu.PrefetchScalarGridSpec(nu...  34.7 us
    pallas_call x2, Pallas kernels, post_back(): pl.pallas_call(post_back_kernel, grid=(4,), in_specs=[full, full, thin, f...  33 us
    pallas_call x2, Pallas kernels, attend_fast(): pl.pallas_call(attend_kernel, grid=(width // 128,), in_specs=[column, key...  31.1 us
    pallas_call x2, Pallas kernels, feed_grad(): pl.pallas_call(functools.partial(feed_grad_kernel, x_first), grid=(8,), i...  25.4 us
  transfers between devices with their start and end apart: 98, of which 20 were waited for; matrix products, arithmetic and copies ran while one was open for 13% of the time, Pallas kernels for 41%

profile of v4, /device:TPU:0, one launch (start us, length us, event | category | flops | bytes accessed | tf_op | source)
XLA Modules:
  0.0 589.1 jit_solution(11039074704872177091)
XLA Ops:
  3.3 3.1 collective-permute-start.1
  8.7 3.8 collective-permute-start
  37.7 2.7 pad_maximum_fusion.4.refs_0_
  42.7 4.7 collective-permute-done.8.refs_3_
  49.0 4.7 collective-permute-start.16
  56.3 4.4 collective-permute-done.16
  65.2 5.8 assemble.6
  77.6 4.7 gather_rows.4.h_ref
  82.3 7.3 %project.2 = (bf16[512,768]{1,0:T(8,128)(2,1)}, bf16[2,512,768]{2,1,0:T(8,128)(2,1)}, bf16[512,384]{1,0:T(8,128)(2,1)}, bf16[512,384]{1,0:T(8,128)(2,1)}) custom-call(bf16[512,768]{1,0:T(8,128)(2,1)} %gather_rows.4.h_ref, bf16[4,768,768]{2,1,0:T(8,128)(2,1)} %bitcast.276, f32[12,768]{1,0:T(8,128)} %squeeze.97.vec_ref, bf16[2,768,384]{2,1,0:T(8,128)(2,1)} %fusion.sel_ref), custom_call_target="tpu_custom_call" | custom-call | flops 7000000000 | bytes 7000000 | tf_op jit(solution)/shard_map/project/pallas_call | solution.py:593
  91.4 16.7 %collective-permute-start.27 = (bf16[544,768]{1,0:T(8,128)(2,1)S(1)}, bf16[544,768]{1,0:T(8,128)(2,1)}, u32[]{:S(2)}, u32[]{:S(2)}) collective-permute-start(bf16[544,768]{1,0:T(8,128)(2,1)S(1)} %pad_maximum_fusion.12), channel_id=1, source_target_pairs={{0,2},{1,3},{2,0},{3,1},{4,6},{5,7},{6,4},{7,5},{8,10},{9,11},{10,... | collective-permute-start | bytes 2506760 | tf_op jit(solution)/shard_map/ppermute | solution.py:441
  116.1 11.4 %collective-permute-done.27 = bf16[544,768]{1,0:T(8,128)(2,1)} collective-permute-done((bf16[544,768]{1,0:T(8,128)(2,1)S(1)}, bf16[544,768]{1,0:T(8,128)(2,1)}, u32[]{:S(2)}, u32[]{:S(2)}) %collective-permute-start.27) | collective-permute-done | bytes 835616 | tf_op jit(solution)/shard_map/ppermute | solution.py:441
  129.3 15.4 %attend_forward.2 = (bf16[512,768]{1,0:T(8,128)(2,1)}, f32[768,512]{1,0:T(8,128)}, f32[6,2,512]{2,1,0:T(2,128)}) custom-call(bf16[512,768]{1,0:T(8,128)(2,1)} %get-tuple-element.162.q_ref, bf16[2,512,768]{2,1,0:T(8,128)(2,1)} %get-tuple-element.163.ka_ref.va_ref, bf16[2,512,768]{2,1,0:T(8,128)(2,1)} %collective-permute-done.15.kb_ref.vb_ref, ...), custom_call_target="tpu_custom_call" | custom-call | flops 15000000512 | bytes 15000000 | tf_op jit(solution)/shard_map/attend_forward/pallas_call | solution.py:671
  157.3 5.8 assemble.8
  165.0 5.8 assemble.7
  170.9 6.3 %collective-permute-done.34.refs_4_ = bf16[3,4,24,768]{3,2,1,0:T(8,128)(2,1)} collective-permute-done((bf16[3,4,24,768]{3,2,1,0:T(8,128)(2,1)}, bf16[3,4,24,768]{3,2,1,0:T(8,128)(2,1)}, u32[]{:S(2)}, u32[]{:S(2)}) %collective-permute-start.34) | collective-permute-done | bytes 442400 | tf_op jit(solution)/shard_map/ppermute | solution.py:441
  177.2 24.2 %post.2 = (f32[512,768]{1,0:T(8,128)}, bf16[512,768]{1,0:T(8,128)(2,1)}, f32[512,768]{1,0:T(8,128)}, f32[512,1]{1,0:T(8,128)}, f32[512,768]{1,0:T(8,128)}, /*ind...) custom-call(s32[3]{0:T(128)} %pad_add_fusion.3.where_ref, ...), custom_call_target="tpu_custom_call" | custom-call | flops 23000000512 | bytes 23000000 | tf_op jit(solution)/shard_map/post/pallas_call | solution.py:850
  204.0 5.8 assemble.9
  209.9 7.6 %project.3 = (bf16[512,768]{1,0:T(8,128)(2,1)}, bf16[2,512,768]{2,1,0:T(8,128)(2,1)}, bf16[512,384]{1,0:T(8,128)(2,1)}, bf16[512,384]{1,0:T(8,128)(2,1)}) custom-call(bf16[512,768]{1,0:T(8,128)(2,1)} %get-tuple-element.172.h_ref, bf16[4,768,768]{2,1,0:T(8,128)(2,1)} %bitcast.298, f32[12,768]{1,0:T(8,128)} %squeeze.102.vec_ref, bf16[2,768,384]{2,1,0:T(8,128)(2,1)} %fusion.sel_ref), custom_call_target="tpu_custom_call" | custom-call | flops 7000000000 | bytes 7000000 | tf_op jit(solution)/shard_map/project/pallas_call | solution.py:593
  217.5 6.4 %collective-permute-done.39.refs_2_ = bf16[3,8,24,768]{3,2,1,0:T(8,128)(2,1)} collective-permute-done((bf16[3,8,24,768]{3,2,1,0:T(8,128)(2,1)}, bf16[3,8,24,768]{3,2,1,0:T(8,128)(2,1)}, u32[]{:S(2)}, u32[]{:S(2)}) %collective-permute-start.39) | collective-permute-done | bytes 884768 | tf_op jit(solution)/shard_map/ppermute | solution.py:441
  229.0 4.7 gather_rows.5.e_ref
  233.7 12.8 %collective-permute-done.43.refs_4_ = bf16[3,8,24,768]{3,2,1,0:T(8,128)(2,1)} collective-permute-done((bf16[3,8,24,768]{3,2,1,0:T(8,128)(2,1)}, bf16[3,8,24,768]{3,2,1,0:T(8,128)(2,1)}, u32[]{:S(2)}, u32[]{:S(2)}) %collective-permute-start.43) | collective-permute-done | bytes 884768 | tf_op jit(solution)/shard_map/ppermute | solution.py:441
  246.7 15.7 %attend_forward.3 = (bf16[512,768]{1,0:T(8,128)(2,1)}, f32[768,512]{1,0:T(8,128)}, f32[6,2,512]{2,1,0:T(2,128)}) custom-call(bf16[512,768]{1,0:T(8,128)(2,1)} %get-tuple-element.183.q_ref, bf16[2,512,768]{2,1,0:T(8,128)(2,1)} %get-tuple-element.184.ka_ref.va_ref, bf16[2,512,768]{2,1,0:T(8,128)(2,1)} %collective-permute-done.38.kb_ref.vb_ref, ...), custom_call_target="tpu_custom_call" | custom-call | flops 15000000512 | bytes 15000000 | tf_op jit(solution)/shard_map/attend_forward/pallas_call | solution.py:671
  263.3 5.8 assemble.11
  269.1 5.7 assemble.10
  274.8 24.8 %post.3 = (f32[512,768]{1,0:T(8,128)}, bf16[512,768]{1,0:T(8,128)(2,1)}, f32[512,768]{1,0:T(8,128)}, f32[512,1]{1,0:T(8,128)}, f32[512,768]{1,0:T(8,128)}, /*ind...) custom-call(s32[3]{0:T(128)} %pad_add_fusion.3.where_ref, ...), custom_call_target="tpu_custom_call" | custom-call | flops 23000000512 | bytes 23000000 | tf_op jit(solution)/shard_map/post/pallas_call | solution.py:850
  299.7 16.3 %post_back.2 = (bf16[6,512,768]{2,1,0:T(8,128)(2,1)}, bf16[512,768]{1,0:T(8,128)(2,1)}, f32[512,768]{1,0:T(8,128)}, f32[12,768]{1,0:T(8,128)}) custom-call(bf16[512,768]{1,0:T(8,128)(2,1)} %gather_rows.5.e_ref, f32[512,768]{1,0:T(8,128)} %get-tuple-element.197.n1_ref, f32[512,1]{1,0:T(8,128)} %get-tuple-element.198.t1_ref, ...), custom_call_target="tpu_custom_call" | custom-call | flops 16000000000 | bytes 16000000 | tf_op jit(solution)/shard_map/post_back/pallas_call | solution.py:944
  319.2 20.7 %attend_backward.2 = (bf16[512,768]{1,0:T(8,128)(2,1)}, f32[2,512,768]{2,1,0:T(8,128)}, bf16[2,512,768]{2,1,0:T(8,128)(2,1)}) custom-call(bf16[512,768]{1,0:T(8,128)(2,1)} %get-tuple-element.183.q_ref, bf16[512,768]{1,0:T(8,128)(2,1)} %get-tuple-element.203.g_ref, bf16[2,512,768]{2,1,0:T(8,128)(2,1)} %get-tuple-element.184.ka_ref.va_ref, ...), custom_call_target="tpu_custom_call" | custom-call | flops 20999999488 | bytes 21000000 | tf_op jit(solution)/shard_map/attend_backward/pallas_call | solution.py:740
  341.7 12.5 %feed_grad.2 = (bf16[4,2,4,24,768]{4,3,2,1,0:T(8,128)(2,1)}, bf16[4,2,4,24,768]{4,3,2,1,0:T(8,128)(2,1)}, bf16[4,2,4,24,768]{4,3,2,1,0:T(8,128)(2,1)}, bf16[4,2,4,24,768]{4,3,2,1,0:T(8,128)(2,1)}) custom-call(s32[2]{0:T(128)} %pad_add_fusion.4.bit_ref, bf16[6,512,384]{2,1,0:T(8,128)(2,1)} %get-tuple-element.192.ym_ref.gm_ref.om_ref, ...), custom_call_target="tpu_custom_call" | custom-call | flops 12000000000 | bytes 12000000 | tf_op jit(solution)/shard_map/feed_grad/pallas_call | solution.py:1133
  358.9 9.2 %project_back.2 = (bf16[3,512,768]{2,1,0:T(8,128)(2,1)}, f32[512,768]{1,0:T(8,128)}, bf16[512,768]{1,0:T(8,128)(2,1)}, f32[2,768]{1,0:T(2,128)}) custom-call(bf16[512,768]{1,0:T(8,128)(2,1)} %get-tuple-element.206.dq_ref, f32[2,512,768]{2,1,0:T(8,128)} %get-tuple-element.211.own_ref, bf16[2,512,768]{2,1,0:T(8,128)(2,1)} %collective-permute-done.56.got_ref, ...), custom_call_target="tpu_custom_call" | custom-call | flops 500000000 | bytes 500000 | tf_op jit(solution)/shard_map/project_back/pallas_call | solution.py:1004
  369.0 4.8 gather_rows.6
  373.8 16.7 %post_back.3 = (bf16[6,512,768]{2,1,0:T(8,128)(2,1)}, bf16[512,768]{1,0:T(8,128)(2,1)}, f32[512,768]{1,0:T(8,128)}, f32[12,768]{1,0:T(8,128)}) custom-call(f32[512,768]{1,0:T(8,128)} %get-tuple-element.221.e_ref, f32[512,768]{1,0:T(8,128)} %get-tuple-element.222.n1_ref, f32[512,1]{1,0:T(8,128)} %get-tuple-element.223.t1_ref, ...), custom_call_target="tpu_custom_call" | custom-call | flops 500000000 | bytes 500000 | tf_op jit(solution)/shard_map/post_back/pallas_call | solution.py:944
  391.1 6.8 %collective-permute-start.57 = (bf16[256,768]{1,0:T(8,128)(2,1)S(1)}, bf16[256,768]{1,0:T(8,128)(2,1)}, u32[]{:S(2)}, u32[]{:S(2)}) collective-permute-start(bf16[256,768]{1,0:T(8,128)(2,1)S(1)} %slice.328), channel_id=1, source_target_pairs={{0,2},{1,3},{2,0},{3,1},{4,6},{5,7},{6,4},{7,5},{8,10},{9,11},{10,... | collective-permute-start | bytes 1179656 | tf_op jit(solution)/shard_map/ppermute | solution.py:441
  397.9 3.7 halve_sum.4
  402.3 20.8 %attend_backward.3 = (bf16[512,768]{1,0:T(8,128)(2,1)}, f32[2,512,768]{2,1,0:T(8,128)}, bf16[2,512,768]{2,1,0:T(8,128)(2,1)}) custom-call(bf16[512,768]{1,0:T(8,128)(2,1)} %get-tuple-element.162.q_ref, bf16[512,768]{1,0:T(8,128)(2,1)} %get-tuple-element.234.g_ref, bf16[2,512,768]{2,1,0:T(8,128)(2,1)} %get-tuple-element.163.ka_ref.va_ref, ...), custom_call_target="tpu_custom_call" | custom-call | flops 44999999488 | bytes 45000000 | tf_op jit(solution)/shard_map/attend_backward/pallas_call | solution.py:740
  423.3 7.7 %front_grad.2 = (bf16[4,2,2,24,768]{4,3,2,1,0:T(8,128)(2,1)}, bf16[4,2,2,24,768]{4,3,2,1,0:T(8,128)(2,1)}, bf16[4,2,2,24,768]{4,3,2,1,0:T(8,128)(2,1)}, bf16[4,2,2,24,768]{4,3,2,1,0:T(8,128)(2,1)}) custom-call(s32[2]{0:T(128)} %pad_add_fusion.4.bit_ref, bf16[512,384]{1,0:T(8,128)(2,1)} %get-tuple-element.241.xm_ref, bf16[512,384]{1,0:T(8,128)(2,1)} %copy-done.24, ...), custom_call_target="tpu_custom_call" | custom-call | flops 500000000 | bytes 500000 | tf_op jit(solution)/shard_map/front_grad/pallas_call | solution.py:1084
  432.3 12.9 %feed_grad.3 = (bf16[4,2,4,24,768]{4,3,2,1,0:T(8,128)(2,1)}, bf16[4,2,4,24,768]{4,3,2,1,0:T(8,128)(2,1)}, bf16[4,2,4,24,768]{4,3,2,1,0:T(8,128)(2,1)}, bf16[4,2,4,24,768]{4,3,2,1,0:T(8,128)(2,1)}) custom-call(s32[2]{0:T(128)} %pad_add_fusion.4.bit_ref, bf16[6,512,384]{2,1,0:T(8,128)(2,1)} %get-tuple-element.247.ym_ref.gm_ref.om_ref, ...), custom_call_target="tpu_custom_call" | custom-call | flops 12000000000 | bytes 12000000 | tf_op jit(solution)/shard_map/feed_grad/pallas_call | solution.py:1133
  449.1 2.6 halve_sum.5
  452.6 9.3 %project_back.3 = (bf16[3,512,768]{2,1,0:T(8,128)(2,1)}, f32[512,768]{1,0:T(8,128)}, bf16[512,768]{1,0:T(8,128)(2,1)}, f32[2,768]{1,0:T(2,128)}) custom-call(bf16[512,768]{1,0:T(8,128)(2,1)} %get-tuple-element.237.dq_ref, f32[2,512,768]{2,1,0:T(8,128)} %get-tuple-element.238.own_ref, bf16[2,512,768]{2,1,0:T(8,128)(2,1)} %collective-permute-done.60.got_ref, ...), custom_call_target="tpu_custom_call" | custom-call | flops 500000000 | bytes 500000 | tf_op jit(solution)/shard_map/project_back/pallas_call | solution.py:1004
  465.1 8.3 %collective-permute-done.70.got_x = bf16[4,2,4,24,768]{4,3,2,1,0:T(8,128)(2,1)} collective-permute-done((bf16[4,2,4,24,768]{4,3,2,1,0:T(8,128)(2,1)}, bf16[4,2,4,24,768]{4,3,2,1,0:T(8,128)(2,1)}, u32[]{:S(2)}, u32[]{:S(2)}) %collective-permute-start.70) | collective-permute-done | bytes 1179680 | tf_op jit(solution)/shard_map/ppermute | solution.py:441
  474.3 3.6 halve_sum.6
  477.9 7.7 %front_grad.3 = (bf16[4,2,2,24,768]{4,3,2,1,0:T(8,128)(2,1)}, bf16[4,2,2,24,768]{4,3,2,1,0:T(8,128)(2,1)}, bf16[4,2,2,24,768]{4,3,2,1,0:T(8,128)(2,1)}, bf16[4,2,2,24,768]{4,3,2,1,0:T(8,128)(2,1)}) custom-call(s32[2]{0:T(128)} %pad_add_fusion.4.bit_ref, bf16[512,384]{1,0:T(8,128)(2,1)} %get-tuple-element.262.xm_ref, bf16[512,384]{1,0:T(8,128)(2,1)} %copy-done.23, ...), custom_call_target="tpu_custom_call" | custom-call | flops 500000000 | bytes 500000 | tf_op jit(solution)/shard_map/front_grad/pallas_call | solution.py:1084
  494.9 4.7 gather_rows.7
  499.5 9.3 %collective-permute-done.77 = bf16[2,2,6,24,768]{4,3,2,1,0:T(8,128)(2,1)S(1)} collective-permute-done((bf16[2,2,6,24,768]{4,3,2,1,0:T(8,128)(2,1)S(1)}, bf16[2,2,6,24,768]{4,3,2,1,0:T(8,128)(2,1)S(1)}, u32[]{:S(2)}, u32[]{:S(2)}) %collective-permute-start.77) | collective-permute-done | bytes 884768 | tf_op jit(solution)/shard_map/ppermute | solution.py:441
  529.1 4.6 collective-permute-done.86
  533.7 2.7 collective-permute-start.83
  539.3 3.6 collective-permute-start.88
  561.7 2.8 collective-permute-done.91
  581.7 2.9 pad_maximum_fusion.1
  (473 shorter events, 172.5 us)
Async XLA Ops:
  6.3 21.8 %collective-permute-start.2 = (bf16[96,768]{1,0:T(8,128)(2,1)}, bf16[96,768]{1,0:T(8,128)(2,1)}, u32[]{:S(2)}, u32[]{:S(2)}) collective-permute-start(bf16[96,768]{1,0:T(8,128)(2,1)} %bitcast.4), channel_id=1, source_target_pairs={{2,4},{3,5},{4,2},{5,3},{10,12},{11,13},{12,10},{13,11},{18,20},{1... | collective-permute-start | bytes 442376 | tf_op jit(solution)/shard_map/ppermute | solution.py:441
  8.7 23.1 %collective-permute-start = (bf16[264,768]{1,0:T(8,128)(2,1)}, bf16[264,768]{1,0:T(8,128)(2,1)}, u32[]{:S(2)}, u32[]{:S(2)}) collective-permute-start(bf16[264,768]{1,0:T(8,128)(2,1)} %maximum_maximum_fusion), channel_id=1, source_target_pairs={{0,2},{1,3},{2,0},{3,1},{4,6},{5,7},{6,4},{7,5},{8,10},{9,11},{10,... | collective-permute-start | bytes 1216520 | tf_op jit(solution)/shard_map/ppermute | solution.py:441
  12.5 22.9 %collective-permute-start.4 = (bf16[264,768]{1,0:T(8,128)(2,1)}, bf16[264,768]{1,0:T(8,128)(2,1)}, u32[]{:S(2)}, u32[]{:S(2)}) collective-permute-start(bf16[264,768]{1,0:T(8,128)(2,1)} %maximum_maximum_fusion), channel_id=1, source_target_pairs={{2,4},{3,5},{4,2},{5,3},{10,12},{11,13},{12,10},{13,11},{18,20},{1... | collective-permute-start | bytes 1216520 | tf_op jit(solution)/shard_map/ppermute | solution.py:441
  14.8 25.7 %collective-permute-start.9 = (bf16[4,4,24,768]{3,2,1,0:T(8,128)(2,1)}, bf16[4,4,24,768]{3,2,1,0:T(8,128)(2,1)}, u32[]{:S(2)}, u32[]{:S(2)}) collective-permute-start(bf16[4,4,24,768]{3,2,1,0:T(8,128)(2,1)} %pad_maximum_fusion.13.refs_0_), channel_id=1, source_target_pairs={{0,1},{1,0},{2,3},{3,2},{4,5},{5,4},{6,7},{7,6},{8,9},{9,8},{10,11... | collective-permute-start | bytes 1769480 | tf_op jit(solution)/shard_map/ppermute | solution.py:441
  40.4 30.6 %collective-permute-start.6 = (bf16[4,264,768]{2,1,0:T(8,128)(2,1)}, bf16[4,264,768]{2,1,0:T(8,128)(2,1)}, u32[]{:S(2)}, u32[]{:S(2)}) collective-permute-start(bf16[4,264,768]{2,1,0:T(8,128)(2,1)} %pad_maximum_fusion.4.refs_0_), channel_id=1, source_target_pairs={{0,1},{1,0},{2,3},{3,2},{4,5},{5,4},{6,7},{7,6},{8,9},{9,8},{10,11... | collective-permute-start | bytes 4866056 | tf_op jit(solution)/shard_map/ppermute | solution.py:441
  60.7 30.8 %collective-permute-start.21 = (bf16[4,8,24,768]{3,2,1,0:T(8,128)(2,1)}, bf16[4,8,24,768]{3,2,1,0:T(8,128)(2,1)}, u32[]{:S(2)}, u32[]{:S(2)}) collective-permute-start(bf16[4,8,24,768]{3,2,1,0:T(8,128)(2,1)} %pad_maximum_fusion.7.refs_0_), channel_id=1, source_target_pairs={{0,1},{1,0},{2,3},{3,2},{4,5},{5,4},{6,7},{7,6},{8,9},{9,8},{10,11... | collective-permute-start | bytes 3538952 | tf_op jit(solution)/shard_map/ppermute | solution.py:441
  71.0 20.4 %collective-permute-start.22 = (bf16[3,8,24,768]{3,2,1,0:T(8,128)(2,1)}, bf16[3,8,24,768]{3,2,1,0:T(8,128)(2,1)}, u32[]{:S(2)}, u32[]{:S(2)}) collective-permute-start(bf16[3,8,24,768]{3,2,1,0:T(8,128)(2,1)} %pad_maximum_fusion.10.refs_1_), channel_id=1, source_target_pairs={{0,1},{1,0},{2,3},{3,2},{4,5},{5,4},{6,7},{7,6},{8,9},{9,8},{10,11... | collective-permute-start | bytes 2654216 | tf_op jit(solution)/shard_map/ppermute | solution.py:441
  71.1 42.8 %collective-permute-start.19 = (bf16[3,8,24,768]{3,2,1,0:T(8,128)(2,1)}, bf16[3,8,24,768]{3,2,1,0:T(8,128)(2,1)}, u32[]{:S(2)}, u32[]{:S(2)}) collective-permute-start(bf16[3,8,24,768]{3,2,1,0:T(8,128)(2,1)} %pad_maximum_fusion.10.refs_1_), channel_id=1, source_target_pairs={{0,8},{1,9},{2,10},{3,11},{4,12},{5,13},{6,14},{7,15},{8,0},{9,1},... | collective-permute-start | bytes 2654216 | tf_op jit(solution)/shard_map/ppermute | solution.py:441
  71.7 42.3 %collective-permute-start.20 = (bf16[3,8,24,768]{3,2,1,0:T(8,128)(2,1)}, bf16[3,8,24,768]{3,2,1,0:T(8,128)(2,1)}, u32[]{:S(2)}, u32[]{:S(2)}) collective-permute-start(bf16[3,8,24,768]{3,2,1,0:T(8,128)(2,1)} %pad_maximum_fusion.10.refs_1_), channel_id=1, source_target_pairs={{0,16},{1,17},{2,18},{3,19},{4,20},{5,21},{6,22},{7,23},{8,24},{9,... | collective-permute-start | bytes 2654216 | tf_op jit(solution)/shard_map/ppermute | solution.py:441
  89.7 25.9 %collective-permute-start.15 = (bf16[2,512,768]{2,1,0:T(8,128)(2,1)}, bf16[2,512,768]{2,1,0:T(8,128)(2,1)}, u32[]{:S(2)}, u32[]{:S(2)}) collective-permute-start(bf16[2,512,768]{2,1,0:T(8,128)(2,1)} %get-tuple-element.163.ka_ref.va_ref), channel_id=1, source_target_pairs={{0,1},{1,0},{2,3},{3,2},{4,5},{5,4},{6,7},{7,6},{8,9},{9,8},{10,11... | collective-permute-start | bytes 4718600 | tf_op jit(solution)/shard_map/ppermute | solution.py:441
  91.4 36.1 %collective-permute-start.27 = (bf16[544,768]{1,0:T(8,128)(2,1)S(1)}, bf16[544,768]{1,0:T(8,128)(2,1)}, u32[]{:S(2)}, u32[]{:S(2)}) collective-permute-start(bf16[544,768]{1,0:T(8,128)(2,1)S(1)} %pad_maximum_fusion.12), channel_id=1, source_target_pairs={{0,2},{1,3},{2,0},{3,1},{4,6},{5,7},{6,4},{7,5},{8,10},{9,11},{10,... | collective-permute-start | bytes 2506760 | tf_op jit(solution)/shard_map/ppermute | solution.py:441
  113.2 33.4 %collective-permute-start.28 = (bf16[544,768]{1,0:T(8,128)(2,1)S(1)}, bf16[544,768]{1,0:T(8,128)(2,1)S(1)}, u32[]{:S(2)}, u32[]{:S(2)}) collective-permute-start(bf16[544,768]{1,0:T(8,128)(2,1)S(1)} %pad_maximum_fusion.12), channel_id=1, source_target_pairs={{2,4},{3,5},{4,2},{5,3},{10,12},{11,13},{12,10},{13,11},{18,20},{1... | collective-permute-start | bytes 2506760 | tf_op jit(solution)/shard_map/ppermute | solution.py:441
  114.0 32.8 %collective-permute-start.23 = (bf16[3,8,24,768]{3,2,1,0:T(8,128)(2,1)}, bf16[3,8,24,768]{3,2,1,0:T(8,128)(2,1)}, u32[]{:S(2)}, u32[]{:S(2)}) collective-permute-start(bf16[3,8,24,768]{3,2,1,0:T(8,128)(2,1)} %collective-permute-done.20.refs_3_), channel_id=1, source_target_pairs={{0,8},{1,9},{2,10},{3,11},{4,12},{5,13},{6,14},{7,15},{8,0},{9,1},... | collective-permute-start | bytes 2654216 | tf_op jit(solution)/shard_map/ppermute | solution.py:441
  115.5 31.8 %collective-permute-start.25 = (bf16[3,8,24,768]{3,2,1,0:T(8,128)(2,1)}, bf16[3,8,24,768]{3,2,1,0:T(8,128)(2,1)}, u32[]{:S(2)}, u32[]{:S(2)}) collective-permute-start(bf16[3,8,24,768]{3,2,1,0:T(8,128)(2,1)} %collective-permute-done.20.refs_3_), channel_id=1, source_target_pairs={{0,1},{1,0},{2,3},{3,2},{4,5},{5,4},{6,7},{7,6},{8,9},{9,8},{10,11... | collective-permute-start | bytes 2654216 | tf_op jit(solution)/shard_map/ppermute | solution.py:441
  115.6 31.8 %collective-permute-start.24 = (bf16[3,8,24,768]{3,2,1,0:T(8,128)(2,1)}, bf16[3,8,24,768]{3,2,1,0:T(8,128)(2,1)}, u32[]{:S(2)}, u32[]{:S(2)}) collective-permute-start(bf16[3,8,24,768]{3,2,1,0:T(8,128)(2,1)} %collective-permute-done.19.refs_2_), channel_id=1, source_target_pairs={{0,1},{1,0},{2,3},{3,2},{4,5},{5,4},{6,7},{7,6},{8,9},{9,8},{10,11... | collective-permute-start | bytes 2654216 | tf_op jit(solution)/shard_map/ppermute | solution.py:441
  127.5 21.0 %collective-permute-start.29 = (bf16[544,768]{1,0:T(8,128)(2,1)}, bf16[544,768]{1,0:T(8,128)(2,1)}, u32[]{:S(2)}, u32[]{:S(2)}) collective-permute-start(bf16[544,768]{1,0:T(8,128)(2,1)} %collective-permute-done.27), channel_id=1, source_target_pairs={{2,4},{3,5},{4,2},{5,3},{10,12},{11,13},{12,10},{13,11},{18,20},{1... | collective-permute-start | bytes 2506760 | tf_op jit(solution)/shard_map/ppermute | solution.py:441
  146.8 63.1 %collective-permute-start.41 = (bf16[4,8,24,768]{3,2,1,0:T(8,128)(2,1)}, bf16[4,8,24,768]{3,2,1,0:T(8,128)(2,1)}, u32[]{:S(2)}, u32[]{:S(2)}) collective-permute-start(bf16[4,8,24,768]{3,2,1,0:T(8,128)(2,1)} %pad_maximum_fusion.8.refs_0_), channel_id=1, source_target_pairs={{0,1},{1,0},{2,3},{3,2},{4,5},{5,4},{6,7},{7,6},{8,9},{9,8},{10,11... | collective-permute-start | bytes 3538952 | tf_op jit(solution)/shard_map/ppermute | solution.py:441
  163.1 65.1 %collective-permute-start.49 = (bf16[4,256,768]{2,1,0:T(8,128)(2,1)S(1)}, bf16[4,256,768]{2,1,0:T(8,128)(2,1)}, u32[]{:S(2)}, u32[]{:S(2)}) collective-permute-start(bf16[4,256,768]{2,1,0:T(8,128)(2,1)S(1)} %pad_maximum_fusion.5.refs_0_), channel_id=1, source_target_pairs={{0,1},{1,0},{2,3},{3,2},{4,5},{5,4},{6,7},{7,6},{8,9},{9,8},{10,11... | collective-permute-start | bytes 4718600 | tf_op jit(solution)/shard_map/ppermute | solution.py:441
  177.2 25.4 %collective-permute-start.37 = (bf16[3,4,24,768]{3,2,1,0:T(8,128)(2,1)}, bf16[3,4,24,768]{3,2,1,0:T(8,128)(2,1)}, u32[]{:S(2)}, u32[]{:S(2)}) collective-permute-start(bf16[3,4,24,768]{3,2,1,0:T(8,128)(2,1)} %collective-permute-done.34.refs_4_), channel_id=1, source_target_pairs={{0,1},{1,0},{2,3},{3,2},{4,5},{5,4},{6,7},{7,6},{8,9},{9,8},{10,11... | collective-permute-start | bytes 1327112 | tf_op jit(solution)/shard_map/ppermute | solution.py:441
  201.4 32.3 %collective-permute-start.51 = (bf16[6,512,384]{2,1,0:T(8,128)(2,1)}, bf16[6,512,384]{2,1,0:T(8,128)(2,1)S(1)}, u32[]{:S(2)}, u32[]{:S(2)}) collective-permute-start(bf16[6,512,384]{2,1,0:T(8,128)(2,1)} %get-tuple-element.195), channel_id=1, source_target_pairs={{0,1},{1,0},{2,3},{3,2},{4,5},{5,4},{6,7},{7,6},{8,9},{9,8},{10,11... | collective-permute-start | bytes 7077896 | tf_op jit(solution)/shard_map/ppermute | solution.py:441
  202.0 21.9 %collective-permute-start.39 = (bf16[3,8,24,768]{3,2,1,0:T(8,128)(2,1)}, bf16[3,8,24,768]{3,2,1,0:T(8,128)(2,1)}, u32[]{:S(2)}, u32[]{:S(2)}) collective-permute-start(bf16[3,8,24,768]{3,2,1,0:T(8,128)(2,1)} %pad_maximum_fusion.11.refs_1_), channel_id=1, source_target_pairs={{0,8},{1,9},{2,10},{3,11},{4,12},{5,13},{6,14},{7,15},{8,0},{9,1},... | collective-permute-start | bytes 2654216 | tf_op jit(solution)/shard_map/ppermute | solution.py:441
  202.5 21.7 %collective-permute-start.40 = (bf16[3,8,24,768]{3,2,1,0:T(8,128)(2,1)}, bf16[3,8,24,768]{3,2,1,0:T(8,128)(2,1)}, u32[]{:S(2)}, u32[]{:S(2)}) collective-permute-start(bf16[3,8,24,768]{3,2,1,0:T(8,128)(2,1)} %pad_maximum_fusion.11.refs_1_), channel_id=1, source_target_pairs={{0,16},{1,17},{2,18},{3,19},{4,20},{5,21},{6,22},{7,23},{8,24},{9,... | collective-permute-start | bytes 2654216 | tf_op jit(solution)/shard_map/ppermute | solution.py:441
  223.9 22.7 %collective-permute-start.38 = (bf16[2,512,768]{2,1,0:T(8,128)(2,1)}, bf16[2,512,768]{2,1,0:T(8,128)(2,1)}, u32[]{:S(2)}, u32[]{:S(2)}) collective-permute-start(bf16[2,512,768]{2,1,0:T(8,128)(2,1)} %get-tuple-element.184.ka_ref.va_ref), channel_id=1, source_target_pairs={{0,1},{1,0},{2,3},{3,2},{4,5},{5,4},{6,7},{7,6},{8,9},{9,8},{10,11... | collective-permute-start | bytes 4718600 | tf_op jit(solution)/shard_map/ppermute | solution.py:441
  224.5 22.1 %collective-permute-start.43 = (bf16[3,8,24,768]{3,2,1,0:T(8,128)(2,1)}, bf16[3,8,24,768]{3,2,1,0:T(8,128)(2,1)}, u32[]{:S(2)}, u32[]{:S(2)}) collective-permute-start(bf16[3,8,24,768]{3,2,1,0:T(8,128)(2,1)} %collective-permute-done.39.refs_2_), channel_id=1, source_target_pairs={{0,16},{1,17},{2,18},{3,19},{4,20},{5,21},{6,22},{7,23},{8,24},{9,... | collective-permute-start | bytes 2654216 | tf_op jit(solution)/shard_map/ppermute | solution.py:441
  316.0 24.3 %collective-permute-start.52 = (bf16[6,512,768]{2,1,0:T(8,128)(2,1)}, bf16[6,512,768]{2,1,0:T(8,128)(2,1)}, u32[]{:S(2)}, u32[]{:S(2)}) collective-permute-start(bf16[6,512,768]{2,1,0:T(8,128)(2,1)} %get-tuple-element.202.dz_ref.df_ref.da_ref), channel_id=1, source_target_pairs={{0,1},{1,0},{2,3},{3,2},{4,5},{5,4},{6,7},{7,6},{8,9},{9,8},{10,11... | collective-permute-start | bytes 14155784 | tf_op jit(solution)/shard_map/ppermute | solution.py:441
  316.3 24.1 %collective-permute-start.48 = (bf16[6,512,384]{2,1,0:T(8,128)(2,1)}, bf16[6,512,384]{2,1,0:T(8,128)(2,1)S(1)}, u32[]{:S(2)}, u32[]{:S(2)}) collective-permute-start(bf16[6,512,384]{2,1,0:T(8,128)(2,1)} %get-tuple-element.193), channel_id=1, source_target_pairs={{0,1},{1,0},{2,3},{3,2},{4,5},{5,4},{6,7},{7,6},{8,9},{9,8},{10,11... | collective-permute-start | bytes 7077896 | tf_op jit(solution)/shard_map/ppermute | solution.py:441
  317.1 22.8 %collective-permute-start.53 = (bf16[512,384]{1,0:T(8,128)(2,1)S(1)}, bf16[512,384]{1,0:T(8,128)(2,1)S(1)}, u32[]{:S(2)}, u32[]{:S(2)}) collective-permute-start(bf16[512,384]{1,0:T(8,128)(2,1)S(1)} %copy-done.59), channel_id=1, source_target_pairs={{0,1},{1,0},{2,3},{3,2},{4,5},{5,4},{6,7},{7,6},{8,9},{9,8},{10,11... | collective-permute-start | bytes 1179656 | tf_op jit(solution)/shard_map/ppermute | solution.py:441
  317.4 22.9 %collective-permute-start.54 = (bf16[512,768]{1,0:T(8,128)(2,1)S(1)}, bf16[512,768]{1,0:T(8,128)(2,1)}, u32[]{:S(2)}, u32[]{:S(2)}) collective-permute-start(bf16[512,768]{1,0:T(8,128)(2,1)S(1)} %copy-done.19), channel_id=1, source_target_pairs={{0,1},{1,0},{2,3},{3,2},{4,5},{5,4},{6,7},{7,6},{8,9},{9,8},{10,11... | collective-permute-start | bytes 2359304 | tf_op jit(solution)/shard_map/ppermute | solution.py:441
  317.7 39.6 %collective-permute-start.47 = (bf16[512,768]{1,0:T(8,128)(2,1)S(1)}, bf16[512,768]{1,0:T(8,128)(2,1)}, u32[]{:S(2)}, u32[]{:S(2)}) collective-permute-start(bf16[512,768]{1,0:T(8,128)(2,1)S(1)} %copy-done.19), channel_id=1, source_target_pairs={{2,4},{3,5},{4,2},{5,3},{10,12},{11,13},{12,10},{13,11},{18,20},{1... | collective-permute-start | bytes 2359304 | tf_op jit(solution)/shard_map/ppermute | solution.py:441
  340.0 18.9 %collective-permute-start.56 = (bf16[2,512,768]{2,1,0:T(8,128)(2,1)}, bf16[2,512,768]{2,1,0:T(8,128)(2,1)}, u32[]{:S(2)}, u32[]{:S(2)}) collective-permute-start(bf16[2,512,768]{2,1,0:T(8,128)(2,1)} %get-tuple-element.212), channel_id=1, source_target_pairs={{0,1},{1,0},{2,3},{3,2},{4,5},{5,4},{6,7},{7,6},{8,9},{9,8},{10,11... | collective-permute-start | bytes 4718600 | tf_op jit(solution)/shard_map/ppermute | solution.py:441
  354.2 43.7 %collective-permute-start.58 = (bf16[4,2,4,24,768]{4,3,2,1,0:T(8,128)(2,1)}, bf16[4,2,4,24,768]{4,3,2,1,0:T(8,128)(2,1)}, u32[]{:S(2)}, u32[]{:S(2)}) collective-permute-start(bf16[4,2,4,24,768]{4,3,2,1,0:T(8,128)(2,1)} %get-tuple-element.228), channel_id=1, source_target_pairs={{0,8},{1,9},{2,10},{3,11},{4,12},{5,13},{6,14},{7,15},{8,0},{9,1},... | collective-permute-start | bytes 3538952 | tf_op jit(solution)/shard_map/ppermute | solution.py:441
  355.8 42.1 %collective-permute-start.59 = (bf16[4,2,4,24,768]{4,3,2,1,0:T(8,128)(2,1)}, bf16[4,2,4,24,768]{4,3,2,1,0:T(8,128)(2,1)}, u32[]{:S(2)}, u32[]{:S(2)}) collective-permute-start(bf16[4,2,4,24,768]{4,3,2,1,0:T(8,128)(2,1)} %get-tuple-element.229), channel_id=1, source_target_pairs={{0,16},{1,17},{2,18},{3,19},{4,20},{5,21},{6,22},{7,23},{8,24},{9,... | collective-permute-start | bytes 3538952 | tf_op jit(solution)/shard_map/ppermute | solution.py:441
  390.5 41.8 %collective-permute-start.64 = (bf16[6,512,768]{2,1,0:T(8,128)(2,1)}, bf16[6,512,768]{2,1,0:T(8,128)(2,1)}, u32[]{:S(2)}, u32[]{:S(2)}) collective-permute-start(bf16[6,512,768]{2,1,0:T(8,128)(2,1)} %get-tuple-element.248.dz_ref.df_ref.da_ref), channel_id=1, source_target_pairs={{0,1},{1,0},{2,3},{3,2},{4,5},{5,4},{6,7},{7,6},{8,9},{9,8},{10,11... | collective-permute-start | bytes 14155784 | tf_op jit(solution)/shard_map/ppermute | solution.py:441
  391.0 32.3 %collective-permute-start.61 = (bf16[3,512,768]{2,1,0:T(8,128)(2,1)S(1)}, bf16[3,512,768]{2,1,0:T(8,128)(2,1)}, u32[]{:S(2)}, u32[]{:S(2)}) collective-permute-start(bf16[3,512,768]{2,1,0:T(8,128)(2,1)S(1)} %copy-done.11), channel_id=1, source_target_pairs={{0,1},{1,0},{2,3},{3,2},{4,5},{5,4},{6,7},{7,6},{8,9},{9,8},{10,11... | collective-permute-start | bytes 7077896 | tf_op jit(solution)/shard_map/ppermute | solution.py:441
  391.1 40.4 %collective-permute-start.57 = (bf16[256,768]{1,0:T(8,128)(2,1)S(1)}, bf16[256,768]{1,0:T(8,128)(2,1)}, u32[]{:S(2)}, u32[]{:S(2)}) collective-permute-start(bf16[256,768]{1,0:T(8,128)(2,1)S(1)} %slice.328), channel_id=1, source_target_pairs={{0,2},{1,3},{2,0},{3,1},{4,6},{5,7},{6,4},{7,5},{8,10},{9,11},{10,... | collective-permute-start | bytes 1179656 | tf_op jit(solution)/shard_map/ppermute | solution.py:441
  401.6 30.7 %collective-permute-start.65 = (bf16[2,2,2,4,24,768]{5,4,3,2,1,0:T(8,128)(2,1)}, bf16[2,2,2,4,24,768]{5,4,3,2,1,0:T(8,128)(2,1)S(1)}, u32[]{:S(2)}, u32[]{:S(2)}) collective-permute-start(bf16[2,2,2,4,24,768]{5,4,3,2,1,0:T(8,128)(2,1)} %get-tuple-element.233), channel_id=1, source_target_pairs={{2,4},{3,5},{4,2},{5,3},{10,12},{11,13},{12,10},{13,11},{18,20},{1... | collective-permute-start | bytes 3538952 | tf_op jit(solution)/shard_map/ppermute | solution.py:441
  423.1 29.5 %collective-permute-start.60 = (bf16[2,512,768]{2,1,0:T(8,128)(2,1)}, bf16[2,512,768]{2,1,0:T(8,128)(2,1)}, u32[]{:S(2)}, u32[]{:S(2)}) collective-permute-start(bf16[2,512,768]{2,1,0:T(8,128)(2,1)} %get-tuple-element.239), channel_id=1, source_target_pairs={{0,1},{1,0},{2,3},{3,2},{4,5},{5,4},{6,7},{7,6},{8,9},{9,8},{10,11... | collective-permute-start | bytes 4718600 | tf_op jit(solution)/shard_map/ppermute | solution.py:441
  445.3 28.1 %collective-permute-start.70 = (bf16[4,2,4,24,768]{4,3,2,1,0:T(8,128)(2,1)}, bf16[4,2,4,24,768]{4,3,2,1,0:T(8,128)(2,1)}, u32[]{:S(2)}, u32[]{:S(2)}) collective-permute-start(bf16[4,2,4,24,768]{4,3,2,1,0:T(8,128)(2,1)} %get-tuple-element.264), channel_id=1, source_target_pairs={{0,16},{1,17},{2,18},{3,19},{4,20},{5,21},{6,22},{7,23},{8,24},{9,... | collective-permute-start | bytes 3538952 | tf_op jit(solution)/shard_map/ppermute | solution.py:441
  446.6 27.7 %collective-permute-start.71 = (bf16[4,2,4,24,768]{4,3,2,1,0:T(8,128)(2,1)}, bf16[4,2,4,24,768]{4,3,2,1,0:T(8,128)(2,1)}, u32[]{:S(2)}, u32[]{:S(2)}) collective-permute-start(bf16[4,2,4,24,768]{4,3,2,1,0:T(8,128)(2,1)} %get-tuple-element.265), channel_id=1, source_target_pairs={{0,8},{1,9},{2,10},{3,11},{4,12},{5,13},{6,14},{7,15},{8,0},{9,1},... | collective-permute-start | bytes 3538952 | tf_op jit(solution)/shard_map/ppermute | solution.py:441
  461.9 27.9 %collective-permute-start.66 = (bf16[512,768]{1,0:T(8,128)(2,1)}, bf16[512,768]{1,0:T(8,128)(2,1)}, u32[]{:S(2)}, u32[]{:S(2)}) collective-permute-start(bf16[512,768]{1,0:T(8,128)(2,1)} %get-tuple-element.256), channel_id=1, source_target_pairs={{2,4},{3,5},{4,2},{5,3},{10,12},{11,13},{12,10},{13,11},{18,20},{1... | collective-permute-start | bytes 2359304 | tf_op jit(solution)/shard_map/ppermute | solution.py:441
  487.6 21.2 %collective-permute-start.77 = (bf16[2,2,6,24,768]{4,3,2,1,0:T(8,128)(2,1)S(1)}, bf16[2,2,6,24,768]{4,3,2,1,0:T(8,128)(2,1)S(1)}, u32[]{:S(2)}, u32[]{:S(2)}) collective-permute-start(bf16[2,2,6,24,768]{4,3,2,1,0:T(8,128)(2,1)S(1)} %fusion.7), channel_id=1, source_target_pairs={{0,2},{1,3},{2,0},{3,1},{4,6},{5,7},{6,4},{7,5},{8,10},{9,11},{10,... | collective-permute-start | bytes 2654216 | tf_op jit(solution)/shard_map/ppermute | solution.py:441
  489.9 35.9 %collective-permute-start.75 = (bf16[2,2,2,4,24,768]{5,4,3,2,1,0:T(8,128)(2,1)}, bf16[2,2,2,4,24,768]{5,4,3,2,1,0:T(8,128)(2,1)}, u32[]{:S(2)}, u32[]{:S(2)}) collective-permute-start(bf16[2,2,2,4,24,768]{5,4,3,2,1,0:T(8,128)(2,1)} %get-tuple-element.269), channel_id=1, source_target_pairs={{2,4},{3,5},{4,2},{5,3},{10,12},{11,13},{12,10},{13,11},{18,20},{1... | collective-permute-start | bytes 3538952 | tf_op jit(solution)/shard_map/ppermute | solution.py:441
  493.5 21.5 %collective-permute-start.81 = (bf16[4,2,2,24,768]{4,3,2,1,0:T(8,128)(2,1)}, bf16[4,2,2,24,768]{4,3,2,1,0:T(8,128)(2,1)}, u32[]{:S(2)}, u32[]{:S(2)}) collective-permute-start(bf16[4,2,2,24,768]{4,3,2,1,0:T(8,128)(2,1)} %get-tuple-element.278), channel_id=1, source_target_pairs={{0,8},{1,9},{2,10},{3,11},{4,12},{5,13},{6,14},{7,15},{8,0},{9,1},... | collective-permute-start | bytes 1769480 | tf_op jit(solution)/shard_map/ppermute | solution.py:441
  494.1 21.6 %collective-permute-start.82 = (bf16[4,2,2,24,768]{4,3,2,1,0:T(8,128)(2,1)}, bf16[4,2,2,24,768]{4,3,2,1,0:T(8,128)(2,1)}, u32[]{:S(2)}, u32[]{:S(2)}) collective-permute-start(bf16[4,2,2,24,768]{4,3,2,1,0:T(8,128)(2,1)} %get-tuple-element.279), channel_id=1, source_target_pairs={{0,16},{1,17},{2,18},{3,19},{4,20},{5,21},{6,22},{7,23},{8,24},{9,... | collective-permute-start | bytes 1769480 | tf_op jit(solution)/shard_map/ppermute | solution.py:441
  515.1 41.9 %collective-permute-start.74 = (bf16[256,768]{1,0:T(8,128)(2,1)}, bf16[256,768]{1,0:T(8,128)(2,1)}, u32[]{:S(2)}, u32[]{:S(2)}) collective-permute-start(bf16[256,768]{1,0:T(8,128)(2,1)} %slice.332), channel_id=1, source_target_pairs={{0,2},{1,3},{2,0},{3,1},{4,6},{5,7},{6,4},{7,5},{8,10},{9,11},{10,... | collective-permute-start | bytes 1179656 | tf_op jit(solution)/shard_map/ppermute | solution.py:441
  533.7 19.6 %collective-permute-start.83 = (bf16[2,2,4,24,768]{4,3,2,1,0:T(8,128)(2,1)}, bf16[2,2,4,24,768]{4,3,2,1,0:T(8,128)(2,1)}, u32[]{:S(2)}, u32[]{:S(2)}) collective-permute-start(bf16[2,2,4,24,768]{4,3,2,1,0:T(8,128)(2,1)} %fusion.8), channel_id=1, source_target_pairs={{0,2},{1,3},{2,0},{3,1},{4,6},{5,7},{6,4},{7,5},{8,10},{9,11},{10,... | collective-permute-start | bytes 1769480 | tf_op jit(solution)/shard_map/ppermute | solution.py:441
  539.3 19.6 %collective-permute-start.88 = (bf16[2,2,2,24,768]{4,3,2,1,0:T(8,128)(2,1)}, bf16[2,2,2,24,768]{4,3,2,1,0:T(8,128)(2,1)}, u32[]{:S(2)}, u32[]{:S(2)}) collective-permute-start(bf16[2,2,2,24,768]{4,3,2,1,0:T(8,128)(2,1)} %fusion.18), channel_id=1, source_target_pairs={{0,2},{1,3},{2,0},{3,1},{4,6},{5,7},{6,4},{7,5},{8,10},{9,11},{10,... | collective-permute-start | bytes 884744 | tf_op jit(solution)/shard_map/ppermute | solution.py:441
  542.9 26.9 %collective-permute-start.97 = (f32[2,1152]{1,0:T(2,128)S(1)}, f32[2,1152]{1,0:T(2,128)}, u32[]{:S(2)}, u32[]{:S(2)}) collective-permute-start(f32[2,1152]{1,0:T(2,128)S(1)} %select_bitcast_fusion), channel_id=1, source_target_pairs={{0,2},{1,3},{2,0},{3,1},{4,6},{5,7},{6,4},{7,5},{8,10},{9,11},{10,... | collective-permute-start | bytes 27656 | tf_op jit(solution)/shard_map/ppermute | solution.py:441
  (116 other events, 1024.4 us)

commit v5 on v4

--- a/solution.py
+++ b/solution.py
@@ -434,7 +434,7 @@
 TO_Y = routes(2, 0, ALL)
 TO_TWIN = routes(0, 1, ALL)
 TO_SIDE = routes(0, 2, ALL)
-TO_MID = routes(0, 6, CORE)
+TO_MID = routes(0, 6, CORE) + routes(0, 1, EDGE)
 
 
 def send(value, route):
@@ -545,7 +545,7 @@
         ),
         out_shape=shaped(shape),
         compiler_params=LIMIT,
-        cost_estimate=cost(6),
+        cost_estimate=cost(0.3),
         name="assemble",
     )(where, *parts)
     return result.reshape(4, 32 * UNIT, width)
@@ -559,14 +559,23 @@
     return list(lax.optimization_barrier(tuple(values) + others)[: len(values)])
 
 
-def spread(own, first, over_x, over_y, x_last):
-    others = [send(own, TO_TWIN), send(first, TO_TWIN)]
-    over_x, over_y = after([over_x, over_y], *others)
-    over_d = send(over_y, TO_X) if x_last else send(over_x, TO_Y)
-    others += [send(over_x, TO_TWIN), send(over_y, TO_TWIN)]
-    over_d = after([over_d], *others)[0]
-    others.append(send(over_d, TO_TWIN))
-    return (own, first, over_x, over_y, over_d) + tuple(others)
+class Spread:
+    def __init__(self, own, first, x_last):
+        self.own, self.first, self.x_last = own, first, x_last
+        self.over = [send(first, TO_X), send(first, TO_Y)]
+        self.twins = [send(own, TO_TWIN), send(first, TO_TWIN)]
+
+    def turn(self, *others):
+        self.over_x, self.over_y = after(self.over, *self.twins, *others)
+        last = self.over_y if self.x_last else self.over_x
+        self.over_d = send(last, TO_X if self.x_last else TO_Y)
+        self.twins += [send(self.over_x, TO_TWIN), send(self.over_y, TO_TWIN)]
+        return self.over_x
+
+    def parts(self, *others):
+        over_d = after([self.over_d], *self.twins, *others)[0]
+        mine = (self.own, self.first, self.over_x, self.over_y, over_d)
+        return mine + tuple(self.twins) + (send(over_d, TO_TWIN),)
 
 
 def project_kernel(h_ref, w_ref, vec_ref, sel_ref, q_ref, kv_ref, mine_ref, theirs_ref):
@@ -612,7 +621,7 @@
             shaped((rows, width // 2)),
         ],
         compiler_params=LIMIT,
-        cost_estimate=cost(7),
+        cost_estimate=cost(0.3),
         name="project",
     )(hidden, weight, vec, sel)
 
@@ -680,7 +689,7 @@
         ],
         scratch_shapes=[pltpu.VMEM((2 * half, half), jnp.float32)],
         compiler_params=LIMIT,
-        cost_estimate=cost(15),
+        cost_estimate=cost(0.3),
         name="attend_forward",
     )(queries, kv, kv_twin, kv, kv_twin, code, member)
 
@@ -872,7 +881,7 @@
             pltpu.VMEM((rows, width), jnp.float32),
         ],
         compiler_params=LIMIT,
-        cost_estimate=cost(23),
+        cost_estimate=cost(0.3),
         name="post",
     )(where, attended, hidden, front, up, down, vec, sel)
 
@@ -1213,15 +1222,46 @@
         return self.sums[0]
 
     def finish(self, *others):
-        results = []
-        for piece, got, first in zip(self.sums, after(self.got, *others), self.firsts):
-            axis = 1 if first else 0
-            bit = self.bits[0] if first else self.bits[1]
-            joined = jnp.where(
-                bit == 0, jnp.stack([piece, got], axis), jnp.stack([got, piece], axis)
-            )
-            results.append(wide(joined).reshape((4,) + piece.shape[1:]))
-        return results
+        return list(zip(self.sums, after(self.got, *others)))
+
+
+def unpack_kernel(plan, bit_ref, *refs):
+    outs = refs[-4:]
+    width = outs[1].shape[1]
+    for index, (x_first, units) in enumerate(plan):
+        piece, got = refs[2 * index], refs[2 * index + 1]
+        bit = bit_ref[0 if x_first else 1]
+        for other in range(2):
+            for side in range(2):
+                rep = (other * 2 + side) if x_first else (side * 2 + other)
+                for unit, (target, place) in enumerate(units):
+                    value = wide(jnp.where(bit == side, piece[other, unit], got[other, unit]))
+                    if target < 3:
+                        rows = slice(rep * UNIT, (rep + 1) * UNIT)
+                        outs[target][rows, place * width : (place + 1) * width] = value
+                    else:
+                        base = (rep * 4 + place) * UNIT
+                        outs[target][base : base + UNIT, :] = value
+
+
+def unpack(bits, pairs, plan, layer, layers, before):
+    width = pairs[0][0].shape[3]
+    shapes = [(4 * UNIT, 3 * width), (4 * UNIT, width), (4 * UNIT, 4 * width), (16 * UNIT, width)]
+    arrays = [item for pair in pairs for item in pair]
+    first = 1 + len(arrays)
+    return pl.pallas_call(
+        functools.partial(unpack_kernel, plan),
+        grid=(1,),
+        in_specs=[SMEM]
+        + [fixed(*item.shape) for item in arrays]
+        + [pl.BlockSpec(memory_space=pl.ANY) for _ in before],
+        out_specs=[pl.BlockSpec((None,) + shape, lambda step: (layer, 0, 0)) for shape in shapes],
+        out_shape=[shaped((layers,) + shape, jnp.float32) for shape in shapes],
+        input_output_aliases={first + index: index for index in range(len(before))},
+        compiler_params=LIMIT,
+        cost_estimate=cost(3),
+        name="unpack",
+    )(bits, *arrays, *before)
 
 
 def body_fast(
@@ -1276,63 +1316,41 @@
     filler = jnp.zeros((7 - extra, width), jnp.bfloat16)
     rows_in = jnp.concatenate([inputs, tail, table, filler], axis=0)
 
+    def group(items, begin, end):
+        return jnp.stack([units_of(item[begin:end]) for item in items])
+
     front_zero = pack_front(entry_weight[0], exit_weight[0])
     piece = own_piece(front_zero)
     near = send(piece, TO_SIDE)
     middle = send(piece, TO_MID)
-    near_in = send(rows_in, TO_SIDE)
-    middle_in = send(rows_in, TO_MID)
+    feed_zero = pack_feed(expand_weight[0], shrink_weight[0])
+    in_rows = rows_in.shape[0]
     far = send(near, TO_MID)
     first = jnp.stack([units_of(item) for item in (near, middle, far)])
-    over_x, over_y = send(first, TO_X), send(first, TO_Y)
-    expand_late, shrink_late, twin_late, near_in = after(
-        [expand_weight[0], shrink_weight[0], twin, near_in], first
-    )
-    far_in = send(near_in, TO_MID)
-    parts = spread(front_zero, first, over_x, over_y, False)
-
-    feed_zero = pack_feed(expand_late, shrink_late)
-    piece = tie(own_piece(feed_zero), parts[5], parts[6])
-    near = send(piece, TO_SIDE)
-    middle = send(piece, TO_MID)
-    mine = jnp.stack([rows_in, near_in, middle_in, far_in])
-    theirs = send(mine, TO_TWIN)
-    far = send(near, TO_MID)
-    first = jnp.stack([units_of(item) for item in (near, middle, far)])
-    first = tie(first, parts[7], parts[8], theirs)
-    over_x, over_y = send(first, TO_X), send(first, TO_Y)
-    feed_parts = spread(feed_zero, first, over_x, over_y, True)
-    fronts = [assemble(where, parts, 0, False)]
+    front_spread = Spread(front_zero, first, False)
+    rows_late, twin_late, lengths = after([rows_in, twin, lengths], first)
+    second = jnp.concatenate([rows_late, own_piece(feed_zero)], axis=0)
+    second_near = send(second, TO_SIDE)
+    second_middle = send(second, TO_MID)
+    second_far = send(second_near, TO_MID)
 
     entry_late, exit_late, expand_late, shrink_late, cotangent_late = after(
         [entry_weight[1], exit_weight[1], expand_weight[1], shrink_weight[1], cotangent], first
     )
     front_one = pack_front(entry_late, exit_late)
     feed_one = pack_feed(expand_late, shrink_late)
-    piece = jnp.concatenate([own_piece(front_one), own_piece(feed_one), cotangent_late], axis=0)
-    piece = tie(piece, feed_parts[5], feed_parts[6])
-    near = send(piece, TO_SIDE)
-    middle = send(piece, TO_MID)
-    far = send(near, TO_MID)
-    four = (piece, near, middle, far)
-    parts = feed_parts
-    ups = [assemble(where, parts, 0, False)]
-    downs = [assemble(where, parts, 4, True)]
-
-    first_split, split = 4 * UNIT, 12 * UNIT
-    first = jnp.stack([units_of(item[:first_split]) for item in four[1:]])
-    first = tie(first, parts[7], parts[8])
-    over_x, over_y = send(first, TO_X), send(first, TO_Y)
-    parts = spread(front_one, first, over_x, over_y, True)
-    fronts.append(assemble(where, parts, 0, False))
-    first = jnp.stack([units_of(item[first_split:split]) for item in four[1:]])
-    first = tie(first, parts[7], parts[8])
-    over_x, over_y = send(first, TO_X), send(first, TO_Y)
-    parts = spread(feed_one, first, over_x, over_y, False)
-    ups.append(assemble(where, parts, 0, False))
-    downs.append(assemble(where, parts, 4, True))
-    cotangent_mine = jnp.stack([item[split:] for item in four])
-    cotangent_theirs = send(cotangent_mine, TO_TWIN)
+    third = jnp.concatenate([own_piece(front_one), own_piece(feed_one), cotangent_late], axis=0)
+    ready = front_spread.turn()
+
+    second_middle, second_far = after([second_middle, second_far], ready)
+    four = (second, second_near, second_middle, second_far)
+    mine = jnp.stack([item[:in_rows] for item in four])
+    theirs = send(mine, TO_TWIN)
+    feed_spread = Spread(feed_zero, tie(group(four[1:], in_rows, in_rows + 8 * UNIT), ready), True)
+    third = tie(third, ready)
+    third_near = send(third, TO_SIDE)
+    third_middle = send(third, TO_MID)
+    fronts = [assemble(where, front_spread.parts(feed_spread.first, mine, third), 0, False)]
 
     header = absolute(tuple(mine[:, rows:]), tuple(theirs[:, rows:]))
     header = header.reshape(8, 8, width)
@@ -1381,8 +1399,9 @@
     ).astype(jnp.int32)
     source_ids = (bases[:, None] + local[None, :]).reshape(8, 1, rows)
     want_in = dealt_near[0].reshape(core_rows, 1)
-    hidden_low = gather_rows((mine, theirs), source_ids, want_in, 5)
-    upstream = gather_rows((cotangent_mine, cotangent_theirs), source_ids, want_in, 5)
+    theirs, third_near = after([theirs, third_near], fronts[0])
+    third_far = send(third_near, TO_MID)
+    hidden_low = gather_rows((mine, tie(theirs, third_near)), source_ids, want_in, 0.3)
 
     result_ids = jnp.stack([dealt_near[0], dealt_far[0], dealt_near[1], dealt_far[1]]).reshape(
         4, 1, core_rows
@@ -1395,18 +1414,61 @@
         return found, send(found[rows:], TO_SIDE)
 
     saved = []
+    def begin(layer):
+        queries, kv, xm, xt = project(hidden_low, fronts[layer], vector_all[layer], sel)
+        return queries, kv, send(kv, TO_TWIN), xm, send(xt, TO_TWIN)
+
+    def attention(queries, kv, kv_twin):
+        return attend_fast(queries, kv, kv_twin, code_half, member_own)
+
+    def complete(layer, attended):
+        results = post(
+            where, attended, hidden, fronts[layer], ups[layer], downs[layer],
+            vector_all[layer], sel,
+        )
+        return results, send(results[8], TO_TWIN)
+
+    def record(start, middle, results, others):
+        queries, kv, kv_twin, xm, xo = start
+        saved.append(
+            (queries, kv, kv_twin) + tuple(middle[1:]) + tuple(results[2:7])
+            + (xm, xo, results[7], others)
+        )
+
     hidden = hidden_low
-    for layer in range(layers):
-        vec = vector_all[layer]
-        queries, kv, xm, xt = project(hidden_low, fronts[layer], vec, sel)
-        kv_twin = send(kv, TO_TWIN)
-        xo = send(xt, TO_TWIN)
-        attended, ot, lse = attend_fast(queries, kv, kv_twin, code_half, member_own)
-        hidden, hidden_low, n1, t1, n2, t2, slope, mine, theirs = post(
-            where, attended, hidden, fronts[layer], ups[layer], downs[layer], vec, sel
-        )
-        others = send(theirs, TO_TWIN)
-        saved.append((queries, kv, kv_twin, ot, lse, n1, t1, n2, t2, slope, xm, xo, mine, others))
+    ready = feed_spread.turn(fronts[0])
+    hidden_low, third_middle = after([hidden_low, third_middle], ready)
+    hidden_low = tie(hidden_low, third_middle)
+    start = begin(0)
+    middle = attention(*start[:3])
+    parts = feed_spread.parts(middle[0])
+    third_far = tie(third_far, middle[0])
+    four = (third, third_near, third_middle, third_far)
+    split = 12 * UNIT
+    front_spread = Spread(front_one, group(four[1:], 0, 4 * UNIT), True)
+    cotangent_mine = jnp.stack([item[split:] for item in four])
+    ups = [assemble(where, parts, 0, False)]
+    downs = [assemble(where, parts, 4, True)]
+    ready = front_spread.turn(ups[0], downs[0])
+    feed_spread = Spread(feed_one, tie(group(four[1:], 4 * UNIT, split), ready), False)
+    cotangent_theirs = send(cotangent_mine, TO_TWIN)
+    held = [feed_spread.first, cotangent_theirs] + front_spread.twins + feed_spread.twins
+    results, others = complete(0, tie(middle[0], ready, *held))
+    hidden, hidden_low = results[:2]
+    record(start, middle, results, others)
+    ready = feed_spread.turn(hidden_low)
+    fronts.append(assemble(where, front_spread.parts(ready), 0, False))
+    start = begin(1)
+    upstream = gather_rows(
+        (cotangent_mine, tie(cotangent_theirs, start[0])), source_ids, want_in, 0.3
+    )
+    middle = attention(tie(start[0], upstream), start[1], start[2])
+    parts = feed_spread.parts(middle[0])
+    ups.append(assemble(where, parts, 0, False))
+    downs.append(assemble(where, parts, 4, True))
+    results, others = complete(1, middle[0])
+    hidden, hidden_low = results[:2]
+    record(start, middle, results, others)
     result_mid = send(hidden_low, TO_MID)
     result_twin = send(hidden_low, TO_TWIN)
 
@@ -1500,35 +1562,30 @@
     vector_keep = jnp.where(is_low, vector_stage[0:2], vector_stage[2:4])
     vector_mid = send(vector_give, TO_MID)
     ready = feed_a.outward(vector_give)
-    done_b = feed_b.finish(ready)
-    up_b, down_b = (item[:, :4] for item in done_b)
-    front_grad_b = jnp.concatenate([item[:, 4:] for item in done_b], axis=1)
-
-    ready = front_a.outward(up_b, down_b, front_grad_b)
+    ups_at = tuple((2, place) for place in range(4))
+    downs_at = tuple((3, place) for place in range(4))
+    early_at, late_at = ((0, 0), (0, 1)), ((0, 2), (1, 0))
+    plan = ((True, ups_at + early_at), (False, downs_at + late_at))
+
+    ready = front_a.outward(ready)
+    grads = unpack(bit_words, feed_b.finish(ready), plan, 1, layers, ())
     vector_stage = vector_keep + tie(vector_mid, ready)
     vector_outer = jnp.where(is_low, vector_stage[0], vector_stage[1])
     vector_inner = jnp.where(is_low, vector_stage[1], vector_stage[0])
     vector_side = send(vector_outer, TO_SIDE)
-    ready = feed_a.turn(vector_outer)
+    ready = feed_a.turn(vector_outer, grads[1])
     output = jnp.where(is_core, found[:rows], output_side)
     input_grad = wide(jnp.where(is_core, found_in[:rows], tie(input_side, ready)))
 
     ready = front_a.turn(ready)
     ready_two = feed_a.share(ready)
     ready = front_a.share(ready_two)
-    up_a, down_a = feed_a.finish(ready)
-    front_grad_a = jnp.concatenate(front_a.finish(up_a, down_a), axis=1)
+    pairs = feed_a.finish(ready) + front_a.finish(ready)
+    plan = ((False, ups_at), (True, downs_at), (True, early_at), (False, late_at))
+    entry_grad, exit_grad, expand_grad, shrink_grad = unpack(
+        bit_words, pairs, plan, 0, layers, grads
+    )
     vector_grad = jnp.where(is_core, vector_inner, tie(vector_side, ready))
-    grads = [(front_grad_a, up_a, down_a), (front_grad_b, up_b, down_b)]
-
-    def columns(units):
-        count = units.shape[1]
-        return units.transpose(0, 2, 1, 3).reshape(4 * UNIT, count * width)
-
-    entry_grad = jnp.stack([columns(item[0][:, 0:3]) for item in grads])
-    exit_grad = jnp.stack([columns(item[0][:, 3:4]) for item in grads])
-    expand_grad = jnp.stack([columns(item[1]) for item in grads])
-    shrink_grad = jnp.stack([item[2].reshape(16 * UNIT, width) for item in grads])
     return (output, input_grad, entry_grad, exit_grad, expand_grad, shrink_grad, vector_grad)
 
 

time: 600 us -> 561 us (0.935); the launches traced: 589 us -> 556 us
  starting transfers between devices: 108 us -> 80.2 us
  other arithmetic: 46.5 us -> 31.7 us
  Pallas kernels: 295 us -> 302 us
    ppermute x98 -> x95, starting transfers between devices: 108 us -> 80.2 us  [send(): return lax.ppermute(value, BOTH, route)]
    another operation x12 -> x8, other arithmetic: 11.7 us -> 1.82 us  [the longest x1 1.36 us: body_fast(): mine = jnp.stack([item[:in_rows] for item in four])]
    another operation x4 -> x2, local copies, waits for them, and re-layouts: 8.58 us -> 2.08 us  [body_fast(): mine = jnp.stack([item[:in_rows] for item in four])]
    pallas_call x0 -> x2, Pallas kernels: none -> 6.5 us  [unpack(): pl.pallas_call(functools.partial(unpack_kernel, plan), grid=(1,), in_spec...]
    ppermute x98 -> x95, waiting for transfers between devices: 81.5 us -> 86.4 us  [send(): return lax.ppermute(value, BOTH, route)]
  transfers between devices with their start and end apart: 98 -> 95, of which waited for: 20 -> 23; matrix products, arithmetic and copies ran while one was open for 13% -> 12% of each run, Pallas kernels for 41% -> 41%
where the time goes in v5:
time: 561 us; the launch traced here: 556 us
  Pallas kernels  302 us (54%)
  waiting for transfers between devices  86.4 us (15%)
  starting transfers between devices  80.2 us (14%)
  local copies, waits for them, and re-layouts  49.6 us (9%)
  other arithmetic  31.7 us (6%)
  between operations  6.59 us (1%)
    ppermute x95, waiting for transfers between devices, send(): return lax.ppermute(value, BOTH, route)  86.4 us
    ppermute x95, starting transfers between devices, send(): return lax.ppermute(value, BOTH, route)  80.2 us
    pallas_call x2, Pallas kernels, post(): pl.pallas_call(post_kernel, grid=(4,), in_specs=[SMEM, full, full, unit_s...  48.7 us
    pallas_call x2, Pallas kernels, attend_back_fast(): pl.pallas_call(attend_back_kernel, grid=(width // 128,), in_specs=[column...  41.1 us
    pallas_call x6, Pallas kernels, assemble(): pl.pallas_call(assemble_kernel, grid_spec=pltpu.PrefetchScalarGridSpec(nu...  34.9 us
    pallas_call x2, Pallas kernels, post_back(): pl.pallas_call(post_back_kernel, grid=(4,), in_specs=[full, full, thin, f...  33.4 us
    pallas_call x2, Pallas kernels, attend_fast(): pl.pallas_call(attend_kernel, grid=(width // 128,), in_specs=[column, key...  31.3 us
    pallas_call x2, Pallas kernels, feed_grad(): pl.pallas_call(functools.partial(feed_grad_kernel, x_first), grid=(8,), i...  25.5 us
  transfers between devices with their start and end apart: 95, of which 23 were waited for; matrix products, arithmetic and copies ran while one was open for 12% of the time, Pallas kernels for 41%

profile of v5, /device:TPU:0, one launch (start us, length us, event | category | flops | bytes accessed | tf_op | source)
XLA Modules:
  0.0 556.1 jit_solution(9707744637146669792)
XLA Ops:
  3.3 3.1 collective-permute-start
  7.9 2.6 slice_bitcast_fusion.1
  17.9 7.5 %collective-permute-start.3 = (bf16[456,768]{1,0:T(8,128)(2,1)}, bf16[456,768]{1,0:T(8,128)(2,1)}, u32[]{:S(2)}, u32[]{:S(2)}) collective-permute-start(bf16[456,768]{1,0:T(8,128)(2,1)} %pad_maximum_fusion.11), channel_id=1, source_target_pairs={{0,2},{1,3},{2,0},{3,1},{4,6},{5,7},{6,4},{7,5},{8,10},{9,11},{10,... | collective-permute-start | bytes 2101256 | tf_op jit(solution)/shard_map/ppermute | solution.py:441
  44.0 8.9 %collective-permute-done.7.refs_3_ = bf16[3,4,24,768]{3,2,1,0:T(8,128)(2,1)S(1)} collective-permute-done((bf16[3,4,24,768]{3,2,1,0:T(8,128)(2,1)}, bf16[3,4,24,768]{3,2,1,0:T(8,128)(2,1)S(1)}, u32[]{:S(2)}, u32[]{:S(2)}) %collective-permute-start.7) | collective-permute-done | bytes 442400 | tf_op jit(solution)/shard_map/ppermute | solution.py:441
  60.7 5.0 collective-permute-done.12.refs_4_
  70.2 5.8 %assemble.6 = bf16[4,4,2,4,24,768]{5,4,3,2,1,0:T(8,128)(2,1)} custom-call(s32[3]{0:T(128)} %pad_add_fusion.3.where_ref, bf16[4,4,24,768]{3,2,1,0:T(8,128)(2,1)} %pad_maximum_fusion.9.refs_0_, bf16[3,4,24,768]{3,2,1,0:T(8,128)(2,1)} %pad_maximum_fusion.12.refs_1_, bf16[3,4,24,768]{3,2,1,0:T(8,128)(2,1)} %collective-permute-done.6.refs_2_, ...), custom_call_target="tpu_custom_call" | custom-call | flops 300000000 | bytes 300000 | tf_op jit(solution)/shard_map/assemble/pallas_call | solution.py:538
  76.3 13.2 %collective-permute-done.17.refs_2_ = bf16[3,8,24,768]{3,2,1,0:T(8,128)(2,1)} collective-permute-done((bf16[3,8,24,768]{3,2,1,0:T(8,128)(2,1)S(1)}, bf16[3,8,24,768]{3,2,1,0:T(8,128)(2,1)}, u32[]{:S(2)}, u32[]{:S(2)}) %collective-permute-start.17) | collective-permute-done | bytes 884768 | tf_op jit(solution)/shard_map/ppermute | solution.py:441
  91.6 5.2 collective-permute-done.11
  99.0 4.7 gather_rows.4.h_ref
  105.3 7.4 %project.2 = (bf16[512,768]{1,0:T(8,128)(2,1)}, bf16[2,512,768]{2,1,0:T(8,128)(2,1)}, bf16[512,384]{1,0:T(8,128)(2,1)}, bf16[512,384]{1,0:T(8,128)(2,1)}) custom-call(bf16[512,768]{1,0:T(8,128)(2,1)} %gather_rows.4.h_ref, bf16[4,768,768]{2,1,0:T(8,128)(2,1)} %bitcast.191, f32[12,768]{1,0:T(8,128)} %squeeze.50.vec_ref, bf16[2,768,384]{2,1,0:T(8,128)(2,1)} %fusion.sel_ref), custom_call_target="tpu_custom_call" | custom-call | flops 300000000 | bytes 300000 | tf_op jit(solution)/shard_map/project/pallas_call | solution.py:602
  122.1 15.4 %attend_forward.2 = (bf16[512,768]{1,0:T(8,128)(2,1)}, f32[768,512]{1,0:T(8,128)}, f32[6,2,512]{2,1,0:T(2,128)}) custom-call(bf16[512,768]{1,0:T(8,128)(2,1)} %get-tuple-element.196.q_ref, bf16[2,512,768]{2,1,0:T(8,128)(2,1)} %get-tuple-element.197.ka_ref.va_ref, bf16[2,512,768]{2,1,0:T(8,128)(2,1)} %copy-done.4, ...), custom_call_target="tpu_custom_call" | custom-call | flops 300000000 | bytes 300000 | tf_op jit(solution)/shard_map/attend_forward/pallas_call | solution.py:680
  146.6 5.8 %assemble.8 = bf16[4,2,4,4,24,768]{5,4,3,2,1,0:T(8,128)(2,1)} custom-call(s32[3]{0:T(128)} %pad_add_fusion.3.where_ref, bf16[4,8,24,768]{3,2,1,0:T(8,128)(2,1)} %copy-done, bf16[3,8,24,768]{3,2,1,0:T(8,128)(2,1)} %copy-done.2, bf16[3,8,24,768]{3,2,1,0:T(8,128)(2,1)} %collective-permute-done.17.refs_2_, ...), custom_call_target="tpu_custom_call" | custom-call | flops 300000000 | bytes 300000 | tf_op jit(solution)/shard_map/assemble/pallas_call | solution.py:538
  152.5 6.0 %assemble.7 = bf16[4,4,2,4,24,768]{5,4,3,2,1,0:T(8,128)(2,1)} custom-call(s32[3]{0:T(128)} %pad_add_fusion.3.where_ref, bf16[4,8,24,768]{3,2,1,0:T(8,128)(2,1)} %copy-done, bf16[3,8,24,768]{3,2,1,0:T(8,128)(2,1)} %copy-done.2, bf16[3,8,24,768]{3,2,1,0:T(8,128)(2,1)} %collective-permute-done.17.refs_2_, ...), custom_call_target="tpu_custom_call" | custom-call | flops 300000000 | bytes 300000 | tf_op jit(solution)/shard_map/assemble/pallas_call | solution.py:538
  166.9 24.2 %post.2 = (f32[512,768]{1,0:T(8,128)}, bf16[512,768]{1,0:T(8,128)(2,1)}, f32[512,768]{1,0:T(8,128)}, f32[512,1]{1,0:T(8,128)}, f32[512,768]{1,0:T(8,128)}, /*ind...) custom-call(s32[3]{0:T(128)} %pad_add_fusion.3.where_ref, ...), custom_call_target="tpu_custom_call" | custom-call | flops 300000000 | bytes 300000 | tf_op jit(solution)/shard_map/post/pallas_call | solution.py:859
  195.7 5.8 %assemble.9 = bf16[4,4,2,4,24,768]{5,4,3,2,1,0:T(8,128)(2,1)} custom-call(s32[3]{0:T(128)} %pad_add_fusion.3.where_ref, bf16[4,4,24,768]{3,2,1,0:T(8,128)(2,1)} %pad_maximum_fusion.10.refs_0_, bf16[3,4,24,768]{3,2,1,0:T(8,128)(2,1)} %copy-done.23, bf16[3,4,24,768]{3,2,1,0:T(8,128)(2,1)} %collective-permute-done.23.refs_2_, ...), custom_call_target="tpu_custom_call" | custom-call | flops 300000000 | bytes 300000 | tf_op jit(solution)/shard_map/assemble/pallas_call | solution.py:538
  201.5 7.4 %project.3 = (bf16[512,768]{1,0:T(8,128)(2,1)}, bf16[2,512,768]{2,1,0:T(8,128)(2,1)}, bf16[512,384]{1,0:T(8,128)(2,1)}, bf16[512,384]{1,0:T(8,128)(2,1)}) custom-call(bf16[512,768]{1,0:T(8,128)(2,1)} %get-tuple-element.206.h_ref, bf16[4,768,768]{2,1,0:T(8,128)(2,1)} %bitcast.195, f32[12,768]{1,0:T(8,128)} %squeeze.51.vec_ref, bf16[2,768,384]{2,1,0:T(8,128)(2,1)} %fusion.sel_ref), custom_call_target="tpu_custom_call" | custom-call | flops 300000000 | bytes 300000 | tf_op jit(solution)/shard_map/project/pallas_call | solution.py:602
  211.4 4.7 gather_rows.5.e_ref
  217.3 15.9 %attend_forward.3 = (bf16[512,768]{1,0:T(8,128)(2,1)}, f32[768,512]{1,0:T(8,128)}, f32[6,2,512]{2,1,0:T(2,128)}) custom-call(bf16[512,768]{1,0:T(8,128)(2,1)} %get-tuple-element.211.q_ref, bf16[2,512,768]{2,1,0:T(8,128)(2,1)} %get-tuple-element.212.ka_ref.va_ref, bf16[2,512,768]{2,1,0:T(8,128)(2,1)} %copy-done.5, ...), custom_call_target="tpu_custom_call" | custom-call | flops 300000000 | bytes 300000 | tf_op jit(solution)/shard_map/attend_forward/pallas_call | solution.py:680
  233.8 2.5 collective-permute-done.47.xt_ref
  237.2 5.7 %assemble.11 = bf16[4,2,4,4,24,768]{5,4,3,2,1,0:T(8,128)(2,1)} custom-call(s32[3]{0:T(128)} %pad_add_fusion.3.where_ref, bf16[4,8,24,768]{3,2,1,0:T(8,128)(2,1)} %copy-done.1, bf16[3,8,24,768]{3,2,1,0:T(8,128)(2,1)} %copy-done.3, bf16[3,8,24,768]{3,2,1,0:T(8,128)(2,1)} %collective-permute-done.37.refs_2_, bf16[3,8,24,768]{3,2,1,0:T(8,128)(2,1)} %copy-done.12, ...), custom_call_target="tpu_custom_call" | custom-call | flops 300000000 | bytes 300000 | tf_op jit(solution)/shard_map/assemble/pallas_call | solution.py:538
  243.0 5.8 %assemble.10 = bf16[4,4,2,4,24,768]{5,4,3,2,1,0:T(8,128)(2,1)} custom-call(s32[3]{0:T(128)} %pad_add_fusion.3.where_ref, bf16[4,8,24,768]{3,2,1,0:T(8,128)(2,1)} %copy-done.1, bf16[3,8,24,768]{3,2,1,0:T(8,128)(2,1)} %copy-done.3, bf16[3,8,24,768]{3,2,1,0:T(8,128)(2,1)} %collective-permute-done.37.refs_2_, bf16[3,8,24,768]{3,2,1,0:T(8,128)(2,1)} %copy-done.12, ...), custom_call_target="tpu_custom_call" | custom-call | flops 300000000 | bytes 300000 | tf_op jit(solution)/shard_map/assemble/pallas_call | solution.py:538
  248.7 24.4 %post.3 = (f32[512,768]{1,0:T(8,128)}, bf16[512,768]{1,0:T(8,128)(2,1)}, f32[512,768]{1,0:T(8,128)}, f32[512,1]{1,0:T(8,128)}, f32[512,768]{1,0:T(8,128)}, /*ind...) custom-call(s32[3]{0:T(128)} %pad_add_fusion.3.where_ref, ...), custom_call_target="tpu_custom_call" | custom-call | flops 300000000 | bytes 300000 | tf_op jit(solution)/shard_map/post/pallas_call | solution.py:859
  273.2 16.6 %post_back.2 = (bf16[6,512,768]{2,1,0:T(8,128)(2,1)}, bf16[512,768]{1,0:T(8,128)(2,1)}, f32[512,768]{1,0:T(8,128)}, f32[12,768]{1,0:T(8,128)}) custom-call(bf16[512,768]{1,0:T(8,128)(2,1)} %gather_rows.5.e_ref, f32[512,768]{1,0:T(8,128)} %get-tuple-element.223.n1_ref, f32[512,1]{1,0:T(8,128)} %get-tuple-element.224.t1_ref, ...), custom_call_target="tpu_custom_call" | custom-call | flops 16000000000 | bytes 16000000 | tf_op jit(solution)/shard_map/post_back/pallas_call | solution.py:953
  291.5 20.5 %attend_backward.2 = (bf16[512,768]{1,0:T(8,128)(2,1)}, f32[2,512,768]{2,1,0:T(8,128)}, bf16[2,512,768]{2,1,0:T(8,128)(2,1)}) custom-call(bf16[512,768]{1,0:T(8,128)(2,1)} %get-tuple-element.211.q_ref, bf16[512,768]{1,0:T(8,128)(2,1)} %get-tuple-element.229.g_ref, bf16[2,512,768]{2,1,0:T(8,128)(2,1)} %get-tuple-element.212.ka_ref.va_ref, ...), custom_call_target="tpu_custom_call" | custom-call | flops 20999999488 | bytes 21000000 | tf_op jit(solution)/shard_map/attend_backward/pallas_call | solution.py:749
  313.9 12.5 %feed_grad.2 = (bf16[4,2,4,24,768]{4,3,2,1,0:T(8,128)(2,1)}, bf16[4,2,4,24,768]{4,3,2,1,0:T(8,128)(2,1)}, bf16[4,2,4,24,768]{4,3,2,1,0:T(8,128)(2,1)}, bf16[4,2,4,24,768]{4,3,2,1,0:T(8,128)(2,1)}) custom-call(s32[2]{0:T(128)} %pad_add_fusion.4.bit_ref, bf16[6,512,384]{2,1,0:T(8,128)(2,1)} %get-tuple-element.218.ym_ref.gm_ref.om_ref, ...), custom_call_target="tpu_custom_call" | custom-call | flops 12000000000 | bytes 12000000 | tf_op jit(solution)/shard_map/feed_grad/pallas_call | solution.py:1142
  330.2 9.2 %project_back.2 = (bf16[3,512,768]{2,1,0:T(8,128)(2,1)}, f32[512,768]{1,0:T(8,128)}, bf16[512,768]{1,0:T(8,128)(2,1)}, f32[2,768]{1,0:T(2,128)}) custom-call(bf16[512,768]{1,0:T(8,128)(2,1)} %get-tuple-element.232.dq_ref, f32[2,512,768]{2,1,0:T(8,128)} %get-tuple-element.237.own_ref, bf16[2,512,768]{2,1,0:T(8,128)(2,1)} %collective-permute-done.53.got_ref, ...), custom_call_target="tpu_custom_call" | custom-call | flops 500000000 | bytes 500000 | tf_op jit(solution)/shard_map/project_back/pallas_call | solution.py:1013
  340.4 4.7 gather_rows.6
  345.1 16.9 %post_back.3 = (bf16[6,512,768]{2,1,0:T(8,128)(2,1)}, bf16[512,768]{1,0:T(8,128)(2,1)}, f32[512,768]{1,0:T(8,128)}, f32[12,768]{1,0:T(8,128)}) custom-call(f32[512,768]{1,0:T(8,128)} %get-tuple-element.247.e_ref, f32[512,768]{1,0:T(8,128)} %get-tuple-element.248.n1_ref, f32[512,1]{1,0:T(8,128)} %get-tuple-element.249.t1_ref, ...), custom_call_target="tpu_custom_call" | custom-call | flops 500000000 | bytes 500000 | tf_op jit(solution)/shard_map/post_back/pallas_call | solution.py:953
  362.6 7.5 %collective-permute-start.54 = (bf16[256,768]{1,0:T(8,128)(2,1)S(1)}, bf16[256,768]{1,0:T(8,128)(2,1)}, u32[]{:S(2)}, u32[]{:S(2)}) collective-permute-start(bf16[256,768]{1,0:T(8,128)(2,1)S(1)} %slice.318), channel_id=1, source_target_pairs={{0,2},{1,3},{2,0},{3,1},{4,6},{5,7},{6,4},{7,5},{8,10},{9,11},{10,... | collective-permute-start | bytes 1179656 | tf_op jit(solution)/shard_map/ppermute | solution.py:441
  370.1 3.6 halve_sum.4
  376.3 20.5 %attend_backward.3 = (bf16[512,768]{1,0:T(8,128)(2,1)}, f32[2,512,768]{2,1,0:T(8,128)}, bf16[2,512,768]{2,1,0:T(8,128)(2,1)}) custom-call(bf16[512,768]{1,0:T(8,128)(2,1)} %get-tuple-element.196.q_ref, bf16[512,768]{1,0:T(8,128)(2,1)} %get-tuple-element.260.g_ref, bf16[2,512,768]{2,1,0:T(8,128)(2,1)} %get-tuple-element.197.ka_ref.va_ref, ...), custom_call_target="tpu_custom_call" | custom-call | flops 44999999488 | bytes 45000000 | tf_op jit(solution)/shard_map/attend_backward/pallas_call | solution.py:749
  397.2 7.7 %front_grad.2 = (bf16[4,2,2,24,768]{4,3,2,1,0:T(8,128)(2,1)}, bf16[4,2,2,24,768]{4,3,2,1,0:T(8,128)(2,1)}, bf16[4,2,2,24,768]{4,3,2,1,0:T(8,128)(2,1)}, bf16[4,2,2,24,768]{4,3,2,1,0:T(8,128)(2,1)}) custom-call(s32[2]{0:T(128)} %pad_add_fusion.4.bit_ref, bf16[512,384]{1,0:T(8,128)(2,1)} %get-tuple-element.267.xm_ref, bf16[512,384]{1,0:T(8,128)(2,1)} %copy-done.48, ...), custom_call_target="tpu_custom_call" | custom-call | flops 500000000 | bytes 500000 | tf_op jit(solution)/shard_map/front_grad/pallas_call | solution.py:1093
  407.0 13.0 %feed_grad.3 = (bf16[4,2,4,24,768]{4,3,2,1,0:T(8,128)(2,1)}, bf16[4,2,4,24,768]{4,3,2,1,0:T(8,128)(2,1)}, bf16[4,2,4,24,768]{4,3,2,1,0:T(8,128)(2,1)}, bf16[4,2,4,24,768]{4,3,2,1,0:T(8,128)(2,1)}) custom-call(s32[2]{0:T(128)} %pad_add_fusion.4.bit_ref, bf16[6,512,384]{2,1,0:T(8,128)(2,1)} %get-tuple-element.273.ym_ref.gm_ref.om_ref, ...), custom_call_target="tpu_custom_call" | custom-call | flops 12000000000 | bytes 12000000 | tf_op jit(solution)/shard_map/feed_grad/pallas_call | solution.py:1142
  423.1 2.6 halve_sum.5
  427.2 9.5 %project_back.3 = (bf16[3,512,768]{2,1,0:T(8,128)(2,1)}, f32[512,768]{1,0:T(8,128)}, bf16[512,768]{1,0:T(8,128)(2,1)}, f32[2,768]{1,0:T(2,128)}) custom-call(bf16[512,768]{1,0:T(8,128)(2,1)} %get-tuple-element.263.dq_ref, f32[2,512,768]{2,1,0:T(8,128)} %get-tuple-element.264.own_ref, bf16[2,512,768]{2,1,0:T(8,128)(2,1)} %collective-permute-done.57.got_ref, ...), custom_call_target="tpu_custom_call" | custom-call | flops 500000000 | bytes 500000 | tf_op jit(solution)/shard_map/project_back/pallas_call | solution.py:1013
  438.8 9.0 %collective-permute-done.67.got_x = bf16[4,2,4,24,768]{4,3,2,1,0:T(8,128)(2,1)} collective-permute-done((bf16[4,2,4,24,768]{4,3,2,1,0:T(8,128)(2,1)}, bf16[4,2,4,24,768]{4,3,2,1,0:T(8,128)(2,1)}, u32[]{:S(2)}, u32[]{:S(2)}) %collective-permute-start.67) | collective-permute-done | bytes 1179680 | tf_op jit(solution)/shard_map/ppermute | solution.py:441
  449.1 3.7 halve_sum.6
  452.7 7.7 %front_grad.3 = (bf16[4,2,2,24,768]{4,3,2,1,0:T(8,128)(2,1)}, bf16[4,2,2,24,768]{4,3,2,1,0:T(8,128)(2,1)}, bf16[4,2,2,24,768]{4,3,2,1,0:T(8,128)(2,1)}, bf16[4,2,2,24,768]{4,3,2,1,0:T(8,128)(2,1)}) custom-call(s32[2]{0:T(128)} %pad_add_fusion.4.bit_ref, bf16[512,384]{1,0:T(8,128)(2,1)} %get-tuple-element.288.xm_ref, bf16[512,384]{1,0:T(8,128)(2,1)} %copy-done.47, ...), custom_call_target="tpu_custom_call" | custom-call | flops 500000000 | bytes 500000 | tf_op jit(solution)/shard_map/front_grad/pallas_call | solution.py:1093
  469.3 4.7 gather_rows.7
  474.0 10.6 %collective-permute-done.74 = bf16[2,2,6,24,768]{4,3,2,1,0:T(8,128)(2,1)} collective-permute-done((bf16[2,2,6,24,768]{4,3,2,1,0:T(8,128)(2,1)}, bf16[2,2,6,24,768]{4,3,2,1,0:T(8,128)(2,1)}, u32[]{:S(2)}, u32[]{:S(2)}) %collective-permute-start.74) | collective-permute-done | bytes 884768 | tf_op jit(solution)/shard_map/ppermute | solution.py:441
  491.3 2.5 halve_sum.7
  495.0 2.7 collective-permute-done.76
  502.3 9.4 %collective-permute-start.80 = (bf16[2,2,4,24,768]{4,3,2,1,0:T(8,128)(2,1)S(1)}, bf16[2,2,4,24,768]{4,3,2,1,0:T(8,128)(2,1)}, u32[]{:S(2)}, u32[]{:S(2)}) collective-permute-start(bf16[2,2,4,24,768]{4,3,2,1,0:T(8,128)(2,1)S(1)} %select_bitcast_fusion.1), channel_id=1, source_target_pairs={{0,2},{1,3},{2,0},{3,1},{4,6},{5,7},{6,4},{7,5},{8,10},{9,11},{10,... | collective-permute-start | bytes 1769480 | tf_op jit(solution)/shard_map/ppermute | solution.py:441
  514.1 3.3 unpack.2
  517.4 8.3 %collective-permute-done.80 = bf16[2,2,4,24,768]{4,3,2,1,0:T(8,128)(2,1)} collective-permute-done((bf16[2,2,4,24,768]{4,3,2,1,0:T(8,128)(2,1)S(1)}, bf16[2,2,4,24,768]{4,3,2,1,0:T(8,128)(2,1)}, u32[]{:S(2)}, u32[]{:S(2)}) %collective-permute-start.80) | collective-permute-done | bytes 589856 | tf_op jit(solution)/shard_map/ppermute | solution.py:441
  535.8 2.9 collective-permute-done.86
  548.4 3.3 collective-permute-done.89.refs_3_
  552.5 3.2 unpack.3
  (482 shorter events, 146.2 us)
Async XLA Ops:
  7.2 33.6 %collective-permute-start.8 = (bf16[4,4,24,768]{3,2,1,0:T(8,128)(2,1)}, bf16[4,4,24,768]{3,2,1,0:T(8,128)(2,1)}, u32[]{:S(2)}, u32[]{:S(2)}) collective-permute-start(bf16[4,4,24,768]{3,2,1,0:T(8,128)(2,1)} %pad_maximum_fusion.9.refs_0_), channel_id=1, source_target_pairs={{0,1},{1,0},{2,3},{3,2},{4,5},{5,4},{6,7},{7,6},{8,9},{9,8},{10,11... | collective-permute-start | bytes 1769480 | tf_op jit(solution)/shard_map/ppermute | solution.py:441
  17.9 24.5 %collective-permute-start.3 = (bf16[456,768]{1,0:T(8,128)(2,1)}, bf16[456,768]{1,0:T(8,128)(2,1)}, u32[]{:S(2)}, u32[]{:S(2)}) collective-permute-start(bf16[456,768]{1,0:T(8,128)(2,1)} %pad_maximum_fusion.11), channel_id=1, source_target_pairs={{0,2},{1,3},{2,0},{3,1},{4,6},{5,7},{6,4},{7,5},{8,10},{9,11},{10,... | collective-permute-start | bytes 2101256 | tf_op jit(solution)/shard_map/ppermute | solution.py:441
  26.1 29.4 %collective-permute-start.4 = (bf16[456,768]{1,0:T(8,128)(2,1)}, bf16[456,768]{1,0:T(8,128)(2,1)}, u32[]{:S(2)}, u32[]{:S(2)}) collective-permute-start(bf16[456,768]{1,0:T(8,128)(2,1)} %pad_maximum_fusion.11), channel_id=1, source_target_pairs={{2,4},{3,5},{4,2},{5,3},{10,12},{11,13},{12,10},{13,11},{18,20},{1... | collective-permute-start | bytes 2101256 | tf_op jit(solution)/shard_map/ppermute | solution.py:441
  26.6 17.4 %collective-permute-start.6 = (bf16[3,4,24,768]{3,2,1,0:T(8,128)(2,1)}, bf16[3,4,24,768]{3,2,1,0:T(8,128)(2,1)}, u32[]{:S(2)}, u32[]{:S(2)}) collective-permute-start(bf16[3,4,24,768]{3,2,1,0:T(8,128)(2,1)} %pad_maximum_fusion.12.refs_1_), channel_id=1, source_target_pairs={{0,8},{1,9},{2,10},{3,11},{4,12},{5,13},{6,14},{7,15},{8,0},{9,1},... | collective-permute-start | bytes 1327112 | tf_op jit(solution)/shard_map/ppermute | solution.py:441
  43.4 32.5 %collective-permute-start.19 = (bf16[4,8,24,768]{3,2,1,0:T(8,128)(2,1)S(1)}, bf16[4,8,24,768]{3,2,1,0:T(8,128)(2,1)}, u32[]{:S(2)}, u32[]{:S(2)}) collective-permute-start(bf16[4,8,24,768]{3,2,1,0:T(8,128)(2,1)S(1)} %pad_maximum_fusion.4.refs_0_), channel_id=1, source_target_pairs={{0,1},{1,0},{2,3},{3,2},{4,5},{5,4},{6,7},{7,6},{8,9},{9,8},{10,11... | collective-permute-start | bytes 3538952 | tf_op jit(solution)/shard_map/ppermute | solution.py:441
  58.2 31.5 %collective-permute-start.10 = (bf16[4,264,768]{2,1,0:T(8,128)(2,1)}, bf16[4,264,768]{2,1,0:T(8,128)(2,1)}, u32[]{:S(2)}, u32[]{:S(2)}) collective-permute-start(bf16[4,264,768]{2,1,0:T(8,128)(2,1)} %pad_maximum_fusion.2.refs_0_), channel_id=1, source_target_pairs={{0,1},{1,0},{2,3},{3,2},{4,5},{5,4},{6,7},{7,6},{8,9},{9,8},{10,11... | collective-permute-start | bytes 4866056 | tf_op jit(solution)/shard_map/ppermute | solution.py:441
  67.3 22.2 %collective-permute-start.17 = (bf16[3,8,24,768]{3,2,1,0:T(8,128)(2,1)S(1)}, bf16[3,8,24,768]{3,2,1,0:T(8,128)(2,1)}, u32[]{:S(2)}, u32[]{:S(2)}) collective-permute-start(bf16[3,8,24,768]{3,2,1,0:T(8,128)(2,1)S(1)} %pad_maximum_fusion.6.refs_1_), channel_id=1, source_target_pairs={{0,8},{1,9},{2,10},{3,11},{4,12},{5,13},{6,14},{7,15},{8,0},{9,1},... | collective-permute-start | bytes 2654216 | tf_op jit(solution)/shard_map/ppermute | solution.py:441
  67.9 21.9 %collective-permute-start.18 = (bf16[3,8,24,768]{3,2,1,0:T(8,128)(2,1)S(1)}, bf16[3,8,24,768]{3,2,1,0:T(8,128)(2,1)}, u32[]{:S(2)}, u32[]{:S(2)}) collective-permute-start(bf16[3,8,24,768]{3,2,1,0:T(8,128)(2,1)S(1)} %pad_maximum_fusion.6.refs_1_), channel_id=1, source_target_pairs={{0,16},{1,17},{2,18},{3,19},{4,20},{5,21},{6,22},{7,23},{8,24},{9,... | collective-permute-start | bytes 2654216 | tf_op jit(solution)/shard_map/ppermute | solution.py:441
  69.4 20.4 %collective-permute-start.20 = (bf16[3,8,24,768]{3,2,1,0:T(8,128)(2,1)S(1)}, bf16[3,8,24,768]{3,2,1,0:T(8,128)(2,1)S(1)}, u32[]{:S(2)}, u32[]{:S(2)}) collective-permute-start(bf16[3,8,24,768]{3,2,1,0:T(8,128)(2,1)S(1)} %pad_maximum_fusion.6.refs_1_), channel_id=1, source_target_pairs={{0,1},{1,0},{2,3},{3,2},{4,5},{5,4},{6,7},{7,6},{8,9},{9,8},{10,11... | collective-permute-start | bytes 2654216 | tf_op jit(solution)/shard_map/ppermute | solution.py:441
  75.9 20.8 %collective-permute-start.11 = (bf16[544,768]{1,0:T(8,128)(2,1)}, bf16[544,768]{1,0:T(8,128)(2,1)}, u32[]{:S(2)}, u32[]{:S(2)}) collective-permute-start(bf16[544,768]{1,0:T(8,128)(2,1)} %pad_maximum_fusion.8), channel_id=1, source_target_pairs={{0,2},{1,3},{2,0},{3,1},{4,6},{5,7},{6,4},{7,5},{8,10},{9,11},{10,... | collective-permute-start | bytes 2506760 | tf_op jit(solution)/shard_map/ppermute | solution.py:441
  113.9 23.7 %collective-permute-start.28 = (bf16[3,8,24,768]{3,2,1,0:T(8,128)(2,1)}, bf16[3,8,24,768]{3,2,1,0:T(8,128)(2,1)}, u32[]{:S(2)}, u32[]{:S(2)}) collective-permute-start(bf16[3,8,24,768]{3,2,1,0:T(8,128)(2,1)} %collective-permute-done.17.refs_2_), channel_id=1, source_target_pairs={{0,1},{1,0},{2,3},{3,2},{4,5},{5,4},{6,7},{7,6},{8,9},{9,8},{10,11... | collective-permute-start | bytes 2654216 | tf_op jit(solution)/shard_map/ppermute | solution.py:441
  114.4 23.1 %collective-permute-start.27 = (bf16[3,8,24,768]{3,2,1,0:T(8,128)(2,1)}, bf16[3,8,24,768]{3,2,1,0:T(8,128)(2,1)}, u32[]{:S(2)}, u32[]{:S(2)}) collective-permute-start(bf16[3,8,24,768]{3,2,1,0:T(8,128)(2,1)} %collective-permute-done.18.refs_3_), channel_id=1, source_target_pairs={{0,8},{1,9},{2,10},{3,11},{4,12},{5,13},{6,14},{7,15},{8,0},{9,1},... | collective-permute-start | bytes 2654216 | tf_op jit(solution)/shard_map/ppermute | solution.py:441
  115.9 21.7 %collective-permute-start.29 = (bf16[3,8,24,768]{3,2,1,0:T(8,128)(2,1)}, bf16[3,8,24,768]{3,2,1,0:T(8,128)(2,1)}, u32[]{:S(2)}, u32[]{:S(2)}) collective-permute-start(bf16[3,8,24,768]{3,2,1,0:T(8,128)(2,1)} %collective-permute-done.18.refs_3_), channel_id=1, source_target_pairs={{0,1},{1,0},{2,3},{3,2},{4,5},{5,4},{6,7},{7,6},{8,9},{9,8},{10,11... | collective-permute-start | bytes 2654216 | tf_op jit(solution)/shard_map/ppermute | solution.py:441
  117.7 23.4 %collective-permute-start.22 = (bf16[544,768]{1,0:T(8,128)(2,1)}, bf16[544,768]{1,0:T(8,128)(2,1)}, u32[]{:S(2)}, u32[]{:S(2)}) collective-permute-start(bf16[544,768]{1,0:T(8,128)(2,1)} %collective-permute-done.11), channel_id=1, source_target_pairs={{2,4},{3,5},{4,2},{5,3},{10,12},{11,13},{12,10},{13,11},{18,20},{1... | collective-permute-start | bytes 2506760 | tf_op jit(solution)/shard_map/ppermute | solution.py:441
  120.8 22.4 %collective-permute-start.25 = (bf16[4,4,24,768]{3,2,1,0:T(8,128)(2,1)}, bf16[4,4,24,768]{3,2,1,0:T(8,128)(2,1)}, u32[]{:S(2)}, u32[]{:S(2)}) collective-permute-start(bf16[4,4,24,768]{3,2,1,0:T(8,128)(2,1)} %pad_maximum_fusion.10.refs_0_), channel_id=1, source_target_pairs={{0,1},{1,0},{2,3},{3,2},{4,5},{5,4},{6,7},{7,6},{8,9},{9,8},{10,11... | collective-permute-start | bytes 1769480 | tf_op jit(solution)/shard_map/ppermute | solution.py:441
  137.5 25.3 %collective-permute-start.34 = (bf16[4,8,24,768]{3,2,1,0:T(8,128)(2,1)S(1)}, bf16[4,8,24,768]{3,2,1,0:T(8,128)(2,1)S(1)}, u32[]{:S(2)}, u32[]{:S(2)}) collective-permute-start(bf16[4,8,24,768]{3,2,1,0:T(8,128)(2,1)S(1)} %pad_maximum_fusion.5.refs_0_), channel_id=1, source_target_pairs={{0,1},{1,0},{2,3},{3,2},{4,5},{5,4},{6,7},{7,6},{8,9},{9,8},{10,11... | collective-permute-start | bytes 3538952 | tf_op jit(solution)/shard_map/ppermute | solution.py:441
  145.7 21.2 %collective-permute-start.31 = (bf16[4,256,768]{2,1,0:T(8,128)(2,1)}, bf16[4,256,768]{2,1,0:T(8,128)(2,1)}, u32[]{:S(2)}, u32[]{:S(2)}) collective-permute-start(bf16[4,256,768]{2,1,0:T(8,128)(2,1)} %pad_maximum_fusion.3.refs_0_), channel_id=1, source_target_pairs={{0,1},{1,0},{2,3},{3,2},{4,5},{5,4},{6,7},{7,6},{8,9},{9,8},{10,11... | collective-permute-start | bytes 4718600 | tf_op jit(solution)/shard_map/ppermute | solution.py:441
  161.3 29.9 %collective-permute-start.37 = (bf16[3,8,24,768]{3,2,1,0:T(8,128)(2,1)S(1)}, bf16[3,8,24,768]{3,2,1,0:T(8,128)(2,1)}, u32[]{:S(2)}, u32[]{:S(2)}) collective-permute-start(bf16[3,8,24,768]{3,2,1,0:T(8,128)(2,1)S(1)} %pad_maximum_fusion.7.refs_1_), channel_id=1, source_target_pairs={{0,8},{1,9},{2,10},{3,11},{4,12},{5,13},{6,14},{7,15},{8,0},{9,1},... | collective-permute-start | bytes 2654216 | tf_op jit(solution)/shard_map/ppermute | solution.py:441
  162.8 28.4 %collective-permute-start.38 = (bf16[3,8,24,768]{3,2,1,0:T(8,128)(2,1)S(1)}, bf16[3,8,24,768]{3,2,1,0:T(8,128)(2,1)S(1)}, u32[]{:S(2)}, u32[]{:S(2)}) collective-permute-start(bf16[3,8,24,768]{3,2,1,0:T(8,128)(2,1)S(1)} %pad_maximum_fusion.7.refs_1_), channel_id=1, source_target_pairs={{0,16},{1,17},{2,18},{3,19},{4,20},{5,21},{6,22},{7,23},{8,24},{9,... | collective-permute-start | bytes 2654216 | tf_op jit(solution)/shard_map/ppermute | solution.py:441
  166.4 26.5 %collective-permute-start.36 = (bf16[3,4,24,768]{3,2,1,0:T(8,128)(2,1)}, bf16[3,4,24,768]{3,2,1,0:T(8,128)(2,1)}, u32[]{:S(2)}, u32[]{:S(2)}) collective-permute-start(bf16[3,4,24,768]{3,2,1,0:T(8,128)(2,1)} %collective-permute-done.24.refs_3_), channel_id=1, source_target_pairs={{0,8},{1,9},{2,10},{3,11},{4,12},{5,13},{6,14},{7,15},{8,0},{9,1},... | collective-permute-start | bytes 1327112 | tf_op jit(solution)/shard_map/ppermute | solution.py:441
  209.0 27.2 %collective-permute-start.48 = (bf16[6,512,384]{2,1,0:T(8,128)(2,1)}, bf16[6,512,384]{2,1,0:T(8,128)(2,1)}, u32[]{:S(2)}, u32[]{:S(2)}) collective-permute-start(bf16[6,512,384]{2,1,0:T(8,128)(2,1)} %get-tuple-element.221), channel_id=1, source_target_pairs={{0,1},{1,0},{2,3},{3,2},{4,5},{5,4},{6,7},{7,6},{8,9},{9,8},{10,11... | collective-permute-start | bytes 7077896 | tf_op jit(solution)/shard_map/ppermute | solution.py:441
  209.4 23.8 %collective-permute-start.41 = (bf16[3,8,24,768]{3,2,1,0:T(8,128)(2,1)}, bf16[3,8,24,768]{3,2,1,0:T(8,128)(2,1)S(1)}, u32[]{:S(2)}, u32[]{:S(2)}) collective-permute-start(bf16[3,8,24,768]{3,2,1,0:T(8,128)(2,1)} %collective-permute-done.37.refs_2_), channel_id=1, source_target_pairs={{0,16},{1,17},{2,18},{3,19},{4,20},{5,21},{6,22},{7,23},{8,24},{9,... | collective-permute-start | bytes 2654216 | tf_op jit(solution)/shard_map/ppermute | solution.py:441
  210.9 22.3 %collective-permute-start.42 = (bf16[3,8,24,768]{3,2,1,0:T(8,128)(2,1)}, bf16[3,8,24,768]{3,2,1,0:T(8,128)(2,1)}, u32[]{:S(2)}, u32[]{:S(2)}) collective-permute-start(bf16[3,8,24,768]{3,2,1,0:T(8,128)(2,1)} %collective-permute-done.37.refs_2_), channel_id=1, source_target_pairs={{0,1},{1,0},{2,3},{3,2},{4,5},{5,4},{6,7},{7,6},{8,9},{9,8},{10,11... | collective-permute-start | bytes 2654216 | tf_op jit(solution)/shard_map/ppermute | solution.py:441
  210.9 22.3 %collective-permute-start.43 = (bf16[3,8,24,768]{3,2,1,0:T(8,128)(2,1)S(1)}, bf16[3,8,24,768]{3,2,1,0:T(8,128)(2,1)}, u32[]{:S(2)}, u32[]{:S(2)}) collective-permute-start(bf16[3,8,24,768]{3,2,1,0:T(8,128)(2,1)S(1)} %copy-done.13), channel_id=1, source_target_pairs={{0,1},{1,0},{2,3},{3,2},{4,5},{5,4},{6,7},{7,6},{8,9},{9,8},{10,11... | collective-permute-start | bytes 2654216 | tf_op jit(solution)/shard_map/ppermute | solution.py:441
  289.7 22.8 %collective-permute-start.49 = (bf16[6,512,768]{2,1,0:T(8,128)(2,1)}, bf16[6,512,768]{2,1,0:T(8,128)(2,1)}, u32[]{:S(2)}, u32[]{:S(2)}) collective-permute-start(bf16[6,512,768]{2,1,0:T(8,128)(2,1)} %get-tuple-element.228.dz_ref.df_ref.da_ref), channel_id=1, source_target_pairs={{0,1},{1,0},{2,3},{3,2},{4,5},{5,4},{6,7},{7,6},{8,9},{9,8},{10,11... | collective-permute-start | bytes 14155784 | tf_op jit(solution)/shard_map/ppermute | solution.py:441
  289.9 22.7 %collective-permute-start.46 = (bf16[6,512,384]{2,1,0:T(8,128)(2,1)}, bf16[6,512,384]{2,1,0:T(8,128)(2,1)S(1)}, u32[]{:S(2)}, u32[]{:S(2)}) collective-permute-start(bf16[6,512,384]{2,1,0:T(8,128)(2,1)} %get-tuple-element.219), channel_id=1, source_target_pairs={{0,1},{1,0},{2,3},{3,2},{4,5},{5,4},{6,7},{7,6},{8,9},{9,8},{10,11... | collective-permute-start | bytes 7077896 | tf_op jit(solution)/shard_map/ppermute | solution.py:441
  290.9 21.2 %collective-permute-start.50 = (bf16[512,384]{1,0:T(8,128)(2,1)S(1)}, bf16[512,384]{1,0:T(8,128)(2,1)S(1)}, u32[]{:S(2)}, u32[]{:S(2)}) collective-permute-start(bf16[512,384]{1,0:T(8,128)(2,1)S(1)} %copy-done.74), channel_id=1, source_target_pairs={{0,1},{1,0},{2,3},{3,2},{4,5},{5,4},{6,7},{7,6},{8,9},{9,8},{10,11... | collective-permute-start | bytes 1179656 | tf_op jit(solution)/shard_map/ppermute | solution.py:441
  291.0 21.5 %collective-permute-start.51 = (bf16[512,768]{1,0:T(8,128)(2,1)S(1)}, bf16[512,768]{1,0:T(8,128)(2,1)}, u32[]{:S(2)}, u32[]{:S(2)}) collective-permute-start(bf16[512,768]{1,0:T(8,128)(2,1)S(1)} %copy-done.32), channel_id=1, source_target_pairs={{0,1},{1,0},{2,3},{3,2},{4,5},{5,4},{6,7},{7,6},{8,9},{9,8},{10,11... | collective-permute-start | bytes 2359304 | tf_op jit(solution)/shard_map/ppermute | solution.py:441
  291.4 37.1 %collective-permute-start.45 = (bf16[512,768]{1,0:T(8,128)(2,1)S(1)}, bf16[512,768]{1,0:T(8,128)(2,1)}, u32[]{:S(2)}, u32[]{:S(2)}) collective-permute-start(bf16[512,768]{1,0:T(8,128)(2,1)S(1)} %copy-done.32), channel_id=1, source_target_pairs={{2,4},{3,5},{4,2},{5,3},{10,12},{11,13},{12,10},{13,11},{18,20},{1... | collective-permute-start | bytes 2359304 | tf_op jit(solution)/shard_map/ppermute | solution.py:441
  312.1 18.1 %collective-permute-start.53 = (bf16[2,512,768]{2,1,0:T(8,128)(2,1)}, bf16[2,512,768]{2,1,0:T(8,128)(2,1)}, u32[]{:S(2)}, u32[]{:S(2)}) collective-permute-start(bf16[2,512,768]{2,1,0:T(8,128)(2,1)} %get-tuple-element.238), channel_id=1, source_target_pairs={{0,1},{1,0},{2,3},{3,2},{4,5},{5,4},{6,7},{7,6},{8,9},{9,8},{10,11... | collective-permute-start | bytes 4718600 | tf_op jit(solution)/shard_map/ppermute | solution.py:441
  326.4 43.7 %collective-permute-start.55 = (bf16[4,2,4,24,768]{4,3,2,1,0:T(8,128)(2,1)}, bf16[4,2,4,24,768]{4,3,2,1,0:T(8,128)(2,1)}, u32[]{:S(2)}, u32[]{:S(2)}) collective-permute-start(bf16[4,2,4,24,768]{4,3,2,1,0:T(8,128)(2,1)} %get-tuple-element.254), channel_id=1, source_target_pairs={{0,8},{1,9},{2,10},{3,11},{4,12},{5,13},{6,14},{7,15},{8,0},{9,1},... | collective-permute-start | bytes 3538952 | tf_op jit(solution)/shard_map/ppermute | solution.py:441
  328.0 42.1 %collective-permute-start.56 = (bf16[4,2,4,24,768]{4,3,2,1,0:T(8,128)(2,1)}, bf16[4,2,4,24,768]{4,3,2,1,0:T(8,128)(2,1)}, u32[]{:S(2)}, u32[]{:S(2)}) collective-permute-start(bf16[4,2,4,24,768]{4,3,2,1,0:T(8,128)(2,1)} %get-tuple-element.255), channel_id=1, source_target_pairs={{0,16},{1,17},{2,18},{3,19},{4,20},{5,21},{6,22},{7,23},{8,24},{9,... | collective-permute-start | bytes 3538952 | tf_op jit(solution)/shard_map/ppermute | solution.py:441
  362.0 45.0 %collective-permute-start.61 = (bf16[6,512,768]{2,1,0:T(8,128)(2,1)}, bf16[6,512,768]{2,1,0:T(8,128)(2,1)}, u32[]{:S(2)}, u32[]{:S(2)}) collective-permute-start(bf16[6,512,768]{2,1,0:T(8,128)(2,1)} %get-tuple-element.274.dz_ref.df_ref.da_ref), channel_id=1, source_target_pairs={{0,1},{1,0},{2,3},{3,2},{4,5},{5,4},{6,7},{7,6},{8,9},{9,8},{10,11... | collective-permute-start | bytes 14155784 | tf_op jit(solution)/shard_map/ppermute | solution.py:441
  362.5 34.8 %collective-permute-start.58 = (bf16[3,512,768]{2,1,0:T(8,128)(2,1)S(1)}, bf16[3,512,768]{2,1,0:T(8,128)(2,1)}, u32[]{:S(2)}, u32[]{:S(2)}) collective-permute-start(bf16[3,512,768]{2,1,0:T(8,128)(2,1)S(1)} %copy-done.22), channel_id=1, source_target_pairs={{0,1},{1,0},{2,3},{3,2},{4,5},{5,4},{6,7},{7,6},{8,9},{9,8},{10,11... | collective-permute-start | bytes 7077896 | tf_op jit(solution)/shard_map/ppermute | solution.py:441
  362.6 43.9 %collective-permute-start.54 = (bf16[256,768]{1,0:T(8,128)(2,1)S(1)}, bf16[256,768]{1,0:T(8,128)(2,1)}, u32[]{:S(2)}, u32[]{:S(2)}) collective-permute-start(bf16[256,768]{1,0:T(8,128)(2,1)S(1)} %slice.318), channel_id=1, source_target_pairs={{0,2},{1,3},{2,0},{3,1},{4,6},{5,7},{6,4},{7,5},{8,10},{9,11},{10,... | collective-permute-start | bytes 1179656 | tf_op jit(solution)/shard_map/ppermute | solution.py:441
  376.1 30.8 %collective-permute-start.62 = (bf16[2,2,2,4,24,768]{5,4,3,2,0,1:T(8,128)(2,1)}, bf16[2,2,2,4,24,768]{5,4,3,2,0,1:T(8,128)(2,1)S(1)}, u32[]{:S(2)}, u32[]{:S(2)}) collective-permute-start(bf16[2,2,2,4,24,768]{5,4,3,2,0,1:T(8,128)(2,1)} %copy.75), channel_id=1, source_target_pairs={{2,4},{3,5},{4,2},{5,3},{10,12},{11,13},{12,10},{13,11},{18,20},{1... | collective-permute-start | bytes 3538952 | tf_op jit(solution)/shard_map/ppermute | solution.py:441
  396.8 30.3 %collective-permute-start.57 = (bf16[2,512,768]{2,1,0:T(8,128)(2,1)}, bf16[2,512,768]{2,1,0:T(8,128)(2,1)}, u32[]{:S(2)}, u32[]{:S(2)}) collective-permute-start(bf16[2,512,768]{2,1,0:T(8,128)(2,1)} %get-tuple-element.265), channel_id=1, source_target_pairs={{0,1},{1,0},{2,3},{3,2},{4,5},{5,4},{6,7},{7,6},{8,9},{9,8},{10,11... | collective-permute-start | bytes 4718600 | tf_op jit(solution)/shard_map/ppermute | solution.py:441
  420.0 27.8 %collective-permute-start.67 = (bf16[4,2,4,24,768]{4,3,2,1,0:T(8,128)(2,1)}, bf16[4,2,4,24,768]{4,3,2,1,0:T(8,128)(2,1)}, u32[]{:S(2)}, u32[]{:S(2)}) collective-permute-start(bf16[4,2,4,24,768]{4,3,2,1,0:T(8,128)(2,1)} %get-tuple-element.290), channel_id=1, source_target_pairs={{0,16},{1,17},{2,18},{3,19},{4,20},{5,21},{6,22},{7,23},{8,24},{9,... | collective-permute-start | bytes 3538952 | tf_op jit(solution)/shard_map/ppermute | solution.py:441
  421.6 27.5 %collective-permute-start.68 = (bf16[4,2,4,24,768]{4,3,2,1,0:T(8,128)(2,1)}, bf16[4,2,4,24,768]{4,3,2,1,0:T(8,128)(2,1)}, u32[]{:S(2)}, u32[]{:S(2)}) collective-permute-start(bf16[4,2,4,24,768]{4,3,2,1,0:T(8,128)(2,1)} %get-tuple-element.291), channel_id=1, source_target_pairs={{0,8},{1,9},{2,10},{3,11},{4,12},{5,13},{6,14},{7,15},{8,0},{9,1},... | collective-permute-start | bytes 3538952 | tf_op jit(solution)/shard_map/ppermute | solution.py:441
  437.2 27.9 %collective-permute-start.63 = (bf16[512,768]{1,0:T(8,128)(2,1)}, bf16[512,768]{1,0:T(8,128)(2,1)}, u32[]{:S(2)}, u32[]{:S(2)}) collective-permute-start(bf16[512,768]{1,0:T(8,128)(2,1)} %get-tuple-element.282), channel_id=1, source_target_pairs={{2,4},{3,5},{4,2},{5,3},{10,12},{11,13},{12,10},{13,11},{18,20},{1... | collective-permute-start | bytes 2359304 | tf_op jit(solution)/shard_map/ppermute | solution.py:441
  463.4 21.2 %collective-permute-start.74 = (bf16[2,2,6,24,768]{4,3,2,1,0:T(8,128)(2,1)}, bf16[2,2,6,24,768]{4,3,2,1,0:T(8,128)(2,1)}, u32[]{:S(2)}, u32[]{:S(2)}) collective-permute-start(bf16[2,2,6,24,768]{4,3,2,1,0:T(8,128)(2,1)} %select_bitcast_fusion), channel_id=1, source_target_pairs={{0,2},{1,3},{2,0},{3,1},{4,6},{5,7},{6,4},{7,5},{8,10},{9,11},{10,... | collective-permute-start | bytes 2654216 | tf_op jit(solution)/shard_map/ppermute | solution.py:441
  466.3 33.4 %collective-permute-start.72 = (bf16[2,2,2,4,24,768]{5,4,3,2,0,1:T(8,128)(2,1)}, bf16[2,2,2,4,24,768]{5,4,3,2,0,1:T(8,128)(2,1)}, u32[]{:S(2)}, u32[]{:S(2)}) collective-permute-start(bf16[2,2,2,4,24,768]{5,4,3,2,0,1:T(8,128)(2,1)} %copy.83), channel_id=1, source_target_pairs={{2,4},{3,5},{4,2},{5,3},{10,12},{11,13},{12,10},{13,11},{18,20},{1... | collective-permute-start | bytes 3538952 | tf_op jit(solution)/shard_map/ppermute | solution.py:441
  466.8 20.7 %collective-permute-start.73 = (f32[4,2,1152]{2,1,0:T(2,128)S(1)}, f32[4,2,1152]{2,1,0:T(2,128)S(1)}, u32[]{:S(2)}, u32[]{:S(2)}) collective-permute-start(f32[4,2,1152]{2,1,0:T(2,128)S(1)} %fusion.10), channel_id=1, source_target_pairs={{0,8},{1,9},{2,10},{3,11},{4,12},{5,13},{6,14},{7,15},{8,0},{9,1},... | collective-permute-start | bytes 110600 | tf_op jit(solution)/shard_map/ppermute | solution.py:441
  467.3 23.3 %collective-permute-start.78 = (bf16[4,2,2,24,768]{4,3,2,1,0:T(8,128)(2,1)}, bf16[4,2,2,24,768]{4,3,2,1,0:T(8,128)(2,1)}, u32[]{:S(2)}, u32[]{:S(2)}) collective-permute-start(bf16[4,2,2,24,768]{4,3,2,1,0:T(8,128)(2,1)} %get-tuple-element.304), channel_id=1, source_target_pairs={{0,8},{1,9},{2,10},{3,11},{4,12},{5,13},{6,14},{7,15},{8,0},{9,1},... | collective-permute-start | bytes 1769480 | tf_op jit(solution)/shard_map/ppermute | solution.py:441
  468.8 21.9 %collective-permute-start.79 = (bf16[4,2,2,24,768]{4,3,2,1,0:T(8,128)(2,1)}, bf16[4,2,2,24,768]{4,3,2,1,0:T(8,128)(2,1)}, u32[]{:S(2)}, u32[]{:S(2)}) collective-permute-start(bf16[4,2,2,24,768]{4,3,2,1,0:T(8,128)(2,1)} %get-tuple-element.305), channel_id=1, source_target_pairs={{0,16},{1,17},{2,18},{3,19},{4,20},{5,21},{6,22},{7,23},{8,24},{9,... | collective-permute-start | bytes 1769480 | tf_op jit(solution)/shard_map/ppermute | solution.py:441
  490.6 40.9 %collective-permute-start.71 = (bf16[256,768]{1,0:T(8,128)(2,1)}, bf16[256,768]{1,0:T(8,128)(2,1)}, u32[]{:S(2)}, u32[]{:S(2)}) collective-permute-start(bf16[256,768]{1,0:T(8,128)(2,1)} %slice.322), channel_id=1, source_target_pairs={{0,2},{1,3},{2,0},{3,1},{4,6},{5,7},{6,4},{7,5},{8,10},{9,11},{10,... | collective-permute-start | bytes 1179656 | tf_op jit(solution)/shard_map/ppermute | solution.py:441
  502.3 23.4 %collective-permute-start.80 = (bf16[2,2,4,24,768]{4,3,2,1,0:T(8,128)(2,1)S(1)}, bf16[2,2,4,24,768]{4,3,2,1,0:T(8,128)(2,1)}, u32[]{:S(2)}, u32[]{:S(2)}) collective-permute-start(bf16[2,2,4,24,768]{4,3,2,1,0:T(8,128)(2,1)S(1)} %select_bitcast_fusion.1), channel_id=1, source_target_pairs={{0,2},{1,3},{2,0},{3,1},{4,6},{5,7},{6,4},{7,5},{8,10},{9,11},{10,... | collective-permute-start | bytes 1769480 | tf_op jit(solution)/shard_map/ppermute | solution.py:441
  512.0 31.3 %collective-permute-start.94 = (f32[2,1152]{1,0:T(2,128)S(1)}, f32[2,1152]{1,0:T(2,128)S(1)}, u32[]{:S(2)}, u32[]{:S(2)}) collective-permute-start(f32[2,1152]{1,0:T(2,128)S(1)} %select_bitcast_fusion.3), channel_id=1, source_target_pairs={{0,2},{1,3},{2,0},{3,1},{4,6},{5,7},{6,4},{7,5},{8,10},{9,11},{10,... | collective-permute-start | bytes 27656 | tf_op jit(solution)/shard_map/ppermute | solution.py:441
  (128 other events, 1185.4 us)

commit v6 on v5

--- a/solution.py
+++ b/solution.py
@@ -1350,7 +1350,7 @@
     third = tie(third, ready)
     third_near = send(third, TO_SIDE)
     third_middle = send(third, TO_MID)
-    fronts = [assemble(where, front_spread.parts(feed_spread.first, mine, third), 0, False)]
+    fronts = [assemble(where, front_spread.parts(feed_spread.first, mine, third_near), 0, False)]
 
     header = absolute(tuple(mine[:, rows:]), tuple(theirs[:, rows:]))
     header = header.reshape(8, 8, width)

time: 561 us -> 559 us (level)
  starting transfers between devices: 80.2 us -> 68.3 us
  waiting for transfers between devices: 86.4 us -> 95.1 us
    ppermute x95, starting transfers between devices: 80.2 us -> 68.3 us  [send(): return lax.ppermute(value, BOTH, route)]
    ppermute x95, waiting for transfers between devices: 86.4 us -> 95.1 us  [send(): return lax.ppermute(value, BOTH, route)]
    unnamed x159 -> x151, local copies, waits for them, and re-layouts: 9.99 us -> 11.7 us
where the time goes in v6:
time: 559 us; the launch traced here: 554 us
  Pallas kernels  301 us (54%)
  waiting for transfers between devices  95.1 us (17%)
  starting transfers between devices  68.3 us (12%)
  local copies, waits for them, and re-layouts  51.5 us (9%)
  other arithmetic  31.1 us (6%)
  between operations  6.58 us (1%)
    ppermute x95, waiting for transfers between devices, send(): return lax.ppermute(value, BOTH, route)  95.1 us
    ppermute x95, starting transfers between devices, send(): return lax.ppermute(value, BOTH, route)  68.3 us
    pallas_call x2, Pallas kernels, post(): pl.pallas_call(post_kernel, grid=(4,), in_specs=[SMEM, full, full, unit_s...  48.7 us
    pallas_call x2, Pallas kernels, attend_back_fast(): pl.pallas_call(attend_back_kernel, grid=(width // 128,), in_specs=[column...  41.1 us
    pallas_call x6, Pallas kernels, assemble(): pl.pallas_call(assemble_kernel, grid_spec=pltpu.PrefetchScalarGridSpec(nu...  34.9 us
    pallas_call x2, Pallas kernels, post_back(): pl.pallas_call(post_back_kernel, grid=(4,), in_specs=[full, full, thin, f...  33.4 us
    pallas_call x2, Pallas kernels, attend_fast(): pl.pallas_call(attend_kernel, grid=(width // 128,), in_specs=[column, key...  31.2 us
    pallas_call x2, Pallas kernels, feed_grad(): pl.pallas_call(functools.partial(feed_grad_kernel, x_first), grid=(8,), i...  25.5 us
  transfers between devices with their start and end apart: 95, of which 23 were waited for; matrix products, arithmetic and copies ran while one was open for 12% of the time, Pallas kernels for 41%

profile of v6, /device:TPU:0, one launch (start us, length us, event | category | flops | bytes accessed | tf_op | source)
XLA Modules:
  0.0 554.0 jit_solution(4629460302037298332)
XLA Ops:
  3.3 3.1 collective-permute-start
  7.9 2.6 slice_bitcast_fusion.1
  17.9 7.5 %collective-permute-start.3 = (bf16[456,768]{1,0:T(8,128)(2,1)}, bf16[456,768]{1,0:T(8,128)(2,1)}, u32[]{:S(2)}, u32[]{:S(2)}) collective-permute-start(bf16[456,768]{1,0:T(8,128)(2,1)} %pad_maximum_fusion.11), channel_id=1, source_target_pairs={{0,2},{1,3},{2,0},{3,1},{4,6},{5,7},{6,4},{7,5},{8,10},{9,11},{10,... | collective-permute-start | bytes 2101256 | tf_op jit(solution)/shard_map/ppermute | solution.py:441
  42.6 10.3 %collective-permute-done.7.refs_3_ = bf16[3,4,24,768]{3,2,1,0:T(8,128)(2,1)S(1)} collective-permute-done((bf16[3,4,24,768]{3,2,1,0:T(8,128)(2,1)}, bf16[3,4,24,768]{3,2,1,0:T(8,128)(2,1)S(1)}, u32[]{:S(2)}, u32[]{:S(2)}) %collective-permute-start.7) | collective-permute-done | bytes 442400 | tf_op jit(solution)/shard_map/ppermute | solution.py:441
  61.1 4.6 collective-permute-done.12.refs_4_
  65.7 9.6 %collective-permute-done.11 = bf16[544,768]{1,0:T(8,128)(2,1)} collective-permute-done((bf16[544,768]{1,0:T(8,128)(2,1)S(1)}, bf16[544,768]{1,0:T(8,128)(2,1)}, u32[]{:S(2)}, u32[]{:S(2)}) %collective-permute-start.11) | collective-permute-done | bytes 835616 | tf_op jit(solution)/shard_map/ppermute | solution.py:441
  78.7 5.8 %assemble.6 = bf16[4,4,2,4,24,768]{5,4,3,2,1,0:T(8,128)(2,1)} custom-call(s32[3]{0:T(128)} %pad_add_fusion.3.where_ref, bf16[4,4,24,768]{3,2,1,0:T(8,128)(2,1)} %pad_maximum_fusion.9.refs_0_, bf16[3,4,24,768]{3,2,1,0:T(8,128)(2,1)} %pad_maximum_fusion.12.refs_1_, bf16[3,4,24,768]{3,2,1,0:T(8,128)(2,1)} %collective-permute-done.6.refs_2_, ...), custom_call_target="tpu_custom_call" | custom-call | flops 300000000 | bytes 300000 | tf_op jit(solution)/shard_map/assemble/pallas_call | solution.py:538
  84.5 14.5 %collective-permute-done.17.refs_2_ = bf16[3,8,24,768]{3,2,1,0:T(8,128)(2,1)} collective-permute-done((bf16[3,8,24,768]{3,2,1,0:T(8,128)(2,1)S(1)}, bf16[3,8,24,768]{3,2,1,0:T(8,128)(2,1)}, u32[]{:S(2)}, u32[]{:S(2)}) %collective-permute-start.17) | collective-permute-done | bytes 884768 | tf_op jit(solution)/shard_map/ppermute | solution.py:441
  102.7 4.7 gather_rows.4.h_ref
  109.1 7.4 %project.2 = (bf16[512,768]{1,0:T(8,128)(2,1)}, bf16[2,512,768]{2,1,0:T(8,128)(2,1)}, bf16[512,384]{1,0:T(8,128)(2,1)}, bf16[512,384]{1,0:T(8,128)(2,1)}) custom-call(bf16[512,768]{1,0:T(8,128)(2,1)} %gather_rows.4.h_ref, bf16[4,768,768]{2,1,0:T(8,128)(2,1)} %bitcast.191, f32[12,768]{1,0:T(8,128)} %squeeze.50.vec_ref, bf16[2,768,384]{2,1,0:T(8,128)(2,1)} %fusion.sel_ref), custom_call_target="tpu_custom_call" | custom-call | flops 300000000 | bytes 300000 | tf_op jit(solution)/shard_map/project/pallas_call | solution.py:602
  125.0 15.4 %attend_forward.2 = (bf16[512,768]{1,0:T(8,128)(2,1)}, f32[768,512]{1,0:T(8,128)}, f32[6,2,512]{2,1,0:T(2,128)}) custom-call(bf16[512,768]{1,0:T(8,128)(2,1)} %get-tuple-element.196.q_ref, bf16[2,512,768]{2,1,0:T(8,128)(2,1)} %get-tuple-element.197.ka_ref.va_ref, bf16[2,512,768]{2,1,0:T(8,128)(2,1)} %copy-done.4, ...), custom_call_target="tpu_custom_call" | custom-call | flops 300000000 | bytes 300000 | tf_op jit(solution)/shard_map/attend_forward/pallas_call | solution.py:680
  150.2 5.8 %assemble.8 = bf16[4,2,4,4,24,768]{5,4,3,2,1,0:T(8,128)(2,1)} custom-call(s32[3]{0:T(128)} %pad_add_fusion.3.where_ref, bf16[4,8,24,768]{3,2,1,0:T(8,128)(2,1)} %copy-done, bf16[3,8,24,768]{3,2,1,0:T(8,128)(2,1)} %copy-done.2, bf16[3,8,24,768]{3,2,1,0:T(8,128)(2,1)} %collective-permute-done.17.refs_2_, ...), custom_call_target="tpu_custom_call" | custom-call | flops 300000000 | bytes 300000 | tf_op jit(solution)/shard_map/assemble/pallas_call | solution.py:538
  155.9 6.0 %assemble.7 = bf16[4,4,2,4,24,768]{5,4,3,2,1,0:T(8,128)(2,1)} custom-call(s32[3]{0:T(128)} %pad_add_fusion.3.where_ref, bf16[4,8,24,768]{3,2,1,0:T(8,128)(2,1)} %copy-done, bf16[3,8,24,768]{3,2,1,0:T(8,128)(2,1)} %copy-done.2, bf16[3,8,24,768]{3,2,1,0:T(8,128)(2,1)} %collective-permute-done.17.refs_2_, ...), custom_call_target="tpu_custom_call" | custom-call | flops 300000000 | bytes 300000 | tf_op jit(solution)/shard_map/assemble/pallas_call | solution.py:538
  170.4 24.2 %post.2 = (f32[512,768]{1,0:T(8,128)}, bf16[512,768]{1,0:T(8,128)(2,1)}, f32[512,768]{1,0:T(8,128)}, f32[512,1]{1,0:T(8,128)}, f32[512,768]{1,0:T(8,128)}, /*ind...) custom-call(s32[3]{0:T(128)} %pad_add_fusion.3.where_ref, ...), custom_call_target="tpu_custom_call" | custom-call | flops 300000000 | bytes 300000 | tf_op jit(solution)/shard_map/post/pallas_call | solution.py:859
  199.2 5.8 %assemble.9 = bf16[4,4,2,4,24,768]{5,4,3,2,1,0:T(8,128)(2,1)} custom-call(s32[3]{0:T(128)} %pad_add_fusion.3.where_ref, bf16[4,4,24,768]{3,2,1,0:T(8,128)(2,1)} %pad_maximum_fusion.10.refs_0_, bf16[3,4,24,768]{3,2,1,0:T(8,128)(2,1)} %copy-done.24, bf16[3,4,24,768]{3,2,1,0:T(8,128)(2,1)} %collective-permute-done.23.refs_2_, ...), custom_call_target="tpu_custom_call" | custom-call | flops 300000000 | bytes 300000 | tf_op jit(solution)/shard_map/assemble/pallas_call | solution.py:538
  205.0 7.4 %project.3 = (bf16[512,768]{1,0:T(8,128)(2,1)}, bf16[2,512,768]{2,1,0:T(8,128)(2,1)}, bf16[512,384]{1,0:T(8,128)(2,1)}, bf16[512,384]{1,0:T(8,128)(2,1)}) custom-call(bf16[512,768]{1,0:T(8,128)(2,1)} %get-tuple-element.206.h_ref, bf16[4,768,768]{2,1,0:T(8,128)(2,1)} %bitcast.195, f32[12,768]{1,0:T(8,128)} %squeeze.51.vec_ref, bf16[2,768,384]{2,1,0:T(8,128)(2,1)} %fusion.sel_ref), custom_call_target="tpu_custom_call" | custom-call | flops 300000000 | bytes 300000 | tf_op jit(solution)/shard_map/project/pallas_call | solution.py:602
  214.9 4.7 gather_rows.5.e_ref
  220.8 15.8 %attend_forward.3 = (bf16[512,768]{1,0:T(8,128)(2,1)}, f32[768,512]{1,0:T(8,128)}, f32[6,2,512]{2,1,0:T(2,128)}) custom-call(bf16[512,768]{1,0:T(8,128)(2,1)} %get-tuple-element.211.q_ref, bf16[2,512,768]{2,1,0:T(8,128)(2,1)} %get-tuple-element.212.ka_ref.va_ref, bf16[2,512,768]{2,1,0:T(8,128)(2,1)} %copy-done.5, ...), custom_call_target="tpu_custom_call" | custom-call | flops 300000000 | bytes 300000 | tf_op jit(solution)/shard_map/attend_forward/pallas_call | solution.py:680
  241.4 5.8 %assemble.11 = bf16[4,2,4,4,24,768]{5,4,3,2,1,0:T(8,128)(2,1)} custom-call(s32[3]{0:T(128)} %pad_add_fusion.3.where_ref, bf16[4,8,24,768]{3,2,1,0:T(8,128)(2,1)} %copy-done.1, bf16[3,8,24,768]{3,2,1,0:T(8,128)(2,1)} %copy-done.3, bf16[3,8,24,768]{3,2,1,0:T(8,128)(2,1)} %collective-permute-done.37.refs_2_, bf16[3,8,24,768]{3,2,1,0:T(8,128)(2,1)} %copy-done.12, ...), custom_call_target="tpu_custom_call" | custom-call | flops 300000000 | bytes 300000 | tf_op jit(solution)/shard_map/assemble/pallas_call | solution.py:538
  247.2 5.7 %assemble.10 = bf16[4,4,2,4,24,768]{5,4,3,2,1,0:T(8,128)(2,1)} custom-call(s32[3]{0:T(128)} %pad_add_fusion.3.where_ref, bf16[4,8,24,768]{3,2,1,0:T(8,128)(2,1)} %copy-done.1, bf16[3,8,24,768]{3,2,1,0:T(8,128)(2,1)} %copy-done.3, bf16[3,8,24,768]{3,2,1,0:T(8,128)(2,1)} %collective-permute-done.37.refs_2_, bf16[3,8,24,768]{3,2,1,0:T(8,128)(2,1)} %copy-done.12, ...), custom_call_target="tpu_custom_call" | custom-call | flops 300000000 | bytes 300000 | tf_op jit(solution)/shard_map/assemble/pallas_call | solution.py:538
  253.0 24.4 %post.3 = (f32[512,768]{1,0:T(8,128)}, bf16[512,768]{1,0:T(8,128)(2,1)}, f32[512,768]{1,0:T(8,128)}, f32[512,1]{1,0:T(8,128)}, f32[512,768]{1,0:T(8,128)}, /*ind...) custom-call(s32[3]{0:T(128)} %pad_add_fusion.3.where_ref, ...), custom_call_target="tpu_custom_call" | custom-call | flops 300000000 | bytes 300000 | tf_op jit(solution)/shard_map/post/pallas_call | solution.py:859
  277.4 16.5 %post_back.2 = (bf16[6,512,768]{2,1,0:T(8,128)(2,1)}, bf16[512,768]{1,0:T(8,128)(2,1)}, f32[512,768]{1,0:T(8,128)}, f32[12,768]{1,0:T(8,128)}) custom-call(bf16[512,768]{1,0:T(8,128)(2,1)} %gather_rows.5.e_ref, f32[512,768]{1,0:T(8,128)} %get-tuple-element.223.n1_ref, f32[512,1]{1,0:T(8,128)} %get-tuple-element.224.t1_ref, ...), custom_call_target="tpu_custom_call" | custom-call | flops 16000000000 | bytes 16000000 | tf_op jit(solution)/shard_map/post_back/pallas_call | solution.py:953
  295.7 20.5 %attend_backward.2 = (bf16[512,768]{1,0:T(8,128)(2,1)}, f32[2,512,768]{2,1,0:T(8,128)}, bf16[2,512,768]{2,1,0:T(8,128)(2,1)}) custom-call(bf16[512,768]{1,0:T(8,128)(2,1)} %get-tuple-element.211.q_ref, bf16[512,768]{1,0:T(8,128)(2,1)} %get-tuple-element.229.g_ref, bf16[2,512,768]{2,1,0:T(8,128)(2,1)} %get-tuple-element.212.ka_ref.va_ref, ...), custom_call_target="tpu_custom_call" | custom-call | flops 20999999488 | bytes 21000000 | tf_op jit(solution)/shard_map/attend_backward/pallas_call | solution.py:749
  318.1 12.4 %feed_grad.2 = (bf16[4,2,4,24,768]{4,3,2,1,0:T(8,128)(2,1)}, bf16[4,2,4,24,768]{4,3,2,1,0:T(8,128)(2,1)}, bf16[4,2,4,24,768]{4,3,2,1,0:T(8,128)(2,1)}, bf16[4,2,4,24,768]{4,3,2,1,0:T(8,128)(2,1)}) custom-call(s32[2]{0:T(128)} %pad_add_fusion.4.bit_ref, bf16[6,512,384]{2,1,0:T(8,128)(2,1)} %get-tuple-element.218.ym_ref.gm_ref.om_ref, ...), custom_call_target="tpu_custom_call" | custom-call | flops 12000000000 | bytes 12000000 | tf_op jit(solution)/shard_map/feed_grad/pallas_call | solution.py:1142
  333.8 9.2 %project_back.2 = (bf16[3,512,768]{2,1,0:T(8,128)(2,1)}, f32[512,768]{1,0:T(8,128)}, bf16[512,768]{1,0:T(8,128)(2,1)}, f32[2,768]{1,0:T(2,128)}) custom-call(bf16[512,768]{1,0:T(8,128)(2,1)} %get-tuple-element.232.dq_ref, f32[2,512,768]{2,1,0:T(8,128)} %get-tuple-element.237.own_ref, bf16[2,512,768]{2,1,0:T(8,128)(2,1)} %collective-permute-done.53.got_ref, ...), custom_call_target="tpu_custom_call" | custom-call | flops 500000000 | bytes 500000 | tf_op jit(solution)/shard_map/project_back/pallas_call | solution.py:1013
  343.9 4.7 gather_rows.6
  348.6 16.9 %post_back.3 = (bf16[6,512,768]{2,1,0:T(8,128)(2,1)}, bf16[512,768]{1,0:T(8,128)(2,1)}, f32[512,768]{1,0:T(8,128)}, f32[12,768]{1,0:T(8,128)}) custom-call(f32[512,768]{1,0:T(8,128)} %get-tuple-element.247.e_ref, f32[512,768]{1,0:T(8,128)} %get-tuple-element.248.n1_ref, f32[512,1]{1,0:T(8,128)} %get-tuple-element.249.t1_ref, ...), custom_call_target="tpu_custom_call" | custom-call | flops 500000000 | bytes 500000 | tf_op jit(solution)/shard_map/post_back/pallas_call | solution.py:953
  367.5 3.6 halve_sum.4
  373.7 20.6 %attend_backward.3 = (bf16[512,768]{1,0:T(8,128)(2,1)}, f32[2,512,768]{2,1,0:T(8,128)}, bf16[2,512,768]{2,1,0:T(8,128)(2,1)}) custom-call(bf16[512,768]{1,0:T(8,128)(2,1)} %get-tuple-element.196.q_ref, bf16[512,768]{1,0:T(8,128)(2,1)} %get-tuple-element.260.g_ref, bf16[2,512,768]{2,1,0:T(8,128)(2,1)} %get-tuple-element.197.ka_ref.va_ref, ...), custom_call_target="tpu_custom_call" | custom-call | flops 44999999488 | bytes 45000000 | tf_op jit(solution)/shard_map/attend_backward/pallas_call | solution.py:749
  394.7 7.7 %front_grad.2 = (bf16[4,2,2,24,768]{4,3,2,1,0:T(8,128)(2,1)}, bf16[4,2,2,24,768]{4,3,2,1,0:T(8,128)(2,1)}, bf16[4,2,2,24,768]{4,3,2,1,0:T(8,128)(2,1)}, bf16[4,2,2,24,768]{4,3,2,1,0:T(8,128)(2,1)}) custom-call(s32[2]{0:T(128)} %pad_add_fusion.4.bit_ref, bf16[512,384]{1,0:T(8,128)(2,1)} %get-tuple-element.267.xm_ref, bf16[512,384]{1,0:T(8,128)(2,1)} %copy-done.49, ...), custom_call_target="tpu_custom_call" | custom-call | flops 500000000 | bytes 500000 | tf_op jit(solution)/shard_map/front_grad/pallas_call | solution.py:1093
  405.2 13.0 %feed_grad.3 = (bf16[4,2,4,24,768]{4,3,2,1,0:T(8,128)(2,1)}, bf16[4,2,4,24,768]{4,3,2,1,0:T(8,128)(2,1)}, bf16[4,2,4,24,768]{4,3,2,1,0:T(8,128)(2,1)}, bf16[4,2,4,24,768]{4,3,2,1,0:T(8,128)(2,1)}) custom-call(s32[2]{0:T(128)} %pad_add_fusion.4.bit_ref, bf16[6,512,384]{2,1,0:T(8,128)(2,1)} %get-tuple-element.273.ym_ref.gm_ref.om_ref, ...), custom_call_target="tpu_custom_call" | custom-call | flops 12000000000 | bytes 12000000 | tf_op jit(solution)/shard_map/feed_grad/pallas_call | solution.py:1142
  420.6 2.6 halve_sum.5
  424.6 9.5 %project_back.3 = (bf16[3,512,768]{2,1,0:T(8,128)(2,1)}, f32[512,768]{1,0:T(8,128)}, bf16[512,768]{1,0:T(8,128)(2,1)}, f32[2,768]{1,0:T(2,128)}) custom-call(bf16[512,768]{1,0:T(8,128)(2,1)} %get-tuple-element.263.dq_ref, f32[2,512,768]{2,1,0:T(8,128)} %get-tuple-element.264.own_ref, bf16[2,512,768]{2,1,0:T(8,128)(2,1)} %collective-permute-done.57.got_ref, ...), custom_call_target="tpu_custom_call" | custom-call | flops 500000000 | bytes 500000 | tf_op jit(solution)/shard_map/project_back/pallas_call | solution.py:1013
  436.2 9.8 %collective-permute-done.67.got_x = bf16[4,2,4,24,768]{4,3,2,1,0:T(8,128)(2,1)} collective-permute-done((bf16[4,2,4,24,768]{4,3,2,1,0:T(8,128)(2,1)}, bf16[4,2,4,24,768]{4,3,2,1,0:T(8,128)(2,1)}, u32[]{:S(2)}, u32[]{:S(2)}) %collective-permute-start.67) | collective-permute-done | bytes 1179680 | tf_op jit(solution)/shard_map/ppermute | solution.py:441
  446.3 3.6 halve_sum.6
  449.9 7.7 %front_grad.3 = (bf16[4,2,2,24,768]{4,3,2,1,0:T(8,128)(2,1)}, bf16[4,2,2,24,768]{4,3,2,1,0:T(8,128)(2,1)}, bf16[4,2,2,24,768]{4,3,2,1,0:T(8,128)(2,1)}, bf16[4,2,2,24,768]{4,3,2,1,0:T(8,128)(2,1)}) custom-call(s32[2]{0:T(128)} %pad_add_fusion.4.bit_ref, bf16[512,384]{1,0:T(8,128)(2,1)} %get-tuple-element.288.xm_ref, bf16[512,384]{1,0:T(8,128)(2,1)} %copy-done.48, ...), custom_call_target="tpu_custom_call" | custom-call | flops 500000000 | bytes 500000 | tf_op jit(solution)/shard_map/front_grad/pallas_call | solution.py:1093
  466.7 4.7 gather_rows.7
  471.3 11.3 %collective-permute-done.74 = bf16[2,2,6,24,768]{4,3,2,1,0:T(8,128)(2,1)} collective-permute-done((bf16[2,2,6,24,768]{4,3,2,1,0:T(8,128)(2,1)}, bf16[2,2,6,24,768]{4,3,2,1,0:T(8,128)(2,1)}, u32[]{:S(2)}, u32[]{:S(2)}) %collective-permute-start.74) | collective-permute-done | bytes 884768 | tf_op jit(solution)/shard_map/ppermute | solution.py:441
  490.3 2.6 halve_sum.7
  494.0 3.0 collective-permute-done.76
  502.2 8.1 %collective-permute-start.80 = (bf16[2,2,4,24,768]{4,3,2,1,0:T(8,128)(2,1)S(1)}, bf16[2,2,4,24,768]{4,3,2,1,0:T(8,128)(2,1)S(1)}, u32[]{:S(2)}, u32[]{:S(2)}) collective-permute-start(bf16[2,2,4,24,768]{4,3,2,1,0:T(8,128)(2,1)S(1)} %select_bitcast_fusion.1), channel_id=1, source_target_pairs={{0,2},{1,3},{2,0},{3,1},{4,6},{5,7},{6,4},{7,5},{8,10},{9,11},{10,... | collective-permute-start | bytes 1769480 | tf_op jit(solution)/shard_map/ppermute | solution.py:441
  512.8 3.3 unpack.2
  516.1 8.3 %collective-permute-done.80 = bf16[2,2,4,24,768]{4,3,2,1,0:T(8,128)(2,1)S(1)} collective-permute-done((bf16[2,2,4,24,768]{4,3,2,1,0:T(8,128)(2,1)S(1)}, bf16[2,2,4,24,768]{4,3,2,1,0:T(8,128)(2,1)S(1)}, u32[]{:S(2)}, u32[]{:S(2)}) %collective-permute-start.80) | collective-permute-done | bytes 589856 | tf_op jit(solution)/shard_map/ppermute | solution.py:441
  524.5 3.1 collective-permute-done.87
  535.2 2.8 collective-permute-done.86
  538.2 2.9 collective-permute-done.90
  546.9 2.7 collective-permute-done.89.refs_3_
  550.3 3.2 unpack.3
  (474 shorter events, 141.9 us)
Async XLA Ops:
  7.2 33.6 %collective-permute-start.8 = (bf16[4,4,24,768]{3,2,1,0:T(8,128)(2,1)}, bf16[4,4,24,768]{3,2,1,0:T(8,128)(2,1)}, u32[]{:S(2)}, u32[]{:S(2)}) collective-permute-start(bf16[4,4,24,768]{3,2,1,0:T(8,128)(2,1)} %pad_maximum_fusion.9.refs_0_), channel_id=1, source_target_pairs={{0,1},{1,0},{2,3},{3,2},{4,5},{5,4},{6,7},{7,6},{8,9},{9,8},{10,11... | collective-permute-start | bytes 1769480 | tf_op jit(solution)/shard_map/ppermute | solution.py:441
  17.9 24.5 %collective-permute-start.3 = (bf16[456,768]{1,0:T(8,128)(2,1)}, bf16[456,768]{1,0:T(8,128)(2,1)}, u32[]{:S(2)}, u32[]{:S(2)}) collective-permute-start(bf16[456,768]{1,0:T(8,128)(2,1)} %pad_maximum_fusion.11), channel_id=1, source_target_pairs={{0,2},{1,3},{2,0},{3,1},{4,6},{5,7},{6,4},{7,5},{8,10},{9,11},{10,... | collective-permute-start | bytes 2101256 | tf_op jit(solution)/shard_map/ppermute | solution.py:441
  26.1 29.7 %collective-permute-start.4 = (bf16[456,768]{1,0:T(8,128)(2,1)}, bf16[456,768]{1,0:T(8,128)(2,1)}, u32[]{:S(2)}, u32[]{:S(2)}) collective-permute-start(bf16[456,768]{1,0:T(8,128)(2,1)} %pad_maximum_fusion.11), channel_id=1, source_target_pairs={{2,4},{3,5},{4,2},{5,3},{10,12},{11,13},{12,10},{13,11},{18,20},{1... | collective-permute-start | bytes 2101256 | tf_op jit(solution)/shard_map/ppermute | solution.py:441
  54.4 20.8 %collective-permute-start.11 = (bf16[544,768]{1,0:T(8,128)(2,1)S(1)}, bf16[544,768]{1,0:T(8,128)(2,1)}, u32[]{:S(2)}, u32[]{:S(2)}) collective-permute-start(bf16[544,768]{1,0:T(8,128)(2,1)S(1)} %pad_maximum_fusion.8), channel_id=1, source_target_pairs={{0,2},{1,3},{2,0},{3,1},{4,6},{5,7},{6,4},{7,5},{8,10},{9,11},{10,... | collective-permute-start | bytes 2506760 | tf_op jit(solution)/shard_map/ppermute | solution.py:441
  58.3 40.9 %collective-permute-start.10 = (bf16[4,264,768]{2,1,0:T(8,128)(2,1)}, bf16[4,264,768]{2,1,0:T(8,128)(2,1)}, u32[]{:S(2)}, u32[]{:S(2)}) collective-permute-start(bf16[4,264,768]{2,1,0:T(8,128)(2,1)} %pad_maximum_fusion.2.refs_0_), channel_id=1, source_target_pairs={{0,1},{1,0},{2,3},{3,2},{4,5},{5,4},{6,7},{7,6},{8,9},{9,8},{10,11... | collective-permute-start | bytes 4866056 | tf_op jit(solution)/shard_map/ppermute | solution.py:441
  61.0 23.4 %collective-permute-start.19 = (bf16[4,8,24,768]{3,2,1,0:T(8,128)(2,1)S(1)}, bf16[4,8,24,768]{3,2,1,0:T(8,128)(2,1)}, u32[]{:S(2)}, u32[]{:S(2)}) collective-permute-start(bf16[4,8,24,768]{3,2,1,0:T(8,128)(2,1)S(1)} %pad_maximum_fusion.4.refs_0_), channel_id=1, source_target_pairs={{0,1},{1,0},{2,3},{3,2},{4,5},{5,4},{6,7},{7,6},{8,9},{9,8},{10,11... | collective-permute-start | bytes 3538952 | tf_op jit(solution)/shard_map/ppermute | solution.py:441
  76.8 22.2 %collective-permute-start.17 = (bf16[3,8,24,768]{3,2,1,0:T(8,128)(2,1)S(1)}, bf16[3,8,24,768]{3,2,1,0:T(8,128)(2,1)}, u32[]{:S(2)}, u32[]{:S(2)}) collective-permute-start(bf16[3,8,24,768]{3,2,1,0:T(8,128)(2,1)S(1)} %pad_maximum_fusion.6.refs_1_), channel_id=1, source_target_pairs={{0,8},{1,9},{2,10},{3,11},{4,12},{5,13},{6,14},{7,15},{8,0},{9,1},... | collective-permute-start | bytes 2654216 | tf_op jit(solution)/shard_map/ppermute | solution.py:441
  77.3 21.9 %collective-permute-start.18 = (bf16[3,8,24,768]{3,2,1,0:T(8,128)(2,1)S(1)}, bf16[3,8,24,768]{3,2,1,0:T(8,128)(2,1)}, u32[]{:S(2)}, u32[]{:S(2)}) collective-permute-start(bf16[3,8,24,768]{3,2,1,0:T(8,128)(2,1)S(1)} %pad_maximum_fusion.6.refs_1_), channel_id=1, source_target_pairs={{0,16},{1,17},{2,18},{3,19},{4,20},{5,21},{6,22},{7,23},{8,24},{9,... | collective-permute-start | bytes 2654216 | tf_op jit(solution)/shard_map/ppermute | solution.py:441
  77.9 21.4 %collective-permute-start.20 = (bf16[3,8,24,768]{3,2,1,0:T(8,128)(2,1)S(1)}, bf16[3,8,24,768]{3,2,1,0:T(8,128)(2,1)S(1)}, u32[]{:S(2)}, u32[]{:S(2)}) collective-permute-start(bf16[3,8,24,768]{3,2,1,0:T(8,128)(2,1)S(1)} %pad_maximum_fusion.6.refs_1_), channel_id=1, source_target_pairs={{0,1},{1,0},{2,3},{3,2},{4,5},{5,4},{6,7},{7,6},{8,9},{9,8},{10,11... | collective-permute-start | bytes 2654216 | tf_op jit(solution)/shard_map/ppermute | solution.py:441
  84.4 23.1 %collective-permute-start.16 = (bf16[544,768]{1,0:T(8,128)(2,1)}, bf16[544,768]{1,0:T(8,128)(2,1)S(1)}, u32[]{:S(2)}, u32[]{:S(2)}) collective-permute-start(bf16[544,768]{1,0:T(8,128)(2,1)} %copy-done.23), channel_id=1, source_target_pairs={{2,4},{3,5},{4,2},{5,3},{10,12},{11,13},{12,10},{13,11},{18,20},{1... | collective-permute-start | bytes 2506760 | tf_op jit(solution)/shard_map/ppermute | solution.py:441
  117.6 22.9 %collective-permute-start.28 = (bf16[3,8,24,768]{3,2,1,0:T(8,128)(2,1)}, bf16[3,8,24,768]{3,2,1,0:T(8,128)(2,1)}, u32[]{:S(2)}, u32[]{:S(2)}) collective-permute-start(bf16[3,8,24,768]{3,2,1,0:T(8,128)(2,1)} %collective-permute-done.17.refs_2_), channel_id=1, source_target_pairs={{0,1},{1,0},{2,3},{3,2},{4,5},{5,4},{6,7},{7,6},{8,9},{9,8},{10,11... | collective-permute-start | bytes 2654216 | tf_op jit(solution)/shard_map/ppermute | solution.py:441
  118.1 22.3 %collective-permute-start.27 = (bf16[3,8,24,768]{3,2,1,0:T(8,128)(2,1)}, bf16[3,8,24,768]{3,2,1,0:T(8,128)(2,1)}, u32[]{:S(2)}, u32[]{:S(2)}) collective-permute-start(bf16[3,8,24,768]{3,2,1,0:T(8,128)(2,1)} %collective-permute-done.18.refs_3_), channel_id=1, source_target_pairs={{0,8},{1,9},{2,10},{3,11},{4,12},{5,13},{6,14},{7,15},{8,0},{9,1},... | collective-permute-start | bytes 2654216 | tf_op jit(solution)/shard_map/ppermute | solution.py:441
  119.6 20.9 %collective-permute-start.29 = (bf16[3,8,24,768]{3,2,1,0:T(8,128)(2,1)}, bf16[3,8,24,768]{3,2,1,0:T(8,128)(2,1)}, u32[]{:S(2)}, u32[]{:S(2)}) collective-permute-start(bf16[3,8,24,768]{3,2,1,0:T(8,128)(2,1)} %collective-permute-done.18.refs_3_), channel_id=1, source_target_pairs={{0,1},{1,0},{2,3},{3,2},{4,5},{5,4},{6,7},{7,6},{8,9},{9,8},{10,11... | collective-permute-start | bytes 2654216 | tf_op jit(solution)/shard_map/ppermute | solution.py:441
  121.4 22.6 %collective-permute-start.22 = (bf16[544,768]{1,0:T(8,128)(2,1)}, bf16[544,768]{1,0:T(8,128)(2,1)}, u32[]{:S(2)}, u32[]{:S(2)}) collective-permute-start(bf16[544,768]{1,0:T(8,128)(2,1)} %collective-permute-done.11), channel_id=1, source_target_pairs={{2,4},{3,5},{4,2},{5,3},{10,12},{11,13},{12,10},{13,11},{18,20},{1... | collective-permute-start | bytes 2506760 | tf_op jit(solution)/shard_map/ppermute | solution.py:441
  123.9 22.9 %collective-permute-start.25 = (bf16[4,4,24,768]{3,2,1,0:T(8,128)(2,1)}, bf16[4,4,24,768]{3,2,1,0:T(8,128)(2,1)}, u32[]{:S(2)}, u32[]{:S(2)}) collective-permute-start(bf16[4,4,24,768]{3,2,1,0:T(8,128)(2,1)} %pad_maximum_fusion.10.refs_0_), channel_id=1, source_target_pairs={{0,1},{1,0},{2,3},{3,2},{4,5},{5,4},{6,7},{7,6},{8,9},{9,8},{10,11... | collective-permute-start | bytes 1769480 | tf_op jit(solution)/shard_map/ppermute | solution.py:441
  140.5 25.3 %collective-permute-start.34 = (bf16[4,8,24,768]{3,2,1,0:T(8,128)(2,1)S(1)}, bf16[4,8,24,768]{3,2,1,0:T(8,128)(2,1)S(1)}, u32[]{:S(2)}, u32[]{:S(2)}) collective-permute-start(bf16[4,8,24,768]{3,2,1,0:T(8,128)(2,1)S(1)} %pad_maximum_fusion.5.refs_0_), channel_id=1, source_target_pairs={{0,1},{1,0},{2,3},{3,2},{4,5},{5,4},{6,7},{7,6},{8,9},{9,8},{10,11... | collective-permute-start | bytes 3538952 | tf_op jit(solution)/shard_map/ppermute | solution.py:441
  149.2 21.2 %collective-permute-start.31 = (bf16[4,256,768]{2,1,0:T(8,128)(2,1)}, bf16[4,256,768]{2,1,0:T(8,128)(2,1)}, u32[]{:S(2)}, u32[]{:S(2)}) collective-permute-start(bf16[4,256,768]{2,1,0:T(8,128)(2,1)} %pad_maximum_fusion.3.refs_0_), channel_id=1, source_target_pairs={{0,1},{1,0},{2,3},{3,2},{4,5},{5,4},{6,7},{7,6},{8,9},{9,8},{10,11... | collective-permute-start | bytes 4718600 | tf_op jit(solution)/shard_map/ppermute | solution.py:441
  164.8 29.9 %collective-permute-start.37 = (bf16[3,8,24,768]{3,2,1,0:T(8,128)(2,1)S(1)}, bf16[3,8,24,768]{3,2,1,0:T(8,128)(2,1)}, u32[]{:S(2)}, u32[]{:S(2)}) collective-permute-start(bf16[3,8,24,768]{3,2,1,0:T(8,128)(2,1)S(1)} %pad_maximum_fusion.7.refs_1_), channel_id=1, source_target_pairs={{0,8},{1,9},{2,10},{3,11},{4,12},{5,13},{6,14},{7,15},{8,0},{9,1},... | collective-permute-start | bytes 2654216 | tf_op jit(solution)/shard_map/ppermute | solution.py:441
  165.8 28.9 %collective-permute-start.38 = (bf16[3,8,24,768]{3,2,1,0:T(8,128)(2,1)S(1)}, bf16[3,8,24,768]{3,2,1,0:T(8,128)(2,1)S(1)}, u32[]{:S(2)}, u32[]{:S(2)}) collective-permute-start(bf16[3,8,24,768]{3,2,1,0:T(8,128)(2,1)S(1)} %pad_maximum_fusion.7.refs_1_), channel_id=1, source_target_pairs={{0,16},{1,17},{2,18},{3,19},{4,20},{5,21},{6,22},{7,23},{8,24},{9,... | collective-permute-start | bytes 2654216 | tf_op jit(solution)/shard_map/ppermute | solution.py:441
  169.3 27.1 %collective-permute-start.36 = (bf16[3,4,24,768]{3,2,1,0:T(8,128)(2,1)}, bf16[3,4,24,768]{3,2,1,0:T(8,128)(2,1)}, u32[]{:S(2)}, u32[]{:S(2)}) collective-permute-start(bf16[3,4,24,768]{3,2,1,0:T(8,128)(2,1)} %collective-permute-done.24.refs_3_), channel_id=1, source_target_pairs={{0,8},{1,9},{2,10},{3,11},{4,12},{5,13},{6,14},{7,15},{8,0},{9,1},... | collective-permute-start | bytes 1327112 | tf_op jit(solution)/shard_map/ppermute | solution.py:441
  212.5 28.0 %collective-permute-start.48 = (bf16[6,512,384]{2,1,0:T(8,128)(2,1)}, bf16[6,512,384]{2,1,0:T(8,128)(2,1)}, u32[]{:S(2)}, u32[]{:S(2)}) collective-permute-start(bf16[6,512,384]{2,1,0:T(8,128)(2,1)} %get-tuple-element.221), channel_id=1, source_target_pairs={{0,1},{1,0},{2,3},{3,2},{4,5},{5,4},{6,7},{7,6},{8,9},{9,8},{10,11... | collective-permute-start | bytes 7077896 | tf_op jit(solution)/shard_map/ppermute | solution.py:441
  212.9 23.8 %collective-permute-start.41 = (bf16[3,8,24,768]{3,2,1,0:T(8,128)(2,1)}, bf16[3,8,24,768]{3,2,1,0:T(8,128)(2,1)S(1)}, u32[]{:S(2)}, u32[]{:S(2)}) collective-permute-start(bf16[3,8,24,768]{3,2,1,0:T(8,128)(2,1)} %collective-permute-done.37.refs_2_), channel_id=1, source_target_pairs={{0,16},{1,17},{2,18},{3,19},{4,20},{5,21},{6,22},{7,23},{8,24},{9,... | collective-permute-start | bytes 2654216 | tf_op jit(solution)/shard_map/ppermute | solution.py:441
  214.4 22.3 %collective-permute-start.42 = (bf16[3,8,24,768]{3,2,1,0:T(8,128)(2,1)}, bf16[3,8,24,768]{3,2,1,0:T(8,128)(2,1)}, u32[]{:S(2)}, u32[]{:S(2)}) collective-permute-start(bf16[3,8,24,768]{3,2,1,0:T(8,128)(2,1)} %collective-permute-done.37.refs_2_), channel_id=1, source_target_pairs={{0,1},{1,0},{2,3},{3,2},{4,5},{5,4},{6,7},{7,6},{8,9},{9,8},{10,11... | collective-permute-start | bytes 2654216 | tf_op jit(solution)/shard_map/ppermute | solution.py:441
  214.4 22.3 %collective-permute-start.43 = (bf16[3,8,24,768]{3,2,1,0:T(8,128)(2,1)S(1)}, bf16[3,8,24,768]{3,2,1,0:T(8,128)(2,1)}, u32[]{:S(2)}, u32[]{:S(2)}) collective-permute-start(bf16[3,8,24,768]{3,2,1,0:T(8,128)(2,1)S(1)} %copy-done.13), channel_id=1, source_target_pairs={{0,1},{1,0},{2,3},{3,2},{4,5},{5,4},{6,7},{7,6},{8,9},{9,8},{10,11... | collective-permute-start | bytes 2654216 | tf_op jit(solution)/shard_map/ppermute | solution.py:441
  293.9 22.8 %collective-permute-start.49 = (bf16[6,512,768]{2,1,0:T(8,128)(2,1)}, bf16[6,512,768]{2,1,0:T(8,128)(2,1)}, u32[]{:S(2)}, u32[]{:S(2)}) collective-permute-start(bf16[6,512,768]{2,1,0:T(8,128)(2,1)} %get-tuple-element.228.dz_ref.df_ref.da_ref), channel_id=1, source_target_pairs={{0,1},{1,0},{2,3},{3,2},{4,5},{5,4},{6,7},{7,6},{8,9},{9,8},{10,11... | collective-permute-start | bytes 14155784 | tf_op jit(solution)/shard_map/ppermute | solution.py:441
  294.0 22.7 %collective-permute-start.46 = (bf16[6,512,384]{2,1,0:T(8,128)(2,1)}, bf16[6,512,384]{2,1,0:T(8,128)(2,1)S(1)}, u32[]{:S(2)}, u32[]{:S(2)}) collective-permute-start(bf16[6,512,384]{2,1,0:T(8,128)(2,1)} %get-tuple-element.219), channel_id=1, source_target_pairs={{0,1},{1,0},{2,3},{3,2},{4,5},{5,4},{6,7},{7,6},{8,9},{9,8},{10,11... | collective-permute-start | bytes 7077896 | tf_op jit(solution)/shard_map/ppermute | solution.py:441
  295.0 21.2 %collective-permute-start.50 = (bf16[512,384]{1,0:T(8,128)(2,1)}, bf16[512,384]{1,0:T(8,128)(2,1)S(1)}, u32[]{:S(2)}, u32[]{:S(2)}) collective-permute-start(bf16[512,384]{1,0:T(8,128)(2,1)} %get-tuple-element.233), channel_id=1, source_target_pairs={{0,1},{1,0},{2,3},{3,2},{4,5},{5,4},{6,7},{7,6},{8,9},{9,8},{10,11... | collective-permute-start | bytes 1179656 | tf_op jit(solution)/shard_map/ppermute | solution.py:441
  295.1 21.5 %collective-permute-start.51 = (bf16[512,768]{1,0:T(8,128)(2,1)S(1)}, bf16[512,768]{1,0:T(8,128)(2,1)}, u32[]{:S(2)}, u32[]{:S(2)}) collective-permute-start(bf16[512,768]{1,0:T(8,128)(2,1)S(1)} %copy-done.33), channel_id=1, source_target_pairs={{0,1},{1,0},{2,3},{3,2},{4,5},{5,4},{6,7},{7,6},{8,9},{9,8},{10,11... | collective-permute-start | bytes 2359304 | tf_op jit(solution)/shard_map/ppermute | solution.py:441
  295.5 36.5 %collective-permute-start.45 = (bf16[512,768]{1,0:T(8,128)(2,1)S(1)}, bf16[512,768]{1,0:T(8,128)(2,1)}, u32[]{:S(2)}, u32[]{:S(2)}) collective-permute-start(bf16[512,768]{1,0:T(8,128)(2,1)S(1)} %copy-done.33), channel_id=1, source_target_pairs={{2,4},{3,5},{4,2},{5,3},{10,12},{11,13},{12,10},{13,11},{18,20},{1... | collective-permute-start | bytes 2359304 | tf_op jit(solution)/shard_map/ppermute | solution.py:441
  316.2 17.6 %collective-permute-start.53 = (bf16[2,512,768]{2,1,0:T(8,128)(2,1)}, bf16[2,512,768]{2,1,0:T(8,128)(2,1)}, u32[]{:S(2)}, u32[]{:S(2)}) collective-permute-start(bf16[2,512,768]{2,1,0:T(8,128)(2,1)} %get-tuple-element.238), channel_id=1, source_target_pairs={{0,1},{1,0},{2,3},{3,2},{4,5},{5,4},{6,7},{7,6},{8,9},{9,8},{10,11... | collective-permute-start | bytes 4718600 | tf_op jit(solution)/shard_map/ppermute | solution.py:441
  330.5 37.0 %collective-permute-start.55 = (bf16[4,2,4,24,768]{4,3,2,1,0:T(8,128)(2,1)}, bf16[4,2,4,24,768]{4,3,2,1,0:T(8,128)(2,1)}, u32[]{:S(2)}, u32[]{:S(2)}) collective-permute-start(bf16[4,2,4,24,768]{4,3,2,1,0:T(8,128)(2,1)} %get-tuple-element.254), channel_id=1, source_target_pairs={{0,8},{1,9},{2,10},{3,11},{4,12},{5,13},{6,14},{7,15},{8,0},{9,1},... | collective-permute-start | bytes 3538952 | tf_op jit(solution)/shard_map/ppermute | solution.py:441
  331.6 36.0 %collective-permute-start.56 = (bf16[4,2,4,24,768]{4,3,2,1,0:T(8,128)(2,1)}, bf16[4,2,4,24,768]{4,3,2,1,0:T(8,128)(2,1)}, u32[]{:S(2)}, u32[]{:S(2)}) collective-permute-start(bf16[4,2,4,24,768]{4,3,2,1,0:T(8,128)(2,1)} %get-tuple-element.255), channel_id=1, source_target_pairs={{0,16},{1,17},{2,18},{3,19},{4,20},{5,21},{6,22},{7,23},{8,24},{9,... | collective-permute-start | bytes 3538952 | tf_op jit(solution)/shard_map/ppermute | solution.py:441
  365.5 39.7 %collective-permute-start.61 = (bf16[6,512,768]{2,1,0:T(8,128)(2,1)}, bf16[6,512,768]{2,1,0:T(8,128)(2,1)}, u32[]{:S(2)}, u32[]{:S(2)}) collective-permute-start(bf16[6,512,768]{2,1,0:T(8,128)(2,1)} %get-tuple-element.274.dz_ref.df_ref.da_ref), channel_id=1, source_target_pairs={{0,1},{1,0},{2,3},{3,2},{4,5},{5,4},{6,7},{7,6},{8,9},{9,8},{10,11... | collective-permute-start | bytes 14155784 | tf_op jit(solution)/shard_map/ppermute | solution.py:441
  366.0 28.7 %collective-permute-start.58 = (bf16[3,512,768]{2,1,0:T(8,128)(2,1)S(1)}, bf16[3,512,768]{2,1,0:T(8,128)(2,1)}, u32[]{:S(2)}, u32[]{:S(2)}) collective-permute-start(bf16[3,512,768]{2,1,0:T(8,128)(2,1)S(1)} %copy-done.22), channel_id=1, source_target_pairs={{0,1},{1,0},{2,3},{3,2},{4,5},{5,4},{6,7},{7,6},{8,9},{9,8},{10,11... | collective-permute-start | bytes 7077896 | tf_op jit(solution)/shard_map/ppermute | solution.py:441
  366.1 37.5 %collective-permute-start.54 = (bf16[256,768]{1,0:T(8,128)(2,1)S(1)}, bf16[256,768]{1,0:T(8,128)(2,1)}, u32[]{:S(2)}, u32[]{:S(2)}) collective-permute-start(bf16[256,768]{1,0:T(8,128)(2,1)S(1)} %slice.318), channel_id=1, source_target_pairs={{0,2},{1,3},{2,0},{3,1},{4,6},{5,7},{6,4},{7,5},{8,10},{9,11},{10,... | collective-permute-start | bytes 1179656 | tf_op jit(solution)/shard_map/ppermute | solution.py:441
  373.6 31.6 %collective-permute-start.62 = (bf16[2,2,2,4,24,768]{5,4,3,2,0,1:T(8,128)(2,1)}, bf16[2,2,2,4,24,768]{5,4,3,2,0,1:T(8,128)(2,1)S(1)}, u32[]{:S(2)}, u32[]{:S(2)}) collective-permute-start(bf16[2,2,2,4,24,768]{5,4,3,2,0,1:T(8,128)(2,1)} %copy.75), channel_id=1, source_target_pairs={{2,4},{3,5},{4,2},{5,3},{10,12},{11,13},{12,10},{13,11},{18,20},{1... | collective-permute-start | bytes 3538952 | tf_op jit(solution)/shard_map/ppermute | solution.py:441
  394.3 30.3 %collective-permute-start.57 = (bf16[2,512,768]{2,1,0:T(8,128)(2,1)}, bf16[2,512,768]{2,1,0:T(8,128)(2,1)}, u32[]{:S(2)}, u32[]{:S(2)}) collective-permute-start(bf16[2,512,768]{2,1,0:T(8,128)(2,1)} %get-tuple-element.265), channel_id=1, source_target_pairs={{0,1},{1,0},{2,3},{3,2},{4,5},{5,4},{6,7},{7,6},{8,9},{9,8},{10,11... | collective-permute-start | bytes 4718600 | tf_op jit(solution)/shard_map/ppermute | solution.py:441
  418.2 27.8 %collective-permute-start.67 = (bf16[4,2,4,24,768]{4,3,2,1,0:T(8,128)(2,1)}, bf16[4,2,4,24,768]{4,3,2,1,0:T(8,128)(2,1)}, u32[]{:S(2)}, u32[]{:S(2)}) collective-permute-start(bf16[4,2,4,24,768]{4,3,2,1,0:T(8,128)(2,1)} %get-tuple-element.290), channel_id=1, source_target_pairs={{0,16},{1,17},{2,18},{3,19},{4,20},{5,21},{6,22},{7,23},{8,24},{9,... | collective-permute-start | bytes 3538952 | tf_op jit(solution)/shard_map/ppermute | solution.py:441
  418.8 27.5 %collective-permute-start.68 = (bf16[4,2,4,24,768]{4,3,2,1,0:T(8,128)(2,1)}, bf16[4,2,4,24,768]{4,3,2,1,0:T(8,128)(2,1)}, u32[]{:S(2)}, u32[]{:S(2)}) collective-permute-start(bf16[4,2,4,24,768]{4,3,2,1,0:T(8,128)(2,1)} %get-tuple-element.291), channel_id=1, source_target_pairs={{0,8},{1,9},{2,10},{3,11},{4,12},{5,13},{6,14},{7,15},{8,0},{9,1},... | collective-permute-start | bytes 3538952 | tf_op jit(solution)/shard_map/ppermute | solution.py:441
  434.6 26.8 %collective-permute-start.63 = (bf16[512,768]{1,0:T(8,128)(2,1)}, bf16[512,768]{1,0:T(8,128)(2,1)}, u32[]{:S(2)}, u32[]{:S(2)}) collective-permute-start(bf16[512,768]{1,0:T(8,128)(2,1)} %get-tuple-element.282), channel_id=1, source_target_pairs={{2,4},{3,5},{4,2},{5,3},{10,12},{11,13},{12,10},{13,11},{18,20},{1... | collective-permute-start | bytes 2359304 | tf_op jit(solution)/shard_map/ppermute | solution.py:441
  460.5 22.2 %collective-permute-start.74 = (bf16[2,2,6,24,768]{4,3,2,1,0:T(8,128)(2,1)}, bf16[2,2,6,24,768]{4,3,2,1,0:T(8,128)(2,1)}, u32[]{:S(2)}, u32[]{:S(2)}) collective-permute-start(bf16[2,2,6,24,768]{4,3,2,1,0:T(8,128)(2,1)} %select_bitcast_fusion), channel_id=1, source_target_pairs={{0,2},{1,3},{2,0},{3,1},{4,6},{5,7},{6,4},{7,5},{8,10},{9,11},{10,... | collective-permute-start | bytes 2654216 | tf_op jit(solution)/shard_map/ppermute | solution.py:441
  462.6 36.9 %collective-permute-start.72 = (bf16[2,2,2,4,24,768]{5,4,3,2,0,1:T(8,128)(2,1)}, bf16[2,2,2,4,24,768]{5,4,3,2,0,1:T(8,128)(2,1)}, u32[]{:S(2)}, u32[]{:S(2)}) collective-permute-start(bf16[2,2,2,4,24,768]{5,4,3,2,0,1:T(8,128)(2,1)} %copy.83), channel_id=1, source_target_pairs={{2,4},{3,5},{4,2},{5,3},{10,12},{11,13},{12,10},{13,11},{18,20},{1... | collective-permute-start | bytes 3538952 | tf_op jit(solution)/shard_map/ppermute | solution.py:441
  463.1 22.2 %collective-permute-start.73 = (f32[4,2,1152]{2,1,0:T(2,128)S(1)}, f32[4,2,1152]{2,1,0:T(2,128)S(1)}, u32[]{:S(2)}, u32[]{:S(2)}) collective-permute-start(f32[4,2,1152]{2,1,0:T(2,128)S(1)} %fusion.10), channel_id=1, source_target_pairs={{0,8},{1,9},{2,10},{3,11},{4,12},{5,13},{6,14},{7,15},{8,0},{9,1},... | collective-permute-start | bytes 110600 | tf_op jit(solution)/shard_map/ppermute | solution.py:441
  464.6 24.0 %collective-permute-start.78 = (bf16[4,2,2,24,768]{4,3,2,1,0:T(8,128)(2,1)}, bf16[4,2,2,24,768]{4,3,2,1,0:T(8,128)(2,1)S(1)}, u32[]{:S(2)}, u32[]{:S(2)}) collective-permute-start(bf16[4,2,2,24,768]{4,3,2,1,0:T(8,128)(2,1)} %get-tuple-element.304), channel_id=1, source_target_pairs={{0,8},{1,9},{2,10},{3,11},{4,12},{5,13},{6,14},{7,15},{8,0},{9,1},... | collective-permute-start | bytes 1769480 | tf_op jit(solution)/shard_map/ppermute | solution.py:441
  465.1 23.6 %collective-permute-start.79 = (bf16[4,2,2,24,768]{4,3,2,1,0:T(8,128)(2,1)}, bf16[4,2,2,24,768]{4,3,2,1,0:T(8,128)(2,1)}, u32[]{:S(2)}, u32[]{:S(2)}) collective-permute-start(bf16[4,2,2,24,768]{4,3,2,1,0:T(8,128)(2,1)} %get-tuple-element.305), channel_id=1, source_target_pairs={{0,16},{1,17},{2,18},{3,19},{4,20},{5,21},{6,22},{7,23},{8,24},{9,... | collective-permute-start | bytes 1769480 | tf_op jit(solution)/shard_map/ppermute | solution.py:441
  488.6 43.6 %collective-permute-start.71 = (bf16[256,768]{1,0:T(8,128)(2,1)}, bf16[256,768]{1,0:T(8,128)(2,1)}, u32[]{:S(2)}, u32[]{:S(2)}) collective-permute-start(bf16[256,768]{1,0:T(8,128)(2,1)} %slice.322), channel_id=1, source_target_pairs={{0,2},{1,3},{2,0},{3,1},{4,6},{5,7},{6,4},{7,5},{8,10},{9,11},{10,... | collective-permute-start | bytes 1179656 | tf_op jit(solution)/shard_map/ppermute | solution.py:441
  502.2 22.1 %collective-permute-start.80 = (bf16[2,2,4,24,768]{4,3,2,1,0:T(8,128)(2,1)S(1)}, bf16[2,2,4,24,768]{4,3,2,1,0:T(8,128)(2,1)S(1)}, u32[]{:S(2)}, u32[]{:S(2)}) collective-permute-start(bf16[2,2,4,24,768]{4,3,2,1,0:T(8,128)(2,1)S(1)} %select_bitcast_fusion.1), channel_id=1, source_target_pairs={{0,2},{1,3},{2,0},{3,1},{4,6},{5,7},{6,4},{7,5},{8,10},{9,11},{10,... | collective-permute-start | bytes 1769480 | tf_op jit(solution)/shard_map/ppermute | solution.py:441
  511.0 30.7 %collective-permute-start.94 = (f32[2,1152]{1,0:T(2,128)S(1)}, f32[2,1152]{1,0:T(2,128)S(1)}, u32[]{:S(2)}, u32[]{:S(2)}) collective-permute-start(f32[2,1152]{1,0:T(2,128)S(1)} %select_bitcast_fusion.3), channel_id=1, source_target_pairs={{0,2},{1,3},{2,0},{3,1},{4,6},{5,7},{6,4},{7,5},{8,10},{9,11},{10,... | collective-permute-start | bytes 27656 | tf_op jit(solution)/shard_map/ppermute | solution.py:441
  (124 other events, 1140.7 us)

commit v7 on v6

--- a/solution.py
+++ b/solution.py
@@ -1453,7 +1453,7 @@
     feed_spread = Spread(feed_one, tie(group(four[1:], 4 * UNIT, split), ready), False)
     cotangent_theirs = send(cotangent_mine, TO_TWIN)
     held = [feed_spread.first, cotangent_theirs] + front_spread.twins + feed_spread.twins
-    results, others = complete(0, tie(middle[0], ready, *held))
+    results, others = complete(0, tie(middle[0], ready, start[4], *held))
     hidden, hidden_low = results[:2]
     record(start, middle, results, others)
     ready = feed_spread.turn(hidden_low)

time: 559 us -> 558 us (level)
    unnamed x151 -> x149, local copies, waits for them, and re-layouts: 11.7 us -> 10.8 us
where the time goes in v7:
time: 558 us; the launch traced here: 553 us
  Pallas kernels  301 us (54%)
  waiting for transfers between devices  95 us (17%)
  starting transfers between devices  68 us (12%)
  local copies, waits for them, and re-layouts  50.6 us (9%)
  other arithmetic  31 us (6%)
  between operations  6.61 us (1%)
    ppermute x95, waiting for transfers between devices, send(): return lax.ppermute(value, BOTH, route)  95 us
    ppermute x95, starting transfers between devices, send(): return lax.ppermute(value, BOTH, route)  68 us
    pallas_call x2, Pallas kernels, post(): pl.pallas_call(post_kernel, grid=(4,), in_specs=[SMEM, full, full, unit_s...  48.7 us
    pallas_call x2, Pallas kernels, attend_back_fast(): pl.pallas_call(attend_back_kernel, grid=(width // 128,), in_specs=[column...  41.1 us
    pallas_call x6, Pallas kernels, assemble(): pl.pallas_call(assemble_kernel, grid_spec=pltpu.PrefetchScalarGridSpec(nu...  34.9 us
    pallas_call x2, Pallas kernels, post_back(): pl.pallas_call(post_back_kernel, grid=(4,), in_specs=[full, full, thin, f...  33.3 us
    pallas_call x2, Pallas kernels, attend_fast(): pl.pallas_call(attend_kernel, grid=(width // 128,), in_specs=[column, key...  31.2 us
    pallas_call x2, Pallas kernels, feed_grad(): pl.pallas_call(functools.partial(feed_grad_kernel, x_first), grid=(8,), i...  25.4 us
  transfers between devices with their start and end apart: 95, of which 23 were waited for; matrix products, arithmetic and copies ran while one was open for 12% of the time, Pallas kernels for 41%

profile of v7, /device:TPU:0, one launch (start us, length us, event | category | flops | bytes accessed | tf_op | source)
XLA Modules:
  0.0 552.5 jit_solution(6482782255131996987)
XLA Ops:
  3.3 3.1 collective-permute-start
  7.9 2.6 slice_bitcast_fusion.1
  17.9 7.5 %collective-permute-start.3 = (bf16[456,768]{1,0:T(8,128)(2,1)}, bf16[456,768]{1,0:T(8,128)(2,1)}, u32[]{:S(2)}, u32[]{:S(2)}) collective-permute-start(bf16[456,768]{1,0:T(8,128)(2,1)} %pad_maximum_fusion.11), channel_id=1, source_target_pairs={{0,2},{1,3},{2,0},{3,1},{4,6},{5,7},{6,4},{7,5},{8,10},{9,11},{10,... | collective-permute-start | bytes 2101256 | tf_op jit(solution)/shard_map/ppermute | solution.py:441
  42.6 10.3 %collective-permute-done.7.refs_3_ = bf16[3,4,24,768]{3,2,1,0:T(8,128)(2,1)S(1)} collective-permute-done((bf16[3,4,24,768]{3,2,1,0:T(8,128)(2,1)}, bf16[3,4,24,768]{3,2,1,0:T(8,128)(2,1)S(1)}, u32[]{:S(2)}, u32[]{:S(2)}) %collective-permute-start.7) | collective-permute-done | bytes 442400 | tf_op jit(solution)/shard_map/ppermute | solution.py:441
  61.1 4.6 collective-permute-done.12.refs_4_
  65.7 9.6 %collective-permute-done.11 = bf16[544,768]{1,0:T(8,128)(2,1)} collective-permute-done((bf16[544,768]{1,0:T(8,128)(2,1)S(1)}, bf16[544,768]{1,0:T(8,128)(2,1)}, u32[]{:S(2)}, u32[]{:S(2)}) %collective-permute-start.11) | collective-permute-done | bytes 835616 | tf_op jit(solution)/shard_map/ppermute | solution.py:441
  78.6 5.8 %assemble.6 = bf16[4,4,2,4,24,768]{5,4,3,2,1,0:T(8,128)(2,1)} custom-call(s32[3]{0:T(128)} %pad_add_fusion.3.where_ref, bf16[4,4,24,768]{3,2,1,0:T(8,128)(2,1)} %pad_maximum_fusion.9.refs_0_, bf16[3,4,24,768]{3,2,1,0:T(8,128)(2,1)} %pad_maximum_fusion.12.refs_1_, bf16[3,4,24,768]{3,2,1,0:T(8,128)(2,1)} %collective-permute-done.6.refs_2_, ...), custom_call_target="tpu_custom_call" | custom-call | flops 300000000 | bytes 300000 | tf_op jit(solution)/shard_map/assemble/pallas_call | solution.py:538
  84.5 14.5 %collective-permute-done.17.refs_2_ = bf16[3,8,24,768]{3,2,1,0:T(8,128)(2,1)} collective-permute-done((bf16[3,8,24,768]{3,2,1,0:T(8,128)(2,1)S(1)}, bf16[3,8,24,768]{3,2,1,0:T(8,128)(2,1)}, u32[]{:S(2)}, u32[]{:S(2)}) %collective-permute-start.17) | collective-permute-done | bytes 884768 | tf_op jit(solution)/shard_map/ppermute | solution.py:441
  102.7 4.7 gather_rows.4.h_ref
  109.0 7.4 %project.2 = (bf16[512,768]{1,0:T(8,128)(2,1)}, bf16[2,512,768]{2,1,0:T(8,128)(2,1)}, bf16[512,384]{1,0:T(8,128)(2,1)}, bf16[512,384]{1,0:T(8,128)(2,1)}) custom-call(bf16[512,768]{1,0:T(8,128)(2,1)} %gather_rows.4.h_ref, bf16[4,768,768]{2,1,0:T(8,128)(2,1)} %bitcast.191, f32[12,768]{1,0:T(8,128)} %squeeze.50.vec_ref, bf16[2,768,384]{2,1,0:T(8,128)(2,1)} %fusion.sel_ref), custom_call_target="tpu_custom_call" | custom-call | flops 300000000 | bytes 300000 | tf_op jit(solution)/shard_map/project/pallas_call | solution.py:602
  125.0 15.4 %attend_forward.2 = (bf16[512,768]{1,0:T(8,128)(2,1)}, f32[768,512]{1,0:T(8,128)}, f32[6,2,512]{2,1,0:T(2,128)}) custom-call(bf16[512,768]{1,0:T(8,128)(2,1)} %get-tuple-element.196.q_ref, bf16[2,512,768]{2,1,0:T(8,128)(2,1)} %get-tuple-element.197.ka_ref.va_ref, bf16[2,512,768]{2,1,0:T(8,128)(2,1)} %copy-done.4, ...), custom_call_target="tpu_custom_call" | custom-call | flops 300000000 | bytes 300000 | tf_op jit(solution)/shard_map/attend_forward/pallas_call | solution.py:680
  150.1 5.8 %assemble.8 = bf16[4,2,4,4,24,768]{5,4,3,2,1,0:T(8,128)(2,1)} custom-call(s32[3]{0:T(128)} %pad_add_fusion.3.where_ref, bf16[4,8,24,768]{3,2,1,0:T(8,128)(2,1)} %copy-done, bf16[3,8,24,768]{3,2,1,0:T(8,128)(2,1)} %copy-done.2, bf16[3,8,24,768]{3,2,1,0:T(8,128)(2,1)} %collective-permute-done.17.refs_2_, ...), custom_call_target="tpu_custom_call" | custom-call | flops 300000000 | bytes 300000 | tf_op jit(solution)/shard_map/assemble/pallas_call | solution.py:538
  155.9 6.0 %assemble.7 = bf16[4,4,2,4,24,768]{5,4,3,2,1,0:T(8,128)(2,1)} custom-call(s32[3]{0:T(128)} %pad_add_fusion.3.where_ref, bf16[4,8,24,768]{3,2,1,0:T(8,128)(2,1)} %copy-done, bf16[3,8,24,768]{3,2,1,0:T(8,128)(2,1)} %copy-done.2, bf16[3,8,24,768]{3,2,1,0:T(8,128)(2,1)} %collective-permute-done.17.refs_2_, ...), custom_call_target="tpu_custom_call" | custom-call | flops 300000000 | bytes 300000 | tf_op jit(solution)/shard_map/assemble/pallas_call | solution.py:538
  170.7 24.2 %post.2 = (f32[512,768]{1,0:T(8,128)}, bf16[512,768]{1,0:T(8,128)(2,1)}, f32[512,768]{1,0:T(8,128)}, f32[512,1]{1,0:T(8,128)}, f32[512,768]{1,0:T(8,128)}, /*ind...) custom-call(s32[3]{0:T(128)} %pad_add_fusion.3.where_ref, ...), custom_call_target="tpu_custom_call" | custom-call | flops 300000000 | bytes 300000 | tf_op jit(solution)/shard_map/post/pallas_call | solution.py:859
  199.2 5.8 %assemble.9 = bf16[4,4,2,4,24,768]{5,4,3,2,1,0:T(8,128)(2,1)} custom-call(s32[3]{0:T(128)} %pad_add_fusion.3.where_ref, bf16[4,4,24,768]{3,2,1,0:T(8,128)(2,1)} %pad_maximum_fusion.10.refs_0_, bf16[3,4,24,768]{3,2,1,0:T(8,128)(2,1)} %copy-done.24, bf16[3,4,24,768]{3,2,1,0:T(8,128)(2,1)} %collective-permute-done.23.refs_2_, ...), custom_call_target="tpu_custom_call" | custom-call | flops 300000000 | bytes 300000 | tf_op jit(solution)/shard_map/assemble/pallas_call | solution.py:538
  205.0 7.4 %project.3 = (bf16[512,768]{1,0:T(8,128)(2,1)}, bf16[2,512,768]{2,1,0:T(8,128)(2,1)}, bf16[512,384]{1,0:T(8,128)(2,1)}, bf16[512,384]{1,0:T(8,128)(2,1)}) custom-call(bf16[512,768]{1,0:T(8,128)(2,1)} %get-tuple-element.207.h_ref, bf16[4,768,768]{2,1,0:T(8,128)(2,1)} %bitcast.195, f32[12,768]{1,0:T(8,128)} %squeeze.51.vec_ref, bf16[2,768,384]{2,1,0:T(8,128)(2,1)} %fusion.sel_ref), custom_call_target="tpu_custom_call" | custom-call | flops 300000000 | bytes 300000 | tf_op jit(solution)/shard_map/project/pallas_call | solution.py:602
  214.9 4.7 gather_rows.5.e_ref
  220.8 15.8 %attend_forward.3 = (bf16[512,768]{1,0:T(8,128)(2,1)}, f32[768,512]{1,0:T(8,128)}, f32[6,2,512]{2,1,0:T(2,128)}) custom-call(bf16[512,768]{1,0:T(8,128)(2,1)} %get-tuple-element.212.q_ref, bf16[2,512,768]{2,1,0:T(8,128)(2,1)} %get-tuple-element.213.ka_ref.va_ref, bf16[2,512,768]{2,1,0:T(8,128)(2,1)} %copy-done.5, ...), custom_call_target="tpu_custom_call" | custom-call | flops 300000000 | bytes 300000 | tf_op jit(solution)/shard_map/attend_forward/pallas_call | solution.py:680
  240.1 5.8 %assemble.11 = bf16[4,2,4,4,24,768]{5,4,3,2,1,0:T(8,128)(2,1)} custom-call(s32[3]{0:T(128)} %pad_add_fusion.3.where_ref, bf16[4,8,24,768]{3,2,1,0:T(8,128)(2,1)} %copy-done.1, bf16[3,8,24,768]{3,2,1,0:T(8,128)(2,1)} %copy-done.3, bf16[3,8,24,768]{3,2,1,0:T(8,128)(2,1)} %copy-done.12, bf16[3,8,24,768]{3,2,1,0:T(8,128)(2,1)} %collective-permute-done.39.refs_3_, ...), custom_call_target="tpu_custom_call" | custom-call | flops 300000000 | bytes 300000 | tf_op jit(solution)/shard_map/assemble/pallas_call | solution.py:538
  245.9 5.7 %assemble.10 = bf16[4,4,2,4,24,768]{5,4,3,2,1,0:T(8,128)(2,1)} custom-call(s32[3]{0:T(128)} %pad_add_fusion.3.where_ref, bf16[4,8,24,768]{3,2,1,0:T(8,128)(2,1)} %copy-done.1, bf16[3,8,24,768]{3,2,1,0:T(8,128)(2,1)} %copy-done.3, bf16[3,8,24,768]{3,2,1,0:T(8,128)(2,1)} %copy-done.12, bf16[3,8,24,768]{3,2,1,0:T(8,128)(2,1)} %collective-permute-done.39.refs_3_, ...), custom_call_target="tpu_custom_call" | custom-call | flops 300000000 | bytes 300000 | tf_op jit(solution)/shard_map/assemble/pallas_call | solution.py:538
  251.6 24.4 %post.3 = (f32[512,768]{1,0:T(8,128)}, bf16[512,768]{1,0:T(8,128)(2,1)}, f32[512,768]{1,0:T(8,128)}, f32[512,1]{1,0:T(8,128)}, f32[512,768]{1,0:T(8,128)}, /*ind...) custom-call(s32[3]{0:T(128)} %pad_add_fusion.3.where_ref, ...), custom_call_target="tpu_custom_call" | custom-call | flops 300000000 | bytes 300000 | tf_op jit(solution)/shard_map/post/pallas_call | solution.py:859
  276.1 16.5 %post_back.2 = (bf16[6,512,768]{2,1,0:T(8,128)(2,1)}, bf16[512,768]{1,0:T(8,128)(2,1)}, f32[512,768]{1,0:T(8,128)}, f32[12,768]{1,0:T(8,128)}) custom-call(bf16[512,768]{1,0:T(8,128)(2,1)} %gather_rows.5.e_ref, f32[512,768]{1,0:T(8,128)} %get-tuple-element.223.n1_ref, f32[512,1]{1,0:T(8,128)} %get-tuple-element.224.t1_ref, ...), custom_call_target="tpu_custom_call" | custom-call | flops 16000000000 | bytes 16000000 | tf_op jit(solution)/shard_map/post_back/pallas_call | solution.py:953
  294.3 20.6 %attend_backward.2 = (bf16[512,768]{1,0:T(8,128)(2,1)}, f32[2,512,768]{2,1,0:T(8,128)}, bf16[2,512,768]{2,1,0:T(8,128)(2,1)}) custom-call(bf16[512,768]{1,0:T(8,128)(2,1)} %get-tuple-element.212.q_ref, bf16[512,768]{1,0:T(8,128)(2,1)} %get-tuple-element.229.g_ref, bf16[2,512,768]{2,1,0:T(8,128)(2,1)} %get-tuple-element.213.ka_ref.va_ref, ...), custom_call_target="tpu_custom_call" | custom-call | flops 20999999488 | bytes 21000000 | tf_op jit(solution)/shard_map/attend_backward/pallas_call | solution.py:749
  316.7 12.5 %feed_grad.2 = (bf16[4,2,4,24,768]{4,3,2,1,0:T(8,128)(2,1)}, bf16[4,2,4,24,768]{4,3,2,1,0:T(8,128)(2,1)}, bf16[4,2,4,24,768]{4,3,2,1,0:T(8,128)(2,1)}, bf16[4,2,4,24,768]{4,3,2,1,0:T(8,128)(2,1)}) custom-call(s32[2]{0:T(128)} %pad_add_fusion.4.bit_ref, bf16[6,512,384]{2,1,0:T(8,128)(2,1)} %get-tuple-element.219.ym_ref.gm_ref.om_ref, ...), custom_call_target="tpu_custom_call" | custom-call | flops 12000000000 | bytes 12000000 | tf_op jit(solution)/shard_map/feed_grad/pallas_call | solution.py:1142
  332.4 9.2 %project_back.2 = (bf16[3,512,768]{2,1,0:T(8,128)(2,1)}, f32[512,768]{1,0:T(8,128)}, bf16[512,768]{1,0:T(8,128)(2,1)}, f32[2,768]{1,0:T(2,128)}) custom-call(bf16[512,768]{1,0:T(8,128)(2,1)} %get-tuple-element.232.dq_ref, f32[2,512,768]{2,1,0:T(8,128)} %get-tuple-element.237.own_ref, bf16[2,512,768]{2,1,0:T(8,128)(2,1)} %collective-permute-done.53.got_ref, ...), custom_call_target="tpu_custom_call" | custom-call | flops 500000000 | bytes 500000 | tf_op jit(solution)/shard_map/project_back/pallas_call | solution.py:1013
  342.5 4.7 gather_rows.6
  347.2 16.9 %post_back.3 = (bf16[6,512,768]{2,1,0:T(8,128)(2,1)}, bf16[512,768]{1,0:T(8,128)(2,1)}, f32[512,768]{1,0:T(8,128)}, f32[12,768]{1,0:T(8,128)}) custom-call(f32[512,768]{1,0:T(8,128)} %get-tuple-element.247.e_ref, f32[512,768]{1,0:T(8,128)} %get-tuple-element.248.n1_ref, f32[512,1]{1,0:T(8,128)} %get-tuple-element.249.t1_ref, ...), custom_call_target="tpu_custom_call" | custom-call | flops 500000000 | bytes 500000 | tf_op jit(solution)/shard_map/post_back/pallas_call | solution.py:953
  366.1 3.6 halve_sum.4
  372.3 20.6 %attend_backward.3 = (bf16[512,768]{1,0:T(8,128)(2,1)}, f32[2,512,768]{2,1,0:T(8,128)}, bf16[2,512,768]{2,1,0:T(8,128)(2,1)}) custom-call(bf16[512,768]{1,0:T(8,128)(2,1)} %get-tuple-element.196.q_ref, bf16[512,768]{1,0:T(8,128)(2,1)} %get-tuple-element.260.g_ref, bf16[2,512,768]{2,1,0:T(8,128)(2,1)} %get-tuple-element.197.ka_ref.va_ref, ...), custom_call_target="tpu_custom_call" | custom-call | flops 44999999488 | bytes 45000000 | tf_op jit(solution)/shard_map/attend_backward/pallas_call | solution.py:749
  393.3 7.6 %front_grad.2 = (bf16[4,2,2,24,768]{4,3,2,1,0:T(8,128)(2,1)}, bf16[4,2,2,24,768]{4,3,2,1,0:T(8,128)(2,1)}, bf16[4,2,2,24,768]{4,3,2,1,0:T(8,128)(2,1)}, bf16[4,2,2,24,768]{4,3,2,1,0:T(8,128)(2,1)}) custom-call(s32[2]{0:T(128)} %pad_add_fusion.4.bit_ref, bf16[512,384]{1,0:T(8,128)(2,1)} %get-tuple-element.267.xm_ref, bf16[512,384]{1,0:T(8,128)(2,1)} %copy-done.49, ...), custom_call_target="tpu_custom_call" | custom-call | flops 500000000 | bytes 500000 | tf_op jit(solution)/shard_map/front_grad/pallas_call | solution.py:1093
  403.8 12.9 %feed_grad.3 = (bf16[4,2,4,24,768]{4,3,2,1,0:T(8,128)(2,1)}, bf16[4,2,4,24,768]{4,3,2,1,0:T(8,128)(2,1)}, bf16[4,2,4,24,768]{4,3,2,1,0:T(8,128)(2,1)}, bf16[4,2,4,24,768]{4,3,2,1,0:T(8,128)(2,1)}) custom-call(s32[2]{0:T(128)} %pad_add_fusion.4.bit_ref, bf16[6,512,384]{2,1,0:T(8,128)(2,1)} %get-tuple-element.273.ym_ref.gm_ref.om_ref, ...), custom_call_target="tpu_custom_call" | custom-call | flops 12000000000 | bytes 12000000 | tf_op jit(solution)/shard_map/feed_grad/pallas_call | solution.py:1142
  419.0 2.6 halve_sum.5
  423.0 9.5 %project_back.3 = (bf16[3,512,768]{2,1,0:T(8,128)(2,1)}, f32[512,768]{1,0:T(8,128)}, bf16[512,768]{1,0:T(8,128)(2,1)}, f32[2,768]{1,0:T(2,128)}) custom-call(bf16[512,768]{1,0:T(8,128)(2,1)} %get-tuple-element.263.dq_ref, f32[2,512,768]{2,1,0:T(8,128)} %get-tuple-element.264.own_ref, bf16[2,512,768]{2,1,0:T(8,128)(2,1)} %collective-permute-done.57.got_ref, ...), custom_call_target="tpu_custom_call" | custom-call | flops 500000000 | bytes 500000 | tf_op jit(solution)/shard_map/project_back/pallas_call | solution.py:1013
  434.6 9.9 %collective-permute-done.67.got_x = bf16[4,2,4,24,768]{4,3,2,1,0:T(8,128)(2,1)} collective-permute-done((bf16[4,2,4,24,768]{4,3,2,1,0:T(8,128)(2,1)}, bf16[4,2,4,24,768]{4,3,2,1,0:T(8,128)(2,1)}, u32[]{:S(2)}, u32[]{:S(2)}) %collective-permute-start.67) | collective-permute-done | bytes 1179680 | tf_op jit(solution)/shard_map/ppermute | solution.py:441
  444.8 3.6 halve_sum.6
  448.4 7.7 %front_grad.3 = (bf16[4,2,2,24,768]{4,3,2,1,0:T(8,128)(2,1)}, bf16[4,2,2,24,768]{4,3,2,1,0:T(8,128)(2,1)}, bf16[4,2,2,24,768]{4,3,2,1,0:T(8,128)(2,1)}, bf16[4,2,2,24,768]{4,3,2,1,0:T(8,128)(2,1)}) custom-call(s32[2]{0:T(128)} %pad_add_fusion.4.bit_ref, bf16[512,384]{1,0:T(8,128)(2,1)} %get-tuple-element.288.xm_ref, bf16[512,384]{1,0:T(8,128)(2,1)} %copy-done.48, ...), custom_call_target="tpu_custom_call" | custom-call | flops 500000000 | bytes 500000 | tf_op jit(solution)/shard_map/front_grad/pallas_call | solution.py:1093
  465.2 4.7 gather_rows.7
  469.9 11.3 %collective-permute-done.74 = bf16[2,2,6,24,768]{4,3,2,1,0:T(8,128)(2,1)} collective-permute-done((bf16[2,2,6,24,768]{4,3,2,1,0:T(8,128)(2,1)}, bf16[2,2,6,24,768]{4,3,2,1,0:T(8,128)(2,1)}, u32[]{:S(2)}, u32[]{:S(2)}) %collective-permute-start.74) | collective-permute-done | bytes 884768 | tf_op jit(solution)/shard_map/ppermute | solution.py:441
  488.8 2.6 halve_sum.7
  492.5 3.0 collective-permute-done.76
  500.8 8.1 %collective-permute-start.80 = (bf16[2,2,4,24,768]{4,3,2,1,0:T(8,128)(2,1)S(1)}, bf16[2,2,4,24,768]{4,3,2,1,0:T(8,128)(2,1)S(1)}, u32[]{:S(2)}, u32[]{:S(2)}) collective-permute-start(bf16[2,2,4,24,768]{4,3,2,1,0:T(8,128)(2,1)S(1)} %select_bitcast_fusion.1), channel_id=1, source_target_pairs={{0,2},{1,3},{2,0},{3,1},{4,6},{5,7},{6,4},{7,5},{8,10},{9,11},{10,... | collective-permute-start | bytes 1769480 | tf_op jit(solution)/shard_map/ppermute | solution.py:441
  511.3 3.3 unpack.2
  514.5 8.3 %collective-permute-done.80 = bf16[2,2,4,24,768]{4,3,2,1,0:T(8,128)(2,1)S(1)} collective-permute-done((bf16[2,2,4,24,768]{4,3,2,1,0:T(8,128)(2,1)S(1)}, bf16[2,2,4,24,768]{4,3,2,1,0:T(8,128)(2,1)S(1)}, u32[]{:S(2)}, u32[]{:S(2)}) %collective-permute-start.80) | collective-permute-done | bytes 589856 | tf_op jit(solution)/shard_map/ppermute | solution.py:441
  523.0 3.1 collective-permute-done.87
  533.7 2.8 collective-permute-done.86
  536.7 2.9 collective-permute-done.90
  545.4 2.7 collective-permute-done.89.refs_3_
  548.9 3.2 unpack.3
  (472 shorter events, 140.2 us)
Async XLA Ops:
  7.3 33.6 %collective-permute-start.8 = (bf16[4,4,24,768]{3,2,1,0:T(8,128)(2,1)}, bf16[4,4,24,768]{3,2,1,0:T(8,128)(2,1)}, u32[]{:S(2)}, u32[]{:S(2)}) collective-permute-start(bf16[4,4,24,768]{3,2,1,0:T(8,128)(2,1)} %pad_maximum_fusion.9.refs_0_), channel_id=1, source_target_pairs={{0,1},{1,0},{2,3},{3,2},{4,5},{5,4},{6,7},{7,6},{8,9},{9,8},{10,11... | collective-permute-start | bytes 1769480 | tf_op jit(solution)/shard_map/ppermute | solution.py:441
  17.9 24.5 %collective-permute-start.3 = (bf16[456,768]{1,0:T(8,128)(2,1)}, bf16[456,768]{1,0:T(8,128)(2,1)}, u32[]{:S(2)}, u32[]{:S(2)}) collective-permute-start(bf16[456,768]{1,0:T(8,128)(2,1)} %pad_maximum_fusion.11), channel_id=1, source_target_pairs={{0,2},{1,3},{2,0},{3,1},{4,6},{5,7},{6,4},{7,5},{8,10},{9,11},{10,... | collective-permute-start | bytes 2101256 | tf_op jit(solution)/shard_map/ppermute | solution.py:441
  26.0 29.7 %collective-permute-start.4 = (bf16[456,768]{1,0:T(8,128)(2,1)}, bf16[456,768]{1,0:T(8,128)(2,1)}, u32[]{:S(2)}, u32[]{:S(2)}) collective-permute-start(bf16[456,768]{1,0:T(8,128)(2,1)} %pad_maximum_fusion.11), channel_id=1, source_target_pairs={{2,4},{3,5},{4,2},{5,3},{10,12},{11,13},{12,10},{13,11},{18,20},{1... | collective-permute-start | bytes 2101256 | tf_op jit(solution)/shard_map/ppermute | solution.py:441
  54.4 20.8 %collective-permute-start.11 = (bf16[544,768]{1,0:T(8,128)(2,1)S(1)}, bf16[544,768]{1,0:T(8,128)(2,1)}, u32[]{:S(2)}, u32[]{:S(2)}) collective-permute-start(bf16[544,768]{1,0:T(8,128)(2,1)S(1)} %pad_maximum_fusion.8), channel_id=1, source_target_pairs={{0,2},{1,3},{2,0},{3,1},{4,6},{5,7},{6,4},{7,5},{8,10},{9,11},{10,... | collective-permute-start | bytes 2506760 | tf_op jit(solution)/shard_map/ppermute | solution.py:441
  58.3 40.9 %collective-permute-start.10 = (bf16[4,264,768]{2,1,0:T(8,128)(2,1)}, bf16[4,264,768]{2,1,0:T(8,128)(2,1)}, u32[]{:S(2)}, u32[]{:S(2)}) collective-permute-start(bf16[4,264,768]{2,1,0:T(8,128)(2,1)} %pad_maximum_fusion.2.refs_0_), channel_id=1, source_target_pairs={{0,1},{1,0},{2,3},{3,2},{4,5},{5,4},{6,7},{7,6},{8,9},{9,8},{10,11... | collective-permute-start | bytes 4866056 | tf_op jit(solution)/shard_map/ppermute | solution.py:441
  61.0 23.4 %collective-permute-start.19 = (bf16[4,8,24,768]{3,2,1,0:T(8,128)(2,1)S(1)}, bf16[4,8,24,768]{3,2,1,0:T(8,128)(2,1)}, u32[]{:S(2)}, u32[]{:S(2)}) collective-permute-start(bf16[4,8,24,768]{3,2,1,0:T(8,128)(2,1)S(1)} %pad_maximum_fusion.4.refs_0_), channel_id=1, source_target_pairs={{0,1},{1,0},{2,3},{3,2},{4,5},{5,4},{6,7},{7,6},{8,9},{9,8},{10,11... | collective-permute-start | bytes 3538952 | tf_op jit(solution)/shard_map/ppermute | solution.py:441
  76.8 22.2 %collective-permute-start.17 = (bf16[3,8,24,768]{3,2,1,0:T(8,128)(2,1)S(1)}, bf16[3,8,24,768]{3,2,1,0:T(8,128)(2,1)}, u32[]{:S(2)}, u32[]{:S(2)}) collective-permute-start(bf16[3,8,24,768]{3,2,1,0:T(8,128)(2,1)S(1)} %pad_maximum_fusion.6.refs_1_), channel_id=1, source_target_pairs={{0,8},{1,9},{2,10},{3,11},{4,12},{5,13},{6,14},{7,15},{8,0},{9,1},... | collective-permute-start | bytes 2654216 | tf_op jit(solution)/shard_map/ppermute | solution.py:441
  77.3 21.9 %collective-permute-start.18 = (bf16[3,8,24,768]{3,2,1,0:T(8,128)(2,1)S(1)}, bf16[3,8,24,768]{3,2,1,0:T(8,128)(2,1)}, u32[]{:S(2)}, u32[]{:S(2)}) collective-permute-start(bf16[3,8,24,768]{3,2,1,0:T(8,128)(2,1)S(1)} %pad_maximum_fusion.6.refs_1_), channel_id=1, source_target_pairs={{0,16},{1,17},{2,18},{3,19},{4,20},{5,21},{6,22},{7,23},{8,24},{9,... | collective-permute-start | bytes 2654216 | tf_op jit(solution)/shard_map/ppermute | solution.py:441
  77.8 21.4 %collective-permute-start.20 = (bf16[3,8,24,768]{3,2,1,0:T(8,128)(2,1)S(1)}, bf16[3,8,24,768]{3,2,1,0:T(8,128)(2,1)S(1)}, u32[]{:S(2)}, u32[]{:S(2)}) collective-permute-start(bf16[3,8,24,768]{3,2,1,0:T(8,128)(2,1)S(1)} %pad_maximum_fusion.6.refs_1_), channel_id=1, source_target_pairs={{0,1},{1,0},{2,3},{3,2},{4,5},{5,4},{6,7},{7,6},{8,9},{9,8},{10,11... | collective-permute-start | bytes 2654216 | tf_op jit(solution)/shard_map/ppermute | solution.py:441
  84.4 23.1 %collective-permute-start.16 = (bf16[544,768]{1,0:T(8,128)(2,1)}, bf16[544,768]{1,0:T(8,128)(2,1)S(1)}, u32[]{:S(2)}, u32[]{:S(2)}) collective-permute-start(bf16[544,768]{1,0:T(8,128)(2,1)} %copy-done.23), channel_id=1, source_target_pairs={{2,4},{3,5},{4,2},{5,3},{10,12},{11,13},{12,10},{13,11},{18,20},{1... | collective-permute-start | bytes 2506760 | tf_op jit(solution)/shard_map/ppermute | solution.py:441
  117.6 22.9 %collective-permute-start.28 = (bf16[3,8,24,768]{3,2,1,0:T(8,128)(2,1)}, bf16[3,8,24,768]{3,2,1,0:T(8,128)(2,1)}, u32[]{:S(2)}, u32[]{:S(2)}) collective-permute-start(bf16[3,8,24,768]{3,2,1,0:T(8,128)(2,1)} %collective-permute-done.17.refs_2_), channel_id=1, source_target_pairs={{0,1},{1,0},{2,3},{3,2},{4,5},{5,4},{6,7},{7,6},{8,9},{9,8},{10,11... | collective-permute-start | bytes 2654216 | tf_op jit(solution)/shard_map/ppermute | solution.py:441
  118.1 22.3 %collective-permute-start.27 = (bf16[3,8,24,768]{3,2,1,0:T(8,128)(2,1)}, bf16[3,8,24,768]{3,2,1,0:T(8,128)(2,1)}, u32[]{:S(2)}, u32[]{:S(2)}) collective-permute-start(bf16[3,8,24,768]{3,2,1,0:T(8,128)(2,1)} %collective-permute-done.18.refs_3_), channel_id=1, source_target_pairs={{0,8},{1,9},{2,10},{3,11},{4,12},{5,13},{6,14},{7,15},{8,0},{9,1},... | collective-permute-start | bytes 2654216 | tf_op jit(solution)/shard_map/ppermute | solution.py:441
  119.6 20.9 %collective-permute-start.29 = (bf16[3,8,24,768]{3,2,1,0:T(8,128)(2,1)}, bf16[3,8,24,768]{3,2,1,0:T(8,128)(2,1)}, u32[]{:S(2)}, u32[]{:S(2)}) collective-permute-start(bf16[3,8,24,768]{3,2,1,0:T(8,128)(2,1)} %collective-permute-done.18.refs_3_), channel_id=1, source_target_pairs={{0,1},{1,0},{2,3},{3,2},{4,5},{5,4},{6,7},{7,6},{8,9},{9,8},{10,11... | collective-permute-start | bytes 2654216 | tf_op jit(solution)/shard_map/ppermute | solution.py:441
  121.4 22.6 %collective-permute-start.22 = (bf16[544,768]{1,0:T(8,128)(2,1)}, bf16[544,768]{1,0:T(8,128)(2,1)}, u32[]{:S(2)}, u32[]{:S(2)}) collective-permute-start(bf16[544,768]{1,0:T(8,128)(2,1)} %collective-permute-done.11), channel_id=1, source_target_pairs={{2,4},{3,5},{4,2},{5,3},{10,12},{11,13},{12,10},{13,11},{18,20},{1... | collective-permute-start | bytes 2506760 | tf_op jit(solution)/shard_map/ppermute | solution.py:441
  123.8 22.9 %collective-permute-start.25 = (bf16[4,4,24,768]{3,2,1,0:T(8,128)(2,1)}, bf16[4,4,24,768]{3,2,1,0:T(8,128)(2,1)}, u32[]{:S(2)}, u32[]{:S(2)}) collective-permute-start(bf16[4,4,24,768]{3,2,1,0:T(8,128)(2,1)} %pad_maximum_fusion.10.refs_0_), channel_id=1, source_target_pairs={{0,1},{1,0},{2,3},{3,2},{4,5},{5,4},{6,7},{7,6},{8,9},{9,8},{10,11... | collective-permute-start | bytes 1769480 | tf_op jit(solution)/shard_map/ppermute | solution.py:441
  140.4 24.8 %collective-permute-start.35 = (bf16[4,8,24,768]{3,2,1,0:T(8,128)(2,1)S(1)}, bf16[4,8,24,768]{3,2,1,0:T(8,128)(2,1)S(1)}, u32[]{:S(2)}, u32[]{:S(2)}) collective-permute-start(bf16[4,8,24,768]{3,2,1,0:T(8,128)(2,1)S(1)} %pad_maximum_fusion.5.refs_0_), channel_id=1, source_target_pairs={{0,1},{1,0},{2,3},{3,2},{4,5},{5,4},{6,7},{7,6},{8,9},{9,8},{10,11... | collective-permute-start | bytes 3538952 | tf_op jit(solution)/shard_map/ppermute | solution.py:441
  149.1 21.6 %collective-permute-start.32 = (bf16[4,256,768]{2,1,0:T(8,128)(2,1)}, bf16[4,256,768]{2,1,0:T(8,128)(2,1)}, u32[]{:S(2)}, u32[]{:S(2)}) collective-permute-start(bf16[4,256,768]{2,1,0:T(8,128)(2,1)} %pad_maximum_fusion.3.refs_0_), channel_id=1, source_target_pairs={{0,1},{1,0},{2,3},{3,2},{4,5},{5,4},{6,7},{7,6},{8,9},{9,8},{10,11... | collective-permute-start | bytes 4718600 | tf_op jit(solution)/shard_map/ppermute | solution.py:441
  165.2 29.8 %collective-permute-start.38 = (bf16[3,8,24,768]{3,2,1,0:T(8,128)(2,1)S(1)}, bf16[3,8,24,768]{3,2,1,0:T(8,128)(2,1)S(1)}, u32[]{:S(2)}, u32[]{:S(2)}) collective-permute-start(bf16[3,8,24,768]{3,2,1,0:T(8,128)(2,1)S(1)} %pad_maximum_fusion.7.refs_1_), channel_id=1, source_target_pairs={{0,8},{1,9},{2,10},{3,11},{4,12},{5,13},{6,14},{7,15},{8,0},{9,1},... | collective-permute-start | bytes 2654216 | tf_op jit(solution)/shard_map/ppermute | solution.py:441
  166.1 28.9 %collective-permute-start.39 = (bf16[3,8,24,768]{3,2,1,0:T(8,128)(2,1)S(1)}, bf16[3,8,24,768]{3,2,1,0:T(8,128)(2,1)}, u32[]{:S(2)}, u32[]{:S(2)}) collective-permute-start(bf16[3,8,24,768]{3,2,1,0:T(8,128)(2,1)S(1)} %pad_maximum_fusion.7.refs_1_), channel_id=1, source_target_pairs={{0,16},{1,17},{2,18},{3,19},{4,20},{5,21},{6,22},{7,23},{8,24},{9,... | collective-permute-start | bytes 2654216 | tf_op jit(solution)/shard_map/ppermute | solution.py:441
  169.6 26.8 %collective-permute-start.37 = (bf16[3,4,24,768]{3,2,1,0:T(8,128)(2,1)}, bf16[3,4,24,768]{3,2,1,0:T(8,128)(2,1)}, u32[]{:S(2)}, u32[]{:S(2)}) collective-permute-start(bf16[3,4,24,768]{3,2,1,0:T(8,128)(2,1)} %collective-permute-done.24.refs_3_), channel_id=1, source_target_pairs={{0,8},{1,9},{2,10},{3,11},{4,12},{5,13},{6,14},{7,15},{8,0},{9,1},... | collective-permute-start | bytes 1327112 | tf_op jit(solution)/shard_map/ppermute | solution.py:441
  212.5 24.2 %collective-permute-start.48 = (bf16[6,512,384]{2,1,0:T(8,128)(2,1)}, bf16[6,512,384]{2,1,0:T(8,128)(2,1)}, u32[]{:S(2)}, u32[]{:S(2)}) collective-permute-start(bf16[6,512,384]{2,1,0:T(8,128)(2,1)} %get-tuple-element.221), channel_id=1, source_target_pairs={{0,1},{1,0},{2,3},{3,2},{4,5},{5,4},{6,7},{7,6},{8,9},{9,8},{10,11... | collective-permute-start | bytes 7077896 | tf_op jit(solution)/shard_map/ppermute | solution.py:441
  212.9 23.7 %collective-permute-start.42 = (bf16[3,8,24,768]{3,2,1,0:T(8,128)(2,1)S(1)}, bf16[3,8,24,768]{3,2,1,0:T(8,128)(2,1)S(1)}, u32[]{:S(2)}, u32[]{:S(2)}) collective-permute-start(bf16[3,8,24,768]{3,2,1,0:T(8,128)(2,1)S(1)} %copy-done.13), channel_id=1, source_target_pairs={{0,16},{1,17},{2,18},{3,19},{4,20},{5,21},{6,22},{7,23},{8,24},{9,... | collective-permute-start | bytes 2654216 | tf_op jit(solution)/shard_map/ppermute | solution.py:441
  214.4 22.2 %collective-permute-start.43 = (bf16[3,8,24,768]{3,2,1,0:T(8,128)(2,1)S(1)}, bf16[3,8,24,768]{3,2,1,0:T(8,128)(2,1)}, u32[]{:S(2)}, u32[]{:S(2)}) collective-permute-start(bf16[3,8,24,768]{3,2,1,0:T(8,128)(2,1)S(1)} %copy-done.13), channel_id=1, source_target_pairs={{0,1},{1,0},{2,3},{3,2},{4,5},{5,4},{6,7},{7,6},{8,9},{9,8},{10,11... | collective-permute-start | bytes 2654216 | tf_op jit(solution)/shard_map/ppermute | solution.py:441
  214.4 22.2 %collective-permute-start.44 = (bf16[3,8,24,768]{3,2,1,0:T(8,128)(2,1)}, bf16[3,8,24,768]{3,2,1,0:T(8,128)(2,1)}, u32[]{:S(2)}, u32[]{:S(2)}) collective-permute-start(bf16[3,8,24,768]{3,2,1,0:T(8,128)(2,1)} %collective-permute-done.39.refs_3_), channel_id=1, source_target_pairs={{0,1},{1,0},{2,3},{3,2},{4,5},{5,4},{6,7},{7,6},{8,9},{9,8},{10,11... | collective-permute-start | bytes 2654216 | tf_op jit(solution)/shard_map/ppermute | solution.py:441
  292.5 22.8 %collective-permute-start.49 = (bf16[6,512,768]{2,1,0:T(8,128)(2,1)}, bf16[6,512,768]{2,1,0:T(8,128)(2,1)}, u32[]{:S(2)}, u32[]{:S(2)}) collective-permute-start(bf16[6,512,768]{2,1,0:T(8,128)(2,1)} %get-tuple-element.228.dz_ref.df_ref.da_ref), channel_id=1, source_target_pairs={{0,1},{1,0},{2,3},{3,2},{4,5},{5,4},{6,7},{7,6},{8,9},{9,8},{10,11... | collective-permute-start | bytes 14155784 | tf_op jit(solution)/shard_map/ppermute | solution.py:441
  292.7 22.6 %collective-permute-start.47 = (bf16[6,512,384]{2,1,0:T(8,128)(2,1)}, bf16[6,512,384]{2,1,0:T(8,128)(2,1)S(1)}, u32[]{:S(2)}, u32[]{:S(2)}) collective-permute-start(bf16[6,512,384]{2,1,0:T(8,128)(2,1)} %get-tuple-element.220), channel_id=1, source_target_pairs={{0,1},{1,0},{2,3},{3,2},{4,5},{5,4},{6,7},{7,6},{8,9},{9,8},{10,11... | collective-permute-start | bytes 7077896 | tf_op jit(solution)/shard_map/ppermute | solution.py:441
  293.6 21.2 %collective-permute-start.50 = (bf16[512,384]{1,0:T(8,128)(2,1)}, bf16[512,384]{1,0:T(8,128)(2,1)S(1)}, u32[]{:S(2)}, u32[]{:S(2)}) collective-permute-start(bf16[512,384]{1,0:T(8,128)(2,1)} %get-tuple-element.233), channel_id=1, source_target_pairs={{0,1},{1,0},{2,3},{3,2},{4,5},{5,4},{6,7},{7,6},{8,9},{9,8},{10,11... | collective-permute-start | bytes 1179656 | tf_op jit(solution)/shard_map/ppermute | solution.py:441
  293.7 21.6 %collective-permute-start.51 = (bf16[512,768]{1,0:T(8,128)(2,1)S(1)}, bf16[512,768]{1,0:T(8,128)(2,1)}, u32[]{:S(2)}, u32[]{:S(2)}) collective-permute-start(bf16[512,768]{1,0:T(8,128)(2,1)S(1)} %copy-done.33), channel_id=1, source_target_pairs={{0,1},{1,0},{2,3},{3,2},{4,5},{5,4},{6,7},{7,6},{8,9},{9,8},{10,11... | collective-permute-start | bytes 2359304 | tf_op jit(solution)/shard_map/ppermute | solution.py:441
  294.1 36.5 %collective-permute-start.46 = (bf16[512,768]{1,0:T(8,128)(2,1)S(1)}, bf16[512,768]{1,0:T(8,128)(2,1)}, u32[]{:S(2)}, u32[]{:S(2)}) collective-permute-start(bf16[512,768]{1,0:T(8,128)(2,1)S(1)} %copy-done.33), channel_id=1, source_target_pairs={{2,4},{3,5},{4,2},{5,3},{10,12},{11,13},{12,10},{13,11},{18,20},{1... | collective-permute-start | bytes 2359304 | tf_op jit(solution)/shard_map/ppermute | solution.py:441
  314.9 17.5 %collective-permute-start.53 = (bf16[2,512,768]{2,1,0:T(8,128)(2,1)}, bf16[2,512,768]{2,1,0:T(8,128)(2,1)}, u32[]{:S(2)}, u32[]{:S(2)}) collective-permute-start(bf16[2,512,768]{2,1,0:T(8,128)(2,1)} %get-tuple-element.238), channel_id=1, source_target_pairs={{0,1},{1,0},{2,3},{3,2},{4,5},{5,4},{6,7},{7,6},{8,9},{9,8},{10,11... | collective-permute-start | bytes 4718600 | tf_op jit(solution)/shard_map/ppermute | solution.py:441
  329.2 37.0 %collective-permute-start.55 = (bf16[4,2,4,24,768]{4,3,2,1,0:T(8,128)(2,1)}, bf16[4,2,4,24,768]{4,3,2,1,0:T(8,128)(2,1)}, u32[]{:S(2)}, u32[]{:S(2)}) collective-permute-start(bf16[4,2,4,24,768]{4,3,2,1,0:T(8,128)(2,1)} %get-tuple-element.254), channel_id=1, source_target_pairs={{0,8},{1,9},{2,10},{3,11},{4,12},{5,13},{6,14},{7,15},{8,0},{9,1},... | collective-permute-start | bytes 3538952 | tf_op jit(solution)/shard_map/ppermute | solution.py:441
  330.1 36.0 %collective-permute-start.56 = (bf16[4,2,4,24,768]{4,3,2,1,0:T(8,128)(2,1)}, bf16[4,2,4,24,768]{4,3,2,1,0:T(8,128)(2,1)}, u32[]{:S(2)}, u32[]{:S(2)}) collective-permute-start(bf16[4,2,4,24,768]{4,3,2,1,0:T(8,128)(2,1)} %get-tuple-element.255), channel_id=1, source_target_pairs={{0,16},{1,17},{2,18},{3,19},{4,20},{5,21},{6,22},{7,23},{8,24},{9,... | collective-permute-start | bytes 3538952 | tf_op jit(solution)/shard_map/ppermute | solution.py:441
  364.1 39.7 %collective-permute-start.61 = (bf16[6,512,768]{2,1,0:T(8,128)(2,1)}, bf16[6,512,768]{2,1,0:T(8,128)(2,1)}, u32[]{:S(2)}, u32[]{:S(2)}) collective-permute-start(bf16[6,512,768]{2,1,0:T(8,128)(2,1)} %get-tuple-element.274.dz_ref.df_ref.da_ref), channel_id=1, source_target_pairs={{0,1},{1,0},{2,3},{3,2},{4,5},{5,4},{6,7},{7,6},{8,9},{9,8},{10,11... | collective-permute-start | bytes 14155784 | tf_op jit(solution)/shard_map/ppermute | solution.py:441
  364.6 28.7 %collective-permute-start.58 = (bf16[3,512,768]{2,1,0:T(8,128)(2,1)S(1)}, bf16[3,512,768]{2,1,0:T(8,128)(2,1)}, u32[]{:S(2)}, u32[]{:S(2)}) collective-permute-start(bf16[3,512,768]{2,1,0:T(8,128)(2,1)S(1)} %copy-done.22), channel_id=1, source_target_pairs={{0,1},{1,0},{2,3},{3,2},{4,5},{5,4},{6,7},{7,6},{8,9},{9,8},{10,11... | collective-permute-start | bytes 7077896 | tf_op jit(solution)/shard_map/ppermute | solution.py:441
  364.7 37.6 %collective-permute-start.54 = (bf16[256,768]{1,0:T(8,128)(2,1)S(1)}, bf16[256,768]{1,0:T(8,128)(2,1)}, u32[]{:S(2)}, u32[]{:S(2)}) collective-permute-start(bf16[256,768]{1,0:T(8,128)(2,1)S(1)} %slice.318), channel_id=1, source_target_pairs={{0,2},{1,3},{2,0},{3,1},{4,6},{5,7},{6,4},{7,5},{8,10},{9,11},{10,... | collective-permute-start | bytes 1179656 | tf_op jit(solution)/shard_map/ppermute | solution.py:441
  372.1 31.6 %collective-permute-start.62 = (bf16[2,2,2,4,24,768]{5,4,3,2,0,1:T(8,128)(2,1)}, bf16[2,2,2,4,24,768]{5,4,3,2,0,1:T(8,128)(2,1)S(1)}, u32[]{:S(2)}, u32[]{:S(2)}) collective-permute-start(bf16[2,2,2,4,24,768]{5,4,3,2,0,1:T(8,128)(2,1)} %copy.75), channel_id=1, source_target_pairs={{2,4},{3,5},{4,2},{5,3},{10,12},{11,13},{12,10},{13,11},{18,20},{1... | collective-permute-start | bytes 3538952 | tf_op jit(solution)/shard_map/ppermute | solution.py:441
  392.9 30.1 %collective-permute-start.57 = (bf16[2,512,768]{2,1,0:T(8,128)(2,1)}, bf16[2,512,768]{2,1,0:T(8,128)(2,1)}, u32[]{:S(2)}, u32[]{:S(2)}) collective-permute-start(bf16[2,512,768]{2,1,0:T(8,128)(2,1)} %get-tuple-element.265), channel_id=1, source_target_pairs={{0,1},{1,0},{2,3},{3,2},{4,5},{5,4},{6,7},{7,6},{8,9},{9,8},{10,11... | collective-permute-start | bytes 4718600 | tf_op jit(solution)/shard_map/ppermute | solution.py:441
  416.7 27.8 %collective-permute-start.67 = (bf16[4,2,4,24,768]{4,3,2,1,0:T(8,128)(2,1)}, bf16[4,2,4,24,768]{4,3,2,1,0:T(8,128)(2,1)}, u32[]{:S(2)}, u32[]{:S(2)}) collective-permute-start(bf16[4,2,4,24,768]{4,3,2,1,0:T(8,128)(2,1)} %get-tuple-element.290), channel_id=1, source_target_pairs={{0,16},{1,17},{2,18},{3,19},{4,20},{5,21},{6,22},{7,23},{8,24},{9,... | collective-permute-start | bytes 3538952 | tf_op jit(solution)/shard_map/ppermute | solution.py:441
  417.3 27.5 %collective-permute-start.68 = (bf16[4,2,4,24,768]{4,3,2,1,0:T(8,128)(2,1)}, bf16[4,2,4,24,768]{4,3,2,1,0:T(8,128)(2,1)}, u32[]{:S(2)}, u32[]{:S(2)}) collective-permute-start(bf16[4,2,4,24,768]{4,3,2,1,0:T(8,128)(2,1)} %get-tuple-element.291), channel_id=1, source_target_pairs={{0,8},{1,9},{2,10},{3,11},{4,12},{5,13},{6,14},{7,15},{8,0},{9,1},... | collective-permute-start | bytes 3538952 | tf_op jit(solution)/shard_map/ppermute | solution.py:441
  433.1 26.9 %collective-permute-start.63 = (bf16[512,768]{1,0:T(8,128)(2,1)}, bf16[512,768]{1,0:T(8,128)(2,1)}, u32[]{:S(2)}, u32[]{:S(2)}) collective-permute-start(bf16[512,768]{1,0:T(8,128)(2,1)} %get-tuple-element.282), channel_id=1, source_target_pairs={{2,4},{3,5},{4,2},{5,3},{10,12},{11,13},{12,10},{13,11},{18,20},{1... | collective-permute-start | bytes 2359304 | tf_op jit(solution)/shard_map/ppermute | solution.py:441
  459.1 22.2 %collective-permute-start.74 = (bf16[2,2,6,24,768]{4,3,2,1,0:T(8,128)(2,1)}, bf16[2,2,6,24,768]{4,3,2,1,0:T(8,128)(2,1)}, u32[]{:S(2)}, u32[]{:S(2)}) collective-permute-start(bf16[2,2,6,24,768]{4,3,2,1,0:T(8,128)(2,1)} %select_bitcast_fusion), channel_id=1, source_target_pairs={{0,2},{1,3},{2,0},{3,1},{4,6},{5,7},{6,4},{7,5},{8,10},{9,11},{10,... | collective-permute-start | bytes 2654216 | tf_op jit(solution)/shard_map/ppermute | solution.py:441
  461.1 36.9 %collective-permute-start.72 = (bf16[2,2,2,4,24,768]{5,4,3,2,0,1:T(8,128)(2,1)}, bf16[2,2,2,4,24,768]{5,4,3,2,0,1:T(8,128)(2,1)}, u32[]{:S(2)}, u32[]{:S(2)}) collective-permute-start(bf16[2,2,2,4,24,768]{5,4,3,2,0,1:T(8,128)(2,1)} %copy.83), channel_id=1, source_target_pairs={{2,4},{3,5},{4,2},{5,3},{10,12},{11,13},{12,10},{13,11},{18,20},{1... | collective-permute-start | bytes 3538952 | tf_op jit(solution)/shard_map/ppermute | solution.py:441
  461.6 22.2 %collective-permute-start.73 = (f32[4,2,1152]{2,1,0:T(2,128)S(1)}, f32[4,2,1152]{2,1,0:T(2,128)S(1)}, u32[]{:S(2)}, u32[]{:S(2)}) collective-permute-start(f32[4,2,1152]{2,1,0:T(2,128)S(1)} %fusion.10), channel_id=1, source_target_pairs={{0,8},{1,9},{2,10},{3,11},{4,12},{5,13},{6,14},{7,15},{8,0},{9,1},... | collective-permute-start | bytes 110600 | tf_op jit(solution)/shard_map/ppermute | solution.py:441
  463.1 24.0 %collective-permute-start.78 = (bf16[4,2,2,24,768]{4,3,2,1,0:T(8,128)(2,1)}, bf16[4,2,2,24,768]{4,3,2,1,0:T(8,128)(2,1)S(1)}, u32[]{:S(2)}, u32[]{:S(2)}) collective-permute-start(bf16[4,2,2,24,768]{4,3,2,1,0:T(8,128)(2,1)} %get-tuple-element.304), channel_id=1, source_target_pairs={{0,8},{1,9},{2,10},{3,11},{4,12},{5,13},{6,14},{7,15},{8,0},{9,1},... | collective-permute-start | bytes 1769480 | tf_op jit(solution)/shard_map/ppermute | solution.py:441
  463.7 23.6 %collective-permute-start.79 = (bf16[4,2,2,24,768]{4,3,2,1,0:T(8,128)(2,1)}, bf16[4,2,2,24,768]{4,3,2,1,0:T(8,128)(2,1)}, u32[]{:S(2)}, u32[]{:S(2)}) collective-permute-start(bf16[4,2,2,24,768]{4,3,2,1,0:T(8,128)(2,1)} %get-tuple-element.305), channel_id=1, source_target_pairs={{0,16},{1,17},{2,18},{3,19},{4,20},{5,21},{6,22},{7,23},{8,24},{9,... | collective-permute-start | bytes 1769480 | tf_op jit(solution)/shard_map/ppermute | solution.py:441
  487.2 43.6 %collective-permute-start.71 = (bf16[256,768]{1,0:T(8,128)(2,1)}, bf16[256,768]{1,0:T(8,128)(2,1)}, u32[]{:S(2)}, u32[]{:S(2)}) collective-permute-start(bf16[256,768]{1,0:T(8,128)(2,1)} %slice.322), channel_id=1, source_target_pairs={{0,2},{1,3},{2,0},{3,1},{4,6},{5,7},{6,4},{7,5},{8,10},{9,11},{10,... | collective-permute-start | bytes 1179656 | tf_op jit(solution)/shard_map/ppermute | solution.py:441
  500.8 22.1 %collective-permute-start.80 = (bf16[2,2,4,24,768]{4,3,2,1,0:T(8,128)(2,1)S(1)}, bf16[2,2,4,24,768]{4,3,2,1,0:T(8,128)(2,1)S(1)}, u32[]{:S(2)}, u32[]{:S(2)}) collective-permute-start(bf16[2,2,4,24,768]{4,3,2,1,0:T(8,128)(2,1)S(1)} %select_bitcast_fusion.1), channel_id=1, source_target_pairs={{0,2},{1,3},{2,0},{3,1},{4,6},{5,7},{6,4},{7,5},{8,10},{9,11},{10,... | collective-permute-start | bytes 1769480 | tf_op jit(solution)/shard_map/ppermute | solution.py:441
  509.6 30.5 %collective-permute-start.94 = (f32[2,1152]{1,0:T(2,128)S(1)}, f32[2,1152]{1,0:T(2,128)S(1)}, u32[]{:S(2)}, u32[]{:S(2)}) collective-permute-start(f32[2,1152]{1,0:T(2,128)S(1)} %select_bitcast_fusion.3), channel_id=1, source_target_pairs={{0,2},{1,3},{2,0},{3,1},{4,6},{5,7},{6,4},{7,5},{8,10},{9,11},{10,... | collective-permute-start | bytes 27656 | tf_op jit(solution)/shard_map/ppermute | solution.py:441
  (123 other events, 1124.3 us)
